TPU v7x, 128 devices: a whole 4x4x4 slice. The times are simulated.
128 devices in a mesh: row: 16 (over x_lo, z, core), col: 8 (over x_hi, y).
Axes of the slice: x: 4 (x_hi: 2, x_lo: 2; x = x_hi * 2 + x_lo), y: 4, z: 4, core: 2. Of those that a mesh axis runs over, the one named last changes fastest.
Arguments:
- psi: bfloat16 [4096, 4096], P(('row', 'col')), may hold values from -6 to 6
- hpsi: bfloat16 [4096, 4096], P(('row', 'col')), may hold values from -0.09375 to 0.09375
- eigvec: bfloat16 [2, 16, 128, 4, 8, 128], P(None, 'row', None, None, 'col'), may hold values from -0.09375 to 0.09375
Outputs:
- correlation_tiles: float32 [2, 16, 128, 4, 8, 128], P(None, 'row', None, None, 'col')
- updated_tiles: float32 [2, 16, 128, 4, 8, 128], P(None, 'row', None, None, 'col')
- diag_part: float32 [16], replicated
- offdiag_part: float32 [16], replicated
- rotated: bfloat16 [4096, 4, 8, 128], P('row', None, 'col')
All inputs are finite; a program needn't handle non-finite values.
Results may differ from a plain program's by a relative error of at most 0.001.
Values may be sent and summed in bfloat16 or wider, within the bound.
No kernel may reach another device: no remote copies, remote signals or barrier semaphores. Data moves between devices by JAX's collectives and lax.ppermute only.
A program may use at most 128 MiB of HBM per device.

v0:
```python
import jax
import jax.numpy as jnp
from jax import lax
from jax.sharding import PartitionSpec as P

PB = 16


def in_one_piece(arrays, axis, split_dim, concat_dim, along):
    both = jnp.concatenate(arrays, axis=along)
    whole, at, gathered = (
        lax.all_to_all(both, axis, split_axis=split_dim, concat_axis=concat_dim, tiled=True),
        0,
        [],
    )
    for a in arrays:
        gathered.append(lax.slice_in_dim(whole, at, at + a.shape[along], axis=along))
        at += a.shape[along]
    return tuple(gathered)


def in_one_piece_2(arrays, axis, dim, along):
    both = jnp.concatenate(arrays, axis=along)
    whole, at, gathered = (lax.all_gather(both, axis, axis=dim, tiled=True), 0, [])
    for a in arrays:
        gathered.append(lax.slice_in_dim(whole, at, at + a.shape[along], axis=along))
        at += a.shape[along]
    return tuple(gathered)


def broadcast(array, axis, root):
    return lax.dynamic_index_in_dim(lax.all_gather(array, axis), root, 0, keepdims=False)


def copy_for_each(array, axis):
    length = lax.axis_size(axis)
    return lax.all_to_all(
        jnp.broadcast_to(array[None], (length, *array.shape)), axis, 0, 0, tiled=True
    )


def joined_along(tiles, dim):
    shape = list(tiles.shape[1:])
    shape[dim] *= tiles.shape[0]
    return jnp.moveaxis(tiles, 0, dim).reshape(shape)


def gather_directly(array, axis, dim):
    tiles = copy_for_each(array, axis)
    return joined_along(tiles, dim)


def over_copies(array, axis):
    everything = copy_for_each(array, axis)
    return jnp.sum(everything, axis=0)


def inner(left, right):
    return lax.dot_general(
        left, right, (((0,), (0,)), ((), ())), preferred_element_type=jnp.float32
    )


def on_device(psi, hpsi, eigvec):
    highest = lax.Precision.HIGHEST
    g_rows = psi.shape[0]
    bands = psi.shape[1]
    row_tiles = eigvec.shape[0]
    tile_size = eigvec.shape[2]
    col_tiles = eigvec.shape[3]
    row_count = lax.axis_size("row")
    col_count = lax.axis_size("col")
    row_id = lax.axis_index("row")
    col_id = lax.axis_index("col")
    gvecs = g_rows * row_count * col_count
    row_width = row_tiles * tile_size
    col_width = col_tiles * tile_size
    lifted = (
        psi.reshape(1, g_rows, row_tiles, row_count, tile_size),
        hpsi.reshape(1, g_rows, row_tiles, row_count, tile_size),
    )
    swapped = in_one_piece((lifted[0], lifted[1]), "row", 3, 0, 1)
    joined = in_one_piece_2((swapped[0], swapped[1]), "col", 1, 0)
    psi_rows = joined[0].reshape(gvecs, row_width)
    hpsi_rows = joined[1].reshape(gvecs, row_width)
    lowered = (
        psi.reshape(g_rows, col_tiles, col_count, tile_size),
        hpsi.reshape(g_rows, col_tiles, col_count, tile_size),
    )
    moved = in_one_piece((lowered[0], lowered[1]), "col", 2, 0, 1)
    stacked = in_one_piece_2((moved[0], moved[1]), "row", 0, 1)
    psi_cols = stacked[0].reshape(gvecs, col_width)
    hpsi_cols = stacked[1].reshape(gvecs, col_width)
    reduced = 0.5 * (inner(psi_rows, hpsi_cols) + inner(hpsi_rows, psi_cols))
    correlation = inner(psi_rows, psi_cols) / float(gvecs)
    blocks = reduced.reshape(row_tiles, tile_size, col_tiles, tile_size)
    leading = blocks[:, :, 0, :PB]
    shared = broadcast(leading, "col", 0)
    panel = gather_directly(shared.reshape(row_tiles, 1, tile_size, PB), "row", 1).reshape(
        bands, PB
    )

    def product(vector):
        local_vec = lax.dynamic_index_in_dim(
            vector.reshape(col_tiles, col_count, tile_size), col_id, 1, keepdims=False
        )
        partial_sum = jnp.einsum("atbs,bs->at", blocks, local_vec, precision=highest)
        summed = over_copies(partial_sum, "col")
        result = gather_directly(summed.reshape(row_tiles, 1, tile_size), "row", 1).reshape(bands)
        return result

    positions = jnp.arange(bands)
    slots = jnp.arange(PB)

    def reflect(step, carry):
        vecs, images, diagonal, offdiag = carry
        column = lax.dynamic_index_in_dim(panel, step, 1, keepdims=False)
        head_v = lax.dynamic_index_in_dim(vecs, step, 0, keepdims=False)
        head_w = lax.dynamic_index_in_dim(images, step, 0, keepdims=False)
        column = (
            column
            - jnp.dot(vecs, head_w, precision=highest)
            - jnp.dot(images, head_v, precision=highest)
        )
        pivot = lax.dynamic_index_in_dim(column, step + 1, 0, keepdims=False)
        below = positions > step + 1
        tail = jnp.sum(jnp.where(below, column * column, 0.0))
        length = jnp.sqrt(pivot * pivot + tail)
        beta = jnp.where(pivot >= 0.0, -length, length)
        tau = (beta - pivot) / beta
        vector = jnp.where(
            positions == step + 1, 1.0, jnp.where(below, column / (pivot - beta), 0.0)
        )
        image = product(vector)
        image = image - jnp.dot(vecs, jnp.dot(vector, images, precision=highest), precision=highest)
        image = image - jnp.dot(images, jnp.dot(vector, vecs, precision=highest), precision=highest)
        image = tau * image
        image = image - 0.5 * tau * jnp.dot(image, vector, precision=highest) * vector
        pick = slots == step
        vecs = jnp.where(pick[None, :], vector[:, None], vecs)
        images = jnp.where(pick[None, :], image[:, None], images)
        diagonal = jnp.where(
            pick, lax.dynamic_index_in_dim(column, step, 0, keepdims=False), diagonal
        )
        offdiag = jnp.where(pick, beta, offdiag)
        return (vecs, images, diagonal, offdiag)

    start_state = (
        jnp.zeros((bands, PB), jnp.float32),
        jnp.zeros((bands, PB), jnp.float32),
        jnp.zeros((PB,), jnp.float32),
        jnp.zeros((PB,), jnp.float32),
    )
    vecs, images, diagonal, offdiag = lax.fori_loop(0, PB, reflect, start_state)

    def rows_of(matrix):
        return lax.dynamic_index_in_dim(
            matrix.reshape(row_tiles, row_count, tile_size, PB), row_id, 1, keepdims=False
        ).reshape(row_width, PB)

    def cols_of(matrix):
        return lax.dynamic_index_in_dim(
            matrix.reshape(col_tiles, col_count, tile_size, PB), col_id, 1, keepdims=False
        ).reshape(col_width, PB)

    updated = (
        reduced
        - jnp.dot(rows_of(vecs), cols_of(images).T, precision=highest)
        - jnp.dot(rows_of(images), cols_of(vecs).T, precision=highest)
    )
    flat = eigvec.reshape(row_width, col_width)
    rotated = lax.psum_scatter(
        jnp.dot(psi_rows, flat, preferred_element_type=jnp.float32),
        "row",
        scatter_dimension=0,
        tiled=True,
    )
    tile_shape = (row_tiles, 1, tile_size, col_tiles, 1, tile_size)
    return (
        correlation.reshape(tile_shape),
        updated.reshape(tile_shape),
        diagonal,
        offdiag,
        rotated.astype(jnp.bfloat16).reshape(rotated.shape[0], col_tiles, 1, tile_size),
    )


def solution(mesh):
    return jax.shard_map(
        on_device,
        mesh=mesh,
        in_specs=(
            P(("row", "col"), None),
            P(("row", "col"), None),
            P(None, "row", None, None, "col", None),
        ),
        out_specs=(
            P(None, "row", None, None, "col", None),
            P(None, "row", None, None, "col", None),
            P(),
            P(),
            P("row", None, "col", None),
        ),
        check_vma=False,
    )
```

profile of v0, /device:TPU:1, one launch (start us, length us, event | category | flops | bytes accessed | tf_op | source)
XLA Modules:
  0.0 919.8 jit_solution(17715437989482282004)
XLA Ops:
  9.5 17.2 %all_to_all.71 = bf16[1,64,2,16,128]{4,1,2,0,3:T(8,128)(2,1)S(1)} all-to-all(bf16[1,64,2,16,128]{4,1,2,0,3:T(8,128)(2,1)S(1)} %copy.78), channel_id=1, replica_groups=mesh['row'=16,'col'=8] {'row'}, dimensions={3} | all-to-all | bytes 1048576 | tf_op jit(solution)/shard_map/all_to_all | solution.py:12
  28.1 15.4 %all_to_all.72 = bf16[32,8,8,128]{3,1,0,2:T(8,128)(2,1)} all-to-all(bf16[32,8,8,128]{3,1,0,2:T(8,128)(2,1)S(1)} %copy.81), channel_id=1, replica_groups=mesh['row'=16,'col'=8] {'col'}, dimensions={2} | all-to-all | bytes 1048576 | tf_op jit(solution)/shard_map/all_to_all | solution.py:12
  43.7 54.6 %all-gather.4.cloned.1.call-done = bf16[32,256,2,1,128]{4,0,3,2,1:T(8,128)(2,1)} async-done(((bf16[32,32,2,1,128]{4,0,3,2,1:T(8,128)(2,1)}), bf16[32,256,2,1,128]{4,0,3,2,1:T(8,128)(2,1)}) %all-gather.4.cloned.1.call-update) | async-done | bytes 4194320 | tf_op jit(solution)/shard_map/all_gather | solution.py:24
  98.3 4.9 fusion.27
  109.4 4.9 copy.80
  116.9 4.5 fusion.22
  121.5 29.7 %all-gather.6.cloned.1.call-done = bf16[4096,8,1,128]{3,1,2,0:T(8,128)(2,1)} async-done(((bf16[256,8,1,128]{3,1,2,0:T(8,128)(2,1)}), bf16[4096,8,1,128]{3,1,2,0:T(8,128)(2,1)}) %all-gather.6.cloned.1.call-update) | async-done | bytes 8388624 | tf_op jit(solution)/shard_map/all_gather | solution.py:24
  151.1 11.5 %fusion.26 = (bf16[4096,4,1,128]{3,1,2,0:T(4,128)(2,1)}, bf16[4096,4,1,128]{3,1,2,0:T(4,128)(2,1)}) fusion(bf16[4096,8,1,128]{3,1,2,0:T(8,128)(2,1)} %all-gather.6.cloned.1.call-done), kind=kLoop, calls=%fused_computation.52 | loop fusion | bytes 16777216 | tf_op jit(solution)/shard_map/slice | solution.py:26
  162.6 7.6 copy.98
  173.8 7.6 copy.97
  181.4 4.2 fusion.21
  186.0 28.7 %all-gather = f32[16,128,1,16]{1,3,2,0:T(8,128)S(1)} all-gather(f32[2,128,1,16]{1,3,2,0:T(8,128)S(1)} %copy.99), channel_id=2, replica_groups=mesh['row'=16,'col'=8] {'col'}, dimensions={0}, use_global_device_ids=true | all-gather | bytes 147456 | tf_op jit(solution)/shard_map/all_gather | solution.py:32
  215.5 10.7 %all-to-all-start.4 = ((f32[16,2,1,128,16]{3,1,4,2,0:T(2,128)}), f32[16,2,1,128,16]{3,1,4,2,0:T(2,128)S(1)}, u32[]{:S(2)}, u32[]{:S(2)}) async-start(f32[16,2,1,128,16]{3,1,4,2,0:T(2,128)} %broadcast_in_dim.157), calls=%async_computation.4 | async-start | bytes 524288 | tf_op jit(solution)/shard_map/all_to_all | solution.py:37
  226.2 4.3 convolution_multiply_fusion
  233.6 673.6 %while.23 = (s32[]{:T(128)}, f32[4096,16]{1,0:T(8,128)}, f32[4096,16]{1,0:T(8,128)}, f32[16]{0:T(128)S(1)}, f32[16]{0:T(128)S(1)}, /*index=5*/f32[4096,16]{0,1:T...) while((s32[]{:T(128)}, f32[4096,16]{1,0:T(8,128)}, ...), condition=%wide.region_3.4_spmd.clone.clone, body=%wide.region_0.3_spmd.clone.clone.sunk | while | flops 6690686 | bytes 10534969 | solution.py:154
  242.8 5.9 all-to-all-start
  257.7 4.5 all-to-all-start.1
  262.8 5.2 all-to-all-done.1
  284.5 7.5 all-to-all-start
  305.5 5.2 all-to-all-done.1
  327.3 6.9 all-to-all-start
  347.8 5.2 all-to-all-done.1
  369.5 6.9 all-to-all-start
  390.0 5.2 all-to-all-done.1
  411.8 6.9 all-to-all-start
  432.2 5.2 all-to-all-done.1
  454.0 6.9 all-to-all-start
  474.5 5.2 all-to-all-done.1
  496.2 6.9 all-to-all-start
  516.7 5.2 all-to-all-done.1
  538.5 6.9 all-to-all-start
  558.9 5.2 all-to-all-done.1
  580.7 6.9 all-to-all-start
  601.2 5.2 all-to-all-done.1
  622.9 6.9 all-to-all-start
  643.4 5.2 all-to-all-done.1
  665.2 6.9 all-to-all-start
  685.6 5.2 all-to-all-done.1
  707.4 6.9 all-to-all-start
  727.9 5.2 all-to-all-done.1
  749.6 6.9 all-to-all-start
  770.1 5.2 all-to-all-done.1
  791.9 6.9 all-to-all-start
  812.3 5.2 all-to-all-done.1
  834.1 6.9 all-to-all-start
  854.6 5.2 all-to-all-done.1
  876.4 6.9 all-to-all-start
  896.8 5.2 all-to-all-done.1
  (510 shorter events, 432.8 us)
Async XLA Ops:
  7.2 91.1 %all-gather.4.cloned.1.call-start = ((), (), s32[]{:S(2)}) async-start(), calls=%async_computation.6 | async-start | bytes 4718592 | tf_op jit(solution)/shard_map/all_gather | solution.py:24
  28.0 123.2 %all-gather.6.cloned.1.call-start = ((), (), s32[]{:S(2)}) async-start(), calls=%async_computation.7 | async-start | bytes 8912896 | tf_op jit(solution)/shard_map/all_gather | solution.py:24
  43.6 867.8 %reduce-scatter.2.cloned.1.call-start = ((), (), s32[]{:S(2)}) async-start(), calls=%async_computation.8 | async-start | bytes 8912896 | tf_op jit(solution)/shard_map/reduce_scatter | solution.py:172
  215.5 17.9 %all-to-all-start.4 = ((f32[16,2,1,128,16]{3,1,4,2,0:T(2,128)}), f32[16,2,1,128,16]{3,1,4,2,0:T(2,128)S(1)}, u32[]{:S(2)}, u32[]{:S(2)}) async-start(f32[16,2,1,128,16]{3,1,4,2,0:T(2,128)} %broadcast_in_dim.157), calls=%async_computation.4 | async-start | bytes 524288 | tf_op jit(solution)/shard_map/all_to_all | solution.py:37
  242.8 14.2 %all-to-all-start = ((f32[8,2,128]{2,1,0:T(2,128)}), f32[8,2,128]{2,1,0:T(2,128)S(1)}, u32[]{:S(2)}, u32[]{:S(2)}) async-start(f32[8,2,128]{2,1,0:T(2,128)} %broadcast_in_dim.225), calls=%async_computation | async-start | bytes 16384 | tf_op jit(solution)/shard_map/while/body/eval_jaxpr/all_to_all | solution.py:37
  248.7 4.0 copy-start.1
  257.7 10.3 %all-to-all-start.1 = ((f32[16,2,1,128]{3,1,2,0:T(2,128)}), f32[16,2,1,128]{3,1,2,0:T(2,128)S(1)}, u32[]{:S(2)}, u32[]{:S(2)}) async-start(f32[16,2,1,128]{3,1,2,0:T(2,128)} %broadcast_in_dim.226), calls=%async_computation.1 | async-start | bytes 32768 | tf_op jit(solution)/shard_map/while/body/eval_jaxpr/all_to_all | solution.py:37
  284.5 15.8 %all-to-all-start = ((f32[8,2,128]{2,1,0:T(2,128)}), f32[8,2,128]{2,1,0:T(2,128)S(1)}, u32[]{:S(2)}, u32[]{:S(2)}) async-start(f32[8,2,128]{2,1,0:T(2,128)} %broadcast_in_dim.225), calls=%async_computation | async-start | bytes 16384 | tf_op jit(solution)/shard_map/while/body/eval_jaxpr/all_to_all | solution.py:37
  292.0 4.0 copy-start.1
  301.0 9.8 %all-to-all-start.1 = ((f32[16,2,1,128]{3,1,2,0:T(2,128)}), f32[16,2,1,128]{3,1,2,0:T(2,128)S(1)}, u32[]{:S(2)}, u32[]{:S(2)}) async-start(f32[16,2,1,128]{3,1,2,0:T(2,128)} %broadcast_in_dim.226), calls=%async_computation.1 | async-start | bytes 32768 | tf_op jit(solution)/shard_map/while/body/eval_jaxpr/all_to_all | solution.py:37
  327.3 15.2 %all-to-all-start = ((f32[8,2,128]{2,1,0:T(2,128)}), f32[8,2,128]{2,1,0:T(2,128)S(1)}, u32[]{:S(2)}, u32[]{:S(2)}) async-start(f32[8,2,128]{2,1,0:T(2,128)} %broadcast_in_dim.225), calls=%async_computation | async-start | bytes 16384 | tf_op jit(solution)/shard_map/while/body/eval_jaxpr/all_to_all | solution.py:37
  334.2 4.0 copy-start.1
  343.2 9.8 %all-to-all-start.1 = ((f32[16,2,1,128]{3,1,2,0:T(2,128)}), f32[16,2,1,128]{3,1,2,0:T(2,128)S(1)}, u32[]{:S(2)}, u32[]{:S(2)}) async-start(f32[16,2,1,128]{3,1,2,0:T(2,128)} %broadcast_in_dim.226), calls=%async_computation.1 | async-start | bytes 32768 | tf_op jit(solution)/shard_map/while/body/eval_jaxpr/all_to_all | solution.py:37
  369.5 15.2 %all-to-all-start = ((f32[8,2,128]{2,1,0:T(2,128)}), f32[8,2,128]{2,1,0:T(2,128)S(1)}, u32[]{:S(2)}, u32[]{:S(2)}) async-start(f32[8,2,128]{2,1,0:T(2,128)} %broadcast_in_dim.225), calls=%async_computation | async-start | bytes 16384 | tf_op jit(solution)/shard_map/while/body/eval_jaxpr/all_to_all | solution.py:37
  385.4 9.8 %all-to-all-start.1 = ((f32[16,2,1,128]{3,1,2,0:T(2,128)}), f32[16,2,1,128]{3,1,2,0:T(2,128)S(1)}, u32[]{:S(2)}, u32[]{:S(2)}) async-start(f32[16,2,1,128]{3,1,2,0:T(2,128)} %broadcast_in_dim.226), calls=%async_computation.1 | async-start | bytes 32768 | tf_op jit(solution)/shard_map/while/body/eval_jaxpr/all_to_all | solution.py:37
  411.8 15.2 %all-to-all-start = ((f32[8,2,128]{2,1,0:T(2,128)}), f32[8,2,128]{2,1,0:T(2,128)S(1)}, u32[]{:S(2)}, u32[]{:S(2)}) async-start(f32[8,2,128]{2,1,0:T(2,128)} %broadcast_in_dim.225), calls=%async_computation | async-start | bytes 16384 | tf_op jit(solution)/shard_map/while/body/eval_jaxpr/all_to_all | solution.py:37
  427.7 9.8 %all-to-all-start.1 = ((f32[16,2,1,128]{3,1,2,0:T(2,128)}), f32[16,2,1,128]{3,1,2,0:T(2,128)S(1)}, u32[]{:S(2)}, u32[]{:S(2)}) async-start(f32[16,2,1,128]{3,1,2,0:T(2,128)} %broadcast_in_dim.226), calls=%async_computation.1 | async-start | bytes 32768 | tf_op jit(solution)/shard_map/while/body/eval_jaxpr/all_to_all | solution.py:37
  454.0 15.2 %all-to-all-start = ((f32[8,2,128]{2,1,0:T(2,128)}), f32[8,2,128]{2,1,0:T(2,128)S(1)}, u32[]{:S(2)}, u32[]{:S(2)}) async-start(f32[8,2,128]{2,1,0:T(2,128)} %broadcast_in_dim.225), calls=%async_computation | async-start | bytes 16384 | tf_op jit(solution)/shard_map/while/body/eval_jaxpr/all_to_all | solution.py:37
  460.9 4.0 copy-start.1
  469.9 9.8 %all-to-all-start.1 = ((f32[16,2,1,128]{3,1,2,0:T(2,128)}), f32[16,2,1,128]{3,1,2,0:T(2,128)S(1)}, u32[]{:S(2)}, u32[]{:S(2)}) async-start(f32[16,2,1,128]{3,1,2,0:T(2,128)} %broadcast_in_dim.226), calls=%async_computation.1 | async-start | bytes 32768 | tf_op jit(solution)/shard_map/while/body/eval_jaxpr/all_to_all | solution.py:37
  496.2 15.2 %all-to-all-start = ((f32[8,2,128]{2,1,0:T(2,128)}), f32[8,2,128]{2,1,0:T(2,128)S(1)}, u32[]{:S(2)}, u32[]{:S(2)}) async-start(f32[8,2,128]{2,1,0:T(2,128)} %broadcast_in_dim.225), calls=%async_computation | async-start | bytes 16384 | tf_op jit(solution)/shard_map/while/body/eval_jaxpr/all_to_all | solution.py:37
  503.2 4.0 copy-start.1
  512.1 9.8 %all-to-all-start.1 = ((f32[16,2,1,128]{3,1,2,0:T(2,128)}), f32[16,2,1,128]{3,1,2,0:T(2,128)S(1)}, u32[]{:S(2)}, u32[]{:S(2)}) async-start(f32[16,2,1,128]{3,1,2,0:T(2,128)} %broadcast_in_dim.226), calls=%async_computation.1 | async-start | bytes 32768 | tf_op jit(solution)/shard_map/while/body/eval_jaxpr/all_to_all | solution.py:37
  538.5 15.2 %all-to-all-start = ((f32[8,2,128]{2,1,0:T(2,128)}), f32[8,2,128]{2,1,0:T(2,128)S(1)}, u32[]{:S(2)}, u32[]{:S(2)}) async-start(f32[8,2,128]{2,1,0:T(2,128)} %broadcast_in_dim.225), calls=%async_computation | async-start | bytes 16384 | tf_op jit(solution)/shard_map/while/body/eval_jaxpr/all_to_all | solution.py:37
  545.4 4.0 copy-start.1
  554.4 9.8 %all-to-all-start.1 = ((f32[16,2,1,128]{3,1,2,0:T(2,128)}), f32[16,2,1,128]{3,1,2,0:T(2,128)S(1)}, u32[]{:S(2)}, u32[]{:S(2)}) async-start(f32[16,2,1,128]{3,1,2,0:T(2,128)} %broadcast_in_dim.226), calls=%async_computation.1 | async-start | bytes 32768 | tf_op jit(solution)/shard_map/while/body/eval_jaxpr/all_to_all | solution.py:37
  580.7 15.2 %all-to-all-start = ((f32[8,2,128]{2,1,0:T(2,128)}), f32[8,2,128]{2,1,0:T(2,128)S(1)}, u32[]{:S(2)}, u32[]{:S(2)}) async-start(f32[8,2,128]{2,1,0:T(2,128)} %broadcast_in_dim.225), calls=%async_computation | async-start | bytes 16384 | tf_op jit(solution)/shard_map/while/body/eval_jaxpr/all_to_all | solution.py:37
  587.6 4.0 copy-start.1
  596.6 9.8 %all-to-all-start.1 = ((f32[16,2,1,128]{3,1,2,0:T(2,128)}), f32[16,2,1,128]{3,1,2,0:T(2,128)S(1)}, u32[]{:S(2)}, u32[]{:S(2)}) async-start(f32[16,2,1,128]{3,1,2,0:T(2,128)} %broadcast_in_dim.226), calls=%async_computation.1 | async-start | bytes 32768 | tf_op jit(solution)/shard_map/while/body/eval_jaxpr/all_to_all | solution.py:37
  622.9 15.2 %all-to-all-start = ((f32[8,2,128]{2,1,0:T(2,128)}), f32[8,2,128]{2,1,0:T(2,128)S(1)}, u32[]{:S(2)}, u32[]{:S(2)}) async-start(f32[8,2,128]{2,1,0:T(2,128)} %broadcast_in_dim.225), calls=%async_computation | async-start | bytes 16384 | tf_op jit(solution)/shard_map/while/body/eval_jaxpr/all_to_all | solution.py:37
  629.9 4.0 copy-start.1
  638.8 9.8 %all-to-all-start.1 = ((f32[16,2,1,128]{3,1,2,0:T(2,128)}), f32[16,2,1,128]{3,1,2,0:T(2,128)S(1)}, u32[]{:S(2)}, u32[]{:S(2)}) async-start(f32[16,2,1,128]{3,1,2,0:T(2,128)} %broadcast_in_dim.226), calls=%async_computation.1 | async-start | bytes 32768 | tf_op jit(solution)/shard_map/while/body/eval_jaxpr/all_to_all | solution.py:37
  665.2 15.2 %all-to-all-start = ((f32[8,2,128]{2,1,0:T(2,128)}), f32[8,2,128]{2,1,0:T(2,128)S(1)}, u32[]{:S(2)}, u32[]{:S(2)}) async-start(f32[8,2,128]{2,1,0:T(2,128)} %broadcast_in_dim.225), calls=%async_computation | async-start | bytes 16384 | tf_op jit(solution)/shard_map/while/body/eval_jaxpr/all_to_all | solution.py:37
  672.1 4.0 copy-start.1
  681.1 9.8 %all-to-all-start.1 = ((f32[16,2,1,128]{3,1,2,0:T(2,128)}), f32[16,2,1,128]{3,1,2,0:T(2,128)S(1)}, u32[]{:S(2)}, u32[]{:S(2)}) async-start(f32[16,2,1,128]{3,1,2,0:T(2,128)} %broadcast_in_dim.226), calls=%async_computation.1 | async-start | bytes 32768 | tf_op jit(solution)/shard_map/while/body/eval_jaxpr/all_to_all | solution.py:37
  707.4 15.2 %all-to-all-start = ((f32[8,2,128]{2,1,0:T(2,128)}), f32[8,2,128]{2,1,0:T(2,128)S(1)}, u32[]{:S(2)}, u32[]{:S(2)}) async-start(f32[8,2,128]{2,1,0:T(2,128)} %broadcast_in_dim.225), calls=%async_computation | async-start | bytes 16384 | tf_op jit(solution)/shard_map/while/body/eval_jaxpr/all_to_all | solution.py:37
  723.3 9.8 %all-to-all-start.1 = ((f32[16,2,1,128]{3,1,2,0:T(2,128)}), f32[16,2,1,128]{3,1,2,0:T(2,128)S(1)}, u32[]{:S(2)}, u32[]{:S(2)}) async-start(f32[16,2,1,128]{3,1,2,0:T(2,128)} %broadcast_in_dim.226), calls=%async_computation.1 | async-start | bytes 32768 | tf_op jit(solution)/shard_map/while/body/eval_jaxpr/all_to_all | solution.py:37
  749.6 15.2 %all-to-all-start = ((f32[8,2,128]{2,1,0:T(2,128)}), f32[8,2,128]{2,1,0:T(2,128)S(1)}, u32[]{:S(2)}, u32[]{:S(2)}) async-start(f32[8,2,128]{2,1,0:T(2,128)} %broadcast_in_dim.225), calls=%async_computation | async-start | bytes 16384 | tf_op jit(solution)/shard_map/while/body/eval_jaxpr/all_to_all | solution.py:37
  765.5 9.8 %all-to-all-start.1 = ((f32[16,2,1,128]{3,1,2,0:T(2,128)}), f32[16,2,1,128]{3,1,2,0:T(2,128)S(1)}, u32[]{:S(2)}, u32[]{:S(2)}) async-start(f32[16,2,1,128]{3,1,2,0:T(2,128)} %broadcast_in_dim.226), calls=%async_computation.1 | async-start | bytes 32768 | tf_op jit(solution)/shard_map/while/body/eval_jaxpr/all_to_all | solution.py:37
  791.9 15.2 %all-to-all-start = ((f32[8,2,128]{2,1,0:T(2,128)}), f32[8,2,128]{2,1,0:T(2,128)S(1)}, u32[]{:S(2)}, u32[]{:S(2)}) async-start(f32[8,2,128]{2,1,0:T(2,128)} %broadcast_in_dim.225), calls=%async_computation | async-start | bytes 16384 | tf_op jit(solution)/shard_map/while/body/eval_jaxpr/all_to_all | solution.py:37
  798.8 4.0 copy-start.1
  807.8 9.8 %all-to-all-start.1 = ((f32[16,2,1,128]{3,1,2,0:T(2,128)}), f32[16,2,1,128]{3,1,2,0:T(2,128)S(1)}, u32[]{:S(2)}, u32[]{:S(2)}) async-start(f32[16,2,1,128]{3,1,2,0:T(2,128)} %broadcast_in_dim.226), calls=%async_computation.1 | async-start | bytes 32768 | tf_op jit(solution)/shard_map/while/body/eval_jaxpr/all_to_all | solution.py:37
  834.1 15.2 %all-to-all-start = ((f32[8,2,128]{2,1,0:T(2,128)}), f32[8,2,128]{2,1,0:T(2,128)S(1)}, u32[]{:S(2)}, u32[]{:S(2)}) async-start(f32[8,2,128]{2,1,0:T(2,128)} %broadcast_in_dim.225), calls=%async_computation | async-start | bytes 16384 | tf_op jit(solution)/shard_map/while/body/eval_jaxpr/all_to_all | solution.py:37
  841.1 4.0 copy-start.1
  850.0 9.8 %all-to-all-start.1 = ((f32[16,2,1,128]{3,1,2,0:T(2,128)}), f32[16,2,1,128]{3,1,2,0:T(2,128)S(1)}, u32[]{:S(2)}, u32[]{:S(2)}) async-start(f32[16,2,1,128]{3,1,2,0:T(2,128)} %broadcast_in_dim.226), calls=%async_computation.1 | async-start | bytes 32768 | tf_op jit(solution)/shard_map/while/body/eval_jaxpr/all_to_all | solution.py:37
  876.4 15.2 %all-to-all-start = ((f32[8,2,128]{2,1,0:T(2,128)}), f32[8,2,128]{2,1,0:T(2,128)S(1)}, u32[]{:S(2)}, u32[]{:S(2)}) async-start(f32[8,2,128]{2,1,0:T(2,128)} %broadcast_in_dim.225), calls=%async_computation | async-start | bytes 16384 | tf_op jit(solution)/shard_map/while/body/eval_jaxpr/all_to_all | solution.py:37
  883.3 4.0 copy-start.1
  892.2 9.8 %all-to-all-start.1 = ((f32[16,2,1,128]{3,1,2,0:T(2,128)}), f32[16,2,1,128]{3,1,2,0:T(2,128)S(1)}, u32[]{:S(2)}, u32[]{:S(2)}) async-start(f32[16,2,1,128]{3,1,2,0:T(2,128)} %broadcast_in_dim.226), calls=%async_computation.1 | async-start | bytes 32768 | tf_op jit(solution)/shard_map/while/body/eval_jaxpr/all_to_all | solution.py:37
  (23 other events, 54.1 us)
Sparse Core Ops, SparseCore 0:
  28.1 70.1 all-gather.3
  100.0 51.1 all-gather.5
  153.5 73.0 reduce-scatter.1
where the time goes:
time: 924 us; the launch traced here: 920 us
  matrix products  205 us (22%)
  starting transfers between devices  185 us (20%)
  waiting for transfers between devices  169 us (18%)
  other arithmetic  131 us (14%)
  local copies, waits for them, and re-layouts  85.7 us (9%)
  loops' own time  68.4 us (7%)
  blocking collectives  61.3 us (7%)
  between operations  14 us (2%)
    all_to_all x33, starting transfers between devices, copy_for_each(): lax.all_to_all(jnp.broadcast_to(array[None], (length, *array.shape)), axi...  185 us
    all_to_all x33, waiting for transfers between devices, copy_for_each(): lax.all_to_all(jnp.broadcast_to(array[None], (length, *array.shape)), axi...  84.9 us
    all_gather x2, waiting for transfers between devices, in_one_piece_2(): lax.all_gather(both, axis, axis=dim, tiled=True)  84.3 us
    another operation x1, loops' own time, on_device(): vecs, images, diagonal, offdiag = lax.fori_loop(0, PB, reflect, start_state)  68.4 us
    select_n x16, other arithmetic, reflect(): images = jnp.where(pick[None, :], image[:, None], images)  61 us
    dot_general x16, matrix products, reflect(): jnp.dot(vector, images, precision=highest)  45.5 us
    while x16, other arithmetic  37.7 us
    all_to_all x2, blocking collectives, in_one_piece(): lax.all_to_all(both, axis, split_axis=split_dim, concat_axis=concat_dim,...  32.6 us
  transfers between devices with their start and end apart: 36, of which 19 were waited for; matrix products, arithmetic and copies ran while one was open for 45% of the time, Pallas kernels for 0%

commit v1 on v0

v1 whole, which is shorter than its diff:
```python
import jax
import jax.numpy as jnp
from jax import lax
from jax.experimental import pallas as pl
from jax.experimental.pallas import tpu as pltpu
from jax.sharding import PartitionSpec as P

PB = 16
LANES = 128
F32 = jnp.float32


def total(x):
    return jnp.sum(jnp.sum(x, axis=-2, keepdims=True), axis=-1, keepdims=True)


def finish_image(recv, vecs, images, vector, tau, tiles):
    half = tiles // 2
    sums = jnp.sum(recv, axis=1)
    image = jnp.concatenate([sums[:, :LANES], sums[:, LANES:]], axis=0).reshape(1, 2 * half, LANES)
    along_w = total(images * vector)
    along_v = total(vecs * vector)
    image = image - jnp.sum(vecs * along_w + images * along_v, axis=0, keepdims=True)
    image = tau * image
    return image - 0.5 * tau * total(image * vector) * vector


def place(into, what, slot):
    slots = lax.broadcasted_iota(jnp.int32, (PB, 1, 1), 0)
    return jnp.where(slots == slot, what, into)


def step_body(
    step_ref, recv_ref, panel_ref, vecs_ref, images_ref, marks_ref, matrix_ref,
    vecs_out, images_out, marks_out, send_out, matrix_vmem, sem,
):
    step = step_ref[0]
    tiles = panel_ref.shape[1]
    copy = pltpu.make_async_copy(matrix_ref, matrix_vmem, sem)
    copy.start()
    lane = lax.broadcasted_iota(jnp.int32, (1, 1, LANES), 2)
    marks = marks_ref[...]
    vecs = vecs_ref[...]
    images = images_ref[...]
    before = jnp.maximum(step - 1, 0)
    vector = vecs_ref[pl.ds(before, 1)]
    tau = marks[2:3, 0:1].reshape(1, 1, 1)
    image = finish_image(recv_ref[...], vecs, images, vector, tau, tiles)
    images = place(images, image, step - 1)
    images_out[...] = images
    head_w = jnp.sum(jnp.where(lane == step, images[:, 0:1, :], 0.0), axis=-1, keepdims=True)
    head_v = jnp.sum(jnp.where(lane == step, vecs[:, 0:1, :], 0.0), axis=-1, keepdims=True)
    column = panel_ref[pl.ds(step, 1)] - jnp.sum(
        vecs * head_w + images * head_v, axis=0, keepdims=True
    )
    shape = (1, tiles, LANES)
    positions = lax.broadcasted_iota(jnp.int32, shape, 1) * LANES + lax.broadcasted_iota(
        jnp.int32, shape, 2
    )
    below = positions > step + 1
    pivot = total(jnp.where(positions == step + 1, column, 0.0))
    tail = total(jnp.where(below, column * column, 0.0))
    corner = total(jnp.where(positions == step, column, 0.0))
    length = jnp.sqrt(pivot * pivot + tail)
    beta = jnp.where(pivot >= 0.0, -length, length)
    tau = (beta - pivot) / beta
    vector = jnp.where(positions == step + 1, 1.0, jnp.where(below, column / (pivot - beta), 0.0))
    vecs_out[...] = place(vecs, vector, step)
    row = lax.broadcasted_iota(jnp.int32, marks.shape, 0)
    spot = lax.broadcasted_iota(jnp.int32, marks.shape, 1) == step
    flat = marks.shape
    marks = jnp.where((row == 0) & spot, jnp.broadcast_to(corner[0], flat), marks)
    marks = jnp.where((row == 1) & spot, jnp.broadcast_to(beta[0], flat), marks)
    marks_out[...] = jnp.where(row == 2, jnp.broadcast_to(tau[0], flat), marks)
    copy.wait()
    col_count, height, width = matrix_vmem.shape
    col_tiles = width // LANES
    sums = jnp.zeros((height, LANES), F32)
    for c in range(col_count):
        for a in range(col_tiles):
            u = a * col_count + c
            sums = sums + matrix_vmem[c, :, a * LANES : (a + 1) * LANES] * vector[0, u : u + 1, :]
    pieces = [
        jnp.sum(sums[k * LANES : (k + 1) * LANES].T, axis=0, keepdims=True)
        for k in range(height // LANES)
    ]
    send_out[...] = jnp.broadcast_to(jnp.concatenate(pieces, axis=1), send_out.shape)


def last_body(
    where_ref, recv_ref, vecs_ref, images_ref, marks_ref, tile_ref, updated_out, vecs_vmem, images_vmem
):
    tiles = vecs_ref.shape[1]
    vecs = vecs_ref[...]
    vector = vecs_ref[PB - 1 : PB]
    tau = marks_ref[2:3, 0:1].reshape(1, 1, 1)
    image = finish_image(recv_ref[...], vecs, images_ref[...], vector, tau, tiles)
    images = place(images_ref[...], image, PB - 1)
    images_vmem[...] = images
    vecs_vmem[...] = vecs
    row_id = where_ref[0]
    col_id = where_ref[1]
    height, width = tile_ref.shape
    row_tiles = height // LANES
    col_tiles = width // LANES

    def part(ref, at):
        return ref[:, pl.ds(at, 1), :].reshape(PB, LANES)

    lefts = [
        jnp.concatenate([part(vecs_vmem, at), part(images_vmem, at)], axis=0)
        for at in (row_id + k * (tiles // row_tiles) for k in range(row_tiles))
    ]
    rights = [
        jnp.concatenate([part(images_vmem, at), part(vecs_vmem, at)], axis=0)
        for at in (col_id + k * (tiles // col_tiles) for k in range(col_tiles))
    ]
    left = jnp.concatenate(lefts, axis=1)
    right = jnp.concatenate(rights, axis=1)
    change = lax.dot_general(
        left, right, (((0,), (0,)), ((), ())),
        precision=lax.Precision.HIGHEST, preferred_element_type=F32,
    )
    updated_out[...] = tile_ref[...] - change


def vmem():
    return pl.BlockSpec(memory_space=pltpu.VMEM)


def on_device(psi, hpsi, eigvec):
    g_rows, bands = psi.shape
    row_tiles, _, tile_size, col_tiles = eigvec.shape[:4]
    row_count = lax.axis_size("row")
    col_count = lax.axis_size("col")
    devices = row_count * col_count
    row_id = lax.axis_index("row")
    col_id = lax.axis_index("col")
    gvecs = g_rows * devices
    height = row_tiles * tile_size
    width = col_tiles * tile_size
    tiles = bands // tile_size

    both = lax.all_gather(jnp.stack([psi, hpsi]), "row")
    k = row_count * 2 * g_rows
    flat = both.reshape(k, bands)
    mine = lax.dynamic_index_in_dim(
        both.reshape(row_count, 2, g_rows, row_tiles, row_count, tile_size), row_id, 4, keepdims=False
    ).reshape(row_count, 2, g_rows, height)
    head = both[:, :, :, :PB]
    only_psi = mine * jnp.array([1, 0], mine.dtype).reshape(1, 2, 1, 1)
    left = jnp.concatenate([mine[:, ::-1], head[:, ::-1], only_psi], axis=3).reshape(
        k, 2 * height + PB
    )
    mixed = lax.dot_general(
        left, flat.reshape(k, col_tiles, col_count, tile_size),
        (((0,), (0,)), ((), ())), preferred_element_type=F32,
    )
    mixed = jnp.transpose(mixed, (2, 0, 1, 3)).reshape(col_count, 2 * height + PB, width)
    matrix = 0.5 * mixed[:, :height]
    strip = 0.5 * mixed[:, height : height + PB]
    overlap = mixed[:, height + PB :] * (1.0 / gvecs)

    strip = jnp.sum(lax.all_to_all(strip, "col", 0, 0, tiled=True), axis=0)
    strip = lax.all_to_all(
        jnp.broadcast_to(strip[None], (col_count, *strip.shape)), "col", 0, 0, tiled=True
    )
    panel = jnp.transpose(
        strip.reshape(col_count, PB, col_tiles, tile_size), (1, 2, 0, 3)
    ).reshape(PB, tiles, tile_size)

    reduced = lax.psum_scatter(
        jnp.concatenate([matrix, overlap], axis=1), "col", scatter_dimension=0, tiled=False
    )

    state = jax.ShapeDtypeStruct((PB, tiles, tile_size), F32)
    marks_shape = jax.ShapeDtypeStruct((8, tile_size), F32)
    advance = pl.pallas_call(
        step_body,
        out_shape=(state, state, marks_shape, jax.ShapeDtypeStruct((devices, height), F32)),
        in_specs=[pl.BlockSpec(memory_space=pltpu.SMEM)]
        + [vmem() for _ in range(5)]
        + [pl.BlockSpec(memory_space=pltpu.HBM)],
        out_specs=tuple(vmem() for _ in range(4)),
        scratch_shapes=[pltpu.VMEM(matrix.shape, F32), pltpu.SemaphoreType.DMA],
        input_output_aliases={3: 0, 4: 1, 5: 2},
        compiler_params=pltpu.CompilerParams(vmem_limit_bytes=24 * 1024 * 1024),
        name="reflect",
    )

    def one(step, carry):
        recv, vecs, images, marks = carry
        vecs, images, marks, send = advance(
            jnp.reshape(step, (1,)).astype(jnp.int32), recv, panel, vecs, images, marks, matrix
        )
        recv = lax.all_to_all(send, ("row", "col"), 0, 0, tiled=True)
        return recv.reshape(row_count, col_count, height), vecs, images, marks

    start = (
        jnp.zeros((row_count, col_count, height), F32),
        jnp.zeros(state.shape, F32),
        jnp.zeros(state.shape, F32),
        jnp.zeros(marks_shape.shape, F32),
    )
    recv, vecs, images, marks = lax.fori_loop(0, PB, one, start)

    where = jnp.stack([row_id, col_id]).astype(jnp.int32)
    updated = pl.pallas_call(
        last_body,
        out_shape=jax.ShapeDtypeStruct((height, width), F32),
        in_specs=[pl.BlockSpec(memory_space=pltpu.SMEM)] + [vmem() for _ in range(5)],
        out_specs=vmem(),
        scratch_shapes=[pltpu.VMEM(state.shape, F32), pltpu.VMEM(state.shape, F32)],
        compiler_params=pltpu.CompilerParams(vmem_limit_bytes=24 * 1024 * 1024),
        name="update",
    )(where, recv, vecs, images, marks, reduced[:height])

    psi_rows = lax.all_gather(psi, "col", axis=0, tiled=True)
    turn = lax.all_gather(eigvec.reshape(row_tiles, tile_size, width), "row", axis=1)
    rotated = jnp.dot(psi_rows, turn.reshape(bands, width), preferred_element_type=F32)
    tile_shape = (row_tiles, 1, tile_size, col_tiles, 1, tile_size)
    return (
        reduced[height:].reshape(tile_shape),
        updated.reshape(tile_shape),
        marks[0, :PB],
        marks[1, :PB],
        rotated.astype(jnp.bfloat16).reshape(g_rows * col_count, col_tiles, 1, tile_size),
    )


def solution(mesh):
    return jax.shard_map(
        on_device,
        mesh=mesh,
        in_specs=(
            P(("row", "col"), None),
            P(("row", "col"), None),
            P(None, "row", None, None, "col", None),
        ),
        out_specs=(
            P(None, "row", None, None, "col", None),
            P(None, "row", None, None, "col", None),
            P(),
            P(),
            P("row", None, "col", None),
        ),
        check_vma=False,
    )
```

time: 924 us -> 483 us (0.52)
  matrix products: 205 us -> 11.5 us
  other arithmetic: 131 us -> 9.63 us
  waiting for transfers between devices: 169 us -> 260 us
  starting transfers between devices: 185 us -> 94.4 us
  loops' own time: 68.4 us -> 0.56 us
  blocking collectives: 61.3 us -> 0 us
  Pallas kernels: 0 us -> 48.7 us
  local copies, waits for them, and re-layouts: 85.7 us -> 42.6 us
    dot_general x102 -> x2, matrix products: 197 us -> 11.5 us  [the longest x1 7.41 us: on_device(): lax.dot_general(left, flat.reshape(k, col_tiles, col_count, tile_size), (...]
    all_to_all x33 -> x18, starting transfers between devices: 185 us -> 94.2 us  [the longest x16 84.2 us: one(): recv = lax.all_to_all(send, ('row', 'col'), 0, 0, tiled=True)]
    all_to_all x33 -> x18, waiting for transfers between devices: 84.9 us -> 167 us  [the longest x16 157 us: one(): recv = lax.all_to_all(send, ('row', 'col'), 0, 0, tiled=True)]
    select_n x64 -> x0, other arithmetic: 72.1 us -> none  [the longest x16 61 us: reflect(): images = jnp.where(pick[None, :], image[:, None], images)]
    another operation x1, loops' own time: 68.4 us -> 0.56 us  [on_device(): recv, vecs, images, marks = lax.fori_loop(0, PB, one, start)]
    pallas_call x0 -> x17, Pallas kernels: none -> 48.7 us  [the longest x16 47.2 us: one(): advance(jnp.reshape(step, (1,)).astype(jnp.int32), recv, panel, vecs, ima...]
    while x16 -> x0, other arithmetic: 37.7 us -> none
    all_to_all x2 -> x0, blocking collectives: 32.6 us -> none  [in_one_piece(): lax.all_to_all(both, axis, split_axis=split_dim, concat_axis=concat_dim,...]
  transfers between devices with their start and end apart: 36 -> 22, of which waited for: 19 -> 19; matrix products, arithmetic and copies ran while one was open for 45% -> 11% of each run, Pallas kernels for 0% -> 10%
where the time goes in v1:
time: 483 us; the launch traced here: 481 us
  waiting for transfers between devices  260 us (54%)
  starting transfers between devices  94.4 us (20%)
  Pallas kernels  48.7 us (10%)
  local copies, waits for them, and re-layouts  42.6 us (9%)
  between operations  13.9 us (3%)
  matrix products  11.5 us (2%)
  other arithmetic  9.63 us (2%)
    all_to_all x16, waiting for transfers between devices, one(): recv = lax.all_to_all(send, ('row', 'col'), 0, 0, tiled=True)  157 us
    all_to_all x16, starting transfers between devices, one(): recv = lax.all_to_all(send, ('row', 'col'), 0, 0, tiled=True)  84.2 us
    all_gather x1, waiting for transfers between devices, on_device(): both = lax.all_gather(jnp.stack([psi, hpsi]), 'row')  54.2 us
    pallas_call x16, Pallas kernels, one(): advance(jnp.reshape(step, (1,)).astype(jnp.int32), recv, panel, vecs, ima...  47.2 us
    all_gather x1, waiting for transfers between devices, on_device(): lax.all_gather(eigvec.reshape(row_tiles, tile_size, width), 'row', axis=1)  38.2 us
    unnamed x7, local copies, waits for them, and re-layouts  14.1 us
    all_to_all x16, local copies, waits for them, and re-layouts, one(): recv = lax.all_to_all(send, ('row', 'col'), 0, 0, tiled=True)  12.7 us
  transfers between devices with their start and end apart: 22, of which 19 were waited for; matrix products, arithmetic and copies ran while one was open for 11% of the time, Pallas kernels for 10%

profile of v1, /device:TPU:1, one launch (start us, length us, event | category | flops | bytes accessed | tf_op | source)
XLA Modules:
  0.0 481.2 jit_solution(2453125220588854486)
XLA Ops:
  11.7 54.2 %all-gather.9.cloned.1.call-done = bf16[32,32,4096]{2,1,0:T(8,128)(2,1)} async-done(((bf16[2,32,4096]{2,1,0:T(8,128)(2,1)}), bf16[32,32,4096]{2,1,0:T(8,128)(2,1)}) %all-gather.9.cloned.1.call-update) | async-done | bytes 8388624 | tf_op jit(solution)/shard_map/all_gather | solution.py:144
  66.0 9.5 %copy.46 = bf16[128,8,32,128]{3,2,1,0:T(8,128)(2,1)} copy(bf16[128,8,32,128]{3,1,2,0:T(8,128)(2,1)} %bitcast.58) | data formatting | bytes 16777216
  75.4 5.8 %dynamic-slice_reduce_fusion = bf16[16,2,32,2,128]{4,3,2,1,0:T(2,128)(2,1)S(1)} fusion(bf16[16,2,32,2,16,128]{5,4,3,2,1,0:T(8,128)(2,1)} %bitcast.55, s32[]{:T(128)S(6)} %select_n.4), kind=kLoop, calls=%fused_computation.10 | loop fusion | bytes 1048580 | tf_op jit(solution)/shard_map/jit(dynamic_index_in_dim)/dynamic_slice | solution.py:147
  83.2 7.4 %fusion.2 = f32[4,8,66,8,128]{4,3,2,1,0:T(8,128)S(1)} fusion(bf16[1024,528,1,1]{1,0,3,2:T(8,128)(2,1)S(1)} %bitcast.61, bf16[1024,4,8,128]{3,2,1,0:T(8,128)(2,1)} %bitcast.56), kind=kOutput, calls=%fused_computation.7 | convolution fusion | flops 4429185024 | bytes 18120704 | tf_op jit(solution)/shard_map/dot_general | solution.py:155
  97.7 4.3 pad_maximum_fusion
  103.7 6.4 %all-to-all-start.1 = ((f32[8,16,512]{2,1,0:T(8,128)}), f32[8,16,512]{2,1,0:T(8,128)S(1)}, u32[]{:S(2)}, u32[]{:S(2)}) async-start(f32[8,16,512]{2,1,0:T(8,128)} %slice_multiply_fusion.2), calls=%async_computation.2 | async-start | bytes 524288 | tf_op jit(solution)/shard_map/all_to_all | solution.py:164
  110.2 9.5 %all-to-all-done.1 = f32[8,16,512]{2,1,0:T(8,128)S(1)} async-done(((f32[8,16,512]{2,1,0:T(8,128)}), f32[8,16,512]{2,1,0:T(8,128)S(1)}, u32[]{:S(2)}, u32[]{:S(2)}) %all-to-all-start.1) | async-done | bytes 262176 | tf_op jit(solution)/shard_map/all_to_all | solution.py:164
  120.4 3.6 all-to-all-start.2
  124.0 38.2 %all-gather.7.cloned.1.call-done = bf16[2,16,128,512]{3,2,1,0:T(8,128)(2,1)} async-done(((bf16[2,1,128,512]{3,2,1,0:T(8,128)(2,1)}), bf16[2,16,128,512]{3,2,1,0:T(8,128)(2,1)}) %all-gather.7.cloned.1.call-update) | async-done | bytes 4194320 | tf_op jit(solution)/shard_map/all_gather | solution.py:219
  162.2 4.1 convolution_convert_fusion
  167.4 302.1 %while.19 = (s32[]{:T(128)}, f32[16,8,256]{2,1,0:T(8,128)S(1)}, f32[16,32,128]{2,1,0:T(8,128)S(1)}, f32[16,32,128]{2,1,0:T(8,128)S(1)}, f32[8,128]{1,0:T(8,128)S...) while((s32[]{:T(128)}, f32[16,8,256]{2,1,0:T(8,128)S(1)}, ...), condition=%wide.region_3.4_spmd, body=%wide.region_2.3_spmd.sunk | while | flops 2 | bytes 917621 | solution.py:205
  167.4 2.9 reflect.5
  171.1 7.8 %all-to-all-start = ((f32[128,1,256]{2,1,0:T(1,128)}), f32[128,1,256]{2,1,0:T(1,128)S(1)}, u32[]{:S(2)}, u32[]{:S(2)}) async-start(f32[128,1,256]{2,1,0:T(1,128)} %copy.60), calls=%async_computation | async-start | bytes 262144 | tf_op jit(solution)/shard_map/while/body/eval_jaxpr/all_to_all | solution.py:196
  178.9 10.8 %all-to-all-done = f32[128,1,256]{2,1,0:T(1,128)S(1)} async-done(((f32[128,1,256]{2,1,0:T(1,128)}), f32[128,1,256]{2,1,0:T(1,128)S(1)}, u32[]{:S(2)}, u32[]{:S(2)}) %all-to-all-start) | async-done | bytes 131104 | tf_op jit(solution)/shard_map/while/body/eval_jaxpr/all_to_all | solution.py:196
  189.7 3.0 reflect.5
  193.5 5.0 %all-to-all-start = ((f32[128,1,256]{2,1,0:T(1,128)}), f32[128,1,256]{2,1,0:T(1,128)S(1)}, u32[]{:S(2)}, u32[]{:S(2)}) async-start(f32[128,1,256]{2,1,0:T(1,128)} %copy.60), calls=%async_computation | async-start | bytes 262144 | tf_op jit(solution)/shard_map/while/body/eval_jaxpr/all_to_all | solution.py:196
  198.5 10.8 %all-to-all-done = f32[128,1,256]{2,1,0:T(1,128)S(1)} async-done(((f32[128,1,256]{2,1,0:T(1,128)}), f32[128,1,256]{2,1,0:T(1,128)S(1)}, u32[]{:S(2)}, u32[]{:S(2)}) %all-to-all-start) | async-done | bytes 131104 | tf_op jit(solution)/shard_map/while/body/eval_jaxpr/all_to_all | solution.py:196
  209.3 3.0 reflect.5
  213.1 11.3 %all-to-all-start = ((f32[128,1,256]{2,1,0:T(1,128)}), f32[128,1,256]{2,1,0:T(1,128)S(1)}, u32[]{:S(2)}, u32[]{:S(2)}) async-start(f32[128,1,256]{2,1,0:T(1,128)} %copy.60), calls=%async_computation | async-start | bytes 262144 | tf_op jit(solution)/shard_map/while/body/eval_jaxpr/all_to_all | solution.py:196
  224.5 9.9 %all-to-all-done = f32[128,1,256]{2,1,0:T(1,128)S(1)} async-done(((f32[128,1,256]{2,1,0:T(1,128)}), f32[128,1,256]{2,1,0:T(1,128)S(1)}, u32[]{:S(2)}, u32[]{:S(2)}) %all-to-all-start) | async-done | bytes 131104 | tf_op jit(solution)/shard_map/while/body/eval_jaxpr/all_to_all | solution.py:196
  238.2 5.2 %all-to-all-start = ((f32[128,1,256]{2,1,0:T(1,128)}), f32[128,1,256]{2,1,0:T(1,128)S(1)}, u32[]{:S(2)}, u32[]{:S(2)}) async-start(f32[128,1,256]{2,1,0:T(1,128)} %copy.60), calls=%async_computation | async-start | bytes 262144 | tf_op jit(solution)/shard_map/while/body/eval_jaxpr/all_to_all | solution.py:196
  243.4 9.6 %all-to-all-done = f32[128,1,256]{2,1,0:T(1,128)S(1)} async-done(((f32[128,1,256]{2,1,0:T(1,128)}), f32[128,1,256]{2,1,0:T(1,128)S(1)}, u32[]{:S(2)}, u32[]{:S(2)}) %all-to-all-start) | async-done | bytes 131104 | tf_op jit(solution)/shard_map/while/body/eval_jaxpr/all_to_all | solution.py:196
  256.7 4.5 all-to-all-start
  261.3 10.8 %all-to-all-done = f32[128,1,256]{2,1,0:T(1,128)S(1)} async-done(((f32[128,1,256]{2,1,0:T(1,128)}), f32[128,1,256]{2,1,0:T(1,128)S(1)}, u32[]{:S(2)}, u32[]{:S(2)}) %all-to-all-start) | async-done | bytes 131104 | tf_op jit(solution)/shard_map/while/body/eval_jaxpr/all_to_all | solution.py:196
  272.1 3.0 reflect.5
  275.9 5.0 %all-to-all-start = ((f32[128,1,256]{2,1,0:T(1,128)}), f32[128,1,256]{2,1,0:T(1,128)S(1)}, u32[]{:S(2)}, u32[]{:S(2)}) async-start(f32[128,1,256]{2,1,0:T(1,128)} %copy.60), calls=%async_computation | async-start | bytes 262144 | tf_op jit(solution)/shard_map/while/body/eval_jaxpr/all_to_all | solution.py:196
  280.9 9.6 %all-to-all-done = f32[128,1,256]{2,1,0:T(1,128)S(1)} async-done(((f32[128,1,256]{2,1,0:T(1,128)}), f32[128,1,256]{2,1,0:T(1,128)S(1)}, u32[]{:S(2)}, u32[]{:S(2)}) %all-to-all-start) | async-done | bytes 131104 | tf_op jit(solution)/shard_map/while/body/eval_jaxpr/all_to_all | solution.py:196
  290.5 2.9 reflect.5
  294.3 4.5 all-to-all-start
  298.8 9.6 %all-to-all-done = f32[128,1,256]{2,1,0:T(1,128)S(1)} async-done(((f32[128,1,256]{2,1,0:T(1,128)}), f32[128,1,256]{2,1,0:T(1,128)S(1)}, u32[]{:S(2)}, u32[]{:S(2)}) %all-to-all-start) | async-done | bytes 131104 | tf_op jit(solution)/shard_map/while/body/eval_jaxpr/all_to_all | solution.py:196
  312.2 4.5 all-to-all-start
  316.7 9.6 %all-to-all-done = f32[128,1,256]{2,1,0:T(1,128)S(1)} async-done(((f32[128,1,256]{2,1,0:T(1,128)}), f32[128,1,256]{2,1,0:T(1,128)S(1)}, u32[]{:S(2)}, u32[]{:S(2)}) %all-to-all-start) | async-done | bytes 131104 | tf_op jit(solution)/shard_map/while/body/eval_jaxpr/all_to_all | solution.py:196
  330.0 4.5 all-to-all-start
  334.6 9.6 %all-to-all-done = f32[128,1,256]{2,1,0:T(1,128)S(1)} async-done(((f32[128,1,256]{2,1,0:T(1,128)}), f32[128,1,256]{2,1,0:T(1,128)S(1)}, u32[]{:S(2)}, u32[]{:S(2)}) %all-to-all-start) | async-done | bytes 131104 | tf_op jit(solution)/shard_map/while/body/eval_jaxpr/all_to_all | solution.py:196
  347.9 4.5 all-to-all-start
  352.5 9.6 %all-to-all-done = f32[128,1,256]{2,1,0:T(1,128)S(1)} async-done(((f32[128,1,256]{2,1,0:T(1,128)}), f32[128,1,256]{2,1,0:T(1,128)S(1)}, u32[]{:S(2)}, u32[]{:S(2)}) %all-to-all-start) | async-done | bytes 131104 | tf_op jit(solution)/shard_map/while/body/eval_jaxpr/all_to_all | solution.py:196
  365.8 4.5 all-to-all-start
  370.4 9.6 %all-to-all-done = f32[128,1,256]{2,1,0:T(1,128)S(1)} async-done(((f32[128,1,256]{2,1,0:T(1,128)}), f32[128,1,256]{2,1,0:T(1,128)S(1)}, u32[]{:S(2)}, u32[]{:S(2)}) %all-to-all-start) | async-done | bytes 131104 | tf_op jit(solution)/shard_map/while/body/eval_jaxpr/all_to_all | solution.py:196
  383.7 4.5 all-to-all-start
  388.3 9.6 %all-to-all-done = f32[128,1,256]{2,1,0:T(1,128)S(1)} async-done(((f32[128,1,256]{2,1,0:T(1,128)}), f32[128,1,256]{2,1,0:T(1,128)S(1)}, u32[]{:S(2)}, u32[]{:S(2)}) %all-to-all-start) | async-done | bytes 131104 | tf_op jit(solution)/shard_map/while/body/eval_jaxpr/all_to_all | solution.py:196
  401.6 4.5 all-to-all-start
  406.2 9.6 %all-to-all-done = f32[128,1,256]{2,1,0:T(1,128)S(1)} async-done(((f32[128,1,256]{2,1,0:T(1,128)}), f32[128,1,256]{2,1,0:T(1,128)S(1)}, u32[]{:S(2)}, u32[]{:S(2)}) %all-to-all-start) | async-done | bytes 131104 | tf_op jit(solution)/shard_map/while/body/eval_jaxpr/all_to_all | solution.py:196
  419.5 4.5 all-to-all-start
  424.0 9.6 %all-to-all-done = f32[128,1,256]{2,1,0:T(1,128)S(1)} async-done(((f32[128,1,256]{2,1,0:T(1,128)}), f32[128,1,256]{2,1,0:T(1,128)S(1)}, u32[]{:S(2)}, u32[]{:S(2)}) %all-to-all-start) | async-done | bytes 131104 | tf_op jit(solution)/shard_map/while/body/eval_jaxpr/all_to_all | solution.py:196
  437.4 4.5 all-to-all-start
  441.9 9.6 %all-to-all-done = f32[128,1,256]{2,1,0:T(1,128)S(1)} async-done(((f32[128,1,256]{2,1,0:T(1,128)}), f32[128,1,256]{2,1,0:T(1,128)S(1)}, u32[]{:S(2)}, u32[]{:S(2)}) %all-to-all-start) | async-done | bytes 131104 | tf_op jit(solution)/shard_map/while/body/eval_jaxpr/all_to_all | solution.py:196
  455.3 4.5 all-to-all-start
  459.8 9.6 %all-to-all-done = f32[128,1,256]{2,1,0:T(1,128)S(1)} async-done(((f32[128,1,256]{2,1,0:T(1,128)}), f32[128,1,256]{2,1,0:T(1,128)S(1)}, u32[]{:S(2)}, u32[]{:S(2)}) %all-to-all-start) | async-done | bytes 131104 | tf_op jit(solution)/shard_map/while/body/eval_jaxpr/all_to_all | solution.py:196
  (86 shorter events, 67.5 us)
Async XLA Ops:
  7.2 58.8 %all-gather.9.cloned.1.call-start = ((), (), s32[]{:S(2)}) async-start(), calls=%async_computation.7 | async-start | bytes 8912896 | tf_op jit(solution)/shard_map/all_gather | solution.py:144
  9.1 114.9 %all-gather.5.cloned.1.call-start = ((), (), s32[]{:S(2)}) async-start(), calls=%async_computation.5 | async-start | bytes 2359296 | tf_op jit(solution)/shard_map/all_gather | solution.py:218
  9.9 152.3 %all-gather.7.cloned.1.call-start = ((), (), s32[]{:S(2)}) async-start(), calls=%async_computation.6 | async-start | bytes 4456448 | tf_op jit(solution)/shard_map/all_gather | solution.py:219
  11.7 458.3 %reduce-scatter.2.cloned.1.call-start = ((), (), s32[]{:S(2)}) async-start(), calls=%async_computation.4 | async-start | bytes 9437184 | tf_op jit(solution)/shard_map/reduce_scatter | solution.py:172
  75.4 7.2 %copy-start.2 = (bf16[2]{0:T(256)(128)(2,1)S(1)}, bf16[2]{0:T(256)(128)(2,1)}, u32[]{:S(2)}) copy-start(bf16[2]{0:T(256)(128)(2,1)} %constant.38.clone) | copy-start | bytes 16
  91.8 3.8 copy-start.1
  95.6 2.0 copy-start
  103.7 16.0 %all-to-all-start.1 = ((f32[8,16,512]{2,1,0:T(8,128)}), f32[8,16,512]{2,1,0:T(8,128)S(1)}, u32[]{:S(2)}, u32[]{:S(2)}) async-start(f32[8,16,512]{2,1,0:T(8,128)} %slice_multiply_fusion.2), calls=%async_computation.2 | async-start | bytes 524288 | tf_op jit(solution)/shard_map/all_to_all | solution.py:164
  120.4 46.6 %all-to-all-start.2 = ((f32[8,16,512]{2,1,0:T(8,128)}), f32[8,16,512]{2,1,0:T(8,128)S(1)}, u32[]{:S(2)}, u32[]{:S(2)}) async-start(f32[8,16,512]{2,1,0:T(8,128)} %broadcast_in_dim.14), calls=%async_computation.3 | async-start | bytes 524288 | tf_op jit(solution)/shard_map/all_to_all | solution.py:165
  171.1 18.6 %all-to-all-start = ((f32[128,1,256]{2,1,0:T(1,128)}), f32[128,1,256]{2,1,0:T(1,128)S(1)}, u32[]{:S(2)}, u32[]{:S(2)}) async-start(f32[128,1,256]{2,1,0:T(1,128)} %copy.60), calls=%async_computation | async-start | bytes 262144 | tf_op jit(solution)/shard_map/while/body/eval_jaxpr/all_to_all | solution.py:196
  193.5 15.8 %all-to-all-start = ((f32[128,1,256]{2,1,0:T(1,128)}), f32[128,1,256]{2,1,0:T(1,128)S(1)}, u32[]{:S(2)}, u32[]{:S(2)}) async-start(f32[128,1,256]{2,1,0:T(1,128)} %copy.60), calls=%async_computation | async-start | bytes 262144 | tf_op jit(solution)/shard_map/while/body/eval_jaxpr/all_to_all | solution.py:196
  213.1 21.3 %all-to-all-start = ((f32[128,1,256]{2,1,0:T(1,128)}), f32[128,1,256]{2,1,0:T(1,128)S(1)}, u32[]{:S(2)}, u32[]{:S(2)}) async-start(f32[128,1,256]{2,1,0:T(1,128)} %copy.60), calls=%async_computation | async-start | bytes 262144 | tf_op jit(solution)/shard_map/while/body/eval_jaxpr/all_to_all | solution.py:196
  238.2 14.8 %all-to-all-start = ((f32[128,1,256]{2,1,0:T(1,128)}), f32[128,1,256]{2,1,0:T(1,128)S(1)}, u32[]{:S(2)}, u32[]{:S(2)}) async-start(f32[128,1,256]{2,1,0:T(1,128)} %copy.60), calls=%async_computation | async-start | bytes 262144 | tf_op jit(solution)/shard_map/while/body/eval_jaxpr/all_to_all | solution.py:196
  256.7 15.3 %all-to-all-start = ((f32[128,1,256]{2,1,0:T(1,128)}), f32[128,1,256]{2,1,0:T(1,128)S(1)}, u32[]{:S(2)}, u32[]{:S(2)}) async-start(f32[128,1,256]{2,1,0:T(1,128)} %copy.60), calls=%async_computation | async-start | bytes 262144 | tf_op jit(solution)/shard_map/while/body/eval_jaxpr/all_to_all | solution.py:196
  275.9 14.6 %all-to-all-start = ((f32[128,1,256]{2,1,0:T(1,128)}), f32[128,1,256]{2,1,0:T(1,128)S(1)}, u32[]{:S(2)}, u32[]{:S(2)}) async-start(f32[128,1,256]{2,1,0:T(1,128)} %copy.60), calls=%async_computation | async-start | bytes 262144 | tf_op jit(solution)/shard_map/while/body/eval_jaxpr/all_to_all | solution.py:196
  294.3 14.1 %all-to-all-start = ((f32[128,1,256]{2,1,0:T(1,128)}), f32[128,1,256]{2,1,0:T(1,128)S(1)}, u32[]{:S(2)}, u32[]{:S(2)}) async-start(f32[128,1,256]{2,1,0:T(1,128)} %copy.60), calls=%async_computation | async-start | bytes 262144 | tf_op jit(solution)/shard_map/while/body/eval_jaxpr/all_to_all | solution.py:196
  312.2 14.1 %all-to-all-start = ((f32[128,1,256]{2,1,0:T(1,128)}), f32[128,1,256]{2,1,0:T(1,128)S(1)}, u32[]{:S(2)}, u32[]{:S(2)}) async-start(f32[128,1,256]{2,1,0:T(1,128)} %copy.60), calls=%async_computation | async-start | bytes 262144 | tf_op jit(solution)/shard_map/while/body/eval_jaxpr/all_to_all | solution.py:196
  330.0 14.1 %all-to-all-start = ((f32[128,1,256]{2,1,0:T(1,128)}), f32[128,1,256]{2,1,0:T(1,128)S(1)}, u32[]{:S(2)}, u32[]{:S(2)}) async-start(f32[128,1,256]{2,1,0:T(1,128)} %copy.60), calls=%async_computation | async-start | bytes 262144 | tf_op jit(solution)/shard_map/while/body/eval_jaxpr/all_to_all | solution.py:196
  347.9 14.1 %all-to-all-start = ((f32[128,1,256]{2,1,0:T(1,128)}), f32[128,1,256]{2,1,0:T(1,128)S(1)}, u32[]{:S(2)}, u32[]{:S(2)}) async-start(f32[128,1,256]{2,1,0:T(1,128)} %copy.60), calls=%async_computation | async-start | bytes 262144 | tf_op jit(solution)/shard_map/while/body/eval_jaxpr/all_to_all | solution.py:196
  365.8 14.1 %all-to-all-start = ((f32[128,1,256]{2,1,0:T(1,128)}), f32[128,1,256]{2,1,0:T(1,128)S(1)}, u32[]{:S(2)}, u32[]{:S(2)}) async-start(f32[128,1,256]{2,1,0:T(1,128)} %copy.60), calls=%async_computation | async-start | bytes 262144 | tf_op jit(solution)/shard_map/while/body/eval_jaxpr/all_to_all | solution.py:196
  383.7 14.1 %all-to-all-start = ((f32[128,1,256]{2,1,0:T(1,128)}), f32[128,1,256]{2,1,0:T(1,128)S(1)}, u32[]{:S(2)}, u32[]{:S(2)}) async-start(f32[128,1,256]{2,1,0:T(1,128)} %copy.60), calls=%async_computation | async-start | bytes 262144 | tf_op jit(solution)/shard_map/while/body/eval_jaxpr/all_to_all | solution.py:196
  401.6 14.1 %all-to-all-start = ((f32[128,1,256]{2,1,0:T(1,128)}), f32[128,1,256]{2,1,0:T(1,128)S(1)}, u32[]{:S(2)}, u32[]{:S(2)}) async-start(f32[128,1,256]{2,1,0:T(1,128)} %copy.60), calls=%async_computation | async-start | bytes 262144 | tf_op jit(solution)/shard_map/while/body/eval_jaxpr/all_to_all | solution.py:196
  419.5 14.1 %all-to-all-start = ((f32[128,1,256]{2,1,0:T(1,128)}), f32[128,1,256]{2,1,0:T(1,128)S(1)}, u32[]{:S(2)}, u32[]{:S(2)}) async-start(f32[128,1,256]{2,1,0:T(1,128)} %copy.60), calls=%async_computation | async-start | bytes 262144 | tf_op jit(solution)/shard_map/while/body/eval_jaxpr/all_to_all | solution.py:196
  437.4 14.1 %all-to-all-start = ((f32[128,1,256]{2,1,0:T(1,128)}), f32[128,1,256]{2,1,0:T(1,128)S(1)}, u32[]{:S(2)}, u32[]{:S(2)}) async-start(f32[128,1,256]{2,1,0:T(1,128)} %copy.60), calls=%async_computation | async-start | bytes 262144 | tf_op jit(solution)/shard_map/while/body/eval_jaxpr/all_to_all | solution.py:196
  455.3 14.1 %all-to-all-start = ((f32[128,1,256]{2,1,0:T(1,128)}), f32[128,1,256]{2,1,0:T(1,128)S(1)}, u32[]{:S(2)}, u32[]{:S(2)}) async-start(f32[128,1,256]{2,1,0:T(1,128)} %copy.60), calls=%async_computation | async-start | bytes 262144 | tf_op jit(solution)/shard_map/while/body/eval_jaxpr/all_to_all | solution.py:196
Sparse Core Ops, SparseCore 0:
  10.3 55.6 all-gather.8
  68.3 53.6 all-gather.4
  124.2 37.8 all-gather.6
  165.8 120.2 reduce-scatter.1

commit v2 on v1

v2 whole, which is shorter than its diff:
```python
import functools

import jax
import jax.numpy as jnp
from jax import lax
from jax.experimental import pallas as pl
from jax.experimental.pallas import tpu as pltpu
from jax.sharding import PartitionSpec as P

PB = 16
LANES = 128
F32 = jnp.float32
MIB = 1024 * 1024


def total(x):
    return jnp.sum(jnp.sum(x, axis=-2, keepdims=True), axis=-1, keepdims=True)


def over_k(left, right):
    return lax.dot_general(left, right, (((1,), (0,)), ((), ())), preferred_element_type=F32)


def products_body(where_ref, *refs, row_tiles, col_tiles, gvecs):
    rows = refs[:row_tiles]
    head_ref = refs[row_tiles]
    cols = refs[row_tiles + 1 : row_tiles + 1 + col_tiles]
    blocks_out, strip_out, send_out, left_vmem, left_psi_vmem = refs[row_tiles + 1 + col_tiles :]
    height = row_tiles * LANES

    def swapped(x):
        return jnp.concatenate([x[:, 1:2], x[:, 0:1]], axis=1).reshape(-1, LANES)

    @pl.when(pl.program_id(0) == 0)
    def _():
        for k, ref in enumerate(rows):
            at = pl.ds(k * LANES, LANES)
            left_vmem[at, :] = swapped(ref[...]).T
            left_psi_vmem[at, :] = ref[:, 0].reshape(-1, LANES).T
        mine = jnp.concatenate([ref[...].reshape(-1, LANES) for ref in rows], axis=1)
        strip = 0.5 * over_k(swapped(head_ref[...]).T, mine)
        strip_out[...] = strip[:PB]
        send = jnp.concatenate([jnp.zeros((1, height), F32), strip[0:1]], axis=1)
        send_out[...] = jnp.broadcast_to(send[:, None, :], send_out.shape)

    both = jnp.concatenate([ref[...].reshape(-1, LANES) for ref in cols], axis=1)
    psi = jnp.concatenate([ref[:, 0].reshape(-1, LANES) for ref in cols], axis=1)
    blocks_out[0, :height, :] = 0.5 * over_k(left_vmem[...], both)
    blocks_out[0, height:, :] = over_k(left_psi_vmem[...], psi) * (1.0 / gvecs)


def gathered(recv_ref, at, counts, halves):
    row_count, col_count = counts
    parts = []
    for h in range(halves):
        start = at + h * LANES
        block = recv_ref[:, :, start : start + LANES].reshape(row_count, col_count, LANES)
        parts.append(jnp.sum(block, axis=1))
    return jnp.concatenate(parts, axis=0).reshape(1, row_count * halves, LANES)


def finish_image(image, vecs, images, vector, tau):
    along_w = total(images * vector)
    along_v = total(vecs * vector)
    image = image - jnp.sum(vecs * along_w + images * along_v, axis=0, keepdims=True)
    image = tau * image
    return image - 0.5 * tau * total(image * vector) * vector


def place(into, what, slot):
    slots = lax.broadcasted_iota(jnp.int32, (PB, 1, 1), 0)
    return jnp.where(slots == slot, what, into)


def step_body(
    step_ref, recv_ref, strip_ref, vecs_ref, images_ref, marks_ref, blocks_ref,
    vecs_out, images_out, marks_out, send_out, matrix_vmem, sem, *, counts,
):
    step = step_ref[0]
    tiles = vecs_ref.shape[1]
    col_count, height, width = matrix_vmem.shape
    halves = height // LANES
    copy = pltpu.make_async_copy(blocks_ref.at[:, :height, :], matrix_vmem, sem)
    copy.start()
    lane = lax.broadcasted_iota(jnp.int32, (1, 1, LANES), 2)
    marks = marks_ref[...]
    vecs = vecs_ref[...]
    images = images_ref[...]
    before = jnp.maximum(step - 1, 0)
    vector = vecs_ref[pl.ds(before, 1)]
    tau = marks[2:3, 0:1].reshape(1, 1, 1)
    image = finish_image(gathered(recv_ref, 0, counts, halves), vecs, images, vector, tau)
    images = place(images, image, step - 1)
    images_out[...] = images
    head_w = jnp.sum(jnp.where(lane == step, images[:, 0:1, :], 0.0), axis=-1, keepdims=True)
    head_v = jnp.sum(jnp.where(lane == step, vecs[:, 0:1, :], 0.0), axis=-1, keepdims=True)
    column = gathered(recv_ref, height, counts, halves) - jnp.sum(
        vecs * head_w + images * head_v, axis=0, keepdims=True
    )
    shape = (1, tiles, LANES)
    positions = lax.broadcasted_iota(jnp.int32, shape, 1) * LANES + lax.broadcasted_iota(
        jnp.int32, shape, 2
    )
    below = positions > step + 1
    pivot = total(jnp.where(positions == step + 1, column, 0.0))
    tail = total(jnp.where(below, column * column, 0.0))
    corner = total(jnp.where(positions == step, column, 0.0))
    length = jnp.sqrt(pivot * pivot + tail)
    beta = jnp.where(pivot >= 0.0, -length, length)
    tau = (beta - pivot) / beta
    vector = jnp.where(positions == step + 1, 1.0, jnp.where(below, column / (pivot - beta), 0.0))
    vecs_out[...] = place(vecs, vector, step)
    row = lax.broadcasted_iota(jnp.int32, marks.shape, 0)
    spot = lax.broadcasted_iota(jnp.int32, marks.shape, 1) == step
    flat = marks.shape
    marks = jnp.where((row == 0) & spot, jnp.broadcast_to(corner[0], flat), marks)
    marks = jnp.where((row == 1) & spot, jnp.broadcast_to(beta[0], flat), marks)
    marks_out[...] = jnp.where(row == 2, jnp.broadcast_to(tau[0], flat), marks)
    after = strip_ref[pl.ds(jnp.minimum(step + 1, PB - 1), 1), :]
    copy.wait()
    col_tiles = width // LANES
    sums = jnp.zeros((height, LANES), F32)
    for c in range(col_count):
        for a in range(col_tiles):
            u = a * col_count + c
            sums = sums + matrix_vmem[c, :, a * LANES : (a + 1) * LANES] * vector[0, u : u + 1, :]
    pieces = [
        jnp.sum(sums[k * LANES : (k + 1) * LANES].T, axis=0, keepdims=True) for k in range(halves)
    ]
    send = jnp.concatenate(pieces + [after], axis=1)
    send_out[...] = jnp.broadcast_to(send[:, None, :], send_out.shape)


def last_body(
    where_ref, recv_ref, vecs_ref, images_ref, marks_ref, tile_ref, psi_ref, turn_ref,
    updated_out, rotated_out, vecs_vmem, images_vmem, *, counts,
):
    rotated_out[...] = over_k(psi_ref[...], turn_ref[...]).astype(rotated_out.dtype)
    tiles = vecs_ref.shape[1]
    row_id = where_ref[0]
    col_id = where_ref[1]
    height, width = updated_out.shape
    row_tiles = height // LANES
    col_tiles = width // LANES
    vecs = vecs_ref[...]
    vector = vecs_ref[PB - 1 : PB]
    tau = marks_ref[2:3, 0:1].reshape(1, 1, 1)
    image = finish_image(gathered(recv_ref, 0, counts, row_tiles), vecs, images_ref[...], vector, tau)
    images_vmem[...] = place(images_ref[...], image, PB - 1)
    vecs_vmem[...] = vecs

    def part(ref, at):
        return ref[:, pl.ds(at, 1), :].reshape(PB, LANES)

    lefts = [
        jnp.concatenate([part(vecs_vmem, at), part(images_vmem, at)], axis=0)
        for at in (row_id + k * (tiles // row_tiles) for k in range(row_tiles))
    ]
    rights = [
        jnp.concatenate([part(images_vmem, at), part(vecs_vmem, at)], axis=0)
        for at in (col_id + k * (tiles // col_tiles) for k in range(col_tiles))
    ]
    left = jnp.concatenate(lefts, axis=1)
    right = jnp.concatenate(rights, axis=1)
    change = lax.dot_general(
        left, right, (((0,), (0,)), ((), ())),
        precision=lax.Precision.HIGHEST, preferred_element_type=F32,
    )
    updated_out[...] = tile_ref[0, :height, :] - change


def vmem():
    return pl.BlockSpec(memory_space=pltpu.VMEM)


def on_device(psi, hpsi, eigvec):
    g_rows, bands = psi.shape
    row_tiles, _, tile_size, col_tiles = eigvec.shape[:4]
    row_count = lax.axis_size("row")
    col_count = lax.axis_size("col")
    devices = row_count * col_count
    counts = (row_count, col_count)
    row_id = lax.axis_index("row")
    col_id = lax.axis_index("col")
    gvecs = g_rows * devices
    height = row_tiles * tile_size
    width = col_tiles * tile_size
    tiles = bands // tile_size
    where = jnp.stack([row_id, col_id]).astype(jnp.int32)

    both = lax.all_gather(jnp.stack([psi, hpsi]), "row")
    psi_rows = lax.all_gather(psi, "col", axis=0, tiled=True)
    turn = lax.all_gather(eigvec.reshape(row_tiles, tile_size, width), "row", axis=1)

    k = row_count * 2 * g_rows
    block = (row_count, 2, g_rows, tile_size)
    sent = jax.ShapeDtypeStruct((devices, 1, 2 * height), F32)

    def column_block(index):
        return pl.BlockSpec(block, lambda c, where: (0, 0, 0, index(c, where)))

    in_specs = (
        [column_block(lambda c, where, a=a: where[0] + a * row_count) for a in range(row_tiles)]
        + [column_block(lambda c, where: 0)]
        + [column_block(lambda c, where, a=a: c + a * col_count) for a in range(col_tiles)]
    )
    blocks, strip, send = pl.pallas_call(
        functools.partial(products_body, row_tiles=row_tiles, col_tiles=col_tiles, gvecs=gvecs),
        out_shape=(
            jax.ShapeDtypeStruct((col_count, 2 * height, width), F32),
            jax.ShapeDtypeStruct((PB, height), F32),
            sent,
        ),
        grid_spec=pltpu.PrefetchScalarGridSpec(
            num_scalar_prefetch=1,
            grid=(col_count,),
            in_specs=in_specs,
            out_specs=(
                pl.BlockSpec((1, 2 * height, width), lambda c, where: (c, 0, 0)),
                pl.BlockSpec((PB, height), lambda c, where: (0, 0)),
                pl.BlockSpec(sent.shape, lambda c, where: (0, 0, 0)),
            ),
            scratch_shapes=[
                pltpu.VMEM((height, k), psi.dtype),
                pltpu.VMEM((height, k // 2), psi.dtype),
            ],
        ),
        compiler_params=pltpu.CompilerParams(vmem_limit_bytes=32 * MIB),
        name="products",
    )(where, *([both] * len(in_specs)))

    reduced = lax.psum_scatter(blocks, "col", scatter_dimension=0, tiled=True)

    state = jax.ShapeDtypeStruct((PB, tiles, tile_size), F32)
    marks_shape = jax.ShapeDtypeStruct((8, tile_size), F32)
    advance = pl.pallas_call(
        functools.partial(step_body, counts=counts),
        out_shape=(state, state, marks_shape, sent),
        in_specs=[pl.BlockSpec(memory_space=pltpu.SMEM)]
        + [vmem() for _ in range(5)]
        + [pl.BlockSpec(memory_space=pltpu.HBM)],
        out_specs=tuple(vmem() for _ in range(4)),
        scratch_shapes=[
            pltpu.VMEM((col_count, height, width), F32),
            pltpu.SemaphoreType.DMA,
        ],
        input_output_aliases={3: 0, 4: 1, 5: 2},
        compiler_params=pltpu.CompilerParams(vmem_limit_bytes=24 * MIB),
        name="reflect",
    )

    def exchange(send):
        return lax.all_to_all(send, ("row", "col"), 0, 0, tiled=True)

    def one(step, carry):
        recv, vecs, images, marks = carry
        vecs, images, marks, send = advance(
            jnp.reshape(step, (1,)).astype(jnp.int32), recv, strip, vecs, images, marks, blocks
        )
        return exchange(send), vecs, images, marks

    start = (
        exchange(send),
        jnp.zeros(state.shape, F32),
        jnp.zeros(state.shape, F32),
        jnp.zeros(marks_shape.shape, F32),
    )
    recv, vecs, images, marks = lax.fori_loop(0, PB, one, start)

    updated, rotated = pl.pallas_call(
        functools.partial(last_body, counts=counts),
        out_shape=(
            jax.ShapeDtypeStruct((height, width), F32),
            jax.ShapeDtypeStruct((g_rows * col_count, width), psi.dtype),
        ),
        in_specs=[pl.BlockSpec(memory_space=pltpu.SMEM)] + [vmem() for _ in range(7)],
        out_specs=(vmem(), vmem()),
        scratch_shapes=[pltpu.VMEM(state.shape, F32), pltpu.VMEM(state.shape, F32)],
        compiler_params=pltpu.CompilerParams(vmem_limit_bytes=24 * MIB),
        name="update",
    )(where, recv, vecs, images, marks, reduced, psi_rows, turn.reshape(bands, width))

    tile_shape = (row_tiles, 1, tile_size, col_tiles, 1, tile_size)
    return (
        reduced[0, height:].reshape(tile_shape),
        updated.reshape(tile_shape),
        marks[0, :PB],
        marks[1, :PB],
        rotated.reshape(g_rows * col_count, col_tiles, 1, tile_size),
    )


def solution(mesh):
    return jax.shard_map(
        on_device,
        mesh=mesh,
        in_specs=(
            P(("row", "col"), None),
            P(("row", "col"), None),
            P(None, "row", None, None, "col", None),
        ),
        out_specs=(
            P(None, "row", None, None, "col", None),
            P(None, "row", None, None, "col", None),
            P(),
            P(),
            P("row", None, "col", None),
        ),
        check_vma=False,
    )
```

time: 483 us -> 453 us (0.938)
  local copies, waits for them, and re-layouts: 42.6 us -> 13.4 us
  Pallas kernels: 48.7 us -> 72.7 us
  waiting for transfers between devices: 260 us -> 237 us
  starting transfers between devices: 94.4 us -> 112 us
  matrix products: 11.5 us -> 0 us
  other arithmetic: 9.63 us -> 1.95 us
    all_gather x1, waiting for transfers between devices: 38.2 us -> 0.01 us  [on_device(): lax.all_gather(eigvec.reshape(row_tiles, tile_size, width), 'row', axis=1)]
    pallas_call x17 -> x18, Pallas kernels: 48.7 us -> 72.7 us  [the longest x16 60.6 us: one(): advance(jnp.reshape(step, (1,)).astype(jnp.int32), recv, strip, vecs, ima...]
    all_to_all x18 -> x17, starting transfers between devices: 94.2 us -> 112 us  [exchange(): return lax.all_to_all(send, ('row', 'col'), 0, 0, tiled=True)]
    all_to_all x18 -> x17, waiting for transfers between devices: 167 us -> 182 us  [exchange(): return lax.all_to_all(send, ('row', 'col'), 0, 0, tiled=True)]
    all_to_all x16 -> x0, local copies, waits for them, and re-layouts: 12.7 us -> none  [one(): recv = lax.all_to_all(send, ('row', 'col'), 0, 0, tiled=True)]
    dot_general x2 -> x0, matrix products: 11.5 us -> none  [the longest x1 7.41 us: on_device(): lax.dot_general(left, flat.reshape(k, col_tiles, col_count, tile_size), (...]
    dynamic_slice x1 -> x0, local copies, waits for them, and re-layouts: 5.79 us -> none  [on_device(): lax.dynamic_index_in_dim(both.reshape(row_count, 2, g_rows, row_tiles, ro...]
    unnamed x7 -> x8, local copies, waits for them, and re-layouts: 14.1 us -> 8.38 us
  transfers between devices with their start and end apart: 22 -> 21, of which waited for: 19 -> 18; matrix products, arithmetic and copies ran while one was open for 11% -> 1% of each run, Pallas kernels for 10% -> 16%
where the time goes in v2:
time: 453 us; the launch traced here: 451 us
  waiting for transfers between devices  237 us (52%)
  starting transfers between devices  112 us (25%)
  Pallas kernels  72.7 us (16%)
  between operations  13.8 us (3%)
  local copies, waits for them, and re-layouts  13.4 us (3%)
    all_to_all x17, waiting for transfers between devices, exchange(): return lax.all_to_all(send, ('row', 'col'), 0, 0, tiled=True)  182 us
    all_to_all x17, starting transfers between devices, exchange(): return lax.all_to_all(send, ('row', 'col'), 0, 0, tiled=True)  112 us
    pallas_call x16, Pallas kernels, one(): advance(jnp.reshape(step, (1,)).astype(jnp.int32), recv, strip, vecs, ima...  60.6 us
    all_gather x1, waiting for transfers between devices, on_device(): both = lax.all_gather(jnp.stack([psi, hpsi]), 'row')  54.2 us
    pallas_call x1, Pallas kernels, on_device(): pl.pallas_call(functools.partial(products_body, row_tiles=row_tiles, col_...  9.75 us
  transfers between devices with their start and end apart: 21, of which 18 were waited for; matrix products, arithmetic and copies ran while one was open for 1% of the time, Pallas kernels for 16%

profile of v2, /device:TPU:1, one launch (start us, length us, event | category | flops | bytes accessed | tf_op | source)
XLA Modules:
  0.0 450.8 jit_solution(1544205007080413179)
XLA Ops:
  11.8 54.2 %all-gather.9.cloned.1.call-done = bf16[32,32,4096]{2,1,0:T(8,128)(2,1)} async-done(((bf16[2,32,4096]{2,1,0:T(8,128)(2,1)}), bf16[32,32,4096]{2,1,0:T(8,128)(2,1)}) %all-gather.9.cloned.1.call-update) | async-done | bytes 8388624 | tf_op jit(solution)/shard_map/all_gather | solution.py:191
  69.4 9.8 %products.1 = (f32[8,512,512]{2,1,0:T(8,128)}, f32[16,256]{1,0:T(8,128)S(1)}, f32[128,1,512]{2,1,0:T(1,128)}) custom-call(s32[2]{0:T(128)S(1)} %pad_add_fusion.where_ref, bf16[16,2,32,4096]{3,2,1,0:T(8,128)(2,1)S(1)} %bitcast.19, bf16[16,2,32,4096]{3,2,1,0:T(8,128)(2,1)S(1)} %bitcast.20, bf16[16,2,32,4096]{3,2,1,0:T(8,128)(2,1)S(1)} %bitcast.21, ...), custom_call_target="tpu_custom_call" | custom-call | tf_op jit(solution)/shard_map/products/pallas_call | solution.py:207
  79.1 8.9 %all-to-all-start.1 = ((f32[128,1,512]{2,1,0:T(1,128)}), f32[128,1,512]{2,1,0:T(1,128)S(1)}, u32[]{:S(2)}, u32[]{:S(2)}) async-start(f32[128,1,512]{2,1,0:T(1,128)} %get-tuple-element.132), calls=%async_computation.2 | async-start | bytes 524288 | tf_op jit(solution)/shard_map/all_to_all | solution.py:253
  88.0 10.2 %all-to-all-done.1 = f32[128,1,512]{2,1,0:T(1,128)S(1)} async-done(((f32[128,1,512]{2,1,0:T(1,128)}), f32[128,1,512]{2,1,0:T(1,128)S(1)}, u32[]{:S(2)}, u32[]{:S(2)}) %all-to-all-start.1) | async-done | bytes 262176 | tf_op jit(solution)/shard_map/all_to_all | solution.py:253
  98.3 335.5 %while.19 = (s32[]{:T(128)}, f32[128,1,512]{2,1,0:T(1,128)S(1)}, f32[16,32,128]{2,1,0:T(8,128)S(1)}, f32[16,32,128]{2,1,0:T(8,128)S(1)}, f32[8,128]{1,0:T(8,128)...) while((s32[]{:T(128)}, f32[128,1,512]{2,1,0:T(1,128)S(1)}, ...), condition=%wide.region_2.0_spmd, body=%wide.region_1.0_spmd.sunk | while | flops 2 | bytes 786549 | solution.py:268
  98.3 3.8 reflect.5
  102.1 5.2 %all-to-all-start = ((f32[128,1,512]{2,1,0:T(1,128)}), f32[128,1,512]{2,1,0:T(1,128)S(1)}, u32[]{:S(2)}, u32[]{:S(2)}) async-start(f32[128,1,512]{2,1,0:T(1,128)} %get-tuple-element.213), calls=%async_computation | async-start | bytes 524288 | tf_op jit(solution)/shard_map/while/body/eval_jaxpr/all_to_all | solution.py:253
  107.3 12.9 %all-to-all-done = f32[128,1,512]{2,1,0:T(1,128)S(1)} async-done(((f32[128,1,512]{2,1,0:T(1,128)}), f32[128,1,512]{2,1,0:T(1,128)S(1)}, u32[]{:S(2)}, u32[]{:S(2)}) %all-to-all-start) | async-done | bytes 262176 | tf_op jit(solution)/shard_map/while/body/eval_jaxpr/all_to_all | solution.py:253
  120.1 3.8 reflect.5
  123.9 5.6 %all-to-all-start = ((f32[128,1,512]{2,1,0:T(1,128)}), f32[128,1,512]{2,1,0:T(1,128)S(1)}, u32[]{:S(2)}, u32[]{:S(2)}) async-start(f32[128,1,512]{2,1,0:T(1,128)} %get-tuple-element.213), calls=%async_computation | async-start | bytes 524288 | tf_op jit(solution)/shard_map/while/body/eval_jaxpr/all_to_all | solution.py:253
  129.6 10.2 %all-to-all-done = f32[128,1,512]{2,1,0:T(1,128)S(1)} async-done(((f32[128,1,512]{2,1,0:T(1,128)}), f32[128,1,512]{2,1,0:T(1,128)S(1)}, u32[]{:S(2)}, u32[]{:S(2)}) %all-to-all-start) | async-done | bytes 262176 | tf_op jit(solution)/shard_map/while/body/eval_jaxpr/all_to_all | solution.py:253
  139.8 3.8 reflect.5
  143.7 5.1 %all-to-all-start = ((f32[128,1,512]{2,1,0:T(1,128)}), f32[128,1,512]{2,1,0:T(1,128)S(1)}, u32[]{:S(2)}, u32[]{:S(2)}) async-start(f32[128,1,512]{2,1,0:T(1,128)} %get-tuple-element.213), calls=%async_computation | async-start | bytes 524288 | tf_op jit(solution)/shard_map/while/body/eval_jaxpr/all_to_all | solution.py:253
  148.8 11.3 %all-to-all-done = f32[128,1,512]{2,1,0:T(1,128)S(1)} async-done(((f32[128,1,512]{2,1,0:T(1,128)}), f32[128,1,512]{2,1,0:T(1,128)S(1)}, u32[]{:S(2)}, u32[]{:S(2)}) %all-to-all-start) | async-done | bytes 262176 | tf_op jit(solution)/shard_map/while/body/eval_jaxpr/all_to_all | solution.py:253
  160.1 3.8 reflect.5
  163.9 6.8 %all-to-all-start = ((f32[128,1,512]{2,1,0:T(1,128)}), f32[128,1,512]{2,1,0:T(1,128)S(1)}, u32[]{:S(2)}, u32[]{:S(2)}) async-start(f32[128,1,512]{2,1,0:T(1,128)} %get-tuple-element.213), calls=%async_computation | async-start | bytes 524288 | tf_op jit(solution)/shard_map/while/body/eval_jaxpr/all_to_all | solution.py:253
  170.8 10.2 %all-to-all-done = f32[128,1,512]{2,1,0:T(1,128)S(1)} async-done(((f32[128,1,512]{2,1,0:T(1,128)}), f32[128,1,512]{2,1,0:T(1,128)S(1)}, u32[]{:S(2)}, u32[]{:S(2)}) %all-to-all-start) | async-done | bytes 262176 | tf_op jit(solution)/shard_map/while/body/eval_jaxpr/all_to_all | solution.py:253
  184.7 5.2 %all-to-all-start = ((f32[128,1,512]{2,1,0:T(1,128)}), f32[128,1,512]{2,1,0:T(1,128)S(1)}, u32[]{:S(2)}, u32[]{:S(2)}) async-start(f32[128,1,512]{2,1,0:T(1,128)} %get-tuple-element.213), calls=%async_computation | async-start | bytes 524288 | tf_op jit(solution)/shard_map/while/body/eval_jaxpr/all_to_all | solution.py:253
  190.0 11.4 %all-to-all-done = f32[128,1,512]{2,1,0:T(1,128)S(1)} async-done(((f32[128,1,512]{2,1,0:T(1,128)}), f32[128,1,512]{2,1,0:T(1,128)S(1)}, u32[]{:S(2)}, u32[]{:S(2)}) %all-to-all-start) | async-done | bytes 262176 | tf_op jit(solution)/shard_map/while/body/eval_jaxpr/all_to_all | solution.py:253
  201.4 3.9 reflect.5
  205.4 4.4 all-to-all-start
  209.8 11.1 %all-to-all-done = f32[128,1,512]{2,1,0:T(1,128)S(1)} async-done(((f32[128,1,512]{2,1,0:T(1,128)}), f32[128,1,512]{2,1,0:T(1,128)S(1)}, u32[]{:S(2)}, u32[]{:S(2)}) %all-to-all-start) | async-done | bytes 262176 | tf_op jit(solution)/shard_map/while/body/eval_jaxpr/all_to_all | solution.py:253
  221.0 3.9 reflect.5
  224.8 5.9 %all-to-all-start = ((f32[128,1,512]{2,1,0:T(1,128)}), f32[128,1,512]{2,1,0:T(1,128)S(1)}, u32[]{:S(2)}, u32[]{:S(2)}) async-start(f32[128,1,512]{2,1,0:T(1,128)} %get-tuple-element.213), calls=%async_computation | async-start | bytes 524288 | tf_op jit(solution)/shard_map/while/body/eval_jaxpr/all_to_all | solution.py:253
  230.7 11.4 %all-to-all-done = f32[128,1,512]{2,1,0:T(1,128)S(1)} async-done(((f32[128,1,512]{2,1,0:T(1,128)}), f32[128,1,512]{2,1,0:T(1,128)S(1)}, u32[]{:S(2)}, u32[]{:S(2)}) %all-to-all-start) | async-done | bytes 262176 | tf_op jit(solution)/shard_map/while/body/eval_jaxpr/all_to_all | solution.py:253
  242.1 3.8 reflect.5
  245.9 15.0 %all-to-all-start = ((f32[128,1,512]{2,1,0:T(1,128)}), f32[128,1,512]{2,1,0:T(1,128)S(1)}, u32[]{:S(2)}, u32[]{:S(2)}) async-start(f32[128,1,512]{2,1,0:T(1,128)} %get-tuple-element.213), calls=%async_computation | async-start | bytes 524288 | tf_op jit(solution)/shard_map/while/body/eval_jaxpr/all_to_all | solution.py:253
  260.9 11.2 %all-to-all-done = f32[128,1,512]{2,1,0:T(1,128)S(1)} async-done(((f32[128,1,512]{2,1,0:T(1,128)}), f32[128,1,512]{2,1,0:T(1,128)S(1)}, u32[]{:S(2)}, u32[]{:S(2)}) %all-to-all-start) | async-done | bytes 262176 | tf_op jit(solution)/shard_map/while/body/eval_jaxpr/all_to_all | solution.py:253
  272.1 3.8 reflect.5
  275.9 13.3 %all-to-all-start = ((f32[128,1,512]{2,1,0:T(1,128)}), f32[128,1,512]{2,1,0:T(1,128)S(1)}, u32[]{:S(2)}, u32[]{:S(2)}) async-start(f32[128,1,512]{2,1,0:T(1,128)} %get-tuple-element.213), calls=%async_computation | async-start | bytes 524288 | tf_op jit(solution)/shard_map/while/body/eval_jaxpr/all_to_all | solution.py:253
  289.3 10.2 %all-to-all-done = f32[128,1,512]{2,1,0:T(1,128)S(1)} async-done(((f32[128,1,512]{2,1,0:T(1,128)}), f32[128,1,512]{2,1,0:T(1,128)S(1)}, u32[]{:S(2)}, u32[]{:S(2)}) %all-to-all-start) | async-done | bytes 262176 | tf_op jit(solution)/shard_map/while/body/eval_jaxpr/all_to_all | solution.py:253
  299.5 3.8 reflect.5
  303.3 5.2 %all-to-all-start = ((f32[128,1,512]{2,1,0:T(1,128)}), f32[128,1,512]{2,1,0:T(1,128)S(1)}, u32[]{:S(2)}, u32[]{:S(2)}) async-start(f32[128,1,512]{2,1,0:T(1,128)} %get-tuple-element.213), calls=%async_computation | async-start | bytes 524288 | tf_op jit(solution)/shard_map/while/body/eval_jaxpr/all_to_all | solution.py:253
  308.5 10.2 %all-to-all-done = f32[128,1,512]{2,1,0:T(1,128)S(1)} async-done(((f32[128,1,512]{2,1,0:T(1,128)}), f32[128,1,512]{2,1,0:T(1,128)S(1)}, u32[]{:S(2)}, u32[]{:S(2)}) %all-to-all-start) | async-done | bytes 262176 | tf_op jit(solution)/shard_map/while/body/eval_jaxpr/all_to_all | solution.py:253
  322.4 5.2 %all-to-all-start = ((f32[128,1,512]{2,1,0:T(1,128)}), f32[128,1,512]{2,1,0:T(1,128)S(1)}, u32[]{:S(2)}, u32[]{:S(2)}) async-start(f32[128,1,512]{2,1,0:T(1,128)} %get-tuple-element.213), calls=%async_computation | async-start | bytes 524288 | tf_op jit(solution)/shard_map/while/body/eval_jaxpr/all_to_all | solution.py:253
  327.6 10.2 %all-to-all-done = f32[128,1,512]{2,1,0:T(1,128)S(1)} async-done(((f32[128,1,512]{2,1,0:T(1,128)}), f32[128,1,512]{2,1,0:T(1,128)S(1)}, u32[]{:S(2)}, u32[]{:S(2)}) %all-to-all-start) | async-done | bytes 262176 | tf_op jit(solution)/shard_map/while/body/eval_jaxpr/all_to_all | solution.py:253
  337.9 3.8 reflect.5
  341.6 5.2 %all-to-all-start = ((f32[128,1,512]{2,1,0:T(1,128)}), f32[128,1,512]{2,1,0:T(1,128)S(1)}, u32[]{:S(2)}, u32[]{:S(2)}) async-start(f32[128,1,512]{2,1,0:T(1,128)} %get-tuple-element.213), calls=%async_computation | async-start | bytes 524288 | tf_op jit(solution)/shard_map/while/body/eval_jaxpr/all_to_all | solution.py:253
  346.8 10.2 %all-to-all-done = f32[128,1,512]{2,1,0:T(1,128)S(1)} async-done(((f32[128,1,512]{2,1,0:T(1,128)}), f32[128,1,512]{2,1,0:T(1,128)S(1)}, u32[]{:S(2)}, u32[]{:S(2)}) %all-to-all-start) | async-done | bytes 262176 | tf_op jit(solution)/shard_map/while/body/eval_jaxpr/all_to_all | solution.py:253
  360.8 5.2 %all-to-all-start = ((f32[128,1,512]{2,1,0:T(1,128)}), f32[128,1,512]{2,1,0:T(1,128)S(1)}, u32[]{:S(2)}, u32[]{:S(2)}) async-start(f32[128,1,512]{2,1,0:T(1,128)} %get-tuple-element.213), calls=%async_computation | async-start | bytes 524288 | tf_op jit(solution)/shard_map/while/body/eval_jaxpr/all_to_all | solution.py:253
  366.0 10.2 %all-to-all-done = f32[128,1,512]{2,1,0:T(1,128)S(1)} async-done(((f32[128,1,512]{2,1,0:T(1,128)}), f32[128,1,512]{2,1,0:T(1,128)S(1)}, u32[]{:S(2)}, u32[]{:S(2)}) %all-to-all-start) | async-done | bytes 262176 | tf_op jit(solution)/shard_map/while/body/eval_jaxpr/all_to_all | solution.py:253
  380.0 5.2 %all-to-all-start = ((f32[128,1,512]{2,1,0:T(1,128)}), f32[128,1,512]{2,1,0:T(1,128)S(1)}, u32[]{:S(2)}, u32[]{:S(2)}) async-start(f32[128,1,512]{2,1,0:T(1,128)} %get-tuple-element.213), calls=%async_computation | async-start | bytes 524288 | tf_op jit(solution)/shard_map/while/body/eval_jaxpr/all_to_all | solution.py:253
  385.2 10.2 %all-to-all-done = f32[128,1,512]{2,1,0:T(1,128)S(1)} async-done(((f32[128,1,512]{2,1,0:T(1,128)}), f32[128,1,512]{2,1,0:T(1,128)S(1)}, u32[]{:S(2)}, u32[]{:S(2)}) %all-to-all-start) | async-done | bytes 262176 | tf_op jit(solution)/shard_map/while/body/eval_jaxpr/all_to_all | solution.py:253
  395.4 3.8 reflect.5
  399.2 5.2 %all-to-all-start = ((f32[128,1,512]{2,1,0:T(1,128)}), f32[128,1,512]{2,1,0:T(1,128)S(1)}, u32[]{:S(2)}, u32[]{:S(2)}) async-start(f32[128,1,512]{2,1,0:T(1,128)} %get-tuple-element.213), calls=%async_computation | async-start | bytes 524288 | tf_op jit(solution)/shard_map/while/body/eval_jaxpr/all_to_all | solution.py:253
  404.4 10.2 %all-to-all-done = f32[128,1,512]{2,1,0:T(1,128)S(1)} async-done(((f32[128,1,512]{2,1,0:T(1,128)}), f32[128,1,512]{2,1,0:T(1,128)S(1)}, u32[]{:S(2)}, u32[]{:S(2)}) %all-to-all-start) | async-done | bytes 262176 | tf_op jit(solution)/shard_map/while/body/eval_jaxpr/all_to_all | solution.py:253
  418.3 5.2 %all-to-all-start = ((f32[128,1,512]{2,1,0:T(1,128)}), f32[128,1,512]{2,1,0:T(1,128)S(1)}, u32[]{:S(2)}, u32[]{:S(2)}) async-start(f32[128,1,512]{2,1,0:T(1,128)} %get-tuple-element.213), calls=%async_computation | async-start | bytes 524288 | tf_op jit(solution)/shard_map/while/body/eval_jaxpr/all_to_all | solution.py:253
  423.5 10.2 %all-to-all-done = f32[128,1,512]{2,1,0:T(1,128)S(1)} async-done(((f32[128,1,512]{2,1,0:T(1,128)}), f32[128,1,512]{2,1,0:T(1,128)S(1)}, u32[]{:S(2)}, u32[]{:S(2)}) %all-to-all-start) | async-done | bytes 262176 | tf_op jit(solution)/shard_map/while/body/eval_jaxpr/all_to_all | solution.py:253
  (37 shorter events, 37.3 us)
Async XLA Ops:
  7.2 58.8 %all-gather.9.cloned.1.call-start = ((), (), s32[]{:S(2)}) async-start(), calls=%async_computation.6 | async-start | bytes 8912896 | tf_op jit(solution)/shard_map/all_gather | solution.py:191
  9.1 425.2 %all-gather.5.cloned.1.call-start = ((), (), s32[]{:S(2)}) async-start(), calls=%async_computation.4 | async-start | bytes 2359296 | tf_op jit(solution)/shard_map/all_gather | solution.py:192
  9.9 424.4 %all-gather.7.cloned.1.call-start = ((), (), s32[]{:S(2)}) async-start(), calls=%async_computation.5 | async-start | bytes 4456448 | tf_op jit(solution)/shard_map/all_gather | solution.py:193
  11.7 422.6 %reduce-scatter.2.cloned.1.call-start = ((), (), s32[]{:S(2)}) async-start(), calls=%async_computation.3 | async-start | bytes 9437184 | tf_op jit(solution)/shard_map/reduce_scatter | solution.py:232
  66.0 3.4 copy-start
  79.1 19.1 %all-to-all-start.1 = ((f32[128,1,512]{2,1,0:T(1,128)}), f32[128,1,512]{2,1,0:T(1,128)S(1)}, u32[]{:S(2)}, u32[]{:S(2)}) async-start(f32[128,1,512]{2,1,0:T(1,128)} %get-tuple-element.132), calls=%async_computation.2 | async-start | bytes 524288 | tf_op jit(solution)/shard_map/all_to_all | solution.py:253
  102.1 18.1 %all-to-all-start = ((f32[128,1,512]{2,1,0:T(1,128)}), f32[128,1,512]{2,1,0:T(1,128)S(1)}, u32[]{:S(2)}, u32[]{:S(2)}) async-start(f32[128,1,512]{2,1,0:T(1,128)} %get-tuple-element.213), calls=%async_computation | async-start | bytes 524288 | tf_op jit(solution)/shard_map/while/body/eval_jaxpr/all_to_all | solution.py:253
  123.9 15.9 %all-to-all-start = ((f32[128,1,512]{2,1,0:T(1,128)}), f32[128,1,512]{2,1,0:T(1,128)S(1)}, u32[]{:S(2)}, u32[]{:S(2)}) async-start(f32[128,1,512]{2,1,0:T(1,128)} %get-tuple-element.213), calls=%async_computation | async-start | bytes 524288 | tf_op jit(solution)/shard_map/while/body/eval_jaxpr/all_to_all | solution.py:253
  143.7 16.5 %all-to-all-start = ((f32[128,1,512]{2,1,0:T(1,128)}), f32[128,1,512]{2,1,0:T(1,128)S(1)}, u32[]{:S(2)}, u32[]{:S(2)}) async-start(f32[128,1,512]{2,1,0:T(1,128)} %get-tuple-element.213), calls=%async_computation | async-start | bytes 524288 | tf_op jit(solution)/shard_map/while/body/eval_jaxpr/all_to_all | solution.py:253
  163.9 17.0 %all-to-all-start = ((f32[128,1,512]{2,1,0:T(1,128)}), f32[128,1,512]{2,1,0:T(1,128)S(1)}, u32[]{:S(2)}, u32[]{:S(2)}) async-start(f32[128,1,512]{2,1,0:T(1,128)} %get-tuple-element.213), calls=%async_computation | async-start | bytes 524288 | tf_op jit(solution)/shard_map/while/body/eval_jaxpr/all_to_all | solution.py:253
  184.7 16.7 %all-to-all-start = ((f32[128,1,512]{2,1,0:T(1,128)}), f32[128,1,512]{2,1,0:T(1,128)S(1)}, u32[]{:S(2)}, u32[]{:S(2)}) async-start(f32[128,1,512]{2,1,0:T(1,128)} %get-tuple-element.213), calls=%async_computation | async-start | bytes 524288 | tf_op jit(solution)/shard_map/while/body/eval_jaxpr/all_to_all | solution.py:253
  205.4 15.6 %all-to-all-start = ((f32[128,1,512]{2,1,0:T(1,128)}), f32[128,1,512]{2,1,0:T(1,128)S(1)}, u32[]{:S(2)}, u32[]{:S(2)}) async-start(f32[128,1,512]{2,1,0:T(1,128)} %get-tuple-element.213), calls=%async_computation | async-start | bytes 524288 | tf_op jit(solution)/shard_map/while/body/eval_jaxpr/all_to_all | solution.py:253
  224.8 17.3 %all-to-all-start = ((f32[128,1,512]{2,1,0:T(1,128)}), f32[128,1,512]{2,1,0:T(1,128)S(1)}, u32[]{:S(2)}, u32[]{:S(2)}) async-start(f32[128,1,512]{2,1,0:T(1,128)} %get-tuple-element.213), calls=%async_computation | async-start | bytes 524288 | tf_op jit(solution)/shard_map/while/body/eval_jaxpr/all_to_all | solution.py:253
  245.9 26.2 %all-to-all-start = ((f32[128,1,512]{2,1,0:T(1,128)}), f32[128,1,512]{2,1,0:T(1,128)S(1)}, u32[]{:S(2)}, u32[]{:S(2)}) async-start(f32[128,1,512]{2,1,0:T(1,128)} %get-tuple-element.213), calls=%async_computation | async-start | bytes 524288 | tf_op jit(solution)/shard_map/while/body/eval_jaxpr/all_to_all | solution.py:253
  275.9 23.6 %all-to-all-start = ((f32[128,1,512]{2,1,0:T(1,128)}), f32[128,1,512]{2,1,0:T(1,128)S(1)}, u32[]{:S(2)}, u32[]{:S(2)}) async-start(f32[128,1,512]{2,1,0:T(1,128)} %get-tuple-element.213), calls=%async_computation | async-start | bytes 524288 | tf_op jit(solution)/shard_map/while/body/eval_jaxpr/all_to_all | solution.py:253
  303.3 15.4 %all-to-all-start = ((f32[128,1,512]{2,1,0:T(1,128)}), f32[128,1,512]{2,1,0:T(1,128)S(1)}, u32[]{:S(2)}, u32[]{:S(2)}) async-start(f32[128,1,512]{2,1,0:T(1,128)} %get-tuple-element.213), calls=%async_computation | async-start | bytes 524288 | tf_op jit(solution)/shard_map/while/body/eval_jaxpr/all_to_all | solution.py:253
  322.4 15.4 %all-to-all-start = ((f32[128,1,512]{2,1,0:T(1,128)}), f32[128,1,512]{2,1,0:T(1,128)S(1)}, u32[]{:S(2)}, u32[]{:S(2)}) async-start(f32[128,1,512]{2,1,0:T(1,128)} %get-tuple-element.213), calls=%async_computation | async-start | bytes 524288 | tf_op jit(solution)/shard_map/while/body/eval_jaxpr/all_to_all | solution.py:253
  341.6 15.4 %all-to-all-start = ((f32[128,1,512]{2,1,0:T(1,128)}), f32[128,1,512]{2,1,0:T(1,128)S(1)}, u32[]{:S(2)}, u32[]{:S(2)}) async-start(f32[128,1,512]{2,1,0:T(1,128)} %get-tuple-element.213), calls=%async_computation | async-start | bytes 524288 | tf_op jit(solution)/shard_map/while/body/eval_jaxpr/all_to_all | solution.py:253
  360.8 15.4 %all-to-all-start = ((f32[128,1,512]{2,1,0:T(1,128)}), f32[128,1,512]{2,1,0:T(1,128)S(1)}, u32[]{:S(2)}, u32[]{:S(2)}) async-start(f32[128,1,512]{2,1,0:T(1,128)} %get-tuple-element.213), calls=%async_computation | async-start | bytes 524288 | tf_op jit(solution)/shard_map/while/body/eval_jaxpr/all_to_all | solution.py:253
  380.0 15.4 %all-to-all-start = ((f32[128,1,512]{2,1,0:T(1,128)}), f32[128,1,512]{2,1,0:T(1,128)S(1)}, u32[]{:S(2)}, u32[]{:S(2)}) async-start(f32[128,1,512]{2,1,0:T(1,128)} %get-tuple-element.213), calls=%async_computation | async-start | bytes 524288 | tf_op jit(solution)/shard_map/while/body/eval_jaxpr/all_to_all | solution.py:253
  399.2 15.4 %all-to-all-start = ((f32[128,1,512]{2,1,0:T(1,128)}), f32[128,1,512]{2,1,0:T(1,128)S(1)}, u32[]{:S(2)}, u32[]{:S(2)}) async-start(f32[128,1,512]{2,1,0:T(1,128)} %get-tuple-element.213), calls=%async_computation | async-start | bytes 524288 | tf_op jit(solution)/shard_map/while/body/eval_jaxpr/all_to_all | solution.py:253
  418.3 15.4 %all-to-all-start = ((f32[128,1,512]{2,1,0:T(1,128)}), f32[128,1,512]{2,1,0:T(1,128)S(1)}, u32[]{:S(2)}, u32[]{:S(2)}) async-start(f32[128,1,512]{2,1,0:T(1,128)} %get-tuple-element.213), calls=%async_computation | async-start | bytes 524288 | tf_op jit(solution)/shard_map/while/body/eval_jaxpr/all_to_all | solution.py:253
  434.3 2.2 copy-start.1
  436.5 1.2 copy-start.2
  437.7 1.6 copy-start.3
  439.3 4.0 slice-start
Sparse Core Ops, SparseCore 0:
  10.3 55.6 all-gather.8
  68.3 57.5 all-gather.4
  128.2 38.7 all-gather.6
  170.6 119.5 reduce-scatter.1

commit v3 on v2

v3 whole, which is shorter than its diff:
```python
import functools

import jax
import jax.numpy as jnp
from jax import lax
from jax.experimental import pallas as pl
from jax.experimental.pallas import tpu as pltpu
from jax.sharding import PartitionSpec as P

PB = 16
WIDE = 5
LANES = 128
F32 = jnp.float32
MIB = 1024 * 1024


def total(x):
    return jnp.sum(jnp.sum(x, axis=-2, keepdims=True), axis=-1, keepdims=True)


def over_k(left, right):
    return lax.dot_general(left, right, (((1,), (0,)), ((), ())), preferred_element_type=F32)


def products_body(where_ref, *refs, row_tiles, col_tiles, gvecs):
    rows = refs[:row_tiles]
    head_ref = refs[row_tiles]
    cols = refs[row_tiles + 1 : row_tiles + 1 + col_tiles]
    matrix_out, overlap_out, strip_out, left_vmem, left_psi_vmem = refs[row_tiles + 1 + col_tiles :]
    height = row_tiles * LANES

    def swapped(x):
        return jnp.concatenate([x[:, 1:2], x[:, 0:1]], axis=1).reshape(-1, LANES)

    @pl.when(pl.program_id(0) == 0)
    def _():
        for k, ref in enumerate(rows):
            at = pl.ds(k * LANES, LANES)
            left_vmem[at, :] = swapped(ref[...]).T
            left_psi_vmem[at, :] = ref[:, 0].reshape(-1, LANES).T
        left_vmem[height:, :] = swapped(head_ref[...]).T[:PB]

    both = jnp.concatenate([ref[...].reshape(-1, LANES) for ref in cols], axis=1)
    psi = jnp.concatenate([ref[:, 0].reshape(-1, LANES) for ref in cols], axis=1)
    mixed = 0.5 * over_k(left_vmem[...], both)
    matrix_out[0] = mixed[:height]
    strip_out[0] = mixed[height:]
    overlap_out[0] = over_k(left_psi_vmem[...], psi) * (1.0 / gvecs)


def gathered(recv_ref, row_count):
    recv = recv_ref[...]
    count = recv.shape[0] // row_count
    if count > 1:
        recv = jnp.sum(recv.reshape(row_count, count, *recv.shape[1:]), axis=1)
    return recv.reshape(1, -1, LANES)


def finish_image(image, vecs, images, vector, tau):
    along_w = total(images * vector)
    along_v = total(vecs * vector)
    image = image - jnp.sum(vecs * along_w + images * along_v, axis=0, keepdims=True)
    image = tau * image
    return image - 0.5 * tau * total(image * vector) * vector


def place(into, what, slot):
    slots = lax.broadcasted_iota(jnp.int32, (PB, 1, 1), 0)
    return jnp.where(slots == slot, what, into)


def spot_of(tile, row_count, row_tiles):
    return (tile % row_count) * row_tiles + tile // row_count


def step_body(
    step_ref, recv_ref, panel_ref, vecs_ref, images_ref, marks_ref, matrix_ref,
    vecs_out, images_out, marks_out, send_out, matrix_vmem, sem, *, row_count,
):
    step = step_ref[0]
    tiles = vecs_ref.shape[1]
    col_count, height, width = matrix_ref.shape
    copy = pltpu.make_async_copy(matrix_ref, matrix_vmem, sem)
    copy.start()
    row_tiles = height // LANES
    col_tiles = width // LANES
    lane = lax.broadcasted_iota(jnp.int32, (1, 1, LANES), 2)
    marks = marks_ref[...]
    vecs = vecs_ref[...]
    images = images_ref[...]
    before = jnp.maximum(step - 1, 0)
    vector = vecs_ref[pl.ds(before, 1)]
    tau = marks[2:3, 0:1].reshape(1, 1, 1)
    image = finish_image(gathered(recv_ref, row_count), vecs, images, vector, tau)
    images = place(images, image, step - 1)
    images_out[...] = images
    head_w = jnp.sum(jnp.where(lane == step, images[:, 0:1, :], 0.0), axis=-1, keepdims=True)
    head_v = jnp.sum(jnp.where(lane == step, vecs[:, 0:1, :], 0.0), axis=-1, keepdims=True)
    column = panel_ref[pl.ds(step, 1)] - jnp.sum(
        vecs * head_w + images * head_v, axis=0, keepdims=True
    )
    shape = (1, tiles, LANES)
    spot = lax.broadcasted_iota(jnp.int32, shape, 1)
    tile = lax.div(spot, row_tiles) + lax.rem(spot, row_tiles) * row_count
    positions = tile * LANES + lax.broadcasted_iota(jnp.int32, shape, 2)
    below = positions > step + 1
    pivot = total(jnp.where(positions == step + 1, column, 0.0))
    tail = total(jnp.where(below, column * column, 0.0))
    corner = total(jnp.where(positions == step, column, 0.0))
    length = jnp.sqrt(pivot * pivot + tail)
    beta = jnp.where(pivot >= 0.0, -length, length)
    tau = (beta - pivot) / beta
    vector = jnp.where(positions == step + 1, 1.0, jnp.where(below, column / (pivot - beta), 0.0))
    vecs_out[...] = place(vecs, vector, step)
    row = lax.broadcasted_iota(jnp.int32, marks.shape, 0)
    mark = lax.broadcasted_iota(jnp.int32, marks.shape, 1) == step
    flat = marks.shape
    marks = jnp.where((row == 0) & mark, jnp.broadcast_to(corner[0], flat), marks)
    marks = jnp.where((row == 1) & mark, jnp.broadcast_to(beta[0], flat), marks)
    marks_out[...] = jnp.where(row == 2, jnp.broadcast_to(tau[0], flat), marks)
    copy.wait()
    sums = jnp.zeros((height, LANES), F32)
    for c in range(col_count):
        for a in range(col_tiles):
            at = spot_of(a * col_count + c, row_count, row_tiles)
            sums = sums + matrix_vmem[c, :, a * LANES : (a + 1) * LANES] * vector[0, at : at + 1, :]
    send = jnp.concatenate(
        [
            jnp.sum(sums[k * LANES : (k + 1) * LANES].T, axis=0, keepdims=True)
            for k in range(row_tiles)
        ],
        axis=0,
    )
    send_out[...] = jnp.broadcast_to(send[None], send_out.shape)


def last_body(
    where_ref, recv_ref, vecs_ref, images_ref, marks_ref, matrix_ref, psi_ref, turn_ref,
    updated_out, rotated_out, tile_vmem, vecs_vmem, images_vmem, sem, *, row_count,
):
    row_id = where_ref[0]
    col_id = where_ref[1]
    copy = pltpu.make_async_copy(matrix_ref.at[col_id], tile_vmem, sem)
    copy.start()
    rotated_out[...] = over_k(psi_ref[...], turn_ref[...]).astype(rotated_out.dtype)
    height, width = updated_out.shape
    row_tiles = height // LANES
    col_tiles = width // LANES
    col_count = matrix_ref.shape[0]
    vecs = vecs_ref[...]
    vector = vecs_ref[PB - 1 : PB]
    tau = marks_ref[2:3, 0:1].reshape(1, 1, 1)
    image = finish_image(gathered(recv_ref, row_count), vecs, images_ref[...], vector, tau)
    images_vmem[...] = place(images_ref[...], image, PB - 1)
    vecs_vmem[...] = vecs

    def part(ref, tile):
        at = lax.rem(tile, row_count) * row_tiles + lax.div(tile, row_count)
        return ref[:, pl.ds(at, 1), :].reshape(PB, LANES)

    lefts = [
        jnp.concatenate([part(vecs_vmem, at), part(images_vmem, at)], axis=0)
        for at in (row_id + k * row_count for k in range(row_tiles))
    ]
    rights = [
        jnp.concatenate([part(images_vmem, at), part(vecs_vmem, at)], axis=0)
        for at in (col_id + k * col_count for k in range(col_tiles))
    ]
    left = jnp.concatenate(lefts, axis=1)
    right = jnp.concatenate(rights, axis=1)
    change = lax.dot_general(
        left, right, (((0,), (0,)), ((), ())),
        precision=lax.Precision.HIGHEST, preferred_element_type=F32,
    )
    copy.wait()
    updated_out[...] = tile_vmem[...] - change


def vmem():
    return pl.BlockSpec(memory_space=pltpu.VMEM)


def on_device(psi, hpsi, eigvec):
    g_rows, bands = psi.shape
    row_tiles, _, tile_size, col_tiles = eigvec.shape[:4]
    row_count = lax.axis_size("row")
    col_count = lax.axis_size("col")
    devices = row_count * col_count
    row_id = lax.axis_index("row")
    col_id = lax.axis_index("col")
    gvecs = g_rows * devices
    height = row_tiles * tile_size
    width = col_tiles * tile_size
    tiles = bands // tile_size
    where = jnp.stack([row_id, col_id]).astype(jnp.int32)

    both = lax.all_gather(jnp.stack([psi, hpsi]), "row")
    psi_rows = lax.all_to_all(
        jnp.broadcast_to(psi[None], (col_count, *psi.shape)), "col", 0, 0, tiled=True
    ).reshape(g_rows * col_count, bands)
    both, psi_rows = lax.optimization_barrier((both, psi_rows))

    k = row_count * 2 * g_rows
    block = (row_count, 2, g_rows, tile_size)

    def column_block(index):
        return pl.BlockSpec(block, lambda c, where: (0, 0, 0, index(c, where)))

    in_specs = (
        [column_block(lambda c, where, a=a: where[0] + a * row_count) for a in range(row_tiles)]
        + [column_block(lambda c, where: 0)]
        + [column_block(lambda c, where, a=a: c + a * col_count) for a in range(col_tiles)]
    )
    blocks_shape = jax.ShapeDtypeStruct((col_count, height, width), F32)
    strip_shape = jax.ShapeDtypeStruct((col_count, PB, width), F32)
    matrix, overlap, strip = pl.pallas_call(
        functools.partial(products_body, row_tiles=row_tiles, col_tiles=col_tiles, gvecs=gvecs),
        out_shape=(blocks_shape, blocks_shape, strip_shape),
        grid_spec=pltpu.PrefetchScalarGridSpec(
            num_scalar_prefetch=1,
            grid=(col_count,),
            in_specs=in_specs,
            out_specs=tuple(
                pl.BlockSpec((1, *made.shape[1:]), lambda c, where: (c, 0, 0))
                for made in (blocks_shape, blocks_shape, strip_shape)
            ),
            scratch_shapes=[
                pltpu.VMEM((height + PB, k), psi.dtype),
                pltpu.VMEM((height, k // 2), psi.dtype),
            ],
        ),
        compiler_params=pltpu.CompilerParams(vmem_limit_bytes=32 * MIB),
        name="products",
    )(where, *([both] * len(in_specs)))

    summed = lax.psum(matrix, "col")
    strip = jnp.sum(lax.all_to_all(strip, "col", 0, 0, tiled=True), axis=0)
    strip = lax.all_to_all(
        jnp.broadcast_to(strip[None], strip_shape.shape), "col", 0, 0, tiled=True
    )
    eigvec, overlap, strip = lax.optimization_barrier((eigvec, overlap, strip))
    panel = jnp.transpose(
        strip.reshape(col_count, PB, row_tiles, col_tiles // row_tiles, tile_size), (1, 3, 0, 2, 4)
    ).reshape(PB, tiles, tile_size)
    turn = lax.all_gather(eigvec.reshape(row_tiles, tile_size, width), "row", axis=1)
    correlation = lax.psum_scatter(overlap, "col", scatter_dimension=0, tiled=True)

    state = jax.ShapeDtypeStruct((PB, tiles, tile_size), F32)
    marks_shape = jax.ShapeDtypeStruct((8, tile_size), F32)

    def advance(peers, step, recv, vecs, images, marks, factor):
        return pl.pallas_call(
            functools.partial(step_body, row_count=row_count),
            out_shape=(
                state, state, marks_shape,
                jax.ShapeDtypeStruct((peers, row_tiles, tile_size), F32),
            ),
            in_specs=[pl.BlockSpec(memory_space=pltpu.SMEM)]
            + [vmem() for _ in range(5)]
            + [pl.BlockSpec(memory_space=pltpu.HBM)],
            out_specs=tuple(vmem() for _ in range(4)),
            scratch_shapes=[pltpu.VMEM(factor.shape, F32), pltpu.SemaphoreType.DMA],
            input_output_aliases={3: 0, 4: 1, 5: 2},
            compiler_params=pltpu.CompilerParams(vmem_limit_bytes=24 * MIB),
            name="reflect",
        )(jnp.reshape(step, (1,)).astype(jnp.int32), recv, panel, vecs, images, marks, factor)

    def wide(step, carry):
        vecs, images, marks, send = advance(devices, step, *carry, matrix)
        return lax.all_to_all(send, ("row", "col"), 0, 0, tiled=True), vecs, images, marks

    def narrow(step, carry):
        vecs, images, marks, send = advance(row_count, step, *carry, summed)
        return lax.all_to_all(send, "row", 0, 0, tiled=True), vecs, images, marks

    carry = (
        jnp.zeros((devices, row_tiles, tile_size), F32),
        jnp.zeros(state.shape, F32),
        jnp.zeros(state.shape, F32),
        jnp.zeros(marks_shape.shape, F32),
    )
    carry = lax.fori_loop(0, WIDE, wide, carry)
    carry = narrow(jnp.int32(WIDE), carry)
    recv, vecs, images, marks = lax.fori_loop(WIDE + 1, PB, narrow, carry)

    updated, rotated = pl.pallas_call(
        functools.partial(last_body, row_count=row_count),
        out_shape=(
            jax.ShapeDtypeStruct((height, width), F32),
            jax.ShapeDtypeStruct((g_rows * col_count, width), psi.dtype),
        ),
        in_specs=[pl.BlockSpec(memory_space=pltpu.SMEM)]
        + [vmem() for _ in range(4)]
        + [pl.BlockSpec(memory_space=pltpu.HBM), vmem(), vmem()],
        out_specs=(vmem(), vmem()),
        scratch_shapes=[
            pltpu.VMEM((height, width), F32),
            pltpu.VMEM(state.shape, F32),
            pltpu.VMEM(state.shape, F32),
            pltpu.SemaphoreType.DMA,
        ],
        compiler_params=pltpu.CompilerParams(vmem_limit_bytes=24 * MIB),
        name="update",
    )(where, recv, vecs, images, marks, summed, psi_rows, turn.reshape(bands, width))

    tile_shape = (row_tiles, 1, tile_size, col_tiles, 1, tile_size)
    return (
        correlation.reshape(tile_shape),
        updated.reshape(tile_shape),
        marks[0, :PB],
        marks[1, :PB],
        rotated.reshape(g_rows * col_count, col_tiles, 1, tile_size),
    )


def solution(mesh):
    return jax.shard_map(
        on_device,
        mesh=mesh,
        in_specs=(
            P(("row", "col"), None),
            P(("row", "col"), None),
            P(None, "row", None, None, "col", None),
        ),
        out_specs=(
            P(None, "row", None, None, "col", None),
            P(None, "row", None, None, "col", None),
            P(),
            P(),
            P("row", None, "col", None),
        ),
        check_vma=False,
    )
```

time: 453 us -> 430 us (0.949)
  waiting for transfers between devices: 237 us -> 183 us
  blocking collectives: 0 us -> 26.2 us
  starting transfers between devices: 112 us -> 122 us
  Pallas kernels: 72.7 us -> 65.3 us
    all_gather x1, waiting for transfers between devices: 54.2 us -> 21.5 us  [on_device(): both = lax.all_gather(jnp.stack([psi, hpsi]), 'row')]
    all_to_all x0 -> x2, blocking collectives: none -> 26.2 us  [the longest x1 17 us: on_device(): lax.all_to_all(jnp.broadcast_to(strip[None], strip_shape.shape), 'col', 0...]
    all_to_all x17, waiting for transfers between devices: 182 us -> 161 us  [the longest x10 58.7 us: narrow(): return (lax.all_to_all(send, 'row', 0, 0, tiled=True), vecs, images, marks)]
    all_to_all x17, starting transfers between devices: 112 us -> 122 us  [the longest x5 70.2 us: wide(): lax.all_to_all(send, ('row', 'col'), 0, 0, tiled=True)]
    pallas_call x17, Pallas kernels: 62.9 us -> 56 us  [the longest x16 52.9 us: advance(): pl.pallas_call(functools.partial(step_body, row_count=row_count), out_sha...]
  transfers between devices with their start and end apart: 21 -> 21, of which waited for: 18 -> 18; matrix products, arithmetic and copies ran while one was open for 1% -> 1% of each run, Pallas kernels for 16% -> 13%
where the time goes in v3:
time: 430 us; the launch traced here: 428 us
  waiting for transfers between devices  183 us (43%)
  starting transfers between devices  122 us (28%)
  Pallas kernels  65.3 us (15%)
  blocking collectives  26.2 us (6%)
  local copies, waits for them, and re-layouts  15.5 us (4%)
  between operations  13.9 us (3%)
    all_to_all x5, starting transfers between devices, wide(): lax.all_to_all(send, ('row', 'col'), 0, 0, tiled=True)  70.2 us
    all_to_all x10, waiting for transfers between devices, narrow(): return (lax.all_to_all(send, 'row', 0, 0, tiled=True), vecs, images, marks)  58.7 us
    pallas_call x16, Pallas kernels, advance(): pl.pallas_call(functools.partial(step_body, row_count=row_count), out_sha...  52.9 us
    all_to_all x5, waiting for transfers between devices, wide(): lax.all_to_all(send, ('row', 'col'), 0, 0, tiled=True)  50.9 us
    all_to_all x1, waiting for transfers between devices, on_device(): lax.all_to_all(jnp.broadcast_to(psi[None], (col_count, *psi.shape)), 'col...  43.6 us
    all_to_all x10, starting transfers between devices, narrow(): return (lax.all_to_all(send, 'row', 0, 0, tiled=True), vecs, images, marks)  36.8 us
    all_gather x1, waiting for transfers between devices, on_device(): both = lax.all_gather(jnp.stack([psi, hpsi]), 'row')  21.5 us
    all_to_all x1, blocking collectives, on_device(): lax.all_to_all(jnp.broadcast_to(strip[None], strip_shape.shape), 'col', 0...  17 us
  transfers between devices with their start and end apart: 21, of which 18 were waited for; matrix products, arithmetic and copies ran while one was open for 1% of the time, Pallas kernels for 13%

profile of v3, /device:TPU:1, one launch (start us, length us, event | category | flops | bytes accessed | tf_op | source)
XLA Modules:
  0.0 428.1 jit_solution(9836146059673878569)
XLA Ops:
  11.7 7.5 %all-to-all-start.2 = ((bf16[8,32,4096]{2,1,0:T(8,128)(2,1)}), bf16[8,32,4096]{2,1,0:T(8,128)(2,1)S(1)}, u32[]{:S(2)}, u32[]{:S(2)}) async-start(bf16[8,32,4096]{2,1,0:T(8,128)(2,1)} %broadcast_in_dim.8), calls=%async_computation.2 | async-start | bytes 4194304 | tf_op jit(solution)/shard_map/all_to_all | solution.py:198
  19.3 43.6 %all-to-all-done.2 = bf16[8,32,4096]{2,1,0:T(8,128)(2,1)S(1)} async-done(((bf16[8,32,4096]{2,1,0:T(8,128)(2,1)}), bf16[8,32,4096]{2,1,0:T(8,128)(2,1)S(1)}, u32[]{:S(2)}, u32[]{:S(2)}) %all-to-all-start.2) | async-done | bytes 2097184 | tf_op jit(solution)/shard_map/all_to_all | solution.py:198
  62.9 21.5 %all-gather.6.cloned.1.call-done = bf16[32,32,4096]{2,1,0:T(8,128)(2,1)} async-done(((bf16[2,32,4096]{2,1,0:T(8,128)(2,1)}), bf16[32,32,4096]{2,1,0:T(8,128)(2,1)}) %all-gather.6.cloned.1.call-update) | async-done | bytes 8388624 | tf_op jit(solution)/shard_map/all_gather | solution.py:197
  84.4 3.4 copy-done
  87.8 9.3 %products.1 = (f32[8,256,512]{2,1,0:T(8,128)}, f32[8,256,512]{2,1,0:T(8,128)S(1)}, f32[8,16,512]{2,1,0:T(8,128)}) custom-call(s32[2]{0:T(128)S(1)} %pad_add_fusion.where_ref, bf16[16,2,32,4096]{3,2,1,0:T(8,128)(2,1)S(1)} %bitcast.25, bf16[16,2,32,4096]{3,2,1,0:T(8,128)(2,1)S(1)} %bitcast.26, bf16[16,2,32,4096]{3,2,1,0:T(8,128)(2,1)S(1)} %bitcast.27, ...), custom_call_target="tpu_custom_call" | custom-call | tf_op jit(solution)/shard_map/products/pallas_call | solution.py:216
  99.1 7.4 %all-to-all-start.3 = ((f32[8,16,512]{2,1,0:T(8,128)}), f32[8,16,512]{2,1,0:T(8,128)S(1)}, u32[]{:S(2)}, u32[]{:S(2)}) async-start(f32[8,16,512]{2,1,0:T(8,128)} %get-tuple-element.263), calls=%async_computation.3 | async-start | bytes 524288 | tf_op jit(solution)/shard_map/all_to_all | solution.py:237
  106.6 7.5 %all-to-all-done.3 = f32[8,16,512]{2,1,0:T(8,128)S(1)} async-done(((f32[8,16,512]{2,1,0:T(8,128)}), f32[8,16,512]{2,1,0:T(8,128)S(1)}, u32[]{:S(2)}, u32[]{:S(2)}) %all-to-all-start.3) | async-done | bytes 262176 | tf_op jit(solution)/shard_map/all_to_all | solution.py:237
  114.1 17.0 %all_to_all.40 = f32[8,16,512]{2,1,0:T(8,128)S(1)} all-to-all(f32[8,16,512]{2,1,0:T(8,128)S(1)} %broadcast_in_dim.9), channel_id=1, replica_groups=mesh['row'=16,'col'=8] {'col'}, dimensions={0} | all-to-all | bytes 524288 | tf_op jit(solution)/shard_map/all_to_all | solution.py:238
  133.0 138.5 %while.38 = (s32[]{:T(128)}, f32[128,2,128]{2,1,0:T(2,128)S(1)}, f32[16,32,128]{2,1,0:T(8,128)S(1)}, f32[16,32,128]{2,1,0:T(8,128)S(1)}, f32[8,128]{1,0:T(8,128)...) while((s32[]{:T(128)}, f32[128,2,128]{2,1,0:T(2,128)S(1)}, ...), condition=%wide.region_3.0_spmd, body=%wide.region_2.0_spmd.sunk | while | flops 2 | bytes 393333 | solution.py:282
  133.0 3.5 reflect.12
  136.5 11.0 %all-to-all-start = ((f32[128,2,128]{2,1,0:T(2,128)}), f32[128,2,128]{2,1,0:T(2,128)S(1)}, u32[]{:S(2)}, u32[]{:S(2)}) async-start(f32[128,2,128]{2,1,0:T(2,128)} %get-tuple-element.415), calls=%async_computation | async-start | bytes 262144 | tf_op jit(solution)/shard_map/while/body/eval_jaxpr/all_to_all | solution.py:270
  147.5 11.7 %all-to-all-done = f32[128,2,128]{2,1,0:T(2,128)S(1)} async-done(((f32[128,2,128]{2,1,0:T(2,128)}), f32[128,2,128]{2,1,0:T(2,128)S(1)}, u32[]{:S(2)}, u32[]{:S(2)}) %all-to-all-start) | async-done | bytes 131104 | tf_op jit(solution)/shard_map/while/body/eval_jaxpr/all_to_all | solution.py:270
  159.2 3.4 reflect.12
  162.6 8.2 %all-to-all-start = ((f32[128,2,128]{2,1,0:T(2,128)}), f32[128,2,128]{2,1,0:T(2,128)S(1)}, u32[]{:S(2)}, u32[]{:S(2)}) async-start(f32[128,2,128]{2,1,0:T(2,128)} %get-tuple-element.415), calls=%async_computation | async-start | bytes 262144 | tf_op jit(solution)/shard_map/while/body/eval_jaxpr/all_to_all | solution.py:270
  170.9 10.1 %all-to-all-done = f32[128,2,128]{2,1,0:T(2,128)S(1)} async-done(((f32[128,2,128]{2,1,0:T(2,128)}), f32[128,2,128]{2,1,0:T(2,128)S(1)}, u32[]{:S(2)}, u32[]{:S(2)}) %all-to-all-start) | async-done | bytes 131104 | tf_op jit(solution)/shard_map/while/body/eval_jaxpr/all_to_all | solution.py:270
  181.0 3.5 reflect.12
  184.5 40.8 %all-to-all-start = ((f32[128,2,128]{2,1,0:T(2,128)}), f32[128,2,128]{2,1,0:T(2,128)S(1)}, u32[]{:S(2)}, u32[]{:S(2)}) async-start(f32[128,2,128]{2,1,0:T(2,128)} %get-tuple-element.415), calls=%async_computation | async-start | bytes 262144 | tf_op jit(solution)/shard_map/while/body/eval_jaxpr/all_to_all | solution.py:270
  225.2 9.6 %all-to-all-done = f32[128,2,128]{2,1,0:T(2,128)S(1)} async-done(((f32[128,2,128]{2,1,0:T(2,128)}), f32[128,2,128]{2,1,0:T(2,128)S(1)}, u32[]{:S(2)}, u32[]{:S(2)}) %all-to-all-start) | async-done | bytes 131104 | tf_op jit(solution)/shard_map/while/body/eval_jaxpr/all_to_all | solution.py:270
  234.8 3.5 reflect.12
  238.3 4.5 %all-to-all-start = ((f32[128,2,128]{2,1,0:T(2,128)}), f32[128,2,128]{2,1,0:T(2,128)S(1)}, u32[]{:S(2)}, u32[]{:S(2)}) async-start(f32[128,2,128]{2,1,0:T(2,128)} %get-tuple-element.415), calls=%async_computation | async-start | bytes 262144 | tf_op jit(solution)/shard_map/while/body/eval_jaxpr/all_to_all | solution.py:270
  242.8 10.0 %all-to-all-done = f32[128,2,128]{2,1,0:T(2,128)S(1)} async-done(((f32[128,2,128]{2,1,0:T(2,128)}), f32[128,2,128]{2,1,0:T(2,128)S(1)}, u32[]{:S(2)}, u32[]{:S(2)}) %all-to-all-start) | async-done | bytes 131104 | tf_op jit(solution)/shard_map/while/body/eval_jaxpr/all_to_all | solution.py:270
  252.8 3.4 reflect.12
  256.2 5.7 %all-to-all-start = ((f32[128,2,128]{2,1,0:T(2,128)}), f32[128,2,128]{2,1,0:T(2,128)S(1)}, u32[]{:S(2)}, u32[]{:S(2)}) async-start(f32[128,2,128]{2,1,0:T(2,128)} %get-tuple-element.415), calls=%async_computation | async-start | bytes 262144 | tf_op jit(solution)/shard_map/while/body/eval_jaxpr/all_to_all | solution.py:270
  261.9 9.6 %all-to-all-done = f32[128,2,128]{2,1,0:T(2,128)S(1)} async-done(((f32[128,2,128]{2,1,0:T(2,128)}), f32[128,2,128]{2,1,0:T(2,128)S(1)}, u32[]{:S(2)}, u32[]{:S(2)}) %all-to-all-start) | async-done | bytes 131104 | tf_op jit(solution)/shard_map/while/body/eval_jaxpr/all_to_all | solution.py:270
  274.6 9.2 %all_to_all.41 = f32[16,2,128]{2,1,0:T(2,128)S(1)} all-to-all(f32[16,2,128]{2,1,0:T(2,128)S(1)} %get-tuple-element.271), channel_id=1, replica_groups=mesh['row'=16,'col'=8] {'row'}, dimensions={0} | all-to-all | bytes 32768 | tf_op jit(solution)/shard_map/all_to_all | solution.py:274
  283.8 128.2 %while.39 = (s32[]{:T(128)}, f32[16,2,128]{2,1,0:T(2,128)S(1)}, f32[16,32,128]{2,1,0:T(8,128)S(1)}, f32[16,32,128]{2,1,0:T(8,128)S(1)}, f32[8,128]{1,0:T(8,128)S...) while((s32[]{:T(128)}, f32[16,2,128]{2,1,0:T(2,128)S(1)}, ...), condition=%wide.region_6.0_spmd, body=%wide.region_5.0_spmd.sunk | while | flops 3 | bytes 49289 | solution.py:284
  283.8 3.4 reflect.13
  287.2 3.6 all-to-all-start.1
  290.8 5.9 %all-to-all-done.1 = f32[16,2,128]{2,1,0:T(2,128)S(1)} async-done(((f32[16,2,128]{2,1,0:T(2,128)}), f32[16,2,128]{2,1,0:T(2,128)S(1)}, u32[]{:S(2)}, u32[]{:S(2)}) %all-to-all-start.1) | async-done | bytes 16416 | tf_op jit(solution)/shard_map/while/body/eval_jaxpr/all_to_all | solution.py:274
  296.6 3.3 reflect.13
  300.0 3.7 all-to-all-start.1
  303.6 5.9 %all-to-all-done.1 = f32[16,2,128]{2,1,0:T(2,128)S(1)} async-done(((f32[16,2,128]{2,1,0:T(2,128)}), f32[16,2,128]{2,1,0:T(2,128)S(1)}, u32[]{:S(2)}, u32[]{:S(2)}) %all-to-all-start.1) | async-done | bytes 16416 | tf_op jit(solution)/shard_map/while/body/eval_jaxpr/all_to_all | solution.py:274
  312.7 3.8 all-to-all-start.1
  316.5 5.9 %all-to-all-done.1 = f32[16,2,128]{2,1,0:T(2,128)S(1)} async-done(((f32[16,2,128]{2,1,0:T(2,128)}), f32[16,2,128]{2,1,0:T(2,128)S(1)}, u32[]{:S(2)}, u32[]{:S(2)}) %all-to-all-start.1) | async-done | bytes 16416 | tf_op jit(solution)/shard_map/while/body/eval_jaxpr/all_to_all | solution.py:274
  325.6 3.7 all-to-all-start.1
  329.3 6.0 %all-to-all-done.1 = f32[16,2,128]{2,1,0:T(2,128)S(1)} async-done(((f32[16,2,128]{2,1,0:T(2,128)}), f32[16,2,128]{2,1,0:T(2,128)S(1)}, u32[]{:S(2)}, u32[]{:S(2)}) %all-to-all-start.1) | async-done | bytes 16416 | tf_op jit(solution)/shard_map/while/body/eval_jaxpr/all_to_all | solution.py:274
  338.6 3.7 all-to-all-start.1
  342.2 5.9 %all-to-all-done.1 = f32[16,2,128]{2,1,0:T(2,128)S(1)} async-done(((f32[16,2,128]{2,1,0:T(2,128)}), f32[16,2,128]{2,1,0:T(2,128)S(1)}, u32[]{:S(2)}, u32[]{:S(2)}) %all-to-all-start.1) | async-done | bytes 16416 | tf_op jit(solution)/shard_map/while/body/eval_jaxpr/all_to_all | solution.py:274
  351.3 3.7 all-to-all-start.1
  355.0 5.9 %all-to-all-done.1 = f32[16,2,128]{2,1,0:T(2,128)S(1)} async-done(((f32[16,2,128]{2,1,0:T(2,128)}), f32[16,2,128]{2,1,0:T(2,128)S(1)}, u32[]{:S(2)}, u32[]{:S(2)}) %all-to-all-start.1) | async-done | bytes 16416 | tf_op jit(solution)/shard_map/while/body/eval_jaxpr/all_to_all | solution.py:274
  364.1 3.7 all-to-all-start.1
  367.8 5.9 %all-to-all-done.1 = f32[16,2,128]{2,1,0:T(2,128)S(1)} async-done(((f32[16,2,128]{2,1,0:T(2,128)}), f32[16,2,128]{2,1,0:T(2,128)S(1)}, u32[]{:S(2)}, u32[]{:S(2)}) %all-to-all-start.1) | async-done | bytes 16416 | tf_op jit(solution)/shard_map/while/body/eval_jaxpr/all_to_all | solution.py:274
  376.9 3.7 all-to-all-start.1
  380.6 5.9 %all-to-all-done.1 = f32[16,2,128]{2,1,0:T(2,128)S(1)} async-done(((f32[16,2,128]{2,1,0:T(2,128)}), f32[16,2,128]{2,1,0:T(2,128)S(1)}, u32[]{:S(2)}, u32[]{:S(2)}) %all-to-all-start.1) | async-done | bytes 16416 | tf_op jit(solution)/shard_map/while/body/eval_jaxpr/all_to_all | solution.py:274
  389.7 3.7 all-to-all-start.1
  393.4 5.9 %all-to-all-done.1 = f32[16,2,128]{2,1,0:T(2,128)S(1)} async-done(((f32[16,2,128]{2,1,0:T(2,128)}), f32[16,2,128]{2,1,0:T(2,128)S(1)}, u32[]{:S(2)}, u32[]{:S(2)}) %all-to-all-start.1) | async-done | bytes 16416 | tf_op jit(solution)/shard_map/while/body/eval_jaxpr/all_to_all | solution.py:274
  402.5 3.7 all-to-all-start.1
  406.2 5.9 %all-to-all-done.1 = f32[16,2,128]{2,1,0:T(2,128)S(1)} async-done(((f32[16,2,128]{2,1,0:T(2,128)}), f32[16,2,128]{2,1,0:T(2,128)S(1)}, u32[]{:S(2)}, u32[]{:S(2)}) %all-to-all-start.1) | async-done | bytes 16416 | tf_op jit(solution)/shard_map/while/body/eval_jaxpr/all_to_all | solution.py:274
  (44 shorter events, 46.8 us)
Async XLA Ops:
  7.2 77.3 %all-gather.6.cloned.1.call-start = ((), (), s32[]{:S(2)}) async-start(), calls=%async_computation.10 | async-start | bytes 8912896 | tf_op jit(solution)/shard_map/all_gather | solution.py:197
  11.7 51.2 %all-to-all-start.2 = ((bf16[8,32,4096]{2,1,0:T(8,128)(2,1)}), bf16[8,32,4096]{2,1,0:T(8,128)(2,1)S(1)}, u32[]{:S(2)}, u32[]{:S(2)}) async-start(bf16[8,32,4096]{2,1,0:T(8,128)(2,1)} %broadcast_in_dim.8), calls=%async_computation.2 | async-start | bytes 4194304 | tf_op jit(solution)/shard_map/all_to_all | solution.py:198
  19.2 252.3 %all-reduce.2.cloned.1.call-start = ((), (), s32[]{:S(2)}) async-start(), calls=%async_computation.8 | async-start | bytes 8388608 | tf_op jit(solution)/shard_map/psum | solution.py:236
  84.4 3.4 copy-start
  97.2 1.9 copy-start.2
  99.1 32.1 %copy-start.3 = (bf16[2,1,128,4,1,128]{5,3,4,2,1,0:T(4,128)(2,1)S(1)}, bf16[2,1,128,4,1,128]{5,3,4,2,1,0:T(4,128)(2,1)}, u32[]{:S(2)}) copy-start(bf16[2,1,128,4,1,128]{5,3,4,2,1,0:T(4,128)(2,1)} %param.9) | copy-start | bytes 786436
  99.1 15.0 %all-to-all-start.3 = ((f32[8,16,512]{2,1,0:T(8,128)}), f32[8,16,512]{2,1,0:T(8,128)S(1)}, u32[]{:S(2)}, u32[]{:S(2)}) async-start(f32[8,16,512]{2,1,0:T(8,128)} %get-tuple-element.263), calls=%async_computation.3 | async-start | bytes 524288 | tf_op jit(solution)/shard_map/all_to_all | solution.py:237
  106.5 306.0 %all-gather.4.cloned.1.call-start = ((), (), s32[]{:S(2)}) async-start(), calls=%async_computation.9 | async-start | bytes 4456448 | tf_op jit(solution)/shard_map/all_gather | solution.py:245
  132.0 287.6 %reduce-scatter.2.cloned.1.call-start = ((), (), s32[]{:S(2)}) async-start(), calls=%async_computation.7 | async-start | bytes 4718592 | tf_op jit(solution)/shard_map/reduce_scatter | solution.py:246
  136.5 22.7 %all-to-all-start = ((f32[128,2,128]{2,1,0:T(2,128)}), f32[128,2,128]{2,1,0:T(2,128)S(1)}, u32[]{:S(2)}, u32[]{:S(2)}) async-start(f32[128,2,128]{2,1,0:T(2,128)} %get-tuple-element.415), calls=%async_computation | async-start | bytes 262144 | tf_op jit(solution)/shard_map/while/body/eval_jaxpr/all_to_all | solution.py:270
  162.6 18.4 %all-to-all-start = ((f32[128,2,128]{2,1,0:T(2,128)}), f32[128,2,128]{2,1,0:T(2,128)S(1)}, u32[]{:S(2)}, u32[]{:S(2)}) async-start(f32[128,2,128]{2,1,0:T(2,128)} %get-tuple-element.415), calls=%async_computation | async-start | bytes 262144 | tf_op jit(solution)/shard_map/while/body/eval_jaxpr/all_to_all | solution.py:270
  184.5 50.4 %all-to-all-start = ((f32[128,2,128]{2,1,0:T(2,128)}), f32[128,2,128]{2,1,0:T(2,128)S(1)}, u32[]{:S(2)}, u32[]{:S(2)}) async-start(f32[128,2,128]{2,1,0:T(2,128)} %get-tuple-element.415), calls=%async_computation | async-start | bytes 262144 | tf_op jit(solution)/shard_map/while/body/eval_jaxpr/all_to_all | solution.py:270
  238.3 14.5 %all-to-all-start = ((f32[128,2,128]{2,1,0:T(2,128)}), f32[128,2,128]{2,1,0:T(2,128)S(1)}, u32[]{:S(2)}, u32[]{:S(2)}) async-start(f32[128,2,128]{2,1,0:T(2,128)} %get-tuple-element.415), calls=%async_computation | async-start | bytes 262144 | tf_op jit(solution)/shard_map/while/body/eval_jaxpr/all_to_all | solution.py:270
  256.2 15.3 %all-to-all-start = ((f32[128,2,128]{2,1,0:T(2,128)}), f32[128,2,128]{2,1,0:T(2,128)S(1)}, u32[]{:S(2)}, u32[]{:S(2)}) async-start(f32[128,2,128]{2,1,0:T(2,128)} %get-tuple-element.415), calls=%async_computation | async-start | bytes 262144 | tf_op jit(solution)/shard_map/while/body/eval_jaxpr/all_to_all | solution.py:270
  287.2 9.4 %all-to-all-start.1 = ((f32[16,2,128]{2,1,0:T(2,128)}), f32[16,2,128]{2,1,0:T(2,128)S(1)}, u32[]{:S(2)}, u32[]{:S(2)}) async-start(f32[16,2,128]{2,1,0:T(2,128)} %get-tuple-element.426), calls=%async_computation.1 | async-start | bytes 32768 | tf_op jit(solution)/shard_map/while/body/eval_jaxpr/all_to_all | solution.py:274
  300.0 9.5 %all-to-all-start.1 = ((f32[16,2,128]{2,1,0:T(2,128)}), f32[16,2,128]{2,1,0:T(2,128)S(1)}, u32[]{:S(2)}, u32[]{:S(2)}) async-start(f32[16,2,128]{2,1,0:T(2,128)} %get-tuple-element.426), calls=%async_computation.1 | async-start | bytes 32768 | tf_op jit(solution)/shard_map/while/body/eval_jaxpr/all_to_all | solution.py:274
  312.7 9.7 %all-to-all-start.1 = ((f32[16,2,128]{2,1,0:T(2,128)}), f32[16,2,128]{2,1,0:T(2,128)S(1)}, u32[]{:S(2)}, u32[]{:S(2)}) async-start(f32[16,2,128]{2,1,0:T(2,128)} %get-tuple-element.426), calls=%async_computation.1 | async-start | bytes 32768 | tf_op jit(solution)/shard_map/while/body/eval_jaxpr/all_to_all | solution.py:274
  325.6 9.7 %all-to-all-start.1 = ((f32[16,2,128]{2,1,0:T(2,128)}), f32[16,2,128]{2,1,0:T(2,128)S(1)}, u32[]{:S(2)}, u32[]{:S(2)}) async-start(f32[16,2,128]{2,1,0:T(2,128)} %get-tuple-element.426), calls=%async_computation.1 | async-start | bytes 32768 | tf_op jit(solution)/shard_map/while/body/eval_jaxpr/all_to_all | solution.py:274
  338.6 9.5 %all-to-all-start.1 = ((f32[16,2,128]{2,1,0:T(2,128)}), f32[16,2,128]{2,1,0:T(2,128)S(1)}, u32[]{:S(2)}, u32[]{:S(2)}) async-start(f32[16,2,128]{2,1,0:T(2,128)} %get-tuple-element.426), calls=%async_computation.1 | async-start | bytes 32768 | tf_op jit(solution)/shard_map/while/body/eval_jaxpr/all_to_all | solution.py:274
  351.3 9.6 %all-to-all-start.1 = ((f32[16,2,128]{2,1,0:T(2,128)}), f32[16,2,128]{2,1,0:T(2,128)S(1)}, u32[]{:S(2)}, u32[]{:S(2)}) async-start(f32[16,2,128]{2,1,0:T(2,128)} %get-tuple-element.426), calls=%async_computation.1 | async-start | bytes 32768 | tf_op jit(solution)/shard_map/while/body/eval_jaxpr/all_to_all | solution.py:274
  364.1 9.6 %all-to-all-start.1 = ((f32[16,2,128]{2,1,0:T(2,128)}), f32[16,2,128]{2,1,0:T(2,128)S(1)}, u32[]{:S(2)}, u32[]{:S(2)}) async-start(f32[16,2,128]{2,1,0:T(2,128)} %get-tuple-element.426), calls=%async_computation.1 | async-start | bytes 32768 | tf_op jit(solution)/shard_map/while/body/eval_jaxpr/all_to_all | solution.py:274
  376.9 9.6 %all-to-all-start.1 = ((f32[16,2,128]{2,1,0:T(2,128)}), f32[16,2,128]{2,1,0:T(2,128)S(1)}, u32[]{:S(2)}, u32[]{:S(2)}) async-start(f32[16,2,128]{2,1,0:T(2,128)} %get-tuple-element.426), calls=%async_computation.1 | async-start | bytes 32768 | tf_op jit(solution)/shard_map/while/body/eval_jaxpr/all_to_all | solution.py:274
  389.7 9.6 %all-to-all-start.1 = ((f32[16,2,128]{2,1,0:T(2,128)}), f32[16,2,128]{2,1,0:T(2,128)S(1)}, u32[]{:S(2)}, u32[]{:S(2)}) async-start(f32[16,2,128]{2,1,0:T(2,128)} %get-tuple-element.426), calls=%async_computation.1 | async-start | bytes 32768 | tf_op jit(solution)/shard_map/while/body/eval_jaxpr/all_to_all | solution.py:274
  402.5 9.6 %all-to-all-start.1 = ((f32[16,2,128]{2,1,0:T(2,128)}), f32[16,2,128]{2,1,0:T(2,128)S(1)}, u32[]{:S(2)}, u32[]{:S(2)}) async-start(f32[16,2,128]{2,1,0:T(2,128)} %get-tuple-element.426), calls=%async_computation.1 | async-start | bytes 32768 | tf_op jit(solution)/shard_map/while/body/eval_jaxpr/all_to_all | solution.py:274
  412.6 2.2 copy-start.1
Sparse Core Ops, SparseCore 0:
  10.3 74.1 all-gather.5
  99.2 117.5 all-reduce.1
  219.1 38.0 all-gather.3
  260.8 82.9 reduce-scatter.1

commit v4 on v3

--- a/solution.py
+++ b/solution.py
@@ -8,7 +8,7 @@
 from jax.sharding import PartitionSpec as P
 
 PB = 16
-WIDE = 5
+WIDE = 2
 LANES = 128
 F32 = jnp.float32
 MIB = 1024 * 1024
@@ -75,13 +75,11 @@
 
 def step_body(
     step_ref, recv_ref, panel_ref, vecs_ref, images_ref, marks_ref, matrix_ref,
-    vecs_out, images_out, marks_out, send_out, matrix_vmem, sem, *, row_count,
+    vecs_out, images_out, marks_out, send_out, *, row_count,
 ):
     step = step_ref[0]
     tiles = vecs_ref.shape[1]
     col_count, height, width = matrix_ref.shape
-    copy = pltpu.make_async_copy(matrix_ref, matrix_vmem, sem)
-    copy.start()
     row_tiles = height // LANES
     col_tiles = width // LANES
     lane = lax.broadcasted_iota(jnp.int32, (1, 1, LANES), 2)
@@ -118,12 +116,11 @@
     marks = jnp.where((row == 0) & mark, jnp.broadcast_to(corner[0], flat), marks)
     marks = jnp.where((row == 1) & mark, jnp.broadcast_to(beta[0], flat), marks)
     marks_out[...] = jnp.where(row == 2, jnp.broadcast_to(tau[0], flat), marks)
-    copy.wait()
     sums = jnp.zeros((height, LANES), F32)
     for c in range(col_count):
         for a in range(col_tiles):
             at = spot_of(a * col_count + c, row_count, row_tiles)
-            sums = sums + matrix_vmem[c, :, a * LANES : (a + 1) * LANES] * vector[0, at : at + 1, :]
+            sums = sums + matrix_ref[c, :, a * LANES : (a + 1) * LANES] * vector[0, at : at + 1, :]
     send = jnp.concatenate(
         [
             jnp.sum(sums[k * LANES : (k + 1) * LANES].T, axis=0, keepdims=True)
@@ -195,10 +192,6 @@
     where = jnp.stack([row_id, col_id]).astype(jnp.int32)
 
     both = lax.all_gather(jnp.stack([psi, hpsi]), "row")
-    psi_rows = lax.all_to_all(
-        jnp.broadcast_to(psi[None], (col_count, *psi.shape)), "col", 0, 0, tiled=True
-    ).reshape(g_rows * col_count, bands)
-    both, psi_rows = lax.optimization_barrier((both, psi_rows))
 
     k = row_count * 2 * g_rows
     block = (row_count, 2, g_rows, tile_size)
@@ -229,7 +222,7 @@
                 pltpu.VMEM((height, k // 2), psi.dtype),
             ],
         ),
-        compiler_params=pltpu.CompilerParams(vmem_limit_bytes=32 * MIB),
+        compiler_params=pltpu.CompilerParams(vmem_limit_bytes=60 * MIB),
         name="products",
     )(where, *([both] * len(in_specs)))
 
@@ -256,10 +249,8 @@
                 jax.ShapeDtypeStruct((peers, row_tiles, tile_size), F32),
             ),
             in_specs=[pl.BlockSpec(memory_space=pltpu.SMEM)]
-            + [vmem() for _ in range(5)]
-            + [pl.BlockSpec(memory_space=pltpu.HBM)],
+            + [vmem() for _ in range(6)],
             out_specs=tuple(vmem() for _ in range(4)),
-            scratch_shapes=[pltpu.VMEM(factor.shape, F32), pltpu.SemaphoreType.DMA],
             input_output_aliases={3: 0, 4: 1, 5: 2},
             compiler_params=pltpu.CompilerParams(vmem_limit_bytes=24 * MIB),
             name="reflect",
@@ -280,8 +271,11 @@
         jnp.zeros(marks_shape.shape, F32),
     )
     carry = lax.fori_loop(0, WIDE, wide, carry)
-    carry = narrow(jnp.int32(WIDE), carry)
-    recv, vecs, images, marks = lax.fori_loop(WIDE + 1, PB, narrow, carry)
+    psi, carry = lax.optimization_barrier((psi, carry))
+    psi_rows = lax.all_gather(psi, "col", axis=0, tiled=True)
+    for step in range(WIDE, PB):
+        carry = narrow(jnp.int32(step), carry)
+    recv, vecs, images, marks = carry
 
     updated, rotated = pl.pallas_call(
         functools.partial(last_body, row_count=row_count),

time: 430 us -> 383 us (0.89)
  starting transfers between devices: 122 us -> 31.4 us
  blocking collectives: 26.2 us -> 115 us
  Pallas kernels: 65.3 us -> 36.3 us
  waiting for transfers between devices: 183 us -> 168 us
    all_to_all x1 -> x13, blocking collectives: 9.23 us -> 115 us  [narrow(): return (lax.all_to_all(send, 'row', 0, 0, tiled=True), vecs, images, marks)]
    all_to_all x10 -> x1, waiting for transfers between devices: 58.7 us -> 5.34 us  [narrow(): return (lax.all_to_all(send, 'row', 0, 0, tiled=True), vecs, images, marks)]
    all_to_all x5 -> x2, starting transfers between devices: 70.2 us -> 16.9 us  [wide(): lax.all_to_all(send, ('row', 'col'), 0, 0, tiled=True)]
    all_gather x1, waiting for transfers between devices: 21.5 us -> 56.2 us  [on_device(): both = lax.all_gather(jnp.stack([psi, hpsi]), 'row')]
    psum x1, waiting for transfers between devices: 0.01 us -> 34.7 us  [on_device(): summed = lax.psum(matrix, 'col')]
    all_to_all x10 -> x1, starting transfers between devices: 36.8 us -> 3.68 us  [narrow(): return (lax.all_to_all(send, 'row', 0, 0, tiled=True), vecs, images, marks)]
    pallas_call x16, Pallas kernels: 52.9 us -> 22.6 us  [advance(): pl.pallas_call(functools.partial(step_body, row_count=row_count), out_sha...]
    all_to_all x1, waiting for transfers between devices: 43.6 us -> 13.6 us  [on_device(): lax.all_to_all(jnp.broadcast_to(strip[None], strip_shape.shape), 'col', 0...]
  transfers between devices with their start and end apart: 21 -> 10, of which waited for: 18 -> 8; matrix products, arithmetic and copies ran while one was open for 1% -> 1% of each run, Pallas kernels for 13% -> 7%
where the time goes in v4:
time: 383 us; the launch traced here: 381 us
  waiting for transfers between devices  168 us (44%)
  blocking collectives  115 us (30%)
  Pallas kernels  36.3 us (9%)
  starting transfers between devices  31.4 us (8%)
  local copies, waits for them, and re-layouts  14.5 us (4%)
  between operations  13.9 us (4%)
    all_to_all x13, blocking collectives, narrow(): return (lax.all_to_all(send, 'row', 0, 0, tiled=True), vecs, images, marks)  115 us
    all_gather x1, waiting for transfers between devices, on_device(): both = lax.all_gather(jnp.stack([psi, hpsi]), 'row')  56.2 us
    psum x1, waiting for transfers between devices, on_device(): summed = lax.psum(matrix, 'col')  34.7 us
    reduce_scatter x1, waiting for transfers between devices, on_device(): lax.psum_scatter(overlap, 'col', scatter_dimension=0, tiled=True)  27.7 us
    pallas_call x16, Pallas kernels, advance(): pl.pallas_call(functools.partial(step_body, row_count=row_count), out_sha...  22.6 us
    all_to_all x2, waiting for transfers between devices, wide(): lax.all_to_all(send, ('row', 'col'), 0, 0, tiled=True)  21.8 us
    all_to_all x2, starting transfers between devices, wide(): lax.all_to_all(send, ('row', 'col'), 0, 0, tiled=True)  16.9 us
    all_to_all x1, waiting for transfers between devices, on_device(): lax.all_to_all(jnp.broadcast_to(strip[None], strip_shape.shape), 'col', 0...  13.6 us
  transfers between devices with their start and end apart: 10, of which 8 were waited for; matrix products, arithmetic and copies ran while one was open for 1% of the time, Pallas kernels for 7%

profile of v4, /device:TPU:1, one launch (start us, length us, event | category | flops | bytes accessed | tf_op | source)
XLA Modules:
  0.0 381.3 jit_solution(16632715579745589538)
XLA Ops:
  7.2 1.9 pad_maximum_fusion
  9.8 56.2 %all-gather.9.cloned.1.call-done = bf16[32,32,4096]{2,1,0:T(8,128)(2,1)} async-done(((bf16[2,32,4096]{2,1,0:T(8,128)(2,1)}), bf16[32,32,4096]{2,1,0:T(8,128)(2,1)}) %all-gather.9.cloned.1.call-update) | async-done | bytes 8388624 | tf_op jit(solution)/shard_map/all_gather | solution.py:194
  66.0 11.3 %products.1 = (f32[8,256,512]{2,1,0:T(8,128)}, f32[8,256,512]{2,1,0:T(8,128)}, f32[8,16,512]{2,1,0:T(8,128)}) custom-call(s32[2]{0:T(128)} %pad_add_fusion.where_ref, bf16[16,2,32,4096]{3,2,1,0:T(8,128)(2,1)} %bitcast.22, bf16[16,2,32,4096]{3,2,1,0:T(8,128)(2,1)} %bitcast.23, bf16[16,2,32,4096]{3,2,1,0:T(8,128)(2,1)} %bitcast.24, ...), custom_call_target="tpu_custom_call" | custom-call | tf_op jit(solution)/shard_map/products/pallas_call | solution.py:209
  77.3 6.4 %all-to-all-start.1 = ((f32[8,16,512]{2,1,0:T(8,128)}), f32[8,16,512]{2,1,0:T(8,128)S(1)}, u32[]{:S(2)}, u32[]{:S(2)}) async-start(f32[8,16,512]{2,1,0:T(8,128)} %get-tuple-element.196), calls=%async_computation.1 | async-start | bytes 524288 | tf_op jit(solution)/shard_map/all_to_all | solution.py:230
  83.8 7.6 %all-to-all-done.1 = f32[8,16,512]{2,1,0:T(8,128)S(1)} async-done(((f32[8,16,512]{2,1,0:T(8,128)}), f32[8,16,512]{2,1,0:T(8,128)S(1)}, u32[]{:S(2)}, u32[]{:S(2)}) %all-to-all-start.1) | async-done | bytes 262176 | tf_op jit(solution)/shard_map/all_to_all | solution.py:230
  92.1 4.3 %all-to-all-start.2 = ((f32[8,16,512]{2,1,0:T(8,128)}), f32[8,16,512]{2,1,0:T(8,128)S(1)}, u32[]{:S(2)}, u32[]{:S(2)}) async-start(f32[8,16,512]{2,1,0:T(8,128)} %broadcast_in_dim.12), calls=%async_computation.2 | async-start | bytes 524288 | tf_op jit(solution)/shard_map/all_to_all | solution.py:231
  96.5 13.6 %all-to-all-done.2 = f32[8,16,512]{2,1,0:T(8,128)S(1)} async-done(((f32[8,16,512]{2,1,0:T(8,128)}), f32[8,16,512]{2,1,0:T(8,128)S(1)}, u32[]{:S(2)}, u32[]{:S(2)}) %all-to-all-start.2) | async-done | bytes 262176 | tf_op jit(solution)/shard_map/all_to_all | solution.py:231
  110.5 46.7 %while.19 = (s32[]{:T(128)}, f32[128,2,128]{2,1,0:T(2,128)S(1)}, f32[16,32,128]{2,1,0:T(8,128)S(1)}, f32[16,32,128]{2,1,0:T(8,128)S(1)}, f32[8,128]{1,0:T(8,128)...) while((s32[]{:T(128)}, f32[128,2,128]{2,1,0:T(2,128)S(1)}, ...), condition=%wide.region_3.0_spmd, body=%wide.region_2.0_spmd.sunk | while | flops 2 | bytes 393333 | solution.py:273
  110.5 4.0 %reflect.33 = (f32[16,32,128]{2,1,0:T(8,128)S(1)}, f32[16,32,128]{2,1,0:T(8,128)S(1)}, f32[8,128]{1,0:T(8,128)S(1)}, f32[128,2,128]{2,1,0:T(2,128)}) custom-call(s32[1]{0:T(128)} %bitcast.20.step_ref, f32[128,2,128]{2,1,0:T(2,128)S(1)} %get-tuple-element.359.recv_ref, ...), custom_call_target="tpu_custom_call", output_to_operand_aliasing={{0}: (3, {}), {1}: (4, {}), {2}: (5, {})} | custom-call | tf_op jit(solution)/shard_map/while/body/eval_jaxpr/reflect/pallas_call | solution.py:245
  114.5 4.1 %all-to-all-start = ((f32[128,2,128]{2,1,0:T(2,128)}), f32[128,2,128]{2,1,0:T(2,128)S(1)}, u32[]{:S(2)}, u32[]{:S(2)}) async-start(f32[128,2,128]{2,1,0:T(2,128)} %get-tuple-element.346), calls=%async_computation | async-start | bytes 262144 | tf_op jit(solution)/shard_map/while/body/eval_jaxpr/all_to_all | solution.py:261
  118.7 11.8 %all-to-all-done = f32[128,2,128]{2,1,0:T(2,128)S(1)} async-done(((f32[128,2,128]{2,1,0:T(2,128)}), f32[128,2,128]{2,1,0:T(2,128)S(1)}, u32[]{:S(2)}, u32[]{:S(2)}) %all-to-all-start) | async-done | bytes 131104 | tf_op jit(solution)/shard_map/while/body/eval_jaxpr/all_to_all | solution.py:261
  130.4 3.9 %reflect.33 = (f32[16,32,128]{2,1,0:T(8,128)S(1)}, f32[16,32,128]{2,1,0:T(8,128)S(1)}, f32[8,128]{1,0:T(8,128)S(1)}, f32[128,2,128]{2,1,0:T(2,128)}) custom-call(s32[1]{0:T(128)} %bitcast.20.step_ref, f32[128,2,128]{2,1,0:T(2,128)S(1)} %get-tuple-element.359.recv_ref, ...), custom_call_target="tpu_custom_call", output_to_operand_aliasing={{0}: (3, {}), {1}: (4, {}), {2}: (5, {})} | custom-call | tf_op jit(solution)/shard_map/while/body/eval_jaxpr/reflect/pallas_call | solution.py:245
  134.4 12.7 %all-to-all-start = ((f32[128,2,128]{2,1,0:T(2,128)}), f32[128,2,128]{2,1,0:T(2,128)S(1)}, u32[]{:S(2)}, u32[]{:S(2)}) async-start(f32[128,2,128]{2,1,0:T(2,128)} %get-tuple-element.346), calls=%async_computation | async-start | bytes 262144 | tf_op jit(solution)/shard_map/while/body/eval_jaxpr/all_to_all | solution.py:261
  147.1 10.0 %all-to-all-done = f32[128,2,128]{2,1,0:T(2,128)S(1)} async-done(((f32[128,2,128]{2,1,0:T(2,128)}), f32[128,2,128]{2,1,0:T(2,128)S(1)}, u32[]{:S(2)}, u32[]{:S(2)}) %all-to-all-start) | async-done | bytes 131104 | tf_op jit(solution)/shard_map/while/body/eval_jaxpr/all_to_all | solution.py:261
  158.6 34.7 %all-reduce.2.cloned.1.call-done.matrix_ref = f32[8,256,512]{2,1,0:T(8,128)} async-done(((f32[8,256,512]{2,1,0:T(8,128)}), f32[8,256,512]{2,1,0:T(8,128)}) %all-reduce.2.cloned.1.call-update) | async-done | bytes 4194320 | tf_op jit(solution)/shard_map/psum | solution.py:229
  193.3 2.2 copy-done
  195.5 1.0 reflect.19
  196.6 10.9 %all_to_all.90.recv_ref = f32[16,2,128]{2,1,0:T(2,128)S(1)} all-to-all(f32[16,2,128]{2,1,0:T(2,128)S(1)} %get-tuple-element.208), channel_id=1, replica_groups=mesh['row'=16,'col'=8] {'row'}, dimensions={0} | all-to-all | bytes 32768 | tf_op jit(solution)/shard_map/all_to_all | solution.py:265
  207.4 1.0 reflect.20
  208.5 8.6 %all_to_all.91.recv_ref = f32[16,2,128]{2,1,0:T(2,128)S(1)} all-to-all(f32[16,2,128]{2,1,0:T(2,128)S(1)} %get-tuple-element.212), channel_id=1, replica_groups=mesh['row'=16,'col'=8] {'row'}, dimensions={0} | all-to-all | bytes 32768 | tf_op jit(solution)/shard_map/all_to_all | solution.py:265
  217.1 1.0 reflect.21
  218.1 8.6 %all_to_all.92.recv_ref = f32[16,2,128]{2,1,0:T(2,128)S(1)} all-to-all(f32[16,2,128]{2,1,0:T(2,128)S(1)} %get-tuple-element.216), channel_id=1, replica_groups=mesh['row'=16,'col'=8] {'row'}, dimensions={0} | all-to-all | bytes 32768 | tf_op jit(solution)/shard_map/all_to_all | solution.py:265
  226.8 1.0 reflect.22
  227.8 8.8 %all_to_all.93.recv_ref = f32[16,2,128]{2,1,0:T(2,128)S(1)} all-to-all(f32[16,2,128]{2,1,0:T(2,128)S(1)} %get-tuple-element.220), channel_id=1, replica_groups=mesh['row'=16,'col'=8] {'row'}, dimensions={0} | all-to-all | bytes 32768 | tf_op jit(solution)/shard_map/all_to_all | solution.py:265
  236.6 1.0 reflect.23
  237.6 8.6 %all_to_all.94.recv_ref = f32[16,2,128]{2,1,0:T(2,128)S(1)} all-to-all(f32[16,2,128]{2,1,0:T(2,128)S(1)} %get-tuple-element.224), channel_id=1, replica_groups=mesh['row'=16,'col'=8] {'row'}, dimensions={0} | all-to-all | bytes 32768 | tf_op jit(solution)/shard_map/all_to_all | solution.py:265
  246.2 1.0 reflect.24
  247.2 8.6 %all_to_all.95.recv_ref = f32[16,2,128]{2,1,0:T(2,128)S(1)} all-to-all(f32[16,2,128]{2,1,0:T(2,128)S(1)} %get-tuple-element.228), channel_id=1, replica_groups=mesh['row'=16,'col'=8] {'row'}, dimensions={0} | all-to-all | bytes 32768 | tf_op jit(solution)/shard_map/all_to_all | solution.py:265
  255.9 1.0 reflect.25
  256.9 8.6 %all_to_all.96.recv_ref = f32[16,2,128]{2,1,0:T(2,128)S(1)} all-to-all(f32[16,2,128]{2,1,0:T(2,128)S(1)} %get-tuple-element.232), channel_id=1, replica_groups=mesh['row'=16,'col'=8] {'row'}, dimensions={0} | all-to-all | bytes 32768 | tf_op jit(solution)/shard_map/all_to_all | solution.py:265
  266.5 8.8 %all_to_all.97.recv_ref = f32[16,2,128]{2,1,0:T(2,128)S(1)} all-to-all(f32[16,2,128]{2,1,0:T(2,128)S(1)} %get-tuple-element.236), channel_id=1, replica_groups=mesh['row'=16,'col'=8] {'row'}, dimensions={0} | all-to-all | bytes 32768 | tf_op jit(solution)/shard_map/all_to_all | solution.py:265
  275.4 1.0 reflect.27
  276.4 8.6 %all_to_all.98.recv_ref = f32[16,2,128]{2,1,0:T(2,128)S(1)} all-to-all(f32[16,2,128]{2,1,0:T(2,128)S(1)} %get-tuple-element.240), channel_id=1, replica_groups=mesh['row'=16,'col'=8] {'row'}, dimensions={0} | all-to-all | bytes 32768 | tf_op jit(solution)/shard_map/all_to_all | solution.py:265
  285.0 1.0 reflect.28
  286.0 8.6 %all_to_all.99.recv_ref = f32[16,2,128]{2,1,0:T(2,128)S(1)} all-to-all(f32[16,2,128]{2,1,0:T(2,128)S(1)} %get-tuple-element.244), channel_id=1, replica_groups=mesh['row'=16,'col'=8] {'row'}, dimensions={0} | all-to-all | bytes 32768 | tf_op jit(solution)/shard_map/all_to_all | solution.py:265
  294.7 1.0 reflect.29
  295.7 8.6 %all_to_all.100.recv_ref = f32[16,2,128]{2,1,0:T(2,128)S(1)} all-to-all(f32[16,2,128]{2,1,0:T(2,128)S(1)} %get-tuple-element.248), channel_id=1, replica_groups=mesh['row'=16,'col'=8] {'row'}, dimensions={0} | all-to-all | bytes 32768 | tf_op jit(solution)/shard_map/all_to_all | solution.py:265
  305.3 8.6 %all_to_all.101.recv_ref = f32[16,2,128]{2,1,0:T(2,128)S(1)} all-to-all(f32[16,2,128]{2,1,0:T(2,128)S(1)} %get-tuple-element.252), channel_id=1, replica_groups=mesh['row'=16,'col'=8] {'row'}, dimensions={0} | all-to-all | bytes 32768 | tf_op jit(solution)/shard_map/all_to_all | solution.py:265
  315.0 8.6 %all_to_all.102.recv_ref = f32[16,2,128]{2,1,0:T(2,128)S(1)} all-to-all(f32[16,2,128]{2,1,0:T(2,128)S(1)} %get-tuple-element.256), channel_id=1, replica_groups=mesh['row'=16,'col'=8] {'row'}, dimensions={0} | all-to-all | bytes 32768 | tf_op jit(solution)/shard_map/all_to_all | solution.py:265
  323.6 1.6 reflect.32
  325.2 3.7 all-to-all-start.16
  329.4 5.3 %all-to-all-done.16.recv_ref = f32[16,2,128]{2,1,0:T(2,128)S(1)} async-done(((f32[16,2,128]{2,1,0:T(2,128)}), f32[16,2,128]{2,1,0:T(2,128)S(1)}, u32[]{:S(2)}, u32[]{:S(2)}) %all-to-all-start.16) | async-done | bytes 16416 | tf_op jit(solution)/shard_map/all_to_all | solution.py:265
  334.8 2.3 copy-done.2
  337.1 2.2 copy-done.3
  339.3 1.6 copy-done.4
  340.9 2.4 update.1
  345.0 27.7 %reduce-scatter.2.cloned.1.call-done = f32[1,256,512]{2,1,0:T(8,128)} async-done(((f32[8,256,512]{2,1,0:T(8,128)}), f32[1,256,512]{2,1,0:T(8,128)}) %reduce-scatter.2.cloned.1.call-update) | async-done | bytes 524304 | tf_op jit(solution)/shard_map/reduce_scatter | solution.py:239
  372.7 2.0 reshape.32
  (38 shorter events, 8.6 us)
Async XLA Ops:
  7.2 58.8 %all-gather.9.cloned.1.call-start = ((), (), s32[]{:S(2)}) async-start(), calls=%async_computation.22 | async-start | bytes 8912896 | tf_op jit(solution)/shard_map/all_gather | solution.py:194
  9.1 184.2 %all-reduce.2.cloned.1.call-start = ((), (), s32[]{:S(2)}) async-start(), calls=%async_computation.19 | async-start | bytes 8388608 | tf_op jit(solution)/shard_map/psum | solution.py:229
  77.3 14.1 %all-to-all-start.1 = ((f32[8,16,512]{2,1,0:T(8,128)}), f32[8,16,512]{2,1,0:T(8,128)S(1)}, u32[]{:S(2)}, u32[]{:S(2)}) async-start(f32[8,16,512]{2,1,0:T(8,128)} %get-tuple-element.196), calls=%async_computation.1 | async-start | bytes 524288 | tf_op jit(solution)/shard_map/all_to_all | solution.py:230
  92.1 17.9 %all-to-all-start.2 = ((f32[8,16,512]{2,1,0:T(8,128)}), f32[8,16,512]{2,1,0:T(8,128)S(1)}, u32[]{:S(2)}, u32[]{:S(2)}) async-start(f32[8,16,512]{2,1,0:T(8,128)} %broadcast_in_dim.12), calls=%async_computation.2 | async-start | bytes 524288 | tf_op jit(solution)/shard_map/all_to_all | solution.py:231
  96.4 233.0 %all-gather.5.cloned.1.call-start = ((), (), s32[]{:S(2)}) async-start(), calls=%async_computation.20 | async-start | bytes 2359296 | tf_op jit(solution)/shard_map/all_gather | solution.py:275
  110.5 46.7 %copy-start.6 = (bf16[2,1,128,4,1,128]{5,3,4,2,1,0:T(4,128)(2,1)S(1)}, bf16[2,1,128,4,1,128]{5,3,4,2,1,0:T(4,128)(2,1)}, u32[]{:S(2)}) copy-start(bf16[2,1,128,4,1,128]{5,3,4,2,1,0:T(4,128)(2,1)} %param.7) | copy-start | bytes 786436
  114.5 15.9 %all-to-all-start = ((f32[128,2,128]{2,1,0:T(2,128)}), f32[128,2,128]{2,1,0:T(2,128)S(1)}, u32[]{:S(2)}, u32[]{:S(2)}) async-start(f32[128,2,128]{2,1,0:T(2,128)} %get-tuple-element.346), calls=%async_computation | async-start | bytes 262144 | tf_op jit(solution)/shard_map/while/body/eval_jaxpr/all_to_all | solution.py:261
  134.4 22.8 %all-to-all-start = ((f32[128,2,128]{2,1,0:T(2,128)}), f32[128,2,128]{2,1,0:T(2,128)S(1)}, u32[]{:S(2)}, u32[]{:S(2)}) async-start(f32[128,2,128]{2,1,0:T(2,128)} %get-tuple-element.346), calls=%async_computation | async-start | bytes 262144 | tf_op jit(solution)/shard_map/while/body/eval_jaxpr/all_to_all | solution.py:261
  157.2 177.6 %all-gather.7.cloned.1.call-start = ((), (), s32[]{:S(2)}) async-start(), calls=%async_computation.21 | async-start | bytes 4456448 | tf_op jit(solution)/shard_map/all_gather | solution.py:238
  158.1 214.7 %reduce-scatter.2.cloned.1.call-start = ((), (), s32[]{:S(2)}) async-start(), calls=%async_computation.18 | async-start | bytes 4718592 | tf_op jit(solution)/shard_map/reduce_scatter | solution.py:239
  193.3 2.2 copy-start
  195.5 11.9 %copy-start.1 = (f32[8,256,512]{2,1,0:T(8,128)S(1)}, f32[8,256,512]{2,1,0:T(8,128)}, u32[]{:S(2)}) copy-start(f32[8,256,512]{2,1,0:T(8,128)} %all-reduce.2.cloned.1.call-done.matrix_ref) | copy-start | bytes 12582916
  314.0 20.8 %copy-start.5 = (s32[2]{0:T(128)S(1)}, s32[2]{0:T(128)}, u32[]{:S(2)}) copy-start(s32[2]{0:T(128)} %pad_add_fusion.where_ref) | copy-start | bytes 28
  325.2 9.5 %all-to-all-start.16 = ((f32[16,2,128]{2,1,0:T(2,128)}), f32[16,2,128]{2,1,0:T(2,128)S(1)}, u32[]{:S(2)}, u32[]{:S(2)}) async-start(f32[16,2,128]{2,1,0:T(2,128)} %get-tuple-element.260), calls=%async_computation.17 | async-start | bytes 32768 | tf_op jit(solution)/shard_map/all_to_all | solution.py:265
  334.8 2.3 copy-start.2
  337.1 2.2 copy-start.3
  339.3 1.6 copy-start.4
Sparse Core Ops, SparseCore 0:
  10.3 55.6 all-gather.8
  77.4 115.8 all-reduce.1
  195.7 51.6 all-gather.4
  249.5 36.3 all-gather.6
  289.6 83.1 reduce-scatter.1

commit v5 on v4

--- a/solution.py
+++ b/solution.py
@@ -8,7 +8,7 @@
 from jax.sharding import PartitionSpec as P
 
 PB = 16
-WIDE = 2
+WIDE = 1
 LANES = 128
 F32 = jnp.float32
 MIB = 1024 * 1024
@@ -132,18 +132,14 @@
 
 
 def last_body(
-    where_ref, recv_ref, vecs_ref, images_ref, marks_ref, matrix_ref, psi_ref, turn_ref,
-    updated_out, rotated_out, tile_vmem, vecs_vmem, images_vmem, sem, *, row_count,
+    where_ref, recv_ref, vecs_ref, images_ref, marks_ref, tile_ref,
+    updated_out, vecs_vmem, images_vmem, *, row_count, col_count,
 ):
     row_id = where_ref[0]
     col_id = where_ref[1]
-    copy = pltpu.make_async_copy(matrix_ref.at[col_id], tile_vmem, sem)
-    copy.start()
-    rotated_out[...] = over_k(psi_ref[...], turn_ref[...]).astype(rotated_out.dtype)
     height, width = updated_out.shape
     row_tiles = height // LANES
     col_tiles = width // LANES
-    col_count = matrix_ref.shape[0]
     vecs = vecs_ref[...]
     vector = vecs_ref[PB - 1 : PB]
     tau = marks_ref[2:3, 0:1].reshape(1, 1, 1)
@@ -169,8 +165,7 @@
         left, right, (((0,), (0,)), ((), ())),
         precision=lax.Precision.HIGHEST, preferred_element_type=F32,
     )
-    copy.wait()
-    updated_out[...] = tile_vmem[...] - change
+    updated_out[...] = tile_ref[...] - change
 
 
 def vmem():
@@ -227,16 +222,14 @@
     )(where, *([both] * len(in_specs)))
 
     summed = lax.psum(matrix, "col")
-    strip = jnp.sum(lax.all_to_all(strip, "col", 0, 0, tiled=True), axis=0)
+    strip = lax.all_to_all(strip, "col", 0, 0, tiled=True)
+    strip = jnp.sum(strip, axis=0)
     strip = lax.all_to_all(
         jnp.broadcast_to(strip[None], strip_shape.shape), "col", 0, 0, tiled=True
     )
-    eigvec, overlap, strip = lax.optimization_barrier((eigvec, overlap, strip))
     panel = jnp.transpose(
         strip.reshape(col_count, PB, row_tiles, col_tiles // row_tiles, tile_size), (1, 3, 0, 2, 4)
     ).reshape(PB, tiles, tile_size)
-    turn = lax.all_gather(eigvec.reshape(row_tiles, tile_size, width), "row", axis=1)
-    correlation = lax.psum_scatter(overlap, "col", scatter_dimension=0, tiled=True)
 
     state = jax.ShapeDtypeStruct((PB, tiles, tile_size), F32)
     marks_shape = jax.ShapeDtypeStruct((8, tile_size), F32)
@@ -270,32 +263,38 @@
         jnp.zeros(state.shape, F32),
         jnp.zeros(marks_shape.shape, F32),
     )
-    carry = lax.fori_loop(0, WIDE, wide, carry)
-    psi, carry = lax.optimization_barrier((psi, carry))
+    bound = jnp.where(row_id >= 0, jnp.int32(WIDE), jnp.int32(0))
+    carry = lax.fori_loop(0, lax.optimization_barrier(bound), wide, carry)
+    psi, eigvec, carry = lax.optimization_barrier((psi, eigvec, carry))
     psi_rows = lax.all_gather(psi, "col", axis=0, tiled=True)
-    for step in range(WIDE, PB):
+    turn = lax.all_to_all(
+        jnp.broadcast_to(
+            eigvec.reshape(1, row_tiles, tile_size, width), (row_count, row_tiles, tile_size, width)
+        ),
+        "row", 0, 0, tiled=True,
+    )
+    turn, carry = lax.optimization_barrier((turn, carry))
+    carry = narrow(jnp.int32(WIDE), carry)
+    tile = lax.dynamic_index_in_dim(summed, col_id, 0, keepdims=False)
+    overlap, carry = lax.optimization_barrier((overlap, carry))
+    correlation = lax.psum_scatter(overlap, "col", scatter_dimension=0, tiled=True)
+    for step in range(WIDE + 1, PB - 1):
         carry = narrow(jnp.int32(step), carry)
-    recv, vecs, images, marks = carry
-
-    updated, rotated = pl.pallas_call(
-        functools.partial(last_body, row_count=row_count),
-        out_shape=(
-            jax.ShapeDtypeStruct((height, width), F32),
-            jax.ShapeDtypeStruct((g_rows * col_count, width), psi.dtype),
-        ),
+    psi_rows, turn, carry = lax.optimization_barrier((psi_rows, turn, carry))
+    turn = jnp.transpose(turn, (1, 0, 2, 3)).reshape(bands, width)
+    rotated = jnp.dot(psi_rows, turn, preferred_element_type=F32).astype(psi.dtype)
+    recv, vecs, images, marks = narrow(jnp.int32(PB - 1), carry)
+
+    updated = pl.pallas_call(
+        functools.partial(last_body, row_count=row_count, col_count=col_count),
+        out_shape=jax.ShapeDtypeStruct((height, width), F32),
         in_specs=[pl.BlockSpec(memory_space=pltpu.SMEM)]
-        + [vmem() for _ in range(4)]
-        + [pl.BlockSpec(memory_space=pltpu.HBM), vmem(), vmem()],
-        out_specs=(vmem(), vmem()),
-        scratch_shapes=[
-            pltpu.VMEM((height, width), F32),
-            pltpu.VMEM(state.shape, F32),
-            pltpu.VMEM(state.shape, F32),
-            pltpu.SemaphoreType.DMA,
-        ],
+        + [vmem() for _ in range(5)],
+        out_specs=vmem(),
+        scratch_shapes=[pltpu.VMEM(state.shape, F32), pltpu.VMEM(state.shape, F32)],
         compiler_params=pltpu.CompilerParams(vmem_limit_bytes=24 * MIB),
         name="update",
-    )(where, recv, vecs, images, marks, summed, psi_rows, turn.reshape(bands, width))
+    )(where, recv, vecs, images, marks, tile)
 
     tile_shape = (row_tiles, 1, tile_size, col_tiles, 1, tile_size)
     return (

time: 383 us -> 416 us (1.086)
  starting transfers between devices: 31.4 us -> 49.2 us
  waiting for transfers between devices: 168 us -> 180 us
  local copies, waits for them, and re-layouts: 14.5 us -> 20.6 us
    all_to_all x1 -> x2, waiting for transfers between devices: 7.63 us -> 88.5 us  [the longest x1 80.8 us: on_device(): lax.all_to_all(jnp.broadcast_to(eigvec.reshape(1, row_tiles, tile_size, w...]
    psum x1, waiting for transfers between devices: 34.7 us -> 0.01 us  [on_device(): summed = lax.psum(matrix, 'col')]
    reduce_scatter x1, waiting for transfers between devices: 27.7 us -> 0.01 us  [on_device(): lax.psum_scatter(overlap, 'col', scatter_dimension=0, tiled=True)]
    all_to_all x2 -> x1, waiting for transfers between devices: 21.8 us -> 9.57 us  [wide(): lax.all_to_all(send, ('row', 'col'), 0, 0, tiled=True)]
    all_to_all x1 -> x3, starting transfers between devices: 3.68 us -> 11 us  [narrow(): return (lax.all_to_all(send, 'row', 0, 0, tiled=True), vecs, images, marks)]
    all_to_all x1 -> x3, waiting for transfers between devices: 5.34 us -> 11.1 us  [narrow(): return (lax.all_to_all(send, 'row', 0, 0, tiled=True), vecs, images, marks)]
    all_to_all x2 -> x1, starting transfers between devices: 16.9 us -> 22.4 us  [wide(): lax.all_to_all(send, ('row', 'col'), 0, 0, tiled=True)]
    all_to_all x1 -> x2, starting transfers between devices: 6.44 us -> 11.7 us  [the longest x1 6.44 us: on_device(): strip = lax.all_to_all(strip, 'col', 0, 0, tiled=True)]
  transfers between devices with their start and end apart: 10 -> 11, of which waited for: 8 -> 8; matrix products, arithmetic and copies ran while one was open for 1% -> 3% of each run, Pallas kernels for 7% -> 5%
where the time goes in v5:
time: 416 us; the launch traced here: 414 us
  waiting for transfers between devices  180 us (43%)
  blocking collectives  113 us (27%)
  starting transfers between devices  49.2 us (12%)
  Pallas kernels  33.8 us (8%)
  local copies, waits for them, and re-layouts  20.6 us (5%)
  between operations  14 us (3%)
    all_to_all x12, blocking collectives, narrow(): return (lax.all_to_all(send, 'row', 0, 0, tiled=True), vecs, images, marks)  113 us
    all_to_all x1, waiting for transfers between devices, on_device(): lax.all_to_all(jnp.broadcast_to(eigvec.reshape(1, row_tiles, tile_size, w...  80.8 us
    all_gather x1, waiting for transfers between devices, on_device(): both = lax.all_gather(jnp.stack([psi, hpsi]), 'row')  56.2 us
    all_to_all x1, starting transfers between devices, wide(): lax.all_to_all(send, ('row', 'col'), 0, 0, tiled=True)  22.4 us
    pallas_call x16, Pallas kernels, advance(): pl.pallas_call(functools.partial(step_body, row_count=row_count), out_sha...  20.9 us
    all_to_all x1, waiting for transfers between devices, on_device(): lax.all_to_all(jnp.broadcast_to(strip[None], strip_shape.shape), 'col', 0...  13.8 us
    pallas_call x1, Pallas kernels, on_device(): pl.pallas_call(functools.partial(products_body, row_tiles=row_tiles, col_...  11.3 us
    all_to_all x3, waiting for transfers between devices, narrow(): return (lax.all_to_all(send, 'row', 0, 0, tiled=True), vecs, images, marks)  11.1 us
  transfers between devices with their start and end apart: 11, of which 8 were waited for; matrix products, arithmetic and copies ran while one was open for 3% of the time, Pallas kernels for 5%

profile of v5, /device:TPU:1, one launch (start us, length us, event | category | flops | bytes accessed | tf_op | source)
XLA Modules:
  0.0 414.1 jit_solution(15403382963653136192)
XLA Ops:
  7.2 1.9 pad_maximum_fusion
  9.8 56.2 %all-gather.6.cloned.1.call-done = bf16[32,32,4096]{2,1,0:T(8,128)(2,1)} async-done(((bf16[2,32,4096]{2,1,0:T(8,128)(2,1)}), bf16[32,32,4096]{2,1,0:T(8,128)(2,1)}) %all-gather.6.cloned.1.call-update) | async-done | bytes 8388624 | tf_op jit(solution)/shard_map/all_gather | solution.py:189
  66.0 11.3 %products.1 = (f32[8,256,512]{2,1,0:T(8,128)}, f32[8,256,512]{2,1,0:T(8,128)}, f32[8,16,512]{2,1,0:T(8,128)}) custom-call(s32[2]{0:T(128)} %pad_add_fusion.where_ref, bf16[16,2,32,4096]{3,2,1,0:T(8,128)(2,1)} %bitcast.26, bf16[16,2,32,4096]{3,2,1,0:T(8,128)(2,1)} %bitcast.27, bf16[16,2,32,4096]{3,2,1,0:T(8,128)(2,1)} %bitcast.28, ...), custom_call_target="tpu_custom_call" | custom-call | tf_op jit(solution)/shard_map/products/pallas_call | solution.py:204
  77.3 6.4 %all-to-all-start.1 = ((f32[8,16,512]{2,1,0:T(8,128)}), f32[8,16,512]{2,1,0:T(8,128)S(1)}, u32[]{:S(2)}, u32[]{:S(2)}) async-start(f32[8,16,512]{2,1,0:T(8,128)} %get-tuple-element.141), calls=%async_computation.1 | async-start | bytes 524288 | tf_op jit(solution)/shard_map/all_to_all | solution.py:225
  83.7 7.6 %all-to-all-done.1 = f32[8,16,512]{2,1,0:T(8,128)S(1)} async-done(((f32[8,16,512]{2,1,0:T(8,128)}), f32[8,16,512]{2,1,0:T(8,128)S(1)}, u32[]{:S(2)}, u32[]{:S(2)}) %all-to-all-start.1) | async-done | bytes 262176 | tf_op jit(solution)/shard_map/all_to_all | solution.py:225
  92.1 4.0 all-to-all-start.2
  96.1 13.8 %all-to-all-done.2 = f32[8,16,512]{2,1,0:T(8,128)S(1)} async-done(((f32[8,16,512]{2,1,0:T(8,128)}), f32[8,16,512]{2,1,0:T(8,128)S(1)}, u32[]{:S(2)}, u32[]{:S(2)}) %all-to-all-start.2) | async-done | bytes 262176 | tf_op jit(solution)/shard_map/all_to_all | solution.py:227
  110.3 35.9 %while.16 = (s32[]{:T(128)}, f32[128,2,128]{2,1,0:T(2,128)S(1)}, f32[16,32,128]{2,1,0:T(8,128)S(1)}, f32[16,32,128]{2,1,0:T(8,128)S(1)}, f32[8,128]{1,0:T(8,128)...) while((s32[]{:T(128)}, f32[128,2,128]{2,1,0:T(2,128)S(1)}, ...), condition=%wide.region_2.3_spmd, body=%wide.region_1.0_spmd.sunk | while | flops 2 | bytes 393341 | solution.py:267
  110.3 4.0 reflect.31
  114.3 22.4 %all-to-all-start = ((f32[128,2,128]{2,1,0:T(2,128)}), f32[128,2,128]{2,1,0:T(2,128)S(1)}, u32[]{:S(2)}, u32[]{:S(2)}) async-start(f32[128,2,128]{2,1,0:T(2,128)} %get-tuple-element.316), calls=%async_computation | async-start | bytes 262144 | tf_op jit(solution)/shard_map/while/body/all_to_all | solution.py:254
  136.7 9.6 %all-to-all-done = f32[128,2,128]{2,1,0:T(2,128)S(1)} async-done(((f32[128,2,128]{2,1,0:T(2,128)}), f32[128,2,128]{2,1,0:T(2,128)S(1)}, u32[]{:S(2)}, u32[]{:S(2)}) %all-to-all-start) | async-done | bytes 131104 | tf_op jit(solution)/shard_map/while/body/all_to_all | solution.py:254
  146.4 2.5 broadcast_in_dim.23
  148.8 5.2 %all-to-all-start.3 = ((bf16[16,2,128,512]{3,2,1,0:T(8,128)(2,1)}), bf16[16,2,128,512]{3,2,1,0:T(8,128)(2,1)}, u32[]{:S(2)}, u32[]{:S(2)}) async-start(bf16[16,2,128,512]{3,2,1,0:T(8,128)(2,1)} %broadcast_in_dim.23), calls=%async_computation.3 | async-start | bytes 8388608 | tf_op jit(solution)/shard_map/all_to_all | solution.py:270
  154.8 80.8 %all-to-all-done.3 = bf16[16,2,128,512]{3,2,1,0:T(8,128)(2,1)} async-done(((bf16[16,2,128,512]{3,2,1,0:T(8,128)(2,1)}), bf16[16,2,128,512]{3,2,1,0:T(8,128)(2,1)}, u32[]{:S(2)}, u32[]{:S(2)}) %all-to-all-start.3) | async-done | bytes 4194336 | tf_op jit(solution)/shard_map/all_to_all | solution.py:270
  235.7 2.2 copy-done
  237.9 1.0 reflect.16
  238.9 17.4 %all_to_all.96.recv_ref = f32[16,2,128]{2,1,0:T(2,128)S(1)} all-to-all(f32[16,2,128]{2,1,0:T(2,128)S(1)} %get-tuple-element.156), channel_id=1, replica_groups=mesh['row'=16,'col'=8] {'row'}, dimensions={0} | all-to-all | bytes 32768 | tf_op jit(solution)/shard_map/all_to_all | solution.py:258
  256.3 2.2 copy-done.1
  259.5 8.9 %all_to_all.97.recv_ref = f32[16,2,128]{2,1,0:T(2,128)S(1)} all-to-all(f32[16,2,128]{2,1,0:T(2,128)S(1)} %get-tuple-element.167), channel_id=1, replica_groups=mesh['row'=16,'col'=8] {'row'}, dimensions={0} | all-to-all | bytes 32768 | tf_op jit(solution)/shard_map/all_to_all | solution.py:258
  268.4 1.0 reflect.18
  269.4 8.6 %all_to_all.98.recv_ref = f32[16,2,128]{2,1,0:T(2,128)S(1)} all-to-all(f32[16,2,128]{2,1,0:T(2,128)S(1)} %get-tuple-element.171), channel_id=1, replica_groups=mesh['row'=16,'col'=8] {'row'}, dimensions={0} | all-to-all | bytes 32768 | tf_op jit(solution)/shard_map/all_to_all | solution.py:258
  278.0 1.0 reflect.19
  279.0 8.6 %all_to_all.99.recv_ref = f32[16,2,128]{2,1,0:T(2,128)S(1)} all-to-all(f32[16,2,128]{2,1,0:T(2,128)S(1)} %get-tuple-element.175), channel_id=1, replica_groups=mesh['row'=16,'col'=8] {'row'}, dimensions={0} | all-to-all | bytes 32768 | tf_op jit(solution)/shard_map/all_to_all | solution.py:258
  288.7 8.8 %all_to_all.100.recv_ref = f32[16,2,128]{2,1,0:T(2,128)S(1)} all-to-all(f32[16,2,128]{2,1,0:T(2,128)S(1)} %get-tuple-element.179), channel_id=1, replica_groups=mesh['row'=16,'col'=8] {'row'}, dimensions={0} | all-to-all | bytes 32768 | tf_op jit(solution)/shard_map/all_to_all | solution.py:258
  297.5 1.0 reflect.21
  298.5 8.6 %all_to_all.101.recv_ref = f32[16,2,128]{2,1,0:T(2,128)S(1)} all-to-all(f32[16,2,128]{2,1,0:T(2,128)S(1)} %get-tuple-element.183), channel_id=1, replica_groups=mesh['row'=16,'col'=8] {'row'}, dimensions={0} | all-to-all | bytes 32768 | tf_op jit(solution)/shard_map/all_to_all | solution.py:258
  307.1 1.0 reflect.22
  308.1 8.6 %all_to_all.102.recv_ref = f32[16,2,128]{2,1,0:T(2,128)S(1)} all-to-all(f32[16,2,128]{2,1,0:T(2,128)S(1)} %get-tuple-element.187), channel_id=1, replica_groups=mesh['row'=16,'col'=8] {'row'}, dimensions={0} | all-to-all | bytes 32768 | tf_op jit(solution)/shard_map/all_to_all | solution.py:258
  317.8 8.6 %all_to_all.103.recv_ref = f32[16,2,128]{2,1,0:T(2,128)S(1)} all-to-all(f32[16,2,128]{2,1,0:T(2,128)S(1)} %get-tuple-element.191), channel_id=1, replica_groups=mesh['row'=16,'col'=8] {'row'}, dimensions={0} | all-to-all | bytes 32768 | tf_op jit(solution)/shard_map/all_to_all | solution.py:258
  327.4 8.6 %all_to_all.104.recv_ref = f32[16,2,128]{2,1,0:T(2,128)S(1)} all-to-all(f32[16,2,128]{2,1,0:T(2,128)S(1)} %get-tuple-element.195), channel_id=1, replica_groups=mesh['row'=16,'col'=8] {'row'}, dimensions={0} | all-to-all | bytes 32768 | tf_op jit(solution)/shard_map/all_to_all | solution.py:258
  337.1 8.6 %all_to_all.105.recv_ref = f32[16,2,128]{2,1,0:T(2,128)S(1)} all-to-all(f32[16,2,128]{2,1,0:T(2,128)S(1)} %get-tuple-element.199), channel_id=1, replica_groups=mesh['row'=16,'col'=8] {'row'}, dimensions={0} | all-to-all | bytes 32768 | tf_op jit(solution)/shard_map/all_to_all | solution.py:258
  346.7 8.8 %all_to_all.106.recv_ref = f32[16,2,128]{2,1,0:T(2,128)S(1)} all-to-all(f32[16,2,128]{2,1,0:T(2,128)S(1)} %get-tuple-element.203), channel_id=1, replica_groups=mesh['row'=16,'col'=8] {'row'}, dimensions={0} | all-to-all | bytes 32768 | tf_op jit(solution)/shard_map/all_to_all | solution.py:258
  356.5 8.6 %all_to_all.107.recv_ref = f32[16,2,128]{2,1,0:T(2,128)S(1)} all-to-all(f32[16,2,128]{2,1,0:T(2,128)S(1)} %get-tuple-element.207), channel_id=1, replica_groups=mesh['row'=16,'col'=8] {'row'}, dimensions={0} | all-to-all | bytes 32768 | tf_op jit(solution)/shard_map/all_to_all | solution.py:258
  365.2 1.6 reflect.28
  366.8 3.7 all-to-all-start.16
  370.5 5.9 %all-to-all-done.16.recv_ref = f32[16,2,128]{2,1,0:T(2,128)S(1)} async-done(((f32[16,2,128]{2,1,0:T(2,128)}), f32[16,2,128]{2,1,0:T(2,128)S(1)}, u32[]{:S(2)}, u32[]{:S(2)}) %all-to-all-start.16) | async-done | bytes 16416 | tf_op jit(solution)/shard_map/all_to_all | solution.py:258
  376.3 2.2 copy-done.2
  378.5 1.6 reflect.29
  380.1 3.7 all-to-all-start.17
  383.8 1.1 dynamic-slice_bitcast_fusion.tile_ref
  384.9 4.8 %all-to-all-done.17.recv_ref = f32[16,2,128]{2,1,0:T(2,128)S(1)} async-done(((f32[16,2,128]{2,1,0:T(2,128)}), f32[16,2,128]{2,1,0:T(2,128)S(1)}, u32[]{:S(2)}, u32[]{:S(2)}) %all-to-all-start.17) | async-done | bytes 16416 | tf_op jit(solution)/shard_map/all_to_all | solution.py:258
  389.7 2.2 copy-done.3
  391.9 1.6 reflect.30
  393.5 3.7 all-to-all-start.18
  397.2 2.8 copy.64
  400.0 1.2 convolution_convert_fusion
  403.0 1.6 update.1
  405.6 2.0 reshape.36
  (42 shorter events, 12.5 us)
Async XLA Ops:
  7.2 58.8 %all-gather.6.cloned.1.call-start = ((), (), s32[]{:S(2)}) async-start(), calls=%async_computation.23 | async-start | bytes 8912896 | tf_op jit(solution)/shard_map/all_gather | solution.py:189
  9.1 226.6 %all-reduce.2.cloned.1.call-start = ((), (), s32[]{:S(2)}) async-start(), calls=%async_computation.20 | async-start | bytes 8388608 | tf_op jit(solution)/shard_map/psum | solution.py:224
  77.3 14.1 %all-to-all-start.1 = ((f32[8,16,512]{2,1,0:T(8,128)}), f32[8,16,512]{2,1,0:T(8,128)S(1)}, u32[]{:S(2)}, u32[]{:S(2)}) async-start(f32[8,16,512]{2,1,0:T(8,128)} %get-tuple-element.141), calls=%async_computation.1 | async-start | bytes 524288 | tf_op jit(solution)/shard_map/all_to_all | solution.py:225
  92.1 17.8 %all-to-all-start.2 = ((f32[8,16,512]{2,1,0:T(8,128)}), f32[8,16,512]{2,1,0:T(8,128)S(1)}, u32[]{:S(2)}, u32[]{:S(2)}) async-start(f32[8,16,512]{2,1,0:T(8,128)} %broadcast_in_dim.21), calls=%async_computation.2 | async-start | bytes 524288 | tf_op jit(solution)/shard_map/all_to_all | solution.py:227
  110.3 36.0 %copy-start.5 = (bf16[2,1,128,4,1,128]{5,3,4,2,1,0:T(4,128)(2,1)S(1)}, bf16[2,1,128,4,1,128]{5,3,4,2,1,0:T(4,128)(2,1)}, u32[]{:S(2)}) copy-start(bf16[2,1,128,4,1,128]{5,3,4,2,1,0:T(4,128)(2,1)} %param.7) | copy-start | bytes 786436
  114.3 31.9 %all-to-all-start = ((f32[128,2,128]{2,1,0:T(2,128)}), f32[128,2,128]{2,1,0:T(2,128)S(1)}, u32[]{:S(2)}, u32[]{:S(2)}) async-start(f32[128,2,128]{2,1,0:T(2,128)} %get-tuple-element.316), calls=%async_computation | async-start | bytes 262144 | tf_op jit(solution)/shard_map/while/body/all_to_all | solution.py:254
  148.8 86.9 %all-to-all-start.3 = ((bf16[16,2,128,512]{3,2,1,0:T(8,128)(2,1)}), bf16[16,2,128,512]{3,2,1,0:T(8,128)(2,1)}, u32[]{:S(2)}, u32[]{:S(2)}) async-start(bf16[16,2,128,512]{3,2,1,0:T(8,128)(2,1)} %broadcast_in_dim.23), calls=%async_computation.3 | async-start | bytes 8388608 | tf_op jit(solution)/shard_map/all_to_all | solution.py:270
  154.1 230.9 %all-gather.4.cloned.1.call-start = ((), (), s32[]{:S(2)}) async-start(), calls=%async_computation.22 | async-start | bytes 2359296 | tf_op jit(solution)/shard_map/all_gather | solution.py:269
  154.8 250.8 %reduce-scatter.2.cloned.1.call-start = ((), (), s32[]{:S(2)}) async-start(), calls=%async_computation.21 | async-start | bytes 4718592 | tf_op jit(solution)/shard_map/reduce_scatter | solution.py:280
  235.7 2.2 copy-start
  256.3 2.2 copy-start.1
  366.8 9.5 %all-to-all-start.16 = ((f32[16,2,128]{2,1,0:T(2,128)}), f32[16,2,128]{2,1,0:T(2,128)S(1)}, u32[]{:S(2)}, u32[]{:S(2)}) async-start(f32[16,2,128]{2,1,0:T(2,128)} %get-tuple-element.211), calls=%async_computation.17 | async-start | bytes 32768 | tf_op jit(solution)/shard_map/all_to_all | solution.py:258
  376.3 2.2 copy-start.2
  380.1 9.5 %all-to-all-start.17 = ((f32[16,2,128]{2,1,0:T(2,128)}), f32[16,2,128]{2,1,0:T(2,128)S(1)}, u32[]{:S(2)}, u32[]{:S(2)}) async-start(f32[16,2,128]{2,1,0:T(2,128)} %get-tuple-element.215), calls=%async_computation.18 | async-start | bytes 32768 | tf_op jit(solution)/shard_map/all_to_all | solution.py:258
  389.7 2.2 copy-start.3
  393.5 9.5 %all-to-all-start.18 = ((f32[16,2,128]{2,1,0:T(2,128)}), f32[16,2,128]{2,1,0:T(2,128)S(1)}, u32[]{:S(2)}, u32[]{:S(2)}) async-start(f32[16,2,128]{2,1,0:T(2,128)} %get-tuple-element.223), calls=%async_computation.19 | async-start | bytes 32768 | tf_op jit(solution)/shard_map/all_to_all | solution.py:258
  397.2 2.9 copy-start.6
  400.0 3.1 copy-start.4
Sparse Core Ops, SparseCore 0:
  10.3 55.6 all-gather.5
  77.4 145.3 all-reduce.1
  225.2 51.5 all-gather.3
  280.4 82.3 reduce-scatter.1

commit v6 on v5

--- a/solution.py
+++ b/solution.py
@@ -8,7 +8,7 @@
 from jax.sharding import PartitionSpec as P
 
 PB = 16
-WIDE = 1
+WIDE = 3
 LANES = 128
 F32 = jnp.float32
 MIB = 1024 * 1024
@@ -168,6 +168,26 @@
     updated_out[...] = tile_ref[...] - change
 
 
+def rotate_body(psi_ref, both_ref, rotated_out, *, row_tiles, tile_size):
+    row_count, _, g_rows, bands = both_ref.shape
+    width = rotated_out.shape[1]
+    pieces = tile_size // g_rows
+    sums = jnp.zeros(rotated_out.shape, F32)
+    for a in range(row_tiles):
+        for r in range(0, row_count, 2):
+            turn = jnp.concatenate(
+                [
+                    both_ref[q, 0, :, (a * pieces + s) * width : (a * pieces + s + 1) * width]
+                    for q in (r, r + 1)
+                    for s in range(pieces)
+                ],
+                axis=0,
+            )
+            at = (a * row_count + r) * tile_size
+            sums = sums + over_k(psi_ref[:, at : at + 2 * tile_size], turn)
+    rotated_out[...] = sums.astype(rotated_out.dtype)
+
+
 def vmem():
     return pl.BlockSpec(memory_space=pltpu.VMEM)
 
@@ -186,7 +206,9 @@
     tiles = bands // tile_size
     where = jnp.stack([row_id, col_id]).astype(jnp.int32)
 
-    both = lax.all_gather(jnp.stack([psi, hpsi]), "row")
+    lanes = bands // width
+    folded = jnp.transpose(eigvec.reshape(lanes, g_rows, width), (1, 0, 2)).reshape(g_rows, bands)
+    both = lax.all_gather(jnp.stack([psi, hpsi, folded]), "row")
 
     k = row_count * 2 * g_rows
     block = (row_count, 2, g_rows, tile_size)
@@ -263,26 +285,28 @@
         jnp.zeros(state.shape, F32),
         jnp.zeros(marks_shape.shape, F32),
     )
-    bound = jnp.where(row_id >= 0, jnp.int32(WIDE), jnp.int32(0))
-    carry = lax.fori_loop(0, lax.optimization_barrier(bound), wide, carry)
-    psi, eigvec, carry = lax.optimization_barrier((psi, eigvec, carry))
+    carry = lax.fori_loop(0, WIDE, wide, carry)
+    psi, carry = lax.optimization_barrier((psi, carry))
     psi_rows = lax.all_gather(psi, "col", axis=0, tiled=True)
-    turn = lax.all_to_all(
-        jnp.broadcast_to(
-            eigvec.reshape(1, row_tiles, tile_size, width), (row_count, row_tiles, tile_size, width)
-        ),
-        "row", 0, 0, tiled=True,
-    )
-    turn, carry = lax.optimization_barrier((turn, carry))
     carry = narrow(jnp.int32(WIDE), carry)
     tile = lax.dynamic_index_in_dim(summed, col_id, 0, keepdims=False)
     overlap, carry = lax.optimization_barrier((overlap, carry))
     correlation = lax.psum_scatter(overlap, "col", scatter_dimension=0, tiled=True)
     for step in range(WIDE + 1, PB - 1):
         carry = narrow(jnp.int32(step), carry)
-    psi_rows, turn, carry = lax.optimization_barrier((psi_rows, turn, carry))
-    turn = jnp.transpose(turn, (1, 0, 2, 3)).reshape(bands, width)
-    rotated = jnp.dot(psi_rows, turn, preferred_element_type=F32).astype(psi.dtype)
+    psi_rows, both, carry = lax.optimization_barrier((psi_rows, both, carry))
+    rotated = pl.pallas_call(
+        functools.partial(rotate_body, row_tiles=row_tiles, tile_size=tile_size),
+        out_shape=jax.ShapeDtypeStruct((g_rows * col_count, width), psi.dtype),
+        grid=(1,),
+        in_specs=[
+            pl.BlockSpec((g_rows * col_count, bands), lambda i: (0, 0)),
+            pl.BlockSpec((row_count, 1, g_rows, bands), lambda i: (0, 2, 0, 0)),
+        ],
+        out_specs=pl.BlockSpec((g_rows * col_count, width), lambda i: (0, 0)),
+        compiler_params=pltpu.CompilerParams(vmem_limit_bytes=60 * MIB),
+        name="rotate",
+    )(psi_rows, both)
     recv, vecs, images, marks = narrow(jnp.int32(PB - 1), carry)
 
     updated = pl.pallas_call(

time: 416 us -> 386 us (0.928)
  waiting for transfers between devices: 180 us -> 141 us
  starting transfers between devices: 49.2 us -> 78.2 us
  blocking collectives: 113 us -> 87.2 us
  Pallas kernels: 33.8 us -> 44.3 us
    all_to_all x1 -> x0, waiting for transfers between devices: 80.8 us -> none  [on_device(): lax.all_to_all(jnp.broadcast_to(eigvec.reshape(1, row_tiles, tile_size, w...]
    all_to_all x1 -> x3, starting transfers between devices: 22.4 us -> 56.8 us  [wide(): lax.all_to_all(send, ('row', 'col'), 0, 0, tiled=True)]
    all_to_all x12 -> x10, blocking collectives: 113 us -> 87.2 us  [narrow(): return (lax.all_to_all(send, 'row', 0, 0, tiled=True), vecs, images, marks)]
    all_to_all x1 -> x3, waiting for transfers between devices: 9.57 us -> 31 us  [wide(): lax.all_to_all(send, ('row', 'col'), 0, 0, tiled=True)]
    all_gather x1, waiting for transfers between devices: 56.2 us -> 74.9 us  [on_device(): both = lax.all_gather(jnp.stack([psi, hpsi, folded]), 'row')]
    pallas_call x16, Pallas kernels: 20.9 us -> 26.8 us  [advance(): pl.pallas_call(functools.partial(step_body, row_count=row_count), out_sha...]
    all_to_all x1 -> x0, starting transfers between devices: 5.22 us -> none  [on_device(): lax.all_to_all(jnp.broadcast_to(eigvec.reshape(1, row_tiles, tile_size, w...]
    pallas_call x0 -> x1, Pallas kernels: none -> 4.81 us  [on_device(): pl.pallas_call(functools.partial(rotate_body, row_tiles=row_tiles, tile_s...]
  transfers between devices with their start and end apart: 11 -> 12, of which waited for: 8 -> 8; matrix products, arithmetic and copies ran while one was open for 3% -> 2% of each run, Pallas kernels for 5% -> 9%
where the time goes in v6:
time: 386 us; the launch traced here: 385 us
  waiting for transfers between devices  141 us (37%)
  blocking collectives  87.2 us (23%)
  starting transfers between devices  78.2 us (20%)
  Pallas kernels  44.3 us (11%)
  local copies, waits for them, and re-layouts  17.5 us (5%)
  between operations  13.9 us (4%)
    all_to_all x10, blocking collectives, narrow(): return (lax.all_to_all(send, 'row', 0, 0, tiled=True), vecs, images, marks)  87.2 us
    all_gather x1, waiting for transfers between devices, on_device(): both = lax.all_gather(jnp.stack([psi, hpsi, folded]), 'row')  74.9 us
    all_to_all x3, starting transfers between devices, wide(): lax.all_to_all(send, ('row', 'col'), 0, 0, tiled=True)  56.8 us
    all_to_all x3, waiting for transfers between devices, wide(): lax.all_to_all(send, ('row', 'col'), 0, 0, tiled=True)  31 us
    pallas_call x16, Pallas kernels, advance(): pl.pallas_call(functools.partial(step_body, row_count=row_count), out_sha...  26.8 us
    all_to_all x1, waiting for transfers between devices, on_device(): lax.all_to_all(jnp.broadcast_to(strip[None], strip_shape.shape), 'col', 0...  16.4 us
    pallas_call x1, Pallas kernels, on_device(): pl.pallas_call(functools.partial(products_body, row_tiles=row_tiles, col_...  11.1 us
    all_to_all x3, starting transfers between devices, narrow(): return (lax.all_to_all(send, 'row', 0, 0, tiled=True), vecs, images, marks)  11 us
  transfers between devices with their start and end apart: 12, of which 8 were waited for; matrix products, arithmetic and copies ran while one was open for 2% of the time, Pallas kernels for 9%

profile of v6, /device:TPU:1, one launch (start us, length us, event | category | flops | bytes accessed | tf_op | source)
XLA Modules:
  0.0 384.7 jit_solution(5327613258007270914)
XLA Ops:
  7.2 1.1 reshape.32
  8.6 2.0 pad_maximum_fusion
  11.3 74.9 %all-gather.6.cloned.1.call-done = bf16[48,32,4096]{2,1,0:T(8,128)(2,1)} async-done(((bf16[3,32,4096]{2,1,0:T(8,128)(2,1)}), bf16[48,32,4096]{2,1,0:T(8,128)(2,1)}) %all-gather.6.cloned.1.call-update) | async-done | bytes 12582928 | tf_op jit(solution)/shard_map/all_gather | solution.py:211
  86.2 11.1 %products.1 = (f32[8,256,512]{2,1,0:T(8,128)}, f32[8,256,512]{2,1,0:T(8,128)}, f32[8,16,512]{2,1,0:T(8,128)}) custom-call(s32[2]{0:T(128)} %pad_add_fusion.where_ref, bf16[16,3,32,4096]{3,2,1,0:T(8,128)(2,1)} %bitcast.24, bf16[16,3,32,4096]{3,2,1,0:T(8,128)(2,1)} %bitcast.25, bf16[16,3,32,4096]{3,2,1,0:T(8,128)(2,1)} %bitcast.26, ...), custom_call_target="tpu_custom_call" | custom-call | tf_op jit(solution)/shard_map/products/pallas_call | solution.py:226
  97.4 6.4 %all-to-all-start.1 = ((f32[8,16,512]{2,1,0:T(8,128)}), f32[8,16,512]{2,1,0:T(8,128)S(1)}, u32[]{:S(2)}, u32[]{:S(2)}) async-start(f32[8,16,512]{2,1,0:T(8,128)} %get-tuple-element.198), calls=%async_computation.1 | async-start | bytes 524288 | tf_op jit(solution)/shard_map/all_to_all | solution.py:247
  103.8 7.6 %all-to-all-done.1 = f32[8,16,512]{2,1,0:T(8,128)S(1)} async-done(((f32[8,16,512]{2,1,0:T(8,128)}), f32[8,16,512]{2,1,0:T(8,128)S(1)}, u32[]{:S(2)}, u32[]{:S(2)}) %all-to-all-start.1) | async-done | bytes 262176 | tf_op jit(solution)/shard_map/all_to_all | solution.py:247
  112.2 3.8 all-to-all-start.2
  116.0 16.4 %all-to-all-done.2 = f32[8,16,512]{2,1,0:T(8,128)S(1)} async-done(((f32[8,16,512]{2,1,0:T(8,128)}), f32[8,16,512]{2,1,0:T(8,128)S(1)}, u32[]{:S(2)}, u32[]{:S(2)}) %all-to-all-start.2) | async-done | bytes 262176 | tf_op jit(solution)/shard_map/all_to_all | solution.py:249
  132.9 99.7 %while.19 = (s32[]{:T(128)}, f32[128,2,128]{2,1,0:T(2,128)S(1)}, f32[16,32,128]{2,1,0:T(8,128)S(1)}, f32[16,32,128]{2,1,0:T(8,128)S(1)}, f32[8,128]{1,0:T(8,128)...) while((s32[]{:T(128)}, f32[128,2,128]{2,1,0:T(2,128)S(1)}, ...), condition=%wide.region_2.0_spmd, body=%wide.region_1.0_spmd.sunk | while | flops 2 | bytes 393333 | solution.py:288
  132.9 3.9 %reflect.31 = (f32[16,32,128]{2,1,0:T(8,128)S(1)}, f32[16,32,128]{2,1,0:T(8,128)S(1)}, f32[8,128]{1,0:T(8,128)S(1)}, f32[128,2,128]{2,1,0:T(2,128)}) custom-call(s32[1]{0:T(128)} %bitcast.23.step_ref, f32[128,2,128]{2,1,0:T(2,128)S(1)} %get-tuple-element.363.recv_ref, ...), custom_call_target="tpu_custom_call", output_to_operand_aliasing={{0}: (3, {}), {1}: (4, {}), {2}: (5, {})} | custom-call | tf_op jit(solution)/shard_map/while/body/eval_jaxpr/reflect/pallas_call | solution.py:260
  136.8 19.9 %all-to-all-start = ((f32[128,2,128]{2,1,0:T(2,128)}), f32[128,2,128]{2,1,0:T(2,128)S(1)}, u32[]{:S(2)}, u32[]{:S(2)}) async-start(f32[128,2,128]{2,1,0:T(2,128)} %get-tuple-element.350), calls=%async_computation | async-start | bytes 262144 | tf_op jit(solution)/shard_map/while/body/eval_jaxpr/all_to_all | solution.py:276
  156.7 9.6 %all-to-all-done = f32[128,2,128]{2,1,0:T(2,128)S(1)} async-done(((f32[128,2,128]{2,1,0:T(2,128)}), f32[128,2,128]{2,1,0:T(2,128)S(1)}, u32[]{:S(2)}, u32[]{:S(2)}) %all-to-all-start) | async-done | bytes 131104 | tf_op jit(solution)/shard_map/while/body/eval_jaxpr/all_to_all | solution.py:276
  166.3 4.0 %reflect.31 = (f32[16,32,128]{2,1,0:T(8,128)S(1)}, f32[16,32,128]{2,1,0:T(8,128)S(1)}, f32[8,128]{1,0:T(8,128)S(1)}, f32[128,2,128]{2,1,0:T(2,128)}) custom-call(s32[1]{0:T(128)} %bitcast.23.step_ref, f32[128,2,128]{2,1,0:T(2,128)S(1)} %get-tuple-element.363.recv_ref, ...), custom_call_target="tpu_custom_call", output_to_operand_aliasing={{0}: (3, {}), {1}: (4, {}), {2}: (5, {})} | custom-call | tf_op jit(solution)/shard_map/while/body/eval_jaxpr/reflect/pallas_call | solution.py:260
  170.3 4.5 %all-to-all-start = ((f32[128,2,128]{2,1,0:T(2,128)}), f32[128,2,128]{2,1,0:T(2,128)S(1)}, u32[]{:S(2)}, u32[]{:S(2)}) async-start(f32[128,2,128]{2,1,0:T(2,128)} %get-tuple-element.350), calls=%async_computation | async-start | bytes 262144 | tf_op jit(solution)/shard_map/while/body/eval_jaxpr/all_to_all | solution.py:276
  174.8 11.9 %all-to-all-done = f32[128,2,128]{2,1,0:T(2,128)S(1)} async-done(((f32[128,2,128]{2,1,0:T(2,128)}), f32[128,2,128]{2,1,0:T(2,128)S(1)}, u32[]{:S(2)}, u32[]{:S(2)}) %all-to-all-start) | async-done | bytes 131104 | tf_op jit(solution)/shard_map/while/body/eval_jaxpr/all_to_all | solution.py:276
  186.6 3.9 %reflect.31 = (f32[16,32,128]{2,1,0:T(8,128)S(1)}, f32[16,32,128]{2,1,0:T(8,128)S(1)}, f32[8,128]{1,0:T(8,128)S(1)}, f32[128,2,128]{2,1,0:T(2,128)}) custom-call(s32[1]{0:T(128)} %bitcast.23.step_ref, f32[128,2,128]{2,1,0:T(2,128)S(1)} %get-tuple-element.363.recv_ref, ...), custom_call_target="tpu_custom_call", output_to_operand_aliasing={{0}: (3, {}), {1}: (4, {}), {2}: (5, {})} | custom-call | tf_op jit(solution)/shard_map/while/body/eval_jaxpr/reflect/pallas_call | solution.py:260
  190.6 32.4 %all-to-all-start = ((f32[128,2,128]{2,1,0:T(2,128)}), f32[128,2,128]{2,1,0:T(2,128)S(1)}, u32[]{:S(2)}, u32[]{:S(2)}) async-start(f32[128,2,128]{2,1,0:T(2,128)} %get-tuple-element.350), calls=%async_computation | async-start | bytes 262144 | tf_op jit(solution)/shard_map/while/body/eval_jaxpr/all_to_all | solution.py:276
  223.0 9.6 %all-to-all-done = f32[128,2,128]{2,1,0:T(2,128)S(1)} async-done(((f32[128,2,128]{2,1,0:T(2,128)}), f32[128,2,128]{2,1,0:T(2,128)S(1)}, u32[]{:S(2)}, u32[]{:S(2)}) %all-to-all-start) | async-done | bytes 131104 | tf_op jit(solution)/shard_map/while/body/eval_jaxpr/all_to_all | solution.py:276
  232.7 2.2 copy-done
  234.9 1.0 reflect.18
  235.9 9.2 %all_to_all.85.recv_ref = f32[16,2,128]{2,1,0:T(2,128)S(1)} all-to-all(f32[16,2,128]{2,1,0:T(2,128)S(1)} %get-tuple-element.208), channel_id=1, replica_groups=mesh['row'=16,'col'=8] {'row'}, dimensions={0} | all-to-all | bytes 32768 | tf_op jit(solution)/shard_map/all_to_all | solution.py:280
  245.1 2.2 copy-done.1
  248.3 8.6 %all_to_all.86.recv_ref = f32[16,2,128]{2,1,0:T(2,128)S(1)} all-to-all(f32[16,2,128]{2,1,0:T(2,128)S(1)} %get-tuple-element.218), channel_id=1, replica_groups=mesh['row'=16,'col'=8] {'row'}, dimensions={0} | all-to-all | bytes 32768 | tf_op jit(solution)/shard_map/all_to_all | solution.py:280
  257.0 1.0 reflect.20
  258.0 8.6 %all_to_all.87.recv_ref = f32[16,2,128]{2,1,0:T(2,128)S(1)} all-to-all(f32[16,2,128]{2,1,0:T(2,128)S(1)} %get-tuple-element.222), channel_id=1, replica_groups=mesh['row'=16,'col'=8] {'row'}, dimensions={0} | all-to-all | bytes 32768 | tf_op jit(solution)/shard_map/all_to_all | solution.py:280
  266.6 1.0 reflect.21
  267.6 8.8 %all_to_all.88.recv_ref = f32[16,2,128]{2,1,0:T(2,128)S(1)} all-to-all(f32[16,2,128]{2,1,0:T(2,128)S(1)} %get-tuple-element.226), channel_id=1, replica_groups=mesh['row'=16,'col'=8] {'row'}, dimensions={0} | all-to-all | bytes 32768 | tf_op jit(solution)/shard_map/all_to_all | solution.py:280
  277.4 8.6 %all_to_all.89.recv_ref = f32[16,2,128]{2,1,0:T(2,128)S(1)} all-to-all(f32[16,2,128]{2,1,0:T(2,128)S(1)} %get-tuple-element.230), channel_id=1, replica_groups=mesh['row'=16,'col'=8] {'row'}, dimensions={0} | all-to-all | bytes 32768 | tf_op jit(solution)/shard_map/all_to_all | solution.py:280
  287.1 8.6 %all_to_all.90.recv_ref = f32[16,2,128]{2,1,0:T(2,128)S(1)} all-to-all(f32[16,2,128]{2,1,0:T(2,128)S(1)} %get-tuple-element.234), channel_id=1, replica_groups=mesh['row'=16,'col'=8] {'row'}, dimensions={0} | all-to-all | bytes 32768 | tf_op jit(solution)/shard_map/all_to_all | solution.py:280
  296.8 8.6 %all_to_all.91.recv_ref = f32[16,2,128]{2,1,0:T(2,128)S(1)} all-to-all(f32[16,2,128]{2,1,0:T(2,128)S(1)} %get-tuple-element.238), channel_id=1, replica_groups=mesh['row'=16,'col'=8] {'row'}, dimensions={0} | all-to-all | bytes 32768 | tf_op jit(solution)/shard_map/all_to_all | solution.py:280
  306.4 8.6 %all_to_all.92.recv_ref = f32[16,2,128]{2,1,0:T(2,128)S(1)} all-to-all(f32[16,2,128]{2,1,0:T(2,128)S(1)} %get-tuple-element.242), channel_id=1, replica_groups=mesh['row'=16,'col'=8] {'row'}, dimensions={0} | all-to-all | bytes 32768 | tf_op jit(solution)/shard_map/all_to_all | solution.py:280
  316.1 8.6 %all_to_all.93.recv_ref = f32[16,2,128]{2,1,0:T(2,128)S(1)} all-to-all(f32[16,2,128]{2,1,0:T(2,128)S(1)} %get-tuple-element.246), channel_id=1, replica_groups=mesh['row'=16,'col'=8] {'row'}, dimensions={0} | all-to-all | bytes 32768 | tf_op jit(solution)/shard_map/all_to_all | solution.py:280
  325.7 8.7 %all_to_all.94.recv_ref = f32[16,2,128]{2,1,0:T(2,128)S(1)} all-to-all(f32[16,2,128]{2,1,0:T(2,128)S(1)} %get-tuple-element.250), channel_id=1, replica_groups=mesh['row'=16,'col'=8] {'row'}, dimensions={0} | all-to-all | bytes 32768 | tf_op jit(solution)/shard_map/all_to_all | solution.py:280
  334.4 1.6 reflect.28
  336.0 3.7 all-to-all-start.13
  339.7 5.9 %all-to-all-done.13.recv_ref = f32[16,2,128]{2,1,0:T(2,128)S(1)} async-done(((f32[16,2,128]{2,1,0:T(2,128)}), f32[16,2,128]{2,1,0:T(2,128)S(1)}, u32[]{:S(2)}, u32[]{:S(2)}) %all-to-all-start.13) | async-done | bytes 16416 | tf_op jit(solution)/shard_map/all_to_all | solution.py:280
  345.6 2.2 copy-done.2
  347.8 1.6 reflect.29
  349.4 3.7 all-to-all-start.14
  353.1 1.1 dynamic-slice_bitcast_fusion.tile_ref
  354.2 4.9 %all-to-all-done.14.recv_ref = f32[16,2,128]{2,1,0:T(2,128)S(1)} async-done(((f32[16,2,128]{2,1,0:T(2,128)}), f32[16,2,128]{2,1,0:T(2,128)S(1)}, u32[]{:S(2)}, u32[]{:S(2)}) %all-to-all-start.14) | async-done | bytes 16416 | tf_op jit(solution)/shard_map/all_to_all | solution.py:280
  359.1 2.2 copy-done.3
  361.3 1.6 reflect.30
  362.9 3.7 all-to-all-start.15
  367.1 4.8 %rotate.1 = bf16[256,512]{1,0:T(8,128)(2,1)} custom-call(bf16[256,4096]{1,0:T(8,128)(2,1)} %all-gather.4.cloned.1.call-done.psi_ref, bf16[16,3,32,4096]{3,2,1,0:T(8,128)(2,1)} %bitcast.31), custom_call_target="tpu_custom_call" | custom-call | tf_op jit(solution)/shard_map/rotate/pallas_call | solution.py:298
  371.9 1.7 reshape.37
  373.6 1.5 update.1
  376.2 2.0 reshape.35
  (38 shorter events, 10.8 us)
Async XLA Ops:
  7.2 79.1 %all-gather.6.cloned.1.call-start = ((), (), s32[]{:S(2)}) async-start(), calls=%async_computation.20 | async-start | bytes 13369344 | tf_op jit(solution)/shard_map/all_gather | solution.py:211
  10.6 222.0 %all-reduce.2.cloned.1.call-start = ((), (), s32[]{:S(2)}) async-start(), calls=%async_computation.17 | async-start | bytes 8388608 | tf_op jit(solution)/shard_map/psum | solution.py:246
  97.4 14.1 %all-to-all-start.1 = ((f32[8,16,512]{2,1,0:T(8,128)}), f32[8,16,512]{2,1,0:T(8,128)S(1)}, u32[]{:S(2)}, u32[]{:S(2)}) async-start(f32[8,16,512]{2,1,0:T(8,128)} %get-tuple-element.198), calls=%async_computation.1 | async-start | bytes 524288 | tf_op jit(solution)/shard_map/all_to_all | solution.py:247
  112.2 20.2 %all-to-all-start.2 = ((f32[8,16,512]{2,1,0:T(8,128)}), f32[8,16,512]{2,1,0:T(8,128)S(1)}, u32[]{:S(2)}, u32[]{:S(2)}) async-start(f32[8,16,512]{2,1,0:T(8,128)} %broadcast_in_dim.14), calls=%async_computation.2 | async-start | bytes 524288 | tf_op jit(solution)/shard_map/all_to_all | solution.py:249
  116.0 238.2 %all-gather.4.cloned.1.call-start = ((), (), s32[]{:S(2)}) async-start(), calls=%async_computation.19 | async-start | bytes 2359296 | tf_op jit(solution)/shard_map/all_gather | solution.py:290
  136.8 29.5 %all-to-all-start = ((f32[128,2,128]{2,1,0:T(2,128)}), f32[128,2,128]{2,1,0:T(2,128)S(1)}, u32[]{:S(2)}, u32[]{:S(2)}) async-start(f32[128,2,128]{2,1,0:T(2,128)} %get-tuple-element.350), calls=%async_computation | async-start | bytes 262144 | tf_op jit(solution)/shard_map/while/body/eval_jaxpr/all_to_all | solution.py:276
  170.3 16.3 %all-to-all-start = ((f32[128,2,128]{2,1,0:T(2,128)}), f32[128,2,128]{2,1,0:T(2,128)S(1)}, u32[]{:S(2)}, u32[]{:S(2)}) async-start(f32[128,2,128]{2,1,0:T(2,128)} %get-tuple-element.350), calls=%async_computation | async-start | bytes 262144 | tf_op jit(solution)/shard_map/while/body/eval_jaxpr/all_to_all | solution.py:276
  190.6 42.0 %all-to-all-start = ((f32[128,2,128]{2,1,0:T(2,128)}), f32[128,2,128]{2,1,0:T(2,128)S(1)}, u32[]{:S(2)}, u32[]{:S(2)}) async-start(f32[128,2,128]{2,1,0:T(2,128)} %get-tuple-element.350), calls=%async_computation | async-start | bytes 262144 | tf_op jit(solution)/shard_map/while/body/eval_jaxpr/all_to_all | solution.py:276
  232.6 143.6 %reduce-scatter.2.cloned.1.call-start = ((), (), s32[]{:S(2)}) async-start(), calls=%async_computation.18 | async-start | bytes 4718592 | tf_op jit(solution)/shard_map/reduce_scatter | solution.py:294
  232.7 2.2 copy-start
  245.1 2.2 copy-start.1
  336.0 9.5 %all-to-all-start.13 = ((f32[16,2,128]{2,1,0:T(2,128)}), f32[16,2,128]{2,1,0:T(2,128)S(1)}, u32[]{:S(2)}, u32[]{:S(2)}) async-start(f32[16,2,128]{2,1,0:T(2,128)} %get-tuple-element.254), calls=%async_computation.14 | async-start | bytes 32768 | tf_op jit(solution)/shard_map/all_to_all | solution.py:280
  345.6 2.2 copy-start.2
  349.4 9.7 %all-to-all-start.14 = ((f32[16,2,128]{2,1,0:T(2,128)}), f32[16,2,128]{2,1,0:T(2,128)S(1)}, u32[]{:S(2)}, u32[]{:S(2)}) async-start(f32[16,2,128]{2,1,0:T(2,128)} %get-tuple-element.258), calls=%async_computation.15 | async-start | bytes 32768 | tf_op jit(solution)/shard_map/all_to_all | solution.py:280
  359.1 2.2 copy-start.3
  362.9 10.7 %all-to-all-start.15 = ((f32[16,2,128]{2,1,0:T(2,128)}), f32[16,2,128]{2,1,0:T(2,128)S(1)}, u32[]{:S(2)}, u32[]{:S(2)}) async-start(f32[16,2,128]{2,1,0:T(2,128)} %get-tuple-element.266), calls=%async_computation.16 | async-start | bytes 32768 | tf_op jit(solution)/shard_map/all_to_all | solution.py:280
  367.1 6.5 %copy-start.4 = (s32[2]{0:T(128)S(1)}, s32[2]{0:T(128)}, u32[]{:S(2)}) copy-start(s32[2]{0:T(128)} %pad_add_fusion.where_ref) | copy-start | bytes 28
Sparse Core Ops, SparseCore 0:
  10.7 75.4 all-gather.5
  97.5 113.9 all-reduce.1
  232.7 49.0 all-gather.3
  285.5 82.4 reduce-scatter.1

commit v7 on v5

--- a/solution.py
+++ b/solution.py
@@ -8,7 +8,7 @@
 from jax.sharding import PartitionSpec as P
 
 PB = 16
-WIDE = 1
+WIDE = 3
 LANES = 128
 F32 = jnp.float32
 MIB = 1024 * 1024
@@ -165,7 +165,12 @@
         left, right, (((0,), (0,)), ((), ())),
         precision=lax.Precision.HIGHEST, preferred_element_type=F32,
     )
-    updated_out[...] = tile_ref[...] - change
+    updated_out[...] = tile_ref[0] - change
+
+
+def rotate_body(psi_ref, turn_ref, marks_ref, rotated_out):
+    del marks_ref
+    rotated_out[...] = over_k(psi_ref[...], turn_ref[...]).astype(rotated_out.dtype)
 
 
 def vmem():
@@ -187,6 +192,7 @@
     where = jnp.stack([row_id, col_id]).astype(jnp.int32)
 
     both = lax.all_gather(jnp.stack([psi, hpsi]), "row")
+    turn = lax.all_gather(eigvec.reshape(row_tiles, tile_size, width), "row", axis=1)
 
     k = row_count * 2 * g_rows
     block = (row_count, 2, g_rows, tile_size)
@@ -221,7 +227,8 @@
         name="products",
     )(where, *([both] * len(in_specs)))
 
-    summed = lax.psum(matrix, "col")
+    turn, shared = lax.optimization_barrier((turn, matrix))
+    summed = lax.psum(shared, "col")
     strip = lax.all_to_all(strip, "col", 0, 0, tiled=True)
     strip = jnp.sum(strip, axis=0)
     strip = lax.all_to_all(
@@ -263,38 +270,49 @@
         jnp.zeros(state.shape, F32),
         jnp.zeros(marks_shape.shape, F32),
     )
-    bound = jnp.where(row_id >= 0, jnp.int32(WIDE), jnp.int32(0))
-    carry = lax.fori_loop(0, lax.optimization_barrier(bound), wide, carry)
-    psi, eigvec, carry = lax.optimization_barrier((psi, eigvec, carry))
+    carry = lax.fori_loop(0, WIDE, wide, carry)
+    psi, overlap, carry = lax.optimization_barrier((psi, overlap, carry))
     psi_rows = lax.all_gather(psi, "col", axis=0, tiled=True)
-    turn = lax.all_to_all(
-        jnp.broadcast_to(
-            eigvec.reshape(1, row_tiles, tile_size, width), (row_count, row_tiles, tile_size, width)
-        ),
-        "row", 0, 0, tiled=True,
-    )
-    turn, carry = lax.optimization_barrier((turn, carry))
-    carry = narrow(jnp.int32(WIDE), carry)
-    tile = lax.dynamic_index_in_dim(summed, col_id, 0, keepdims=False)
-    overlap, carry = lax.optimization_barrier((overlap, carry))
     correlation = lax.psum_scatter(overlap, "col", scatter_dimension=0, tiled=True)
-    for step in range(WIDE + 1, PB - 1):
+    for step in range(WIDE, PB - 1):
         carry = narrow(jnp.int32(step), carry)
-    psi_rows, turn, carry = lax.optimization_barrier((psi_rows, turn, carry))
-    turn = jnp.transpose(turn, (1, 0, 2, 3)).reshape(bands, width)
-    rotated = jnp.dot(psi_rows, turn, preferred_element_type=F32).astype(psi.dtype)
+    rotated = pl.pallas_call(
+        rotate_body,
+        out_shape=jax.ShapeDtypeStruct((g_rows * col_count, width), psi.dtype),
+        grid=(1,),
+        in_specs=[
+            pl.BlockSpec((g_rows * col_count, bands), lambda i: (0, 0)),
+            pl.BlockSpec((bands, width), lambda i: (0, 0)),
+            pl.BlockSpec(marks_shape.shape, lambda i: (0, 0)),
+        ],
+        out_specs=pl.BlockSpec((g_rows * col_count, width), lambda i: (0, 0)),
+        compiler_params=pltpu.CompilerParams(vmem_limit_bytes=24 * MIB),
+        name="rotate",
+    )(psi_rows, turn.reshape(bands, width), carry[3])
     recv, vecs, images, marks = narrow(jnp.int32(PB - 1), carry)
+
+    def whole(shape):
+        return pl.BlockSpec(shape, lambda i, where: (0,) * len(shape))
 
     updated = pl.pallas_call(
         functools.partial(last_body, row_count=row_count, col_count=col_count),
         out_shape=jax.ShapeDtypeStruct((height, width), F32),
-        in_specs=[pl.BlockSpec(memory_space=pltpu.SMEM)]
-        + [vmem() for _ in range(5)],
-        out_specs=vmem(),
-        scratch_shapes=[pltpu.VMEM(state.shape, F32), pltpu.VMEM(state.shape, F32)],
+        grid_spec=pltpu.PrefetchScalarGridSpec(
+            num_scalar_prefetch=1,
+            grid=(1,),
+            in_specs=[
+                whole(recv.shape),
+                whole(state.shape),
+                whole(state.shape),
+                whole(marks_shape.shape),
+                pl.BlockSpec((1, height, width), lambda i, where: (where[1], 0, 0)),
+            ],
+            out_specs=whole((height, width)),
+            scratch_shapes=[pltpu.VMEM(state.shape, F32), pltpu.VMEM(state.shape, F32)],
+        ),
         compiler_params=pltpu.CompilerParams(vmem_limit_bytes=24 * MIB),
         name="update",
-    )(where, recv, vecs, images, marks, tile)
+    )(where, recv, vecs, images, marks, summed)
 
     tile_shape = (row_tiles, 1, tile_size, col_tiles, 1, tile_size)
     return (

time: 416 us -> 393 us (0.945)
  waiting for transfers between devices: 180 us -> 142 us
  starting transfers between devices: 49.2 us -> 79.4 us
  blocking collectives: 113 us -> 96.1 us
  Pallas kernels: 33.8 us -> 40.2 us
    all_to_all x1 -> x0, waiting for transfers between devices: 80.8 us -> none  [on_device(): lax.all_to_all(jnp.broadcast_to(eigvec.reshape(1, row_tiles, tile_size, w...]
    all_to_all x1 -> x3, starting transfers between devices: 22.4 us -> 59.6 us  [wide(): lax.all_to_all(send, ('row', 'col'), 0, 0, tiled=True)]
    all_gather x0 -> x1, waiting for transfers between devices: none -> 29.2 us  [on_device(): lax.all_gather(eigvec.reshape(row_tiles, tile_size, width), 'row', axis=1)]
    all_to_all x1 -> x3, waiting for transfers between devices: 9.57 us -> 31.3 us  [wide(): lax.all_to_all(send, ('row', 'col'), 0, 0, tiled=True)]
    all_to_all x12 -> x11, blocking collectives: 113 us -> 96.1 us  [narrow(): return (lax.all_to_all(send, 'row', 0, 0, tiled=True), vecs, images, marks)]
    all_to_all x3 -> x2, waiting for transfers between devices: 11.1 us -> 5.28 us  [narrow(): return (lax.all_to_all(send, 'row', 0, 0, tiled=True), vecs, images, marks)]
    pallas_call x16, Pallas kernels: 20.9 us -> 26.1 us  [advance(): pl.pallas_call(functools.partial(step_body, row_count=row_count), out_sha...]
    all_to_all x1 -> x0, starting transfers between devices: 5.22 us -> none  [on_device(): lax.all_to_all(jnp.broadcast_to(eigvec.reshape(1, row_tiles, tile_size, w...]
  transfers between devices with their start and end apart: 11 -> 12, of which waited for: 8 -> 8; matrix products, arithmetic and copies ran while one was open for 3% -> 1% of each run, Pallas kernels for 5% -> 10%
where the time goes in v7:
time: 393 us; the launch traced here: 392 us
  waiting for transfers between devices  142 us (36%)
  blocking collectives  96.1 us (24%)
  starting transfers between devices  79.4 us (20%)
  Pallas kernels  40.2 us (10%)
  local copies, waits for them, and re-layouts  17.8 us (5%)
  between operations  14 us (4%)
    all_to_all x11, blocking collectives, narrow(): return (lax.all_to_all(send, 'row', 0, 0, tiled=True), vecs, images, marks)  96.1 us
    all_to_all x3, starting transfers between devices, wide(): lax.all_to_all(send, ('row', 'col'), 0, 0, tiled=True)  59.6 us
    all_gather x1, waiting for transfers between devices, on_device(): both = lax.all_gather(jnp.stack([psi, hpsi]), 'row')  54.4 us
    all_to_all x3, waiting for transfers between devices, wide(): lax.all_to_all(send, ('row', 'col'), 0, 0, tiled=True)  31.3 us
    all_gather x1, waiting for transfers between devices, on_device(): lax.all_gather(eigvec.reshape(row_tiles, tile_size, width), 'row', axis=1)  29.2 us
    pallas_call x16, Pallas kernels, advance(): pl.pallas_call(functools.partial(step_body, row_count=row_count), out_sha...  26.1 us
    all_to_all x1, waiting for transfers between devices, on_device(): lax.all_to_all(jnp.broadcast_to(strip[None], strip_shape.shape), 'col', 0...  13.3 us
    pallas_call x1, Pallas kernels, on_device(): pl.pallas_call(functools.partial(products_body, row_tiles=row_tiles, col_...  11.3 us
  transfers between devices with their start and end apart: 12, of which 8 were waited for; matrix products, arithmetic and copies ran while one was open for 1% of the time, Pallas kernels for 10%

profile of v7, /device:TPU:1, one launch (start us, length us, event | category | flops | bytes accessed | tf_op | source)
XLA Modules:
  0.0 391.7 jit_solution(6617639441565815161)
XLA Ops:
  7.2 1.9 pad_maximum_fusion
  9.2 1.8 all_gather_reshape.3
  11.6 54.4 %all-gather.9.cloned.1.call-done = bf16[32,32,4096]{2,1,0:T(8,128)(2,1)} async-done(((bf16[2,32,4096]{2,1,0:T(8,128)(2,1)}), bf16[32,32,4096]{2,1,0:T(8,128)(2,1)}) %all-gather.9.cloned.1.call-update) | async-done | bytes 8388624 | tf_op jit(solution)/shard_map/all_gather | solution.py:194
  66.0 11.3 %products.1 = (f32[8,256,512]{2,1,0:T(8,128)}, f32[8,256,512]{2,1,0:T(8,128)}, f32[8,16,512]{2,1,0:T(8,128)}) custom-call(s32[2]{0:T(128)} %pad_add_fusion.where_ref, bf16[16,2,32,4096]{3,2,1,0:T(8,128)(2,1)} %bitcast.22, bf16[16,2,32,4096]{3,2,1,0:T(8,128)(2,1)} %bitcast.23, bf16[16,2,32,4096]{3,2,1,0:T(8,128)(2,1)} %bitcast.24, ...), custom_call_target="tpu_custom_call" | custom-call | tf_op jit(solution)/shard_map/products/pallas_call | solution.py:210
  77.3 29.2 %all-gather.5.cloned.1.call-done = bf16[2,16,128,512]{3,2,1,0:T(8,128)(2,1)} async-done(((bf16[2,1,128,512]{3,2,1,0:T(8,128)(2,1)}), bf16[2,16,128,512]{3,2,1,0:T(8,128)(2,1)}) %all-gather.5.cloned.1.call-update) | async-done | bytes 4194320 | tf_op jit(solution)/shard_map/all_gather | solution.py:195
  106.6 6.2 %all-to-all-start.1 = ((f32[8,16,512]{2,1,0:T(8,128)}), f32[8,16,512]{2,1,0:T(8,128)S(1)}, u32[]{:S(2)}, u32[]{:S(2)}) async-start(f32[8,16,512]{2,1,0:T(8,128)} %get-tuple-element.190), calls=%async_computation.1 | async-start | bytes 524288 | tf_op jit(solution)/shard_map/all_to_all | solution.py:232
  112.7 7.6 %all-to-all-done.1 = f32[8,16,512]{2,1,0:T(8,128)S(1)} async-done(((f32[8,16,512]{2,1,0:T(8,128)}), f32[8,16,512]{2,1,0:T(8,128)S(1)}, u32[]{:S(2)}, u32[]{:S(2)}) %all-to-all-start.1) | async-done | bytes 262176 | tf_op jit(solution)/shard_map/all_to_all | solution.py:232
  121.0 3.9 all-to-all-start.2
  125.0 13.3 %all-to-all-done.2 = f32[8,16,512]{2,1,0:T(8,128)S(1)} async-done(((f32[8,16,512]{2,1,0:T(8,128)}), f32[8,16,512]{2,1,0:T(8,128)S(1)}, u32[]{:S(2)}, u32[]{:S(2)}) %all-to-all-start.2) | async-done | bytes 262176 | tf_op jit(solution)/shard_map/all_to_all | solution.py:234
  138.7 102.9 %while.19 = (s32[]{:T(128)}, f32[128,2,128]{2,1,0:T(2,128)S(1)}, f32[16,32,128]{2,1,0:T(8,128)S(1)}, f32[16,32,128]{2,1,0:T(8,128)S(1)}, f32[8,128]{1,0:T(8,128)...) while((s32[]{:T(128)}, f32[128,2,128]{2,1,0:T(2,128)S(1)}, ...), condition=%wide.region_2.0_spmd, body=%wide.region_1.0_spmd.sunk | while | flops 2 | bytes 393333 | solution.py:273
  138.7 4.0 %reflect.31 = (f32[16,32,128]{2,1,0:T(8,128)S(1)}, f32[16,32,128]{2,1,0:T(8,128)S(1)}, f32[8,128]{1,0:T(8,128)S(1)}, f32[128,2,128]{2,1,0:T(2,128)}) custom-call(s32[1]{0:T(128)} %bitcast.20.step_ref, f32[128,2,128]{2,1,0:T(2,128)S(1)} %get-tuple-element.347.recv_ref, ...), custom_call_target="tpu_custom_call", output_to_operand_aliasing={{0}: (3, {}), {1}: (4, {}), {2}: (5, {})} | custom-call | tf_op jit(solution)/shard_map/while/body/eval_jaxpr/reflect/pallas_call | solution.py:245
  142.7 9.8 %all-to-all-start = ((f32[128,2,128]{2,1,0:T(2,128)}), f32[128,2,128]{2,1,0:T(2,128)S(1)}, u32[]{:S(2)}, u32[]{:S(2)}) async-start(f32[128,2,128]{2,1,0:T(2,128)} %get-tuple-element.334), calls=%async_computation | async-start | bytes 262144 | tf_op jit(solution)/shard_map/while/body/eval_jaxpr/all_to_all | solution.py:261
  152.5 11.6 %all-to-all-done = f32[128,2,128]{2,1,0:T(2,128)S(1)} async-done(((f32[128,2,128]{2,1,0:T(2,128)}), f32[128,2,128]{2,1,0:T(2,128)S(1)}, u32[]{:S(2)}, u32[]{:S(2)}) %all-to-all-start) | async-done | bytes 131104 | tf_op jit(solution)/shard_map/while/body/eval_jaxpr/all_to_all | solution.py:261
  164.1 4.0 %reflect.31 = (f32[16,32,128]{2,1,0:T(8,128)S(1)}, f32[16,32,128]{2,1,0:T(8,128)S(1)}, f32[8,128]{1,0:T(8,128)S(1)}, f32[128,2,128]{2,1,0:T(2,128)}) custom-call(s32[1]{0:T(128)} %bitcast.20.step_ref, f32[128,2,128]{2,1,0:T(2,128)S(1)} %get-tuple-element.347.recv_ref, ...), custom_call_target="tpu_custom_call", output_to_operand_aliasing={{0}: (3, {}), {1}: (4, {}), {2}: (5, {})} | custom-call | tf_op jit(solution)/shard_map/while/body/eval_jaxpr/reflect/pallas_call | solution.py:245
  168.1 9.2 %all-to-all-start = ((f32[128,2,128]{2,1,0:T(2,128)}), f32[128,2,128]{2,1,0:T(2,128)S(1)}, u32[]{:S(2)}, u32[]{:S(2)}) async-start(f32[128,2,128]{2,1,0:T(2,128)} %get-tuple-element.334), calls=%async_computation | async-start | bytes 262144 | tf_op jit(solution)/shard_map/while/body/eval_jaxpr/all_to_all | solution.py:261
  177.3 10.1 %all-to-all-done = f32[128,2,128]{2,1,0:T(2,128)S(1)} async-done(((f32[128,2,128]{2,1,0:T(2,128)}), f32[128,2,128]{2,1,0:T(2,128)S(1)}, u32[]{:S(2)}, u32[]{:S(2)}) %all-to-all-start) | async-done | bytes 131104 | tf_op jit(solution)/shard_map/while/body/eval_jaxpr/all_to_all | solution.py:261
  187.4 3.9 %reflect.31 = (f32[16,32,128]{2,1,0:T(8,128)S(1)}, f32[16,32,128]{2,1,0:T(8,128)S(1)}, f32[8,128]{1,0:T(8,128)S(1)}, f32[128,2,128]{2,1,0:T(2,128)}) custom-call(s32[1]{0:T(128)} %bitcast.20.step_ref, f32[128,2,128]{2,1,0:T(2,128)S(1)} %get-tuple-element.347.recv_ref, ...), custom_call_target="tpu_custom_call", output_to_operand_aliasing={{0}: (3, {}), {1}: (4, {}), {2}: (5, {})} | custom-call | tf_op jit(solution)/shard_map/while/body/eval_jaxpr/reflect/pallas_call | solution.py:245
  191.4 40.6 %all-to-all-start = ((f32[128,2,128]{2,1,0:T(2,128)}), f32[128,2,128]{2,1,0:T(2,128)S(1)}, u32[]{:S(2)}, u32[]{:S(2)}) async-start(f32[128,2,128]{2,1,0:T(2,128)} %get-tuple-element.334), calls=%async_computation | async-start | bytes 262144 | tf_op jit(solution)/shard_map/while/body/eval_jaxpr/all_to_all | solution.py:261
  232.0 9.6 %all-to-all-done = f32[128,2,128]{2,1,0:T(2,128)S(1)} async-done(((f32[128,2,128]{2,1,0:T(2,128)}), f32[128,2,128]{2,1,0:T(2,128)S(1)}, u32[]{:S(2)}, u32[]{:S(2)}) %all-to-all-start) | async-done | bytes 131104 | tf_op jit(solution)/shard_map/while/body/eval_jaxpr/all_to_all | solution.py:261
  242.2 2.2 copy-done
  244.4 1.0 reflect.18
  245.4 9.3 %all_to_all.85.recv_ref = f32[16,2,128]{2,1,0:T(2,128)S(1)} all-to-all(f32[16,2,128]{2,1,0:T(2,128)S(1)} %get-tuple-element.202), channel_id=1, replica_groups=mesh['row'=16,'col'=8] {'row'}, dimensions={0} | all-to-all | bytes 32768 | tf_op jit(solution)/shard_map/all_to_all | solution.py:265
  254.8 1.0 reflect.19
  255.8 8.6 %all_to_all.86.recv_ref = f32[16,2,128]{2,1,0:T(2,128)S(1)} all-to-all(f32[16,2,128]{2,1,0:T(2,128)S(1)} %get-tuple-element.206), channel_id=1, replica_groups=mesh['row'=16,'col'=8] {'row'}, dimensions={0} | all-to-all | bytes 32768 | tf_op jit(solution)/shard_map/all_to_all | solution.py:265
  264.4 1.0 reflect.20
  265.4 8.6 %all_to_all.87.recv_ref = f32[16,2,128]{2,1,0:T(2,128)S(1)} all-to-all(f32[16,2,128]{2,1,0:T(2,128)S(1)} %get-tuple-element.210), channel_id=1, replica_groups=mesh['row'=16,'col'=8] {'row'}, dimensions={0} | all-to-all | bytes 32768 | tf_op jit(solution)/shard_map/all_to_all | solution.py:265
  274.1 1.0 reflect.21
  275.1 8.8 %all_to_all.88.recv_ref = f32[16,2,128]{2,1,0:T(2,128)S(1)} all-to-all(f32[16,2,128]{2,1,0:T(2,128)S(1)} %get-tuple-element.214), channel_id=1, replica_groups=mesh['row'=16,'col'=8] {'row'}, dimensions={0} | all-to-all | bytes 32768 | tf_op jit(solution)/shard_map/all_to_all | solution.py:265
  283.9 1.0 reflect.22
  284.9 8.6 %all_to_all.89.recv_ref = f32[16,2,128]{2,1,0:T(2,128)S(1)} all-to-all(f32[16,2,128]{2,1,0:T(2,128)S(1)} %get-tuple-element.218), channel_id=1, replica_groups=mesh['row'=16,'col'=8] {'row'}, dimensions={0} | all-to-all | bytes 32768 | tf_op jit(solution)/shard_map/all_to_all | solution.py:265
  294.6 8.6 %all_to_all.90.recv_ref = f32[16,2,128]{2,1,0:T(2,128)S(1)} all-to-all(f32[16,2,128]{2,1,0:T(2,128)S(1)} %get-tuple-element.222), channel_id=1, replica_groups=mesh['row'=16,'col'=8] {'row'}, dimensions={0} | all-to-all | bytes 32768 | tf_op jit(solution)/shard_map/all_to_all | solution.py:265
  304.2 8.6 %all_to_all.91.recv_ref = f32[16,2,128]{2,1,0:T(2,128)S(1)} all-to-all(f32[16,2,128]{2,1,0:T(2,128)S(1)} %get-tuple-element.226), channel_id=1, replica_groups=mesh['row'=16,'col'=8] {'row'}, dimensions={0} | all-to-all | bytes 32768 | tf_op jit(solution)/shard_map/all_to_all | solution.py:265
  313.9 8.8 %all_to_all.92.recv_ref = f32[16,2,128]{2,1,0:T(2,128)S(1)} all-to-all(f32[16,2,128]{2,1,0:T(2,128)S(1)} %get-tuple-element.230), channel_id=1, replica_groups=mesh['row'=16,'col'=8] {'row'}, dimensions={0} | all-to-all | bytes 32768 | tf_op jit(solution)/shard_map/all_to_all | solution.py:265
  323.7 8.6 %all_to_all.93.recv_ref = f32[16,2,128]{2,1,0:T(2,128)S(1)} all-to-all(f32[16,2,128]{2,1,0:T(2,128)S(1)} %get-tuple-element.234), channel_id=1, replica_groups=mesh['row'=16,'col'=8] {'row'}, dimensions={0} | all-to-all | bytes 32768 | tf_op jit(solution)/shard_map/all_to_all | solution.py:265
  333.3 8.6 %all_to_all.94.recv_ref = f32[16,2,128]{2,1,0:T(2,128)S(1)} all-to-all(f32[16,2,128]{2,1,0:T(2,128)S(1)} %get-tuple-element.238), channel_id=1, replica_groups=mesh['row'=16,'col'=8] {'row'}, dimensions={0} | all-to-all | bytes 32768 | tf_op jit(solution)/shard_map/all_to_all | solution.py:265
  343.0 8.6 %all_to_all.95.recv_ref = f32[16,2,128]{2,1,0:T(2,128)S(1)} all-to-all(f32[16,2,128]{2,1,0:T(2,128)S(1)} %get-tuple-element.242), channel_id=1, replica_groups=mesh['row'=16,'col'=8] {'row'}, dimensions={0} | all-to-all | bytes 32768 | tf_op jit(solution)/shard_map/all_to_all | solution.py:265
  351.6 1.6 reflect.29
  353.3 3.7 all-to-all-start.14
  357.0 2.2 copy-done.4
  359.1 1.9 copy-done.5
  361.1 1.2 rotate.1
  363.1 2.2 copy-done.2
  365.3 1.6 reflect.30
  366.9 5.8 %all-to-all-start.15 = ((f32[16,2,128]{2,1,0:T(2,128)}), f32[16,2,128]{2,1,0:T(2,128)S(1)}, u32[]{:S(2)}, u32[]{:S(2)}) async-start(f32[16,2,128]{2,1,0:T(2,128)} %get-tuple-element.250), calls=%async_computation.16 | async-start | bytes 32768 | tf_op jit(solution)/shard_map/all_to_all | solution.py:265
  373.2 5.3 %all-to-all-done.15.recv_ref = f32[16,2,128]{2,1,0:T(2,128)S(1)} async-done(((f32[16,2,128]{2,1,0:T(2,128)}), f32[16,2,128]{2,1,0:T(2,128)S(1)}, u32[]{:S(2)}, u32[]{:S(2)}) %all-to-all-start.15) | async-done | bytes 16416 | tf_op jit(solution)/shard_map/all_to_all | solution.py:265
  378.5 2.2 copy-done.3
  380.7 1.6 update.1
  383.2 2.0 reshape.34
  (41 shorter events, 10.9 us)
Async XLA Ops:
  7.2 58.8 %all-gather.9.cloned.1.call-start = ((), (), s32[]{:S(2)}) async-start(), calls=%async_computation.21 | async-start | bytes 8912896 | tf_op jit(solution)/shard_map/all_gather | solution.py:194
  9.1 97.4 %all-gather.5.cloned.1.call-start = ((), (), s32[]{:S(2)}) async-start(), calls=%async_computation.18 | async-start | bytes 4456448 | tf_op jit(solution)/shard_map/all_gather | solution.py:195
  10.9 231.3 %all-reduce.2.cloned.1.call-start = ((), (), s32[]{:S(2)}) async-start(), calls=%async_computation.19 | async-start | bytes 8388608 | tf_op jit(solution)/shard_map/psum | solution.py:231
  106.6 13.7 %all-to-all-start.1 = ((f32[8,16,512]{2,1,0:T(8,128)}), f32[8,16,512]{2,1,0:T(8,128)S(1)}, u32[]{:S(2)}, u32[]{:S(2)}) async-start(f32[8,16,512]{2,1,0:T(8,128)} %get-tuple-element.190), calls=%async_computation.1 | async-start | bytes 524288 | tf_op jit(solution)/shard_map/all_to_all | solution.py:232
  121.0 17.2 %all-to-all-start.2 = ((f32[8,16,512]{2,1,0:T(8,128)}), f32[8,16,512]{2,1,0:T(8,128)S(1)}, u32[]{:S(2)}, u32[]{:S(2)}) async-start(f32[8,16,512]{2,1,0:T(8,128)} %broadcast_in_dim.14), calls=%async_computation.2 | async-start | bytes 524288 | tf_op jit(solution)/shard_map/all_to_all | solution.py:234
  124.9 232.0 %all-gather.7.cloned.1.call-start = ((), (), s32[]{:S(2)}) async-start(), calls=%async_computation.20 | async-start | bytes 2359296 | tf_op jit(solution)/shard_map/all_gather | solution.py:275
  142.7 21.5 %all-to-all-start = ((f32[128,2,128]{2,1,0:T(2,128)}), f32[128,2,128]{2,1,0:T(2,128)S(1)}, u32[]{:S(2)}, u32[]{:S(2)}) async-start(f32[128,2,128]{2,1,0:T(2,128)} %get-tuple-element.334), calls=%async_computation | async-start | bytes 262144 | tf_op jit(solution)/shard_map/while/body/eval_jaxpr/all_to_all | solution.py:261
  168.1 19.3 %all-to-all-start = ((f32[128,2,128]{2,1,0:T(2,128)}), f32[128,2,128]{2,1,0:T(2,128)S(1)}, u32[]{:S(2)}, u32[]{:S(2)}) async-start(f32[128,2,128]{2,1,0:T(2,128)} %get-tuple-element.334), calls=%async_computation | async-start | bytes 262144 | tf_op jit(solution)/shard_map/while/body/eval_jaxpr/all_to_all | solution.py:261
  191.4 50.2 %all-to-all-start = ((f32[128,2,128]{2,1,0:T(2,128)}), f32[128,2,128]{2,1,0:T(2,128)S(1)}, u32[]{:S(2)}, u32[]{:S(2)}) async-start(f32[128,2,128]{2,1,0:T(2,128)} %get-tuple-element.334), calls=%async_computation | async-start | bytes 262144 | tf_op jit(solution)/shard_map/while/body/eval_jaxpr/all_to_all | solution.py:261
  241.6 141.6 %reduce-scatter.2.cloned.1.call-start = ((), (), s32[]{:S(2)}) async-start(), calls=%async_computation.17 | async-start | bytes 4718592 | tf_op jit(solution)/shard_map/reduce_scatter | solution.py:276
  242.2 2.2 copy-start
  244.4 10.4 %copy-start.1 = (f32[8,256,512]{2,1,0:T(8,128)S(1)}, f32[8,256,512]{2,1,0:T(8,128)}, u32[]{:S(2)}) copy-start(f32[8,256,512]{2,1,0:T(8,128)} %all-reduce.2.cloned.1.call-done.matrix_ref.tile_ref) | copy-start | bytes 12582916
  353.3 9.8 %all-to-all-start.14 = ((f32[16,2,128]{2,1,0:T(2,128)}), f32[16,2,128]{2,1,0:T(2,128)S(1)}, u32[]{:S(2)}, u32[]{:S(2)}) async-start(f32[16,2,128]{2,1,0:T(2,128)} %get-tuple-element.246), calls=%async_computation.15 | async-start | bytes 32768 | tf_op jit(solution)/shard_map/all_to_all | solution.py:265
  356.9 2.2 copy-start.4
  359.1 1.9 copy-start.5
  362.3 16.2 %copy-start.6 = (s32[2]{0:T(128)S(1)}, s32[2]{0:T(128)}, u32[]{:S(2)}) copy-start(s32[2]{0:T(128)} %pad_add_fusion.where_ref) | copy-start | bytes 28
  363.1 2.2 copy-start.2
  366.9 11.6 %all-to-all-start.15 = ((f32[16,2,128]{2,1,0:T(2,128)}), f32[16,2,128]{2,1,0:T(2,128)S(1)}, u32[]{:S(2)}, u32[]{:S(2)}) async-start(f32[16,2,128]{2,1,0:T(2,128)} %get-tuple-element.250), calls=%async_computation.16 | async-start | bytes 32768 | tf_op jit(solution)/shard_map/all_to_all | solution.py:265
  378.5 2.2 copy-start.3
Sparse Core Ops, SparseCore 0:
  10.3 55.6 all-gather.8
  68.2 38.2 all-gather.4
  109.1 114.0 all-reduce.1
  241.7 49.0 all-gather.6
  294.5 82.2 reduce-scatter.1

commit v8 on v7

--- a/solution.py
+++ b/solution.py
@@ -8,7 +8,7 @@
 from jax.sharding import PartitionSpec as P
 
 PB = 16
-WIDE = 3
+WIDE = 2
 LANES = 128
 F32 = jnp.float32
 MIB = 1024 * 1024
@@ -168,9 +168,25 @@
     updated_out[...] = tile_ref[0] - change
 
 
-def rotate_body(psi_ref, turn_ref, marks_ref, rotated_out):
+def rotate_body(psi_ref, both_ref, marks_ref, rotated_out, *, row_tiles, tile_size):
     del marks_ref
-    rotated_out[...] = over_k(psi_ref[...], turn_ref[...]).astype(rotated_out.dtype)
+    row_count, _, g_rows, bands = both_ref.shape
+    width = rotated_out.shape[1]
+    pieces = tile_size // g_rows
+    sums = jnp.zeros(rotated_out.shape, F32)
+    for a in range(row_tiles):
+        for r in range(0, row_count, 2):
+            turn = jnp.concatenate(
+                [
+                    both_ref[q, 0, :, (a * pieces + s) * width : (a * pieces + s + 1) * width]
+                    for q in (r, r + 1)
+                    for s in range(pieces)
+                ],
+                axis=0,
+            )
+            at = (a * row_count + r) * tile_size
+            sums = sums + over_k(psi_ref[:, at : at + 2 * tile_size], turn)
+    rotated_out[...] = sums.astype(rotated_out.dtype)
 
 
 def vmem():
@@ -191,8 +207,9 @@
     tiles = bands // tile_size
     where = jnp.stack([row_id, col_id]).astype(jnp.int32)
 
-    both = lax.all_gather(jnp.stack([psi, hpsi]), "row")
-    turn = lax.all_gather(eigvec.reshape(row_tiles, tile_size, width), "row", axis=1)
+    lanes = bands // width
+    folded = jnp.transpose(eigvec.reshape(lanes, g_rows, width), (1, 0, 2)).reshape(g_rows, bands)
+    both = lax.all_gather(jnp.stack([psi, hpsi, folded]), "row")
 
     k = row_count * 2 * g_rows
     block = (row_count, 2, g_rows, tile_size)
@@ -227,8 +244,7 @@
         name="products",
     )(where, *([both] * len(in_specs)))
 
-    turn, shared = lax.optimization_barrier((turn, matrix))
-    summed = lax.psum(shared, "col")
+    summed = lax.psum(matrix, "col")
     strip = lax.all_to_all(strip, "col", 0, 0, tiled=True)
     strip = jnp.sum(strip, axis=0)
     strip = lax.all_to_all(
@@ -277,18 +293,18 @@
     for step in range(WIDE, PB - 1):
         carry = narrow(jnp.int32(step), carry)
     rotated = pl.pallas_call(
-        rotate_body,
+        functools.partial(rotate_body, row_tiles=row_tiles, tile_size=tile_size),
         out_shape=jax.ShapeDtypeStruct((g_rows * col_count, width), psi.dtype),
         grid=(1,),
         in_specs=[
             pl.BlockSpec((g_rows * col_count, bands), lambda i: (0, 0)),
-            pl.BlockSpec((bands, width), lambda i: (0, 0)),
+            pl.BlockSpec((row_count, 1, g_rows, bands), lambda i: (0, 2, 0, 0)),
             pl.BlockSpec(marks_shape.shape, lambda i: (0, 0)),
         ],
         out_specs=pl.BlockSpec((g_rows * col_count, width), lambda i: (0, 0)),
-        compiler_params=pltpu.CompilerParams(vmem_limit_bytes=24 * MIB),
+        compiler_params=pltpu.CompilerParams(vmem_limit_bytes=60 * MIB),
         name="rotate",
-    )(psi_rows, turn.reshape(bands, width), carry[3])
+    )(psi_rows, both, carry[3])
     recv, vecs, images, marks = narrow(jnp.int32(PB - 1), carry)
 
     def whole(shape):
@@ -310,7 +326,7 @@
             out_specs=whole((height, width)),
             scratch_shapes=[pltpu.VMEM(state.shape, F32), pltpu.VMEM(state.shape, F32)],
         ),
-        compiler_params=pltpu.CompilerParams(vmem_limit_bytes=24 * MIB),
+        compiler_params=pltpu.CompilerParams(vmem_limit_bytes=60 * MIB),
         name="update",
     )(where, recv, vecs, images, marks, summed)
 

time: 393 us -> 376 us (0.957)
  starting transfers between devices: 79.4 us -> 47.4 us
  blocking collectives: 96.1 us -> 106 us
  waiting for transfers between devices: 142 us -> 148 us
  local copies, waits for them, and re-layouts: 17.8 us -> 13.7 us
    all_to_all x3 -> x2, starting transfers between devices: 59.6 us -> 27.5 us  [wide(): lax.all_to_all(send, ('row', 'col'), 0, 0, tiled=True)]
    psum x1, waiting for transfers between devices: 0.02 us -> 21.3 us  [on_device(): summed = lax.psum(matrix, 'col')]
    all_to_all x11 -> x12, blocking collectives: 96.1 us -> 106 us  [narrow(): return (lax.all_to_all(send, 'row', 0, 0, tiled=True), vecs, images, marks)]
    all_to_all x3 -> x2, waiting for transfers between devices: 31.3 us -> 21.4 us  [wide(): lax.all_to_all(send, ('row', 'col'), 0, 0, tiled=True)]
    all_gather x2 -> x1, waiting for transfers between devices: 83.6 us -> 75 us  [on_device(): both = lax.all_gather(jnp.stack([psi, hpsi, folded]), 'row')]
    unnamed x14 -> x8, local copies, waits for them, and re-layouts: 10.7 us -> 5.06 us
  transfers between devices with their start and end apart: 12 -> 10, of which waited for: 8 -> 7; matrix products, arithmetic and copies ran while one was open for 1% -> 2% of each run, Pallas kernels for 10% -> 8%
where the time goes in v8:
time: 376 us; the launch traced here: 374 us
  waiting for transfers between devices  148 us (39%)
  blocking collectives  106 us (28%)
  starting transfers between devices  47.4 us (13%)
  Pallas kernels  42.6 us (11%)
  between operations  13.9 us (4%)
  local copies, waits for them, and re-layouts  13.7 us (4%)
    all_to_all x12, blocking collectives, narrow(): return (lax.all_to_all(send, 'row', 0, 0, tiled=True), vecs, images, marks)  106 us
    all_gather x1, waiting for transfers between devices, on_device(): both = lax.all_gather(jnp.stack([psi, hpsi, folded]), 'row')  75 us
    all_to_all x2, starting transfers between devices, wide(): lax.all_to_all(send, ('row', 'col'), 0, 0, tiled=True)  27.5 us
    pallas_call x16, Pallas kernels, advance(): pl.pallas_call(functools.partial(step_body, row_count=row_count), out_sha...  23.2 us
    all_to_all x2, waiting for transfers between devices, wide(): lax.all_to_all(send, ('row', 'col'), 0, 0, tiled=True)  21.4 us
    psum x1, waiting for transfers between devices, on_device(): summed = lax.psum(matrix, 'col')  21.3 us
    all_to_all x1, waiting for transfers between devices, on_device(): lax.all_to_all(jnp.broadcast_to(strip[None], strip_shape.shape), 'col', 0...  16.4 us
    pallas_call x1, Pallas kernels, on_device(): pl.pallas_call(functools.partial(products_body, row_tiles=row_tiles, col_...  11.1 us
  transfers between devices with their start and end apart: 10, of which 7 were waited for; matrix products, arithmetic and copies ran while one was open for 2% of the time, Pallas kernels for 8%

profile of v8, /device:TPU:1, one launch (start us, length us, event | category | flops | bytes accessed | tf_op | source)
XLA Modules:
  0.0 374.1 jit_solution(584750036103793837)
XLA Ops:
  7.2 1.1 reshape.32
  8.6 2.0 pad_maximum_fusion
  11.2 75.0 %all-gather.6.cloned.1.call-done = bf16[48,32,4096]{2,1,0:T(8,128)(2,1)} async-done(((bf16[3,32,4096]{2,1,0:T(8,128)(2,1)}), bf16[48,32,4096]{2,1,0:T(8,128)(2,1)}) %all-gather.6.cloned.1.call-update) | async-done | bytes 12582928 | tf_op jit(solution)/shard_map/all_gather | solution.py:212
  86.2 11.1 %products.1 = (f32[8,256,512]{2,1,0:T(8,128)}, f32[8,256,512]{2,1,0:T(8,128)}, f32[8,16,512]{2,1,0:T(8,128)}) custom-call(s32[2]{0:T(128)} %pad_add_fusion.where_ref, bf16[16,3,32,4096]{3,2,1,0:T(8,128)(2,1)} %bitcast.22, bf16[16,3,32,4096]{3,2,1,0:T(8,128)(2,1)} %bitcast.23, bf16[16,3,32,4096]{3,2,1,0:T(8,128)(2,1)} %bitcast.24, ...), custom_call_target="tpu_custom_call" | custom-call | tf_op jit(solution)/shard_map/products/pallas_call | solution.py:227
  97.4 6.4 %all-to-all-start.1 = ((f32[8,16,512]{2,1,0:T(8,128)}), f32[8,16,512]{2,1,0:T(8,128)S(1)}, u32[]{:S(2)}, u32[]{:S(2)}) async-start(f32[8,16,512]{2,1,0:T(8,128)} %get-tuple-element.192), calls=%async_computation.1 | async-start | bytes 524288 | tf_op jit(solution)/shard_map/all_to_all | solution.py:248
  103.8 7.6 %all-to-all-done.1 = f32[8,16,512]{2,1,0:T(8,128)S(1)} async-done(((f32[8,16,512]{2,1,0:T(8,128)}), f32[8,16,512]{2,1,0:T(8,128)S(1)}, u32[]{:S(2)}, u32[]{:S(2)}) %all-to-all-start.1) | async-done | bytes 262176 | tf_op jit(solution)/shard_map/all_to_all | solution.py:248
  112.2 3.9 %all-to-all-start.2 = ((f32[8,16,512]{2,1,0:T(8,128)}), f32[8,16,512]{2,1,0:T(8,128)S(1)}, u32[]{:S(2)}, u32[]{:S(2)}) async-start(f32[8,16,512]{2,1,0:T(8,128)} %broadcast_in_dim.14), calls=%async_computation.2 | async-start | bytes 524288 | tf_op jit(solution)/shard_map/all_to_all | solution.py:250
  116.1 16.4 %all-to-all-done.2 = f32[8,16,512]{2,1,0:T(8,128)S(1)} async-done(((f32[8,16,512]{2,1,0:T(8,128)}), f32[8,16,512]{2,1,0:T(8,128)S(1)}, u32[]{:S(2)}, u32[]{:S(2)}) %all-to-all-start.2) | async-done | bytes 262176 | tf_op jit(solution)/shard_map/all_to_all | solution.py:250
  132.9 56.7 %while.19 = (s32[]{:T(128)}, f32[128,2,128]{2,1,0:T(2,128)S(1)}, f32[16,32,128]{2,1,0:T(8,128)S(1)}, f32[16,32,128]{2,1,0:T(8,128)S(1)}, f32[8,128]{1,0:T(8,128)...) while((s32[]{:T(128)}, f32[128,2,128]{2,1,0:T(2,128)S(1)}, ...), condition=%wide.region_2.0_spmd, body=%wide.region_1.0_spmd.sunk | while | flops 2 | bytes 393333 | solution.py:289
  132.9 3.9 %reflect.33 = (f32[16,32,128]{2,1,0:T(8,128)S(1)}, f32[16,32,128]{2,1,0:T(8,128)S(1)}, f32[8,128]{1,0:T(8,128)S(1)}, f32[128,2,128]{2,1,0:T(2,128)}) custom-call(s32[1]{0:T(128)} %bitcast.21.step_ref, f32[128,2,128]{2,1,0:T(2,128)S(1)} %get-tuple-element.351.recv_ref, ...), custom_call_target="tpu_custom_call", output_to_operand_aliasing={{0}: (3, {}), {1}: (4, {}), {2}: (5, {})} | custom-call | tf_op jit(solution)/shard_map/while/body/eval_jaxpr/reflect/pallas_call | solution.py:261
  136.8 22.7 %all-to-all-start = ((f32[128,2,128]{2,1,0:T(2,128)}), f32[128,2,128]{2,1,0:T(2,128)S(1)}, u32[]{:S(2)}, u32[]{:S(2)}) async-start(f32[128,2,128]{2,1,0:T(2,128)} %get-tuple-element.338), calls=%async_computation | async-start | bytes 262144 | tf_op jit(solution)/shard_map/while/body/eval_jaxpr/all_to_all | solution.py:277
  159.5 9.6 %all-to-all-done = f32[128,2,128]{2,1,0:T(2,128)S(1)} async-done(((f32[128,2,128]{2,1,0:T(2,128)}), f32[128,2,128]{2,1,0:T(2,128)S(1)}, u32[]{:S(2)}, u32[]{:S(2)}) %all-to-all-start) | async-done | bytes 131104 | tf_op jit(solution)/shard_map/while/body/eval_jaxpr/all_to_all | solution.py:277
  169.1 3.9 %reflect.33 = (f32[16,32,128]{2,1,0:T(8,128)S(1)}, f32[16,32,128]{2,1,0:T(8,128)S(1)}, f32[8,128]{1,0:T(8,128)S(1)}, f32[128,2,128]{2,1,0:T(2,128)}) custom-call(s32[1]{0:T(128)} %bitcast.21.step_ref, f32[128,2,128]{2,1,0:T(2,128)S(1)} %get-tuple-element.351.recv_ref, ...), custom_call_target="tpu_custom_call", output_to_operand_aliasing={{0}: (3, {}), {1}: (4, {}), {2}: (5, {})} | custom-call | tf_op jit(solution)/shard_map/while/body/eval_jaxpr/reflect/pallas_call | solution.py:261
  173.0 4.8 %all-to-all-start = ((f32[128,2,128]{2,1,0:T(2,128)}), f32[128,2,128]{2,1,0:T(2,128)S(1)}, u32[]{:S(2)}, u32[]{:S(2)}) async-start(f32[128,2,128]{2,1,0:T(2,128)} %get-tuple-element.338), calls=%async_computation | async-start | bytes 262144 | tf_op jit(solution)/shard_map/while/body/eval_jaxpr/all_to_all | solution.py:277
  177.8 11.9 %all-to-all-done = f32[128,2,128]{2,1,0:T(2,128)S(1)} async-done(((f32[128,2,128]{2,1,0:T(2,128)}), f32[128,2,128]{2,1,0:T(2,128)S(1)}, u32[]{:S(2)}, u32[]{:S(2)}) %all-to-all-start) | async-done | bytes 131104 | tf_op jit(solution)/shard_map/while/body/eval_jaxpr/all_to_all | solution.py:277
  190.2 21.3 %all-reduce.2.cloned.1.call-done.matrix_ref.tile_ref = f32[8,256,512]{2,1,0:T(8,128)} async-done(((f32[8,256,512]{2,1,0:T(8,128)}), f32[8,256,512]{2,1,0:T(8,128)}) %all-reduce.2.cloned.1.call-update) | async-done | bytes 4194320 | tf_op jit(solution)/shard_map/psum | solution.py:247
  211.5 2.2 copy-done
  213.7 1.0 reflect.19
  214.7 11.0 %all_to_all.90.recv_ref = f32[16,2,128]{2,1,0:T(2,128)S(1)} all-to-all(f32[16,2,128]{2,1,0:T(2,128)S(1)} %get-tuple-element.203), channel_id=1, replica_groups=mesh['row'=16,'col'=8] {'row'}, dimensions={0} | all-to-all | bytes 32768 | tf_op jit(solution)/shard_map/all_to_all | solution.py:281
  225.7 1.0 reflect.20
  226.7 8.6 %all_to_all.91.recv_ref = f32[16,2,128]{2,1,0:T(2,128)S(1)} all-to-all(f32[16,2,128]{2,1,0:T(2,128)S(1)} %get-tuple-element.207), channel_id=1, replica_groups=mesh['row'=16,'col'=8] {'row'}, dimensions={0} | all-to-all | bytes 32768 | tf_op jit(solution)/shard_map/all_to_all | solution.py:281
  235.4 1.0 reflect.21
  236.4 8.6 %all_to_all.92.recv_ref = f32[16,2,128]{2,1,0:T(2,128)S(1)} all-to-all(f32[16,2,128]{2,1,0:T(2,128)S(1)} %get-tuple-element.211), channel_id=1, replica_groups=mesh['row'=16,'col'=8] {'row'}, dimensions={0} | all-to-all | bytes 32768 | tf_op jit(solution)/shard_map/all_to_all | solution.py:281
  245.0 1.0 reflect.22
  246.1 8.8 %all_to_all.93.recv_ref = f32[16,2,128]{2,1,0:T(2,128)S(1)} all-to-all(f32[16,2,128]{2,1,0:T(2,128)S(1)} %get-tuple-element.215), channel_id=1, replica_groups=mesh['row'=16,'col'=8] {'row'}, dimensions={0} | all-to-all | bytes 32768 | tf_op jit(solution)/shard_map/all_to_all | solution.py:281
  254.9 1.0 reflect.23
  255.9 8.6 %all_to_all.94.recv_ref = f32[16,2,128]{2,1,0:T(2,128)S(1)} all-to-all(f32[16,2,128]{2,1,0:T(2,128)S(1)} %get-tuple-element.219), channel_id=1, replica_groups=mesh['row'=16,'col'=8] {'row'}, dimensions={0} | all-to-all | bytes 32768 | tf_op jit(solution)/shard_map/all_to_all | solution.py:281
  264.5 1.0 reflect.24
  265.5 8.6 %all_to_all.95.recv_ref = f32[16,2,128]{2,1,0:T(2,128)S(1)} all-to-all(f32[16,2,128]{2,1,0:T(2,128)S(1)} %get-tuple-element.223), channel_id=1, replica_groups=mesh['row'=16,'col'=8] {'row'}, dimensions={0} | all-to-all | bytes 32768 | tf_op jit(solution)/shard_map/all_to_all | solution.py:281
  274.2 1.0 reflect.25
  275.2 8.7 %all_to_all.96.recv_ref = f32[16,2,128]{2,1,0:T(2,128)S(1)} all-to-all(f32[16,2,128]{2,1,0:T(2,128)S(1)} %get-tuple-element.227), channel_id=1, replica_groups=mesh['row'=16,'col'=8] {'row'}, dimensions={0} | all-to-all | bytes 32768 | tf_op jit(solution)/shard_map/all_to_all | solution.py:281
  283.9 1.0 reflect.26
  284.9 8.6 %all_to_all.97.recv_ref = f32[16,2,128]{2,1,0:T(2,128)S(1)} all-to-all(f32[16,2,128]{2,1,0:T(2,128)S(1)} %get-tuple-element.231), channel_id=1, replica_groups=mesh['row'=16,'col'=8] {'row'}, dimensions={0} | all-to-all | bytes 32768 | tf_op jit(solution)/shard_map/all_to_all | solution.py:281
  294.6 8.6 %all_to_all.98.recv_ref = f32[16,2,128]{2,1,0:T(2,128)S(1)} all-to-all(f32[16,2,128]{2,1,0:T(2,128)S(1)} %get-tuple-element.235), channel_id=1, replica_groups=mesh['row'=16,'col'=8] {'row'}, dimensions={0} | all-to-all | bytes 32768 | tf_op jit(solution)/shard_map/all_to_all | solution.py:281
  304.2 8.6 %all_to_all.99.recv_ref = f32[16,2,128]{2,1,0:T(2,128)S(1)} all-to-all(f32[16,2,128]{2,1,0:T(2,128)S(1)} %get-tuple-element.239), channel_id=1, replica_groups=mesh['row'=16,'col'=8] {'row'}, dimensions={0} | all-to-all | bytes 32768 | tf_op jit(solution)/shard_map/all_to_all | solution.py:281
  313.9 8.6 %all_to_all.100.recv_ref = f32[16,2,128]{2,1,0:T(2,128)S(1)} all-to-all(f32[16,2,128]{2,1,0:T(2,128)S(1)} %get-tuple-element.243), channel_id=1, replica_groups=mesh['row'=16,'col'=8] {'row'}, dimensions={0} | all-to-all | bytes 32768 | tf_op jit(solution)/shard_map/all_to_all | solution.py:281
  323.6 8.6 %all_to_all.101.recv_ref = f32[16,2,128]{2,1,0:T(2,128)S(1)} all-to-all(f32[16,2,128]{2,1,0:T(2,128)S(1)} %get-tuple-element.247), channel_id=1, replica_groups=mesh['row'=16,'col'=8] {'row'}, dimensions={0} | all-to-all | bytes 32768 | tf_op jit(solution)/shard_map/all_to_all | solution.py:281
  332.2 1.6 reflect.31
  333.8 3.7 all-to-all-start.15
  337.5 4.8 %rotate.1 = bf16[256,512]{1,0:T(8,128)(2,1)} custom-call(bf16[256,4096]{1,0:T(8,128)(2,1)} %all-gather.4.cloned.1.call-done.psi_ref, bf16[16,3,32,4096]{3,2,1,0:T(8,128)(2,1)} %bitcast.29, f32[8,128]{1,0:T(8,128)S(1)} %get-tuple-element.254.marks_ref), custom_call_target="tpu_custom_call" | custom-call | tf_op jit(solution)/shard_map/rotate/pallas_call | solution.py:295
  342.3 1.7 reshape.37
  344.0 2.3 copy-done.2
  346.3 1.6 reflect.32
  347.9 5.8 %all-to-all-start.16 = ((f32[16,2,128]{2,1,0:T(2,128)}), f32[16,2,128]{2,1,0:T(2,128)S(1)}, u32[]{:S(2)}, u32[]{:S(2)}) async-start(f32[16,2,128]{2,1,0:T(2,128)} %get-tuple-element.255), calls=%async_computation.17 | async-start | bytes 32768 | tf_op jit(solution)/shard_map/all_to_all | solution.py:281
  354.2 5.3 %all-to-all-done.16.recv_ref = f32[16,2,128]{2,1,0:T(2,128)S(1)} async-done(((f32[16,2,128]{2,1,0:T(2,128)}), f32[16,2,128]{2,1,0:T(2,128)S(1)}, u32[]{:S(2)}, u32[]{:S(2)}) %all-to-all-start.16) | async-done | bytes 16416 | tf_op jit(solution)/shard_map/all_to_all | solution.py:281
  360.1 3.5 update.1
  363.6 2.0 reshape.36
  365.6 2.0 reshape.35
  (33 shorter events, 7.9 us)
Async XLA Ops:
  7.2 79.1 %all-gather.6.cloned.1.call-start = ((), (), s32[]{:S(2)}) async-start(), calls=%async_computation.21 | async-start | bytes 13369344 | tf_op jit(solution)/shard_map/all_gather | solution.py:212
  10.6 200.9 %all-reduce.2.cloned.1.call-start = ((), (), s32[]{:S(2)}) async-start(), calls=%async_computation.19 | async-start | bytes 8388608 | tf_op jit(solution)/shard_map/psum | solution.py:247
  97.4 14.1 %all-to-all-start.1 = ((f32[8,16,512]{2,1,0:T(8,128)}), f32[8,16,512]{2,1,0:T(8,128)S(1)}, u32[]{:S(2)}, u32[]{:S(2)}) async-start(f32[8,16,512]{2,1,0:T(8,128)} %get-tuple-element.192), calls=%async_computation.1 | async-start | bytes 524288 | tf_op jit(solution)/shard_map/all_to_all | solution.py:248
  112.2 20.3 %all-to-all-start.2 = ((f32[8,16,512]{2,1,0:T(8,128)}), f32[8,16,512]{2,1,0:T(8,128)S(1)}, u32[]{:S(2)}, u32[]{:S(2)}) async-start(f32[8,16,512]{2,1,0:T(8,128)} %broadcast_in_dim.14), calls=%async_computation.2 | async-start | bytes 524288 | tf_op jit(solution)/shard_map/all_to_all | solution.py:250
  116.0 221.5 %all-gather.4.cloned.1.call-start = ((), (), s32[]{:S(2)}) async-start(), calls=%async_computation.20 | async-start | bytes 2359296 | tf_op jit(solution)/shard_map/all_gather | solution.py:291
  136.8 32.3 %all-to-all-start = ((f32[128,2,128]{2,1,0:T(2,128)}), f32[128,2,128]{2,1,0:T(2,128)S(1)}, u32[]{:S(2)}, u32[]{:S(2)}) async-start(f32[128,2,128]{2,1,0:T(2,128)} %get-tuple-element.338), calls=%async_computation | async-start | bytes 262144 | tf_op jit(solution)/shard_map/while/body/eval_jaxpr/all_to_all | solution.py:277
  173.0 16.6 %all-to-all-start = ((f32[128,2,128]{2,1,0:T(2,128)}), f32[128,2,128]{2,1,0:T(2,128)S(1)}, u32[]{:S(2)}, u32[]{:S(2)}) async-start(f32[128,2,128]{2,1,0:T(2,128)} %get-tuple-element.338), calls=%async_computation | async-start | bytes 262144 | tf_op jit(solution)/shard_map/while/body/eval_jaxpr/all_to_all | solution.py:277
  189.6 176.0 %reduce-scatter.2.cloned.1.call-start = ((), (), s32[]{:S(2)}) async-start(), calls=%async_computation.18 | async-start | bytes 4718592 | tf_op jit(solution)/shard_map/reduce_scatter | solution.py:292
  211.5 2.2 copy-start
  213.7 12.0 %copy-start.1 = (f32[8,256,512]{2,1,0:T(8,128)S(1)}, f32[8,256,512]{2,1,0:T(8,128)}, u32[]{:S(2)}) copy-start(f32[8,256,512]{2,1,0:T(8,128)} %all-reduce.2.cloned.1.call-done.matrix_ref.tile_ref) | copy-start | bytes 12582916
  333.8 10.2 %all-to-all-start.15 = ((f32[16,2,128]{2,1,0:T(2,128)}), f32[16,2,128]{2,1,0:T(2,128)S(1)}, u32[]{:S(2)}, u32[]{:S(2)}) async-start(f32[16,2,128]{2,1,0:T(2,128)} %get-tuple-element.251), calls=%async_computation.16 | async-start | bytes 32768 | tf_op jit(solution)/shard_map/all_to_all | solution.py:281
  344.0 2.3 copy-start.2
  347.9 11.6 %all-to-all-start.16 = ((f32[16,2,128]{2,1,0:T(2,128)}), f32[16,2,128]{2,1,0:T(2,128)S(1)}, u32[]{:S(2)}, u32[]{:S(2)}) async-start(f32[16,2,128]{2,1,0:T(2,128)} %get-tuple-element.255), calls=%async_computation.17 | async-start | bytes 32768 | tf_op jit(solution)/shard_map/all_to_all | solution.py:281
  359.5 0.6 copy-start.3
Sparse Core Ops, SparseCore 0:
  10.7 75.4 all-gather.5
  97.5 113.9 all-reduce.1
  213.9 51.9 all-gather.3
  269.6 82.3 reduce-scatter.1

commit v9 on v6

--- a/solution.py
+++ b/solution.py
@@ -8,7 +8,7 @@
 from jax.sharding import PartitionSpec as P
 
 PB = 16
-WIDE = 3
+WIDE = 2
 LANES = 128
 F32 = jnp.float32
 MIB = 1024 * 1024
@@ -22,11 +22,11 @@
     return lax.dot_general(left, right, (((1,), (0,)), ((), ())), preferred_element_type=F32)
 
 
-def products_body(where_ref, *refs, row_tiles, col_tiles, gvecs):
+def matrix_body(where_ref, *refs, row_tiles, col_tiles):
     rows = refs[:row_tiles]
     head_ref = refs[row_tiles]
     cols = refs[row_tiles + 1 : row_tiles + 1 + col_tiles]
-    matrix_out, overlap_out, strip_out, left_vmem, left_psi_vmem = refs[row_tiles + 1 + col_tiles :]
+    matrix_out, strip_out, left_vmem = refs[row_tiles + 1 + col_tiles :]
     height = row_tiles * LANES
 
     def swapped(x):
@@ -35,17 +35,27 @@
     @pl.when(pl.program_id(0) == 0)
     def _():
         for k, ref in enumerate(rows):
-            at = pl.ds(k * LANES, LANES)
-            left_vmem[at, :] = swapped(ref[...]).T
-            left_psi_vmem[at, :] = ref[:, 0].reshape(-1, LANES).T
+            left_vmem[pl.ds(k * LANES, LANES), :] = swapped(ref[...]).T
         left_vmem[height:, :] = swapped(head_ref[...]).T[:PB]
 
     both = jnp.concatenate([ref[...].reshape(-1, LANES) for ref in cols], axis=1)
-    psi = jnp.concatenate([ref[:, 0].reshape(-1, LANES) for ref in cols], axis=1)
     mixed = 0.5 * over_k(left_vmem[...], both)
     matrix_out[0] = mixed[:height]
     strip_out[0] = mixed[height:]
-    overlap_out[0] = over_k(left_psi_vmem[...], psi) * (1.0 / gvecs)
+
+
+def overlap_body(where_ref, *refs, row_tiles, col_tiles, gvecs):
+    rows = refs[:row_tiles]
+    cols = refs[row_tiles : row_tiles + col_tiles]
+    overlap_out, left_vmem = refs[row_tiles + col_tiles :]
+
+    @pl.when(pl.program_id(0) == 0)
+    def _():
+        for k, ref in enumerate(rows):
+            left_vmem[pl.ds(k * LANES, LANES), :] = ref[...].reshape(-1, LANES).T
+
+    psi = jnp.concatenate([ref[...].reshape(-1, LANES) for ref in cols], axis=1)
+    overlap_out[0] = over_k(left_vmem[...], psi) * (1.0 / gvecs)
 
 
 def gathered(recv_ref, row_count):
@@ -168,7 +178,11 @@
     updated_out[...] = tile_ref[...] - change
 
 
-def rotate_body(psi_ref, both_ref, rotated_out, *, row_tiles, tile_size):
+def rotate_body(
+    where_ref, psi_ref, both_ref, marks_ref, block_ref, rotated_out, tile_out, *, row_tiles, tile_size
+):
+    del where_ref, marks_ref
+    tile_out[...] = block_ref[0]
     row_count, _, g_rows, bands = both_ref.shape
     width = rotated_out.shape[1]
     pieces = tile_size // g_rows
@@ -210,44 +224,56 @@
     folded = jnp.transpose(eigvec.reshape(lanes, g_rows, width), (1, 0, 2)).reshape(g_rows, bands)
     both = lax.all_gather(jnp.stack([psi, hpsi, folded]), "row")
 
-    k = row_count * 2 * g_rows
-    block = (row_count, 2, g_rows, tile_size)
-
-    def column_block(index):
-        return pl.BlockSpec(block, lambda c, where: (0, 0, 0, index(c, where)))
-
-    in_specs = (
-        [column_block(lambda c, where, a=a: where[0] + a * row_count) for a in range(row_tiles)]
-        + [column_block(lambda c, where: 0)]
-        + [column_block(lambda c, where, a=a: c + a * col_count) for a in range(col_tiles)]
-    )
     blocks_shape = jax.ShapeDtypeStruct((col_count, height, width), F32)
     strip_shape = jax.ShapeDtypeStruct((col_count, PB, width), F32)
-    matrix, overlap, strip = pl.pallas_call(
-        functools.partial(products_body, row_tiles=row_tiles, col_tiles=col_tiles, gvecs=gvecs),
-        out_shape=(blocks_shape, blocks_shape, strip_shape),
-        grid_spec=pltpu.PrefetchScalarGridSpec(
-            num_scalar_prefetch=1,
-            grid=(col_count,),
-            in_specs=in_specs,
-            out_specs=tuple(
-                pl.BlockSpec((1, *made.shape[1:]), lambda c, where: (c, 0, 0))
-                for made in (blocks_shape, blocks_shape, strip_shape)
+
+    def products(body, source, kinds, with_head, made, name):
+        def column_block(index):
+            return pl.BlockSpec(
+                (row_count, kinds, g_rows, tile_size), lambda c, where: (0, 0, 0, index(c, where))
+            )
+
+        in_specs = [
+            column_block(lambda c, where, a=a: where[0] + a * row_count) for a in range(row_tiles)
+        ]
+        if with_head:
+            in_specs.append(column_block(lambda c, where: 0))
+        in_specs += [
+            column_block(lambda c, where, a=a: c + a * col_count) for a in range(col_tiles)
+        ]
+        left = (height + PB * with_head, row_count * kinds * g_rows)
+        return pl.pallas_call(
+            body,
+            out_shape=made,
+            grid_spec=pltpu.PrefetchScalarGridSpec(
+                num_scalar_prefetch=1,
+                grid=(col_count,),
+                in_specs=in_specs,
+                out_specs=tuple(
+                    pl.BlockSpec((1, *one.shape[1:]), lambda c, where: (c, 0, 0)) for one in made
+                ),
+                scratch_shapes=[pltpu.VMEM(left, psi.dtype)],
             ),
-            scratch_shapes=[
-                pltpu.VMEM((height + PB, k), psi.dtype),
-                pltpu.VMEM((height, k // 2), psi.dtype),
-            ],
-        ),
-        compiler_params=pltpu.CompilerParams(vmem_limit_bytes=60 * MIB),
-        name="products",
-    )(where, *([both] * len(in_specs)))
+            compiler_params=pltpu.CompilerParams(vmem_limit_bytes=60 * MIB),
+            name=name,
+        )(where, *([source] * len(in_specs)))
+
+    matrix, strip = products(
+        functools.partial(matrix_body, row_tiles=row_tiles, col_tiles=col_tiles),
+        both, 2, 1, (blocks_shape, strip_shape), "products",
+    )
 
     summed = lax.psum(matrix, "col")
     strip = lax.all_to_all(strip, "col", 0, 0, tiled=True)
     strip = jnp.sum(strip, axis=0)
     strip = lax.all_to_all(
         jnp.broadcast_to(strip[None], strip_shape.shape), "col", 0, 0, tiled=True
+    )
+    (overlap,) = products(
+        functools.partial(
+            overlap_body, row_tiles=row_tiles, col_tiles=col_tiles, gvecs=gvecs
+        ),
+        both, 1, 0, (blocks_shape,), "overlaps",
     )
     panel = jnp.transpose(
         strip.reshape(col_count, PB, row_tiles, col_tiles // row_tiles, tile_size), (1, 3, 0, 2, 4)
@@ -286,34 +312,40 @@
         jnp.zeros(marks_shape.shape, F32),
     )
     carry = lax.fori_loop(0, WIDE, wide, carry)
-    psi, carry = lax.optimization_barrier((psi, carry))
+    psi, overlap, carry = lax.optimization_barrier((psi, overlap, carry))
     psi_rows = lax.all_gather(psi, "col", axis=0, tiled=True)
-    carry = narrow(jnp.int32(WIDE), carry)
-    tile = lax.dynamic_index_in_dim(summed, col_id, 0, keepdims=False)
-    overlap, carry = lax.optimization_barrier((overlap, carry))
     correlation = lax.psum_scatter(overlap, "col", scatter_dimension=0, tiled=True)
-    for step in range(WIDE + 1, PB - 1):
+    for step in range(WIDE, PB - 1):
         carry = narrow(jnp.int32(step), carry)
-    psi_rows, both, carry = lax.optimization_barrier((psi_rows, both, carry))
-    rotated = pl.pallas_call(
+    rotated, tile = pl.pallas_call(
         functools.partial(rotate_body, row_tiles=row_tiles, tile_size=tile_size),
-        out_shape=jax.ShapeDtypeStruct((g_rows * col_count, width), psi.dtype),
-        grid=(1,),
-        in_specs=[
-            pl.BlockSpec((g_rows * col_count, bands), lambda i: (0, 0)),
-            pl.BlockSpec((row_count, 1, g_rows, bands), lambda i: (0, 2, 0, 0)),
-        ],
-        out_specs=pl.BlockSpec((g_rows * col_count, width), lambda i: (0, 0)),
+        out_shape=(
+            jax.ShapeDtypeStruct((g_rows * col_count, width), psi.dtype),
+            jax.ShapeDtypeStruct((height, width), F32),
+        ),
+        grid_spec=pltpu.PrefetchScalarGridSpec(
+            num_scalar_prefetch=1,
+            grid=(1,),
+            in_specs=[
+                pl.BlockSpec((g_rows * col_count, bands), lambda i, where: (0, 0)),
+                pl.BlockSpec((row_count, 1, g_rows, bands), lambda i, where: (0, 2, 0, 0)),
+                pl.BlockSpec(marks_shape.shape, lambda i, where: (0, 0)),
+                pl.BlockSpec((1, height, width), lambda i, where: (where[1], 0, 0)),
+            ],
+            out_specs=(
+                pl.BlockSpec((g_rows * col_count, width), lambda i, where: (0, 0)),
+                pl.BlockSpec((height, width), lambda i, where: (0, 0)),
+            ),
+        ),
         compiler_params=pltpu.CompilerParams(vmem_limit_bytes=60 * MIB),
         name="rotate",
-    )(psi_rows, both)
+    )(where, psi_rows, both, carry[3], summed)
     recv, vecs, images, marks = narrow(jnp.int32(PB - 1), carry)
 
     updated = pl.pallas_call(
         functools.partial(last_body, row_count=row_count, col_count=col_count),
         out_shape=jax.ShapeDtypeStruct((height, width), F32),
-        in_specs=[pl.BlockSpec(memory_space=pltpu.SMEM)]
-        + [vmem() for _ in range(5)],
+        in_specs=[pl.BlockSpec(memory_space=pltpu.SMEM)] + [vmem() for _ in range(5)],
         out_specs=vmem(),
         scratch_shapes=[pltpu.VMEM(state.shape, F32), pltpu.VMEM(state.shape, F32)],
         compiler_params=pltpu.CompilerParams(vmem_limit_bytes=24 * MIB),

time: 386 us -> 372 us (0.964)
  starting transfers between devices: 78.2 us -> 44.2 us
  blocking collectives: 87.2 us -> 106 us
  local copies, waits for them, and re-layouts: 17.5 us -> 12.2 us
  Pallas kernels: 44.3 us -> 49.5 us
    all_to_all x3 -> x2, starting transfers between devices: 56.8 us -> 24.3 us  [wide(): lax.all_to_all(send, ('row', 'col'), 0, 0, tiled=True)]
    psum x1, waiting for transfers between devices: 0.02 us -> 24.4 us  [on_device(): summed = lax.psum(matrix, 'col')]
    all_to_all x10 -> x12, blocking collectives: 87.2 us -> 106 us  [narrow(): return (lax.all_to_all(send, 'row', 0, 0, tiled=True), vecs, images, marks)]
    all_to_all x3 -> x2, waiting for transfers between devices: 31 us -> 21.4 us  [wide(): lax.all_to_all(send, ('row', 'col'), 0, 0, tiled=True)]
    all_to_all x1, waiting for transfers between devices: 16.4 us -> 7.68 us  [on_device(): lax.all_to_all(jnp.broadcast_to(strip[None], strip_shape.shape), 'col', 0...]
    pallas_call x1 -> x2, Pallas kernels: 11.1 us -> 19 us  [products(): pl.pallas_call(body, out_shape=made, grid_spec=pltpu.PrefetchScalarGridSp...]
    all_to_all x3 -> x2, waiting for transfers between devices: 10.8 us -> 5.28 us  [narrow(): return (lax.all_to_all(send, 'row', 0, 0, tiled=True), vecs, images, marks)]
    unnamed x10, local copies, waits for them, and re-layouts: 8.79 us -> 4.47 us
  transfers between devices with their start and end apart: 12 -> 10, of which waited for: 8 -> 7; matrix products, arithmetic and copies ran while one was open for 2% -> 1% of each run, Pallas kernels for 9% -> 11%
where the time goes in v9:
time: 372 us; the launch traced here: 371 us
  waiting for transfers between devices  142 us (38%)
  blocking collectives  106 us (28%)
  Pallas kernels  49.5 us (13%)
  starting transfers between devices  44.2 us (12%)
  between operations  13.9 us (4%)
  local copies, waits for them, and re-layouts  12.2 us (3%)
    all_to_all x12, blocking collectives, narrow(): return (lax.all_to_all(send, 'row', 0, 0, tiled=True), vecs, images, marks)  106 us
    all_gather x1, waiting for transfers between devices, on_device(): both = lax.all_gather(jnp.stack([psi, hpsi, folded]), 'row')  74.9 us
    psum x1, waiting for transfers between devices, on_device(): summed = lax.psum(matrix, 'col')  24.4 us
    all_to_all x2, starting transfers between devices, wide(): lax.all_to_all(send, ('row', 'col'), 0, 0, tiled=True)  24.3 us
    pallas_call x16, Pallas kernels, advance(): pl.pallas_call(functools.partial(step_body, row_count=row_count), out_sha...  23.3 us
    all_to_all x2, waiting for transfers between devices, wide(): lax.all_to_all(send, ('row', 'col'), 0, 0, tiled=True)  21.4 us
    pallas_call x2, Pallas kernels, products(): pl.pallas_call(body, out_shape=made, grid_spec=pltpu.PrefetchScalarGridSp...  19 us
    all_to_all x2, starting transfers between devices, narrow(): return (lax.all_to_all(send, 'row', 0, 0, tiled=True), vecs, images, marks)  9.42 us
  transfers between devices with their start and end apart: 10, of which 7 were waited for; matrix products, arithmetic and copies ran while one was open for 1% of the time, Pallas kernels for 11%

profile of v9, /device:TPU:1, one launch (start us, length us, event | category | flops | bytes accessed | tf_op | source)
XLA Modules:
  0.0 370.8 jit_solution(3607680579505017604)
XLA Ops:
  7.2 1.1 reshape.32
  8.6 2.0 pad_maximum_fusion
  11.3 74.9 %all-gather.6.cloned.1.call-done = bf16[48,32,4096]{2,1,0:T(8,128)(2,1)} async-done(((bf16[3,32,4096]{2,1,0:T(8,128)(2,1)}), bf16[48,32,4096]{2,1,0:T(8,128)(2,1)}) %all-gather.6.cloned.1.call-update) | async-done | bytes 12582928 | tf_op jit(solution)/shard_map/all_gather | solution.py:225
  86.2 10.3 %products.1 = (f32[8,256,512]{2,1,0:T(8,128)}, f32[8,16,512]{2,1,0:T(8,128)}) custom-call(s32[2]{0:T(128)} %pad_add_fusion.where_ref, bf16[16,3,32,4096]{3,2,1,0:T(8,128)(2,1)} %bitcast.22, bf16[16,3,32,4096]{3,2,1,0:T(8,128)(2,1)} %bitcast.23, bf16[16,3,32,4096]{3,2,1,0:T(8,128)(2,1)} %bitcast.24, bf16[16,3,32,4096]{3,2,1,0:T(8,128)(2,1)} %bitcast.25, ...), custom_call_target="tpu_custom_call" | custom-call | tf_op jit(solution)/shard_map/products/pallas_call | solution.py:245
  96.5 6.4 %all-to-all-start.1 = ((f32[8,16,512]{2,1,0:T(8,128)}), f32[8,16,512]{2,1,0:T(8,128)S(1)}, u32[]{:S(2)}, u32[]{:S(2)}) async-start(f32[8,16,512]{2,1,0:T(8,128)} %get-tuple-element.192), calls=%async_computation.1 | async-start | bytes 524288 | tf_op jit(solution)/shard_map/all_to_all | solution.py:267
  103.0 7.6 %all-to-all-done.1 = f32[8,16,512]{2,1,0:T(8,128)S(1)} async-done(((f32[8,16,512]{2,1,0:T(8,128)}), f32[8,16,512]{2,1,0:T(8,128)S(1)}, u32[]{:S(2)}, u32[]{:S(2)}) %all-to-all-start.1) | async-done | bytes 262176 | tf_op jit(solution)/shard_map/all_to_all | solution.py:267
  111.3 3.8 %all-to-all-start.2 = ((f32[8,16,512]{2,1,0:T(8,128)}), f32[8,16,512]{2,1,0:T(8,128)S(1)}, u32[]{:S(2)}, u32[]{:S(2)}) async-start(f32[8,16,512]{2,1,0:T(8,128)} %broadcast_in_dim.14), calls=%async_computation.2 | async-start | bytes 524288 | tf_op jit(solution)/shard_map/all_to_all | solution.py:269
  115.2 8.7 %overlaps.1 = f32[8,256,512]{2,1,0:T(8,128)} custom-call(s32[2]{0:T(128)} %pad_add_fusion.where_ref, bf16[16,3,32,4096]{3,2,1,0:T(8,128)(2,1)} %bitcast.29, bf16[16,3,32,4096]{3,2,1,0:T(8,128)(2,1)} %bitcast.30, bf16[16,3,32,4096]{3,2,1,0:T(8,128)(2,1)} %bitcast.31, bf16[16,3,32,4096]{3,2,1,0:T(8,128)(2,1)} %bitcast.32, bf16[16,3,32,4096]{3,2,1,0:T(8,128)(2,1)} %bitcast.33, ...), custom_call_target="tpu_custom_call" | custom-call | tf_op jit(solution)/shard_map/overlaps/pallas_call | solution.py:245
  123.9 7.7 %all-to-all-done.2 = f32[8,16,512]{2,1,0:T(8,128)S(1)} async-done(((f32[8,16,512]{2,1,0:T(8,128)}), f32[8,16,512]{2,1,0:T(8,128)S(1)}, u32[]{:S(2)}, u32[]{:S(2)}) %all-to-all-start.2) | async-done | bytes 262176 | tf_op jit(solution)/shard_map/all_to_all | solution.py:269
  132.0 53.8 %while.19 = (s32[]{:T(128)}, f32[128,2,128]{2,1,0:T(2,128)S(1)}, f32[16,32,128]{2,1,0:T(8,128)S(1)}, f32[16,32,128]{2,1,0:T(8,128)S(1)}, f32[8,128]{1,0:T(8,128)...) while((s32[]{:T(128)}, f32[128,2,128]{2,1,0:T(2,128)S(1)}, ...), condition=%wide.region_2.0_spmd, body=%wide.region_1.0_spmd.sunk | while | flops 2 | bytes 393333 | solution.py:314
  132.0 3.9 %reflect.33 = (f32[16,32,128]{2,1,0:T(8,128)S(1)}, f32[16,32,128]{2,1,0:T(8,128)S(1)}, f32[8,128]{1,0:T(8,128)S(1)}, f32[128,2,128]{2,1,0:T(2,128)}) custom-call(s32[1]{0:T(128)} %bitcast.21.step_ref, f32[128,2,128]{2,1,0:T(2,128)S(1)} %get-tuple-element.353.recv_ref, ...), custom_call_target="tpu_custom_call", output_to_operand_aliasing={{0}: (3, {}), {1}: (4, {}), {2}: (5, {})} | custom-call | tf_op jit(solution)/shard_map/while/body/eval_jaxpr/reflect/pallas_call | solution.py:286
  135.9 19.9 %all-to-all-start = ((f32[128,2,128]{2,1,0:T(2,128)}), f32[128,2,128]{2,1,0:T(2,128)S(1)}, u32[]{:S(2)}, u32[]{:S(2)}) async-start(f32[128,2,128]{2,1,0:T(2,128)} %get-tuple-element.340), calls=%async_computation | async-start | bytes 262144 | tf_op jit(solution)/shard_map/while/body/eval_jaxpr/all_to_all | solution.py:302
  155.9 9.6 %all-to-all-done = f32[128,2,128]{2,1,0:T(2,128)S(1)} async-done(((f32[128,2,128]{2,1,0:T(2,128)}), f32[128,2,128]{2,1,0:T(2,128)S(1)}, u32[]{:S(2)}, u32[]{:S(2)}) %all-to-all-start) | async-done | bytes 131104 | tf_op jit(solution)/shard_map/while/body/eval_jaxpr/all_to_all | solution.py:302
  165.4 4.0 %reflect.33 = (f32[16,32,128]{2,1,0:T(8,128)S(1)}, f32[16,32,128]{2,1,0:T(8,128)S(1)}, f32[8,128]{1,0:T(8,128)S(1)}, f32[128,2,128]{2,1,0:T(2,128)}) custom-call(s32[1]{0:T(128)} %bitcast.21.step_ref, f32[128,2,128]{2,1,0:T(2,128)S(1)} %get-tuple-element.353.recv_ref, ...), custom_call_target="tpu_custom_call", output_to_operand_aliasing={{0}: (3, {}), {1}: (4, {}), {2}: (5, {})} | custom-call | tf_op jit(solution)/shard_map/while/body/eval_jaxpr/reflect/pallas_call | solution.py:286
  169.5 4.4 %all-to-all-start = ((f32[128,2,128]{2,1,0:T(2,128)}), f32[128,2,128]{2,1,0:T(2,128)S(1)}, u32[]{:S(2)}, u32[]{:S(2)}) async-start(f32[128,2,128]{2,1,0:T(2,128)} %get-tuple-element.340), calls=%async_computation | async-start | bytes 262144 | tf_op jit(solution)/shard_map/while/body/eval_jaxpr/all_to_all | solution.py:302
  173.9 11.9 %all-to-all-done = f32[128,2,128]{2,1,0:T(2,128)S(1)} async-done(((f32[128,2,128]{2,1,0:T(2,128)}), f32[128,2,128]{2,1,0:T(2,128)S(1)}, u32[]{:S(2)}, u32[]{:S(2)}) %all-to-all-start) | async-done | bytes 131104 | tf_op jit(solution)/shard_map/while/body/eval_jaxpr/all_to_all | solution.py:302
  186.4 24.4 %all-reduce.2.cloned.1.call-done.matrix_ref.block_ref = f32[8,256,512]{2,1,0:T(8,128)} async-done(((f32[8,256,512]{2,1,0:T(8,128)}), f32[8,256,512]{2,1,0:T(8,128)}) %all-reduce.2.cloned.1.call-update) | async-done | bytes 4194320 | tf_op jit(solution)/shard_map/psum | solution.py:266
  210.8 2.2 copy-done
  213.0 1.0 reflect.19
  214.0 11.0 %all_to_all.90.recv_ref = f32[16,2,128]{2,1,0:T(2,128)S(1)} all-to-all(f32[16,2,128]{2,1,0:T(2,128)S(1)} %get-tuple-element.203), channel_id=1, replica_groups=mesh['row'=16,'col'=8] {'row'}, dimensions={0} | all-to-all | bytes 32768 | tf_op jit(solution)/shard_map/all_to_all | solution.py:306
  225.0 1.0 reflect.20
  226.0 8.6 %all_to_all.91.recv_ref = f32[16,2,128]{2,1,0:T(2,128)S(1)} all-to-all(f32[16,2,128]{2,1,0:T(2,128)S(1)} %get-tuple-element.207), channel_id=1, replica_groups=mesh['row'=16,'col'=8] {'row'}, dimensions={0} | all-to-all | bytes 32768 | tf_op jit(solution)/shard_map/all_to_all | solution.py:306
  234.7 1.0 reflect.21
  235.7 8.6 %all_to_all.92.recv_ref = f32[16,2,128]{2,1,0:T(2,128)S(1)} all-to-all(f32[16,2,128]{2,1,0:T(2,128)S(1)} %get-tuple-element.211), channel_id=1, replica_groups=mesh['row'=16,'col'=8] {'row'}, dimensions={0} | all-to-all | bytes 32768 | tf_op jit(solution)/shard_map/all_to_all | solution.py:306
  244.3 1.0 reflect.22
  245.3 8.8 %all_to_all.93.recv_ref = f32[16,2,128]{2,1,0:T(2,128)S(1)} all-to-all(f32[16,2,128]{2,1,0:T(2,128)S(1)} %get-tuple-element.215), channel_id=1, replica_groups=mesh['row'=16,'col'=8] {'row'}, dimensions={0} | all-to-all | bytes 32768 | tf_op jit(solution)/shard_map/all_to_all | solution.py:306
  254.1 1.0 reflect.23
  255.1 8.6 %all_to_all.94.recv_ref = f32[16,2,128]{2,1,0:T(2,128)S(1)} all-to-all(f32[16,2,128]{2,1,0:T(2,128)S(1)} %get-tuple-element.219), channel_id=1, replica_groups=mesh['row'=16,'col'=8] {'row'}, dimensions={0} | all-to-all | bytes 32768 | tf_op jit(solution)/shard_map/all_to_all | solution.py:306
  263.8 1.0 reflect.24
  264.8 8.6 %all_to_all.95.recv_ref = f32[16,2,128]{2,1,0:T(2,128)S(1)} all-to-all(f32[16,2,128]{2,1,0:T(2,128)S(1)} %get-tuple-element.223), channel_id=1, replica_groups=mesh['row'=16,'col'=8] {'row'}, dimensions={0} | all-to-all | bytes 32768 | tf_op jit(solution)/shard_map/all_to_all | solution.py:306
  273.4 1.0 reflect.25
  274.4 8.7 %all_to_all.96.recv_ref = f32[16,2,128]{2,1,0:T(2,128)S(1)} all-to-all(f32[16,2,128]{2,1,0:T(2,128)S(1)} %get-tuple-element.227), channel_id=1, replica_groups=mesh['row'=16,'col'=8] {'row'}, dimensions={0} | all-to-all | bytes 32768 | tf_op jit(solution)/shard_map/all_to_all | solution.py:306
  284.2 8.6 %all_to_all.97.recv_ref = f32[16,2,128]{2,1,0:T(2,128)S(1)} all-to-all(f32[16,2,128]{2,1,0:T(2,128)S(1)} %get-tuple-element.231), channel_id=1, replica_groups=mesh['row'=16,'col'=8] {'row'}, dimensions={0} | all-to-all | bytes 32768 | tf_op jit(solution)/shard_map/all_to_all | solution.py:306
  293.9 8.6 %all_to_all.98.recv_ref = f32[16,2,128]{2,1,0:T(2,128)S(1)} all-to-all(f32[16,2,128]{2,1,0:T(2,128)S(1)} %get-tuple-element.235), channel_id=1, replica_groups=mesh['row'=16,'col'=8] {'row'}, dimensions={0} | all-to-all | bytes 32768 | tf_op jit(solution)/shard_map/all_to_all | solution.py:306
  302.5 1.0 reflect.28
  303.5 8.6 %all_to_all.99.recv_ref = f32[16,2,128]{2,1,0:T(2,128)S(1)} all-to-all(f32[16,2,128]{2,1,0:T(2,128)S(1)} %get-tuple-element.239), channel_id=1, replica_groups=mesh['row'=16,'col'=8] {'row'}, dimensions={0} | all-to-all | bytes 32768 | tf_op jit(solution)/shard_map/all_to_all | solution.py:306
  313.2 8.6 %all_to_all.100.recv_ref = f32[16,2,128]{2,1,0:T(2,128)S(1)} all-to-all(f32[16,2,128]{2,1,0:T(2,128)S(1)} %get-tuple-element.243), channel_id=1, replica_groups=mesh['row'=16,'col'=8] {'row'}, dimensions={0} | all-to-all | bytes 32768 | tf_op jit(solution)/shard_map/all_to_all | solution.py:306
  322.8 8.6 %all_to_all.101.recv_ref = f32[16,2,128]{2,1,0:T(2,128)S(1)} all-to-all(f32[16,2,128]{2,1,0:T(2,128)S(1)} %get-tuple-element.247), channel_id=1, replica_groups=mesh['row'=16,'col'=8] {'row'}, dimensions={0} | all-to-all | bytes 32768 | tf_op jit(solution)/shard_map/all_to_all | solution.py:306
  331.5 1.6 reflect.31
  333.1 3.7 all-to-all-start.15
  336.8 5.7 %rotate.1 = (bf16[256,512]{1,0:T(8,128)(2,1)}, f32[256,512]{1,0:T(8,128)}) custom-call(s32[2]{0:T(128)} %pad_add_fusion.where_ref, bf16[256,4096]{1,0:T(8,128)(2,1)} %all-gather.4.cloned.1.call-done.psi_ref, bf16[16,3,32,4096]{3,2,1,0:T(8,128)(2,1)} %bitcast.35, f32[8,128]{1,0:T(8,128)S(1)} %get-tuple-element.254.marks_ref, ...), custom_call_target="tpu_custom_call" | custom-call | tf_op jit(solution)/shard_map/rotate/pallas_call | solution.py:320
  342.5 1.8 reshape.37
  344.3 2.3 copy-done.2
  346.5 1.6 reflect.32
  348.2 5.8 %all-to-all-start.16 = ((f32[16,2,128]{2,1,0:T(2,128)}), f32[16,2,128]{2,1,0:T(2,128)S(1)}, u32[]{:S(2)}, u32[]{:S(2)}) async-start(f32[16,2,128]{2,1,0:T(2,128)} %get-tuple-element.255), calls=%async_computation.17 | async-start | bytes 32768 | tf_op jit(solution)/shard_map/all_to_all | solution.py:306
  354.4 5.3 %all-to-all-done.16.recv_ref = f32[16,2,128]{2,1,0:T(2,128)S(1)} async-done(((f32[16,2,128]{2,1,0:T(2,128)}), f32[16,2,128]{2,1,0:T(2,128)S(1)}, u32[]{:S(2)}, u32[]{:S(2)}) %all-to-all-start.16) | async-done | bytes 16416 | tf_op jit(solution)/shard_map/all_to_all | solution.py:306
  359.7 1.6 update.1
  362.2 2.0 reshape.35
  (36 shorter events, 8.3 us)
Async XLA Ops:
  7.2 79.1 %all-gather.6.cloned.1.call-start = ((), (), s32[]{:S(2)}) async-start(), calls=%async_computation.21 | async-start | bytes 13369344 | tf_op jit(solution)/shard_map/all_gather | solution.py:225
  10.6 200.2 %all-reduce.2.cloned.1.call-start = ((), (), s32[]{:S(2)}) async-start(), calls=%async_computation.19 | async-start | bytes 8388608 | tf_op jit(solution)/shard_map/psum | solution.py:266
  96.5 14.1 %all-to-all-start.1 = ((f32[8,16,512]{2,1,0:T(8,128)}), f32[8,16,512]{2,1,0:T(8,128)S(1)}, u32[]{:S(2)}, u32[]{:S(2)}) async-start(f32[8,16,512]{2,1,0:T(8,128)} %get-tuple-element.192), calls=%async_computation.1 | async-start | bytes 524288 | tf_op jit(solution)/shard_map/all_to_all | solution.py:267
  111.3 20.2 %all-to-all-start.2 = ((f32[8,16,512]{2,1,0:T(8,128)}), f32[8,16,512]{2,1,0:T(8,128)S(1)}, u32[]{:S(2)}, u32[]{:S(2)}) async-start(f32[8,16,512]{2,1,0:T(8,128)} %broadcast_in_dim.14), calls=%async_computation.2 | async-start | bytes 524288 | tf_op jit(solution)/shard_map/all_to_all | solution.py:269
  115.1 221.6 %all-gather.4.cloned.1.call-start = ((), (), s32[]{:S(2)}) async-start(), calls=%async_computation.20 | async-start | bytes 2359296 | tf_op jit(solution)/shard_map/all_gather | solution.py:316
  135.9 29.5 %all-to-all-start = ((f32[128,2,128]{2,1,0:T(2,128)}), f32[128,2,128]{2,1,0:T(2,128)S(1)}, u32[]{:S(2)}, u32[]{:S(2)}) async-start(f32[128,2,128]{2,1,0:T(2,128)} %get-tuple-element.340), calls=%async_computation | async-start | bytes 262144 | tf_op jit(solution)/shard_map/while/body/eval_jaxpr/all_to_all | solution.py:302
  169.5 16.3 %all-to-all-start = ((f32[128,2,128]{2,1,0:T(2,128)}), f32[128,2,128]{2,1,0:T(2,128)S(1)}, u32[]{:S(2)}, u32[]{:S(2)}) async-start(f32[128,2,128]{2,1,0:T(2,128)} %get-tuple-element.340), calls=%async_computation | async-start | bytes 262144 | tf_op jit(solution)/shard_map/while/body/eval_jaxpr/all_to_all | solution.py:302
  185.8 176.4 %reduce-scatter.2.cloned.1.call-start = ((), (), s32[]{:S(2)}) async-start(), calls=%async_computation.18 | async-start | bytes 4718592 | tf_op jit(solution)/shard_map/reduce_scatter | solution.py:317
  210.8 2.2 copy-start
  213.0 12.0 %copy-start.1 = (f32[8,256,512]{2,1,0:T(8,128)S(1)}, f32[8,256,512]{2,1,0:T(8,128)}, u32[]{:S(2)}) copy-start(f32[8,256,512]{2,1,0:T(8,128)} %all-reduce.2.cloned.1.call-done.matrix_ref.block_ref) | copy-start | bytes 12582916
  333.1 11.2 %all-to-all-start.15 = ((f32[16,2,128]{2,1,0:T(2,128)}), f32[16,2,128]{2,1,0:T(2,128)S(1)}, u32[]{:S(2)}, u32[]{:S(2)}) async-start(f32[16,2,128]{2,1,0:T(2,128)} %get-tuple-element.251), calls=%async_computation.16 | async-start | bytes 32768 | tf_op jit(solution)/shard_map/all_to_all | solution.py:306
  342.5 17.2 %copy-start.3 = (f32[256,512]{1,0:T(8,128)S(1)}, f32[256,512]{1,0:T(8,128)}, u32[]{:S(2)}) copy-start(f32[256,512]{1,0:T(8,128)} %get-tuple-element.260.tile_ref) | copy-start | bytes 1572868
  342.5 17.2 %copy-start.4 = (s32[2]{0:T(128)S(1)}, s32[2]{0:T(128)}, u32[]{:S(2)}) copy-start(s32[2]{0:T(128)} %pad_add_fusion.where_ref) | copy-start | bytes 28
  344.3 2.3 copy-start.2
  348.2 11.5 %all-to-all-start.16 = ((f32[16,2,128]{2,1,0:T(2,128)}), f32[16,2,128]{2,1,0:T(2,128)S(1)}, u32[]{:S(2)}, u32[]{:S(2)}) async-start(f32[16,2,128]{2,1,0:T(2,128)} %get-tuple-element.255), calls=%async_computation.17 | async-start | bytes 32768 | tf_op jit(solution)/shard_map/all_to_all | solution.py:306
Sparse Core Ops, SparseCore 0:
  10.7 75.4 all-gather.5
  96.6 114.0 all-reduce.1
  213.1 51.8 all-gather.3
  268.7 82.4 reduce-scatter.1

commit v10 on v9

--- a/solution.py
+++ b/solution.py
@@ -22,11 +22,9 @@
     return lax.dot_general(left, right, (((1,), (0,)), ((), ())), preferred_element_type=F32)
 
 
-def matrix_body(where_ref, *refs, row_tiles, col_tiles):
+def matrix_body(where_ref, *refs, row_tiles):
     rows = refs[:row_tiles]
-    head_ref = refs[row_tiles]
-    cols = refs[row_tiles + 1 : row_tiles + 1 + col_tiles]
-    matrix_out, strip_out, left_vmem = refs[row_tiles + 1 + col_tiles :]
+    head_ref, cols_ref, matrix_out, strip_out, left_vmem = refs[row_tiles:]
     height = row_tiles * LANES
 
     def swapped(x):
@@ -38,7 +36,7 @@
             left_vmem[pl.ds(k * LANES, LANES), :] = swapped(ref[...]).T
         left_vmem[height:, :] = swapped(head_ref[...]).T[:PB]
 
-    both = jnp.concatenate([ref[...].reshape(-1, LANES) for ref in cols], axis=1)
+    both = cols_ref[...].reshape(left_vmem.shape[1], -1)
     mixed = 0.5 * over_k(left_vmem[...], both)
     matrix_out[0] = mixed[:height]
     strip_out[0] = mixed[height:]
@@ -129,7 +127,7 @@
     sums = jnp.zeros((height, LANES), F32)
     for c in range(col_count):
         for a in range(col_tiles):
-            at = spot_of(a * col_count + c, row_count, row_tiles)
+            at = spot_of(c * col_tiles + a, row_count, row_tiles)
             sums = sums + matrix_ref[c, :, a * LANES : (a + 1) * LANES] * vector[0, at : at + 1, :]
     send = jnp.concatenate(
         [
@@ -179,10 +177,12 @@
 
 
 def rotate_body(
-    where_ref, psi_ref, both_ref, marks_ref, block_ref, rotated_out, tile_out, *, row_tiles, tile_size
+    where_ref, psi_ref, both_ref, marks_ref, *refs, row_tiles, tile_size
 ):
+    *blocks, rotated_out, tile_out = refs
     del where_ref, marks_ref
-    tile_out[...] = block_ref[0]
+    for a, ref in enumerate(blocks):
+        tile_out[:, a * LANES : (a + 1) * LANES] = ref[0]
     row_count, _, g_rows, bands = both_ref.shape
     width = rotated_out.shape[1]
     pieces = tile_size // g_rows
@@ -228,9 +228,9 @@
     strip_shape = jax.ShapeDtypeStruct((col_count, PB, width), F32)
 
     def products(body, source, kinds, with_head, made, name):
-        def column_block(index):
+        def column_block(index, wide=tile_size):
             return pl.BlockSpec(
-                (row_count, kinds, g_rows, tile_size), lambda c, where: (0, 0, 0, index(c, where))
+                (row_count, kinds, g_rows, wide), lambda c, where: (0, 0, 0, index(c, where))
             )
 
         in_specs = [
@@ -238,9 +238,11 @@
         ]
         if with_head:
             in_specs.append(column_block(lambda c, where: 0))
-        in_specs += [
-            column_block(lambda c, where, a=a: c + a * col_count) for a in range(col_tiles)
-        ]
+            in_specs.append(column_block(lambda c, where: c, width))
+        else:
+            in_specs += [
+                column_block(lambda c, where, a=a: c + a * col_count) for a in range(col_tiles)
+            ]
         left = (height + PB * with_head, row_count * kinds * g_rows)
         return pl.pallas_call(
             body,
@@ -259,7 +261,7 @@
         )(where, *([source] * len(in_specs)))
 
     matrix, strip = products(
-        functools.partial(matrix_body, row_tiles=row_tiles, col_tiles=col_tiles),
+        functools.partial(matrix_body, row_tiles=row_tiles),
         both, 2, 1, (blocks_shape, strip_shape), "products",
     )
 
@@ -276,7 +278,7 @@
         both, 1, 0, (blocks_shape,), "overlaps",
     )
     panel = jnp.transpose(
-        strip.reshape(col_count, PB, row_tiles, col_tiles // row_tiles, tile_size), (1, 3, 0, 2, 4)
+        strip.reshape(row_tiles, col_count // row_tiles, PB, col_tiles, tile_size), (2, 1, 3, 0, 4)
     ).reshape(PB, tiles, tile_size)
 
     state = jax.ShapeDtypeStruct((PB, tiles, tile_size), F32)
@@ -317,6 +319,13 @@
     correlation = lax.psum_scatter(overlap, "col", scatter_dimension=0, tiled=True)
     for step in range(WIDE, PB - 1):
         carry = narrow(jnp.int32(step), carry)
+    def own_tile(a):
+        def index(i, where):
+            tile = where[1] + a * col_count
+            return lax.div(tile, col_tiles), 0, lax.rem(tile, col_tiles)
+
+        return pl.BlockSpec((1, height, tile_size), index)
+
     rotated, tile = pl.pallas_call(
         functools.partial(rotate_body, row_tiles=row_tiles, tile_size=tile_size),
         out_shape=(
@@ -330,8 +339,8 @@
                 pl.BlockSpec((g_rows * col_count, bands), lambda i, where: (0, 0)),
                 pl.BlockSpec((row_count, 1, g_rows, bands), lambda i, where: (0, 2, 0, 0)),
                 pl.BlockSpec(marks_shape.shape, lambda i, where: (0, 0)),
-                pl.BlockSpec((1, height, width), lambda i, where: (where[1], 0, 0)),
-            ],
+            ]
+            + [own_tile(a) for a in range(col_tiles)],
             out_specs=(
                 pl.BlockSpec((g_rows * col_count, width), lambda i, where: (0, 0)),
                 pl.BlockSpec((height, width), lambda i, where: (0, 0)),
@@ -339,7 +348,7 @@
         ),
         compiler_params=pltpu.CompilerParams(vmem_limit_bytes=60 * MIB),
         name="rotate",
-    )(where, psi_rows, both, carry[3], summed)
+    )(where, psi_rows, both, carry[3], *([summed] * col_tiles))
     recv, vecs, images, marks = narrow(jnp.int32(PB - 1), carry)
 
     updated = pl.pallas_call(

time: 372 us -> 374 us (level)
  waiting for transfers between devices: 142 us -> 151 us
  starting transfers between devices: 44.2 us -> 36.6 us
    psum x1, waiting for transfers between devices: 24.4 us -> 35.8 us  [on_device(): summed = lax.psum(matrix, 'col')]
    all_to_all x2, starting transfers between devices: 24.3 us -> 16.4 us  [wide(): lax.all_to_all(send, ('row', 'col'), 0, 0, tiled=True)]
where the time goes in v10:
time: 374 us; the launch traced here: 372 us
  waiting for transfers between devices  151 us (40%)
  blocking collectives  106 us (28%)
  Pallas kernels  49.5 us (13%)
  starting transfers between devices  36.6 us (10%)
  between operations  13.9 us (4%)
  local copies, waits for them, and re-layouts  12.1 us (3%)
    all_to_all x12, blocking collectives, narrow(): return (lax.all_to_all(send, 'row', 0, 0, tiled=True), vecs, images, marks)  106 us
    all_gather x1, waiting for transfers between devices, on_device(): both = lax.all_gather(jnp.stack([psi, hpsi, folded]), 'row')  74.9 us
    psum x1, waiting for transfers between devices, on_device(): summed = lax.psum(matrix, 'col')  35.8 us
    pallas_call x16, Pallas kernels, advance(): pl.pallas_call(functools.partial(step_body, row_count=row_count), out_sha...  23.2 us
    all_to_all x2, waiting for transfers between devices, wide(): lax.all_to_all(send, ('row', 'col'), 0, 0, tiled=True)  21.9 us
    pallas_call x2, Pallas kernels, products(): pl.pallas_call(body, out_shape=made, grid_spec=pltpu.PrefetchScalarGridSp...  19 us
    all_to_all x2, starting transfers between devices, wide(): lax.all_to_all(send, ('row', 'col'), 0, 0, tiled=True)  16.4 us
    all_to_all x2, starting transfers between devices, narrow(): return (lax.all_to_all(send, 'row', 0, 0, tiled=True), vecs, images, marks)  9.42 us
  transfers between devices with their start and end apart: 10, of which 7 were waited for; matrix products, arithmetic and copies ran while one was open for 1% of the time, Pallas kernels for 11%

profile of v10, /device:TPU:1, one launch (start us, length us, event | category | flops | bytes accessed | tf_op | source)
XLA Modules:
  0.0 372.0 jit_solution(15336608772388022299)
XLA Ops:
  7.2 1.1 reshape.32
  8.6 2.0 pad_maximum_fusion
  11.3 74.9 %all-gather.6.cloned.1.call-done = bf16[48,32,4096]{2,1,0:T(8,128)(2,1)} async-done(((bf16[3,32,4096]{2,1,0:T(8,128)(2,1)}), bf16[48,32,4096]{2,1,0:T(8,128)(2,1)}) %all-gather.6.cloned.1.call-update) | async-done | bytes 12582928 | tf_op jit(solution)/shard_map/all_gather | solution.py:225
  86.2 10.2 %products.1 = (f32[8,256,512]{2,1,0:T(8,128)}, f32[8,16,512]{2,1,0:T(8,128)}) custom-call(s32[2]{0:T(128)} %pad_add_fusion.where_ref, bf16[16,3,32,4096]{3,2,1,0:T(8,128)(2,1)} %bitcast.22, bf16[16,3,32,4096]{3,2,1,0:T(8,128)(2,1)} %bitcast.23, bf16[16,3,32,4096]{3,2,1,0:T(8,128)(2,1)} %bitcast.24, bf16[16,3,32,4096]{3,2,1,0:T(8,128)(2,1)} %bitcast.25), custom_call_target="tpu_custom_call" | custom-call | tf_op jit(solution)/shard_map/products/pallas_call | solution.py:247
  96.5 6.4 %all-to-all-start.1 = ((f32[8,16,512]{2,1,0:T(8,128)}), f32[8,16,512]{2,1,0:T(8,128)S(1)}, u32[]{:S(2)}, u32[]{:S(2)}) async-start(f32[8,16,512]{2,1,0:T(8,128)} %get-tuple-element.192), calls=%async_computation.1 | async-start | bytes 524288 | tf_op jit(solution)/shard_map/all_to_all | solution.py:269
  102.9 7.6 %all-to-all-done.1 = f32[8,16,512]{2,1,0:T(8,128)S(1)} async-done(((f32[8,16,512]{2,1,0:T(8,128)}), f32[8,16,512]{2,1,0:T(8,128)S(1)}, u32[]{:S(2)}, u32[]{:S(2)}) %all-to-all-start.1) | async-done | bytes 262176 | tf_op jit(solution)/shard_map/all_to_all | solution.py:269
  111.3 4.1 %all-to-all-start.2 = ((f32[8,16,512]{2,1,0:T(8,128)}), f32[8,16,512]{2,1,0:T(8,128)S(1)}, u32[]{:S(2)}, u32[]{:S(2)}) async-start(f32[8,16,512]{2,1,0:T(8,128)} %broadcast_in_dim.14), calls=%async_computation.2 | async-start | bytes 524288 | tf_op jit(solution)/shard_map/all_to_all | solution.py:271
  115.5 8.8 %overlaps.1 = f32[8,256,512]{2,1,0:T(8,128)} custom-call(s32[2]{0:T(128)} %pad_add_fusion.where_ref, bf16[16,3,32,4096]{3,2,1,0:T(8,128)(2,1)} %bitcast.26, bf16[16,3,32,4096]{3,2,1,0:T(8,128)(2,1)} %bitcast.27, bf16[16,3,32,4096]{3,2,1,0:T(8,128)(2,1)} %bitcast.28, bf16[16,3,32,4096]{3,2,1,0:T(8,128)(2,1)} %bitcast.29, bf16[16,3,32,4096]{3,2,1,0:T(8,128)(2,1)} %bitcast.30, ...), custom_call_target="tpu_custom_call" | custom-call | tf_op jit(solution)/shard_map/overlaps/pallas_call | solution.py:247
  124.2 5.0 %all-to-all-done.2 = f32[8,16,512]{2,1,0:T(8,128)S(1)} async-done(((f32[8,16,512]{2,1,0:T(8,128)}), f32[8,16,512]{2,1,0:T(8,128)S(1)}, u32[]{:S(2)}, u32[]{:S(2)}) %all-to-all-start.2) | async-done | bytes 262176 | tf_op jit(solution)/shard_map/all_to_all | solution.py:271
  129.6 46.2 %while.19 = (s32[]{:T(128)}, f32[128,2,128]{2,1,0:T(2,128)S(1)}, f32[16,32,128]{2,1,0:T(8,128)S(1)}, f32[16,32,128]{2,1,0:T(8,128)S(1)}, f32[8,128]{1,0:T(8,128)...) while((s32[]{:T(128)}, f32[128,2,128]{2,1,0:T(2,128)S(1)}, ...), condition=%wide.region_2.0_spmd, body=%wide.region_1.0_spmd.sunk | while | flops 2 | bytes 393333 | solution.py:316
  129.6 4.0 %reflect.33 = (f32[16,32,128]{2,1,0:T(8,128)S(1)}, f32[16,32,128]{2,1,0:T(8,128)S(1)}, f32[8,128]{1,0:T(8,128)S(1)}, f32[128,2,128]{2,1,0:T(2,128)}) custom-call(s32[1]{0:T(128)} %bitcast.21.step_ref, f32[128,2,128]{2,1,0:T(2,128)S(1)} %get-tuple-element.353.recv_ref, ...), custom_call_target="tpu_custom_call", output_to_operand_aliasing={{0}: (3, {}), {1}: (4, {}), {2}: (5, {})} | custom-call | tf_op jit(solution)/shard_map/while/body/eval_jaxpr/reflect/pallas_call | solution.py:288
  133.6 6.1 %all-to-all-start = ((f32[128,2,128]{2,1,0:T(2,128)}), f32[128,2,128]{2,1,0:T(2,128)S(1)}, u32[]{:S(2)}, u32[]{:S(2)}) async-start(f32[128,2,128]{2,1,0:T(2,128)} %get-tuple-element.340), calls=%async_computation | async-start | bytes 262144 | tf_op jit(solution)/shard_map/while/body/eval_jaxpr/all_to_all | solution.py:304
  139.7 11.7 %all-to-all-done = f32[128,2,128]{2,1,0:T(2,128)S(1)} async-done(((f32[128,2,128]{2,1,0:T(2,128)}), f32[128,2,128]{2,1,0:T(2,128)S(1)}, u32[]{:S(2)}, u32[]{:S(2)}) %all-to-all-start) | async-done | bytes 131104 | tf_op jit(solution)/shard_map/while/body/eval_jaxpr/all_to_all | solution.py:304
  151.4 3.9 %reflect.33 = (f32[16,32,128]{2,1,0:T(8,128)S(1)}, f32[16,32,128]{2,1,0:T(8,128)S(1)}, f32[8,128]{1,0:T(8,128)S(1)}, f32[128,2,128]{2,1,0:T(2,128)}) custom-call(s32[1]{0:T(128)} %bitcast.21.step_ref, f32[128,2,128]{2,1,0:T(2,128)S(1)} %get-tuple-element.353.recv_ref, ...), custom_call_target="tpu_custom_call", output_to_operand_aliasing={{0}: (3, {}), {1}: (4, {}), {2}: (5, {})} | custom-call | tf_op jit(solution)/shard_map/while/body/eval_jaxpr/reflect/pallas_call | solution.py:288
  155.3 10.3 %all-to-all-start = ((f32[128,2,128]{2,1,0:T(2,128)}), f32[128,2,128]{2,1,0:T(2,128)S(1)}, u32[]{:S(2)}, u32[]{:S(2)}) async-start(f32[128,2,128]{2,1,0:T(2,128)} %get-tuple-element.340), calls=%async_computation | async-start | bytes 262144 | tf_op jit(solution)/shard_map/while/body/eval_jaxpr/all_to_all | solution.py:304
  165.7 10.2 %all-to-all-done = f32[128,2,128]{2,1,0:T(2,128)S(1)} async-done(((f32[128,2,128]{2,1,0:T(2,128)}), f32[128,2,128]{2,1,0:T(2,128)S(1)}, u32[]{:S(2)}, u32[]{:S(2)}) %all-to-all-start) | async-done | bytes 131104 | tf_op jit(solution)/shard_map/while/body/eval_jaxpr/all_to_all | solution.py:304
  176.4 35.8 %all-reduce.2.cloned.1.call-done.matrix_ref.refs_0_.refs_1_.refs_2_.refs_3_ = f32[8,256,512]{2,1,0:T(8,128)} async-done(((f32[8,256,512]{2,1,0:T(8,128)}), f32[8,256,512]{2,1,0:T(8,128)}) %all-reduce.2.cloned.1.call-update) | async-done | bytes 4194320 | tf_op jit(solution)/shard_map/psum | solution.py:268
  212.2 2.2 copy-done
  214.4 1.0 reflect.19
  215.4 10.8 %all_to_all.90.recv_ref = f32[16,2,128]{2,1,0:T(2,128)S(1)} all-to-all(f32[16,2,128]{2,1,0:T(2,128)S(1)} %get-tuple-element.203), channel_id=1, replica_groups=mesh['row'=16,'col'=8] {'row'}, dimensions={0} | all-to-all | bytes 32768 | tf_op jit(solution)/shard_map/all_to_all | solution.py:308
  226.2 1.0 reflect.20
  227.2 8.6 %all_to_all.91.recv_ref = f32[16,2,128]{2,1,0:T(2,128)S(1)} all-to-all(f32[16,2,128]{2,1,0:T(2,128)S(1)} %get-tuple-element.207), channel_id=1, replica_groups=mesh['row'=16,'col'=8] {'row'}, dimensions={0} | all-to-all | bytes 32768 | tf_op jit(solution)/shard_map/all_to_all | solution.py:308
  235.9 1.0 reflect.21
  236.9 8.6 %all_to_all.92.recv_ref = f32[16,2,128]{2,1,0:T(2,128)S(1)} all-to-all(f32[16,2,128]{2,1,0:T(2,128)S(1)} %get-tuple-element.211), channel_id=1, replica_groups=mesh['row'=16,'col'=8] {'row'}, dimensions={0} | all-to-all | bytes 32768 | tf_op jit(solution)/shard_map/all_to_all | solution.py:308
  245.5 1.0 reflect.22
  246.5 8.8 %all_to_all.93.recv_ref = f32[16,2,128]{2,1,0:T(2,128)S(1)} all-to-all(f32[16,2,128]{2,1,0:T(2,128)S(1)} %get-tuple-element.215), channel_id=1, replica_groups=mesh['row'=16,'col'=8] {'row'}, dimensions={0} | all-to-all | bytes 32768 | tf_op jit(solution)/shard_map/all_to_all | solution.py:308
  256.4 8.6 %all_to_all.94.recv_ref = f32[16,2,128]{2,1,0:T(2,128)S(1)} all-to-all(f32[16,2,128]{2,1,0:T(2,128)S(1)} %get-tuple-element.219), channel_id=1, replica_groups=mesh['row'=16,'col'=8] {'row'}, dimensions={0} | all-to-all | bytes 32768 | tf_op jit(solution)/shard_map/all_to_all | solution.py:308
  265.0 1.0 reflect.24
  266.0 8.6 %all_to_all.95.recv_ref = f32[16,2,128]{2,1,0:T(2,128)S(1)} all-to-all(f32[16,2,128]{2,1,0:T(2,128)S(1)} %get-tuple-element.223), channel_id=1, replica_groups=mesh['row'=16,'col'=8] {'row'}, dimensions={0} | all-to-all | bytes 32768 | tf_op jit(solution)/shard_map/all_to_all | solution.py:308
  274.7 1.0 reflect.25
  275.7 8.8 %all_to_all.96.recv_ref = f32[16,2,128]{2,1,0:T(2,128)S(1)} all-to-all(f32[16,2,128]{2,1,0:T(2,128)S(1)} %get-tuple-element.227), channel_id=1, replica_groups=mesh['row'=16,'col'=8] {'row'}, dimensions={0} | all-to-all | bytes 32768 | tf_op jit(solution)/shard_map/all_to_all | solution.py:308
  285.5 8.6 %all_to_all.97.recv_ref = f32[16,2,128]{2,1,0:T(2,128)S(1)} all-to-all(f32[16,2,128]{2,1,0:T(2,128)S(1)} %get-tuple-element.231), channel_id=1, replica_groups=mesh['row'=16,'col'=8] {'row'}, dimensions={0} | all-to-all | bytes 32768 | tf_op jit(solution)/shard_map/all_to_all | solution.py:308
  295.1 8.6 %all_to_all.98.recv_ref = f32[16,2,128]{2,1,0:T(2,128)S(1)} all-to-all(f32[16,2,128]{2,1,0:T(2,128)S(1)} %get-tuple-element.235), channel_id=1, replica_groups=mesh['row'=16,'col'=8] {'row'}, dimensions={0} | all-to-all | bytes 32768 | tf_op jit(solution)/shard_map/all_to_all | solution.py:308
  303.8 1.0 reflect.28
  304.8 8.6 %all_to_all.99.recv_ref = f32[16,2,128]{2,1,0:T(2,128)S(1)} all-to-all(f32[16,2,128]{2,1,0:T(2,128)S(1)} %get-tuple-element.239), channel_id=1, replica_groups=mesh['row'=16,'col'=8] {'row'}, dimensions={0} | all-to-all | bytes 32768 | tf_op jit(solution)/shard_map/all_to_all | solution.py:308
  313.4 1.0 reflect.29
  314.4 8.7 %all_to_all.100.recv_ref = f32[16,2,128]{2,1,0:T(2,128)S(1)} all-to-all(f32[16,2,128]{2,1,0:T(2,128)S(1)} %get-tuple-element.243), channel_id=1, replica_groups=mesh['row'=16,'col'=8] {'row'}, dimensions={0} | all-to-all | bytes 32768 | tf_op jit(solution)/shard_map/all_to_all | solution.py:308
  324.1 8.6 %all_to_all.101.recv_ref = f32[16,2,128]{2,1,0:T(2,128)S(1)} all-to-all(f32[16,2,128]{2,1,0:T(2,128)S(1)} %get-tuple-element.247), channel_id=1, replica_groups=mesh['row'=16,'col'=8] {'row'}, dimensions={0} | all-to-all | bytes 32768 | tf_op jit(solution)/shard_map/all_to_all | solution.py:308
  332.8 1.6 reflect.31
  334.4 3.7 all-to-all-start.15
  338.0 5.7 %rotate.1 = (bf16[256,512]{1,0:T(8,128)(2,1)}, f32[256,512]{1,0:T(8,128)}) custom-call(s32[2]{0:T(128)} %pad_add_fusion.where_ref, bf16[256,4096]{1,0:T(8,128)(2,1)} %all-gather.4.cloned.1.call-done.psi_ref, bf16[16,3,32,4096]{3,2,1,0:T(8,128)(2,1)} %bitcast.32, f32[8,128]{1,0:T(8,128)S(1)} %get-tuple-element.254.marks_ref, ...), custom_call_target="tpu_custom_call" | custom-call | tf_op jit(solution)/shard_map/rotate/pallas_call | solution.py:329
  343.8 1.8 reshape.37
  345.5 2.3 copy-done.2
  347.8 1.6 reflect.32
  349.4 5.8 %all-to-all-start.16 = ((f32[16,2,128]{2,1,0:T(2,128)}), f32[16,2,128]{2,1,0:T(2,128)S(1)}, u32[]{:S(2)}, u32[]{:S(2)}) async-start(f32[16,2,128]{2,1,0:T(2,128)} %get-tuple-element.255), calls=%async_computation.17 | async-start | bytes 32768 | tf_op jit(solution)/shard_map/all_to_all | solution.py:308
  355.7 5.3 %all-to-all-done.16.recv_ref = f32[16,2,128]{2,1,0:T(2,128)S(1)} async-done(((f32[16,2,128]{2,1,0:T(2,128)}), f32[16,2,128]{2,1,0:T(2,128)S(1)}, u32[]{:S(2)}, u32[]{:S(2)}) %all-to-all-start.16) | async-done | bytes 16416 | tf_op jit(solution)/shard_map/all_to_all | solution.py:308
  361.0 1.6 update.1
  363.5 2.0 reshape.35
  (36 shorter events, 8.3 us)
Async XLA Ops:
  7.2 79.1 %all-gather.6.cloned.1.call-start = ((), (), s32[]{:S(2)}) async-start(), calls=%async_computation.21 | async-start | bytes 13369344 | tf_op jit(solution)/shard_map/all_gather | solution.py:225
  10.6 201.6 %all-reduce.2.cloned.1.call-start = ((), (), s32[]{:S(2)}) async-start(), calls=%async_computation.19 | async-start | bytes 8388608 | tf_op jit(solution)/shard_map/psum | solution.py:268
  96.5 14.1 %all-to-all-start.1 = ((f32[8,16,512]{2,1,0:T(8,128)}), f32[8,16,512]{2,1,0:T(8,128)S(1)}, u32[]{:S(2)}, u32[]{:S(2)}) async-start(f32[8,16,512]{2,1,0:T(8,128)} %get-tuple-element.192), calls=%async_computation.1 | async-start | bytes 524288 | tf_op jit(solution)/shard_map/all_to_all | solution.py:269
  111.3 17.9 %all-to-all-start.2 = ((f32[8,16,512]{2,1,0:T(8,128)}), f32[8,16,512]{2,1,0:T(8,128)S(1)}, u32[]{:S(2)}, u32[]{:S(2)}) async-start(f32[8,16,512]{2,1,0:T(8,128)} %broadcast_in_dim.14), calls=%async_computation.2 | async-start | bytes 524288 | tf_op jit(solution)/shard_map/all_to_all | solution.py:271
  115.4 222.6 %all-gather.4.cloned.1.call-start = ((), (), s32[]{:S(2)}) async-start(), calls=%async_computation.20 | async-start | bytes 2359296 | tf_op jit(solution)/shard_map/all_gather | solution.py:318
  133.6 17.8 %all-to-all-start = ((f32[128,2,128]{2,1,0:T(2,128)}), f32[128,2,128]{2,1,0:T(2,128)S(1)}, u32[]{:S(2)}, u32[]{:S(2)}) async-start(f32[128,2,128]{2,1,0:T(2,128)} %get-tuple-element.340), calls=%async_computation | async-start | bytes 262144 | tf_op jit(solution)/shard_map/while/body/eval_jaxpr/all_to_all | solution.py:304
  155.3 20.5 %all-to-all-start = ((f32[128,2,128]{2,1,0:T(2,128)}), f32[128,2,128]{2,1,0:T(2,128)S(1)}, u32[]{:S(2)}, u32[]{:S(2)}) async-start(f32[128,2,128]{2,1,0:T(2,128)} %get-tuple-element.340), calls=%async_computation | async-start | bytes 262144 | tf_op jit(solution)/shard_map/while/body/eval_jaxpr/all_to_all | solution.py:304
  175.8 187.7 %reduce-scatter.2.cloned.1.call-start = ((), (), s32[]{:S(2)}) async-start(), calls=%async_computation.18 | async-start | bytes 4718592 | tf_op jit(solution)/shard_map/reduce_scatter | solution.py:319
  212.2 2.2 copy-start
  214.4 11.8 %copy-start.1 = (f32[8,256,512]{2,1,0:T(8,128)S(1)}, f32[8,256,512]{2,1,0:T(8,128)}, u32[]{:S(2)}) copy-start(f32[8,256,512]{2,1,0:T(8,128)} %all-reduce.2.cloned.1.call-done.matrix_ref.refs_0_.refs_1_.refs_2_.refs_3_) | copy-start | bytes 12582916
  334.4 11.2 %all-to-all-start.15 = ((f32[16,2,128]{2,1,0:T(2,128)}), f32[16,2,128]{2,1,0:T(2,128)S(1)}, u32[]{:S(2)}, u32[]{:S(2)}) async-start(f32[16,2,128]{2,1,0:T(2,128)} %get-tuple-element.251), calls=%async_computation.16 | async-start | bytes 32768 | tf_op jit(solution)/shard_map/all_to_all | solution.py:308
  343.8 17.2 %copy-start.3 = (f32[256,512]{1,0:T(8,128)S(1)}, f32[256,512]{1,0:T(8,128)}, u32[]{:S(2)}) copy-start(f32[256,512]{1,0:T(8,128)} %get-tuple-element.260.tile_ref) | copy-start | bytes 1572868
  343.8 17.2 %copy-start.4 = (s32[2]{0:T(128)S(1)}, s32[2]{0:T(128)}, u32[]{:S(2)}) copy-start(s32[2]{0:T(128)} %pad_add_fusion.where_ref) | copy-start | bytes 28
  345.5 2.3 copy-start.2
  349.4 11.5 %all-to-all-start.16 = ((f32[16,2,128]{2,1,0:T(2,128)}), f32[16,2,128]{2,1,0:T(2,128)S(1)}, u32[]{:S(2)}, u32[]{:S(2)}) async-start(f32[16,2,128]{2,1,0:T(2,128)} %get-tuple-element.255), calls=%async_computation.17 | async-start | bytes 32768 | tf_op jit(solution)/shard_map/all_to_all | solution.py:308
Sparse Core Ops, SparseCore 0:
  10.7 75.4 all-gather.5
  96.6 115.5 all-reduce.1
  214.6 51.5 all-gather.3
  269.8 82.3 reduce-scatter.1

commit v11 on v9

--- a/solution.py
+++ b/solution.py
@@ -337,7 +337,7 @@
                 pl.BlockSpec((height, width), lambda i, where: (0, 0)),
             ),
         ),
-        compiler_params=pltpu.CompilerParams(vmem_limit_bytes=60 * MIB),
+        compiler_params=pltpu.CompilerParams(vmem_limit_bytes=48 * MIB),
         name="rotate",
     )(where, psi_rows, both, carry[3], summed)
     recv, vecs, images, marks = narrow(jnp.int32(PB - 1), carry)

time: 372 us -> 371 us (level)
  transfers between devices with their start and end apart: 10 -> 10, of which waited for: 7 -> 7; matrix products, arithmetic and copies ran while one was open for 1% -> 1% of each run, Pallas kernels for 11% -> 10%
where the time goes in v11:
time: 371 us; the launch traced here: 370 us
  waiting for transfers between devices  142 us (38%)
  blocking collectives  106 us (29%)
  Pallas kernels  48 us (13%)
  starting transfers between devices  44.2 us (12%)
  between operations  13.9 us (4%)
  local copies, waits for them, and re-layouts  12.7 us (3%)
    all_to_all x12, blocking collectives, narrow(): return (lax.all_to_all(send, 'row', 0, 0, tiled=True), vecs, images, marks)  106 us
    all_gather x1, waiting for transfers between devices, on_device(): both = lax.all_gather(jnp.stack([psi, hpsi, folded]), 'row')  75 us
    psum x1, waiting for transfers between devices, on_device(): summed = lax.psum(matrix, 'col')  24.4 us
    all_to_all x2, starting transfers between devices, wide(): lax.all_to_all(send, ('row', 'col'), 0, 0, tiled=True)  24.3 us
    pallas_call x16, Pallas kernels, advance(): pl.pallas_call(functools.partial(step_body, row_count=row_count), out_sha...  23.3 us
    all_to_all x2, waiting for transfers between devices, wide(): lax.all_to_all(send, ('row', 'col'), 0, 0, tiled=True)  21.4 us
    pallas_call x2, Pallas kernels, products(): pl.pallas_call(body, out_shape=made, grid_spec=pltpu.PrefetchScalarGridSp...  19 us
    all_to_all x2, starting transfers between devices, narrow(): return (lax.all_to_all(send, 'row', 0, 0, tiled=True), vecs, images, marks)  9.45 us
  transfers between devices with their start and end apart: 10, of which 7 were waited for; matrix products, arithmetic and copies ran while one was open for 1% of the time, Pallas kernels for 10%

profile of v11, /device:TPU:1, one launch (start us, length us, event | category | flops | bytes accessed | tf_op | source)
XLA Modules:
  0.0 369.9 jit_solution(12996193717304477799)
XLA Ops:
  7.2 1.1 reshape.32
  8.6 2.0 pad_maximum_fusion
  11.3 75.0 %all-gather.6.cloned.1.call-done = bf16[48,32,4096]{2,1,0:T(8,128)(2,1)} async-done(((bf16[3,32,4096]{2,1,0:T(8,128)(2,1)}), bf16[48,32,4096]{2,1,0:T(8,128)(2,1)}) %all-gather.6.cloned.1.call-update) | async-done | bytes 12582928 | tf_op jit(solution)/shard_map/all_gather | solution.py:225
  86.2 10.3 %products.1 = (f32[8,256,512]{2,1,0:T(8,128)}, f32[8,16,512]{2,1,0:T(8,128)}) custom-call(s32[2]{0:T(128)} %pad_add_fusion.where_ref, bf16[16,3,32,4096]{3,2,1,0:T(8,128)(2,1)} %bitcast.22, bf16[16,3,32,4096]{3,2,1,0:T(8,128)(2,1)} %bitcast.23, bf16[16,3,32,4096]{3,2,1,0:T(8,128)(2,1)} %bitcast.24, bf16[16,3,32,4096]{3,2,1,0:T(8,128)(2,1)} %bitcast.25, ...), custom_call_target="tpu_custom_call" | custom-call | tf_op jit(solution)/shard_map/products/pallas_call | solution.py:245
  96.5 6.4 %all-to-all-start.1 = ((f32[8,16,512]{2,1,0:T(8,128)}), f32[8,16,512]{2,1,0:T(8,128)S(1)}, u32[]{:S(2)}, u32[]{:S(2)}) async-start(f32[8,16,512]{2,1,0:T(8,128)} %get-tuple-element.192), calls=%async_computation.1 | async-start | bytes 524288 | tf_op jit(solution)/shard_map/all_to_all | solution.py:267
  103.0 7.6 %all-to-all-done.1 = f32[8,16,512]{2,1,0:T(8,128)S(1)} async-done(((f32[8,16,512]{2,1,0:T(8,128)}), f32[8,16,512]{2,1,0:T(8,128)S(1)}, u32[]{:S(2)}, u32[]{:S(2)}) %all-to-all-start.1) | async-done | bytes 262176 | tf_op jit(solution)/shard_map/all_to_all | solution.py:267
  111.3 3.8 %all-to-all-start.2 = ((f32[8,16,512]{2,1,0:T(8,128)}), f32[8,16,512]{2,1,0:T(8,128)S(1)}, u32[]{:S(2)}, u32[]{:S(2)}) async-start(f32[8,16,512]{2,1,0:T(8,128)} %broadcast_in_dim.14), calls=%async_computation.2 | async-start | bytes 524288 | tf_op jit(solution)/shard_map/all_to_all | solution.py:269
  115.2 8.7 %overlaps.1 = f32[8,256,512]{2,1,0:T(8,128)} custom-call(s32[2]{0:T(128)} %pad_add_fusion.where_ref, bf16[16,3,32,4096]{3,2,1,0:T(8,128)(2,1)} %bitcast.29, bf16[16,3,32,4096]{3,2,1,0:T(8,128)(2,1)} %bitcast.30, bf16[16,3,32,4096]{3,2,1,0:T(8,128)(2,1)} %bitcast.31, bf16[16,3,32,4096]{3,2,1,0:T(8,128)(2,1)} %bitcast.32, bf16[16,3,32,4096]{3,2,1,0:T(8,128)(2,1)} %bitcast.33, ...), custom_call_target="tpu_custom_call" | custom-call | tf_op jit(solution)/shard_map/overlaps/pallas_call | solution.py:245
  123.9 7.7 %all-to-all-done.2 = f32[8,16,512]{2,1,0:T(8,128)S(1)} async-done(((f32[8,16,512]{2,1,0:T(8,128)}), f32[8,16,512]{2,1,0:T(8,128)S(1)}, u32[]{:S(2)}, u32[]{:S(2)}) %all-to-all-start.2) | async-done | bytes 262176 | tf_op jit(solution)/shard_map/all_to_all | solution.py:269
  132.0 53.8 %while.19 = (s32[]{:T(128)}, f32[128,2,128]{2,1,0:T(2,128)S(1)}, f32[16,32,128]{2,1,0:T(8,128)S(1)}, f32[16,32,128]{2,1,0:T(8,128)S(1)}, f32[8,128]{1,0:T(8,128)...) while((s32[]{:T(128)}, f32[128,2,128]{2,1,0:T(2,128)S(1)}, ...), condition=%wide.region_2.0_spmd, body=%wide.region_1.0_spmd.sunk | while | flops 2 | bytes 393333 | solution.py:314
  132.0 3.9 %reflect.33 = (f32[16,32,128]{2,1,0:T(8,128)S(1)}, f32[16,32,128]{2,1,0:T(8,128)S(1)}, f32[8,128]{1,0:T(8,128)S(1)}, f32[128,2,128]{2,1,0:T(2,128)}) custom-call(s32[1]{0:T(128)} %bitcast.21.step_ref, f32[128,2,128]{2,1,0:T(2,128)S(1)} %get-tuple-element.353.recv_ref, ...), custom_call_target="tpu_custom_call", output_to_operand_aliasing={{0}: (3, {}), {1}: (4, {}), {2}: (5, {})} | custom-call | tf_op jit(solution)/shard_map/while/body/eval_jaxpr/reflect/pallas_call | solution.py:286
  135.9 19.9 %all-to-all-start = ((f32[128,2,128]{2,1,0:T(2,128)}), f32[128,2,128]{2,1,0:T(2,128)S(1)}, u32[]{:S(2)}, u32[]{:S(2)}) async-start(f32[128,2,128]{2,1,0:T(2,128)} %get-tuple-element.340), calls=%async_computation | async-start | bytes 262144 | tf_op jit(solution)/shard_map/while/body/eval_jaxpr/all_to_all | solution.py:302
  155.9 9.6 %all-to-all-done = f32[128,2,128]{2,1,0:T(2,128)S(1)} async-done(((f32[128,2,128]{2,1,0:T(2,128)}), f32[128,2,128]{2,1,0:T(2,128)S(1)}, u32[]{:S(2)}, u32[]{:S(2)}) %all-to-all-start) | async-done | bytes 131104 | tf_op jit(solution)/shard_map/while/body/eval_jaxpr/all_to_all | solution.py:302
  165.4 4.0 %reflect.33 = (f32[16,32,128]{2,1,0:T(8,128)S(1)}, f32[16,32,128]{2,1,0:T(8,128)S(1)}, f32[8,128]{1,0:T(8,128)S(1)}, f32[128,2,128]{2,1,0:T(2,128)}) custom-call(s32[1]{0:T(128)} %bitcast.21.step_ref, f32[128,2,128]{2,1,0:T(2,128)S(1)} %get-tuple-element.353.recv_ref, ...), custom_call_target="tpu_custom_call", output_to_operand_aliasing={{0}: (3, {}), {1}: (4, {}), {2}: (5, {})} | custom-call | tf_op jit(solution)/shard_map/while/body/eval_jaxpr/reflect/pallas_call | solution.py:286
  169.5 4.4 %all-to-all-start = ((f32[128,2,128]{2,1,0:T(2,128)}), f32[128,2,128]{2,1,0:T(2,128)S(1)}, u32[]{:S(2)}, u32[]{:S(2)}) async-start(f32[128,2,128]{2,1,0:T(2,128)} %get-tuple-element.340), calls=%async_computation | async-start | bytes 262144 | tf_op jit(solution)/shard_map/while/body/eval_jaxpr/all_to_all | solution.py:302
  173.9 11.9 %all-to-all-done = f32[128,2,128]{2,1,0:T(2,128)S(1)} async-done(((f32[128,2,128]{2,1,0:T(2,128)}), f32[128,2,128]{2,1,0:T(2,128)S(1)}, u32[]{:S(2)}, u32[]{:S(2)}) %all-to-all-start) | async-done | bytes 131104 | tf_op jit(solution)/shard_map/while/body/eval_jaxpr/all_to_all | solution.py:302
  186.4 24.4 %all-reduce.2.cloned.1.call-done.matrix_ref.block_ref = f32[8,256,512]{2,1,0:T(8,128)} async-done(((f32[8,256,512]{2,1,0:T(8,128)}), f32[8,256,512]{2,1,0:T(8,128)}) %all-reduce.2.cloned.1.call-update) | async-done | bytes 4194320 | tf_op jit(solution)/shard_map/psum | solution.py:266
  210.8 2.2 copy-done
  213.0 1.0 reflect.19
  214.0 11.0 %all_to_all.90.recv_ref = f32[16,2,128]{2,1,0:T(2,128)S(1)} all-to-all(f32[16,2,128]{2,1,0:T(2,128)S(1)} %get-tuple-element.203), channel_id=1, replica_groups=mesh['row'=16,'col'=8] {'row'}, dimensions={0} | all-to-all | bytes 32768 | tf_op jit(solution)/shard_map/all_to_all | solution.py:306
  225.0 1.0 reflect.20
  226.0 8.6 %all_to_all.91.recv_ref = f32[16,2,128]{2,1,0:T(2,128)S(1)} all-to-all(f32[16,2,128]{2,1,0:T(2,128)S(1)} %get-tuple-element.207), channel_id=1, replica_groups=mesh['row'=16,'col'=8] {'row'}, dimensions={0} | all-to-all | bytes 32768 | tf_op jit(solution)/shard_map/all_to_all | solution.py:306
  234.7 1.0 reflect.21
  235.7 8.6 %all_to_all.92.recv_ref = f32[16,2,128]{2,1,0:T(2,128)S(1)} all-to-all(f32[16,2,128]{2,1,0:T(2,128)S(1)} %get-tuple-element.211), channel_id=1, replica_groups=mesh['row'=16,'col'=8] {'row'}, dimensions={0} | all-to-all | bytes 32768 | tf_op jit(solution)/shard_map/all_to_all | solution.py:306
  245.3 8.8 %all_to_all.93.recv_ref = f32[16,2,128]{2,1,0:T(2,128)S(1)} all-to-all(f32[16,2,128]{2,1,0:T(2,128)S(1)} %get-tuple-element.215), channel_id=1, replica_groups=mesh['row'=16,'col'=8] {'row'}, dimensions={0} | all-to-all | bytes 32768 | tf_op jit(solution)/shard_map/all_to_all | solution.py:306
  254.1 1.0 reflect.23
  255.1 8.6 %all_to_all.94.recv_ref = f32[16,2,128]{2,1,0:T(2,128)S(1)} all-to-all(f32[16,2,128]{2,1,0:T(2,128)S(1)} %get-tuple-element.219), channel_id=1, replica_groups=mesh['row'=16,'col'=8] {'row'}, dimensions={0} | all-to-all | bytes 32768 | tf_op jit(solution)/shard_map/all_to_all | solution.py:306
  263.8 1.0 reflect.24
  264.8 8.6 %all_to_all.95.recv_ref = f32[16,2,128]{2,1,0:T(2,128)S(1)} all-to-all(f32[16,2,128]{2,1,0:T(2,128)S(1)} %get-tuple-element.223), channel_id=1, replica_groups=mesh['row'=16,'col'=8] {'row'}, dimensions={0} | all-to-all | bytes 32768 | tf_op jit(solution)/shard_map/all_to_all | solution.py:306
  274.4 8.7 %all_to_all.96.recv_ref = f32[16,2,128]{2,1,0:T(2,128)S(1)} all-to-all(f32[16,2,128]{2,1,0:T(2,128)S(1)} %get-tuple-element.227), channel_id=1, replica_groups=mesh['row'=16,'col'=8] {'row'}, dimensions={0} | all-to-all | bytes 32768 | tf_op jit(solution)/shard_map/all_to_all | solution.py:306
  283.2 1.0 reflect.26
  284.2 8.6 %all_to_all.97.recv_ref = f32[16,2,128]{2,1,0:T(2,128)S(1)} all-to-all(f32[16,2,128]{2,1,0:T(2,128)S(1)} %get-tuple-element.231), channel_id=1, replica_groups=mesh['row'=16,'col'=8] {'row'}, dimensions={0} | all-to-all | bytes 32768 | tf_op jit(solution)/shard_map/all_to_all | solution.py:306
  293.9 8.6 %all_to_all.98.recv_ref = f32[16,2,128]{2,1,0:T(2,128)S(1)} all-to-all(f32[16,2,128]{2,1,0:T(2,128)S(1)} %get-tuple-element.235), channel_id=1, replica_groups=mesh['row'=16,'col'=8] {'row'}, dimensions={0} | all-to-all | bytes 32768 | tf_op jit(solution)/shard_map/all_to_all | solution.py:306
  303.5 8.6 %all_to_all.99.recv_ref = f32[16,2,128]{2,1,0:T(2,128)S(1)} all-to-all(f32[16,2,128]{2,1,0:T(2,128)S(1)} %get-tuple-element.239), channel_id=1, replica_groups=mesh['row'=16,'col'=8] {'row'}, dimensions={0} | all-to-all | bytes 32768 | tf_op jit(solution)/shard_map/all_to_all | solution.py:306
  312.2 1.0 reflect.29
  313.2 8.6 %all_to_all.100.recv_ref = f32[16,2,128]{2,1,0:T(2,128)S(1)} all-to-all(f32[16,2,128]{2,1,0:T(2,128)S(1)} %get-tuple-element.243), channel_id=1, replica_groups=mesh['row'=16,'col'=8] {'row'}, dimensions={0} | all-to-all | bytes 32768 | tf_op jit(solution)/shard_map/all_to_all | solution.py:306
  321.8 1.0 reflect.30
  322.8 8.6 %all_to_all.101.recv_ref = f32[16,2,128]{2,1,0:T(2,128)S(1)} all-to-all(f32[16,2,128]{2,1,0:T(2,128)S(1)} %get-tuple-element.247), channel_id=1, replica_groups=mesh['row'=16,'col'=8] {'row'}, dimensions={0} | all-to-all | bytes 32768 | tf_op jit(solution)/shard_map/all_to_all | solution.py:306
  331.5 1.6 reflect.31
  333.1 3.7 all-to-all-start.15
  336.8 1.6 copy-done.3
  338.4 4.2 %rotate.1 = (bf16[256,512]{1,0:T(8,128)(2,1)S(1)}, f32[256,512]{1,0:T(8,128)S(1)}) custom-call(s32[2]{0:T(128)S(1)} %copy-done.4, bf16[256,4096]{1,0:T(8,128)(2,1)S(1)} %copy-done.3, bf16[16,3,32,4096]{3,2,1,0:T(8,128)(2,1)} %bitcast.35, f32[8,128]{1,0:T(8,128)S(1)} %get-tuple-element.254.marks_ref, ...), custom_call_target="tpu_custom_call" | custom-call | tf_op jit(solution)/shard_map/rotate/pallas_call | solution.py:320
  343.4 2.3 copy-done.2
  345.6 1.6 reflect.32
  347.2 5.8 %all-to-all-start.16 = ((f32[16,2,128]{2,1,0:T(2,128)}), f32[16,2,128]{2,1,0:T(2,128)S(1)}, u32[]{:S(2)}, u32[]{:S(2)}) async-start(f32[16,2,128]{2,1,0:T(2,128)} %get-tuple-element.255), calls=%async_computation.17 | async-start | bytes 32768 | tf_op jit(solution)/shard_map/all_to_all | solution.py:306
  353.5 5.3 %all-to-all-done.16.recv_ref = f32[16,2,128]{2,1,0:T(2,128)S(1)} async-done(((f32[16,2,128]{2,1,0:T(2,128)}), f32[16,2,128]{2,1,0:T(2,128)S(1)}, u32[]{:S(2)}, u32[]{:S(2)}) %all-to-all-start.16) | async-done | bytes 16416 | tf_op jit(solution)/shard_map/all_to_all | solution.py:306
  358.8 1.6 update.1
  361.3 2.0 reshape.35
  (36 shorter events, 9.0 us)
Async XLA Ops:
  7.2 79.1 %all-gather.6.cloned.1.call-start = ((), (), s32[]{:S(2)}) async-start(), calls=%async_computation.21 | async-start | bytes 13369344 | tf_op jit(solution)/shard_map/all_gather | solution.py:225
  10.6 200.2 %all-reduce.2.cloned.1.call-start = ((), (), s32[]{:S(2)}) async-start(), calls=%async_computation.19 | async-start | bytes 8388608 | tf_op jit(solution)/shard_map/psum | solution.py:266
  96.5 14.1 %all-to-all-start.1 = ((f32[8,16,512]{2,1,0:T(8,128)}), f32[8,16,512]{2,1,0:T(8,128)S(1)}, u32[]{:S(2)}, u32[]{:S(2)}) async-start(f32[8,16,512]{2,1,0:T(8,128)} %get-tuple-element.192), calls=%async_computation.1 | async-start | bytes 524288 | tf_op jit(solution)/shard_map/all_to_all | solution.py:267
  111.3 20.2 %all-to-all-start.2 = ((f32[8,16,512]{2,1,0:T(8,128)}), f32[8,16,512]{2,1,0:T(8,128)S(1)}, u32[]{:S(2)}, u32[]{:S(2)}) async-start(f32[8,16,512]{2,1,0:T(8,128)} %broadcast_in_dim.14), calls=%async_computation.2 | async-start | bytes 524288 | tf_op jit(solution)/shard_map/all_to_all | solution.py:269
  115.1 221.7 %all-gather.4.cloned.1.call-start = ((), (), s32[]{:S(2)}) async-start(), calls=%async_computation.20 | async-start | bytes 2359296 | tf_op jit(solution)/shard_map/all_gather | solution.py:316
  135.9 29.5 %all-to-all-start = ((f32[128,2,128]{2,1,0:T(2,128)}), f32[128,2,128]{2,1,0:T(2,128)S(1)}, u32[]{:S(2)}, u32[]{:S(2)}) async-start(f32[128,2,128]{2,1,0:T(2,128)} %get-tuple-element.340), calls=%async_computation | async-start | bytes 262144 | tf_op jit(solution)/shard_map/while/body/eval_jaxpr/all_to_all | solution.py:302
  169.5 16.3 %all-to-all-start = ((f32[128,2,128]{2,1,0:T(2,128)}), f32[128,2,128]{2,1,0:T(2,128)S(1)}, u32[]{:S(2)}, u32[]{:S(2)}) async-start(f32[128,2,128]{2,1,0:T(2,128)} %get-tuple-element.340), calls=%async_computation | async-start | bytes 262144 | tf_op jit(solution)/shard_map/while/body/eval_jaxpr/all_to_all | solution.py:302
  185.8 175.5 %reduce-scatter.2.cloned.1.call-start = ((), (), s32[]{:S(2)}) async-start(), calls=%async_computation.18 | async-start | bytes 4718592 | tf_op jit(solution)/shard_map/reduce_scatter | solution.py:317
  210.8 2.2 copy-start
  213.0 12.0 %copy-start.1 = (f32[8,256,512]{2,1,0:T(8,128)S(1)}, f32[8,256,512]{2,1,0:T(8,128)}, u32[]{:S(2)}) copy-start(f32[8,256,512]{2,1,0:T(8,128)} %all-reduce.2.cloned.1.call-done.matrix_ref.block_ref) | copy-start | bytes 12582916
  321.8 15.0 %copy-start.4 = (s32[2]{0:T(128)S(1)}, s32[2]{0:T(128)}, u32[]{:S(2)}) copy-start(s32[2]{0:T(128)} %pad_add_fusion.where_ref) | copy-start | bytes 28
  333.1 10.3 %all-to-all-start.15 = ((f32[16,2,128]{2,1,0:T(2,128)}), f32[16,2,128]{2,1,0:T(2,128)S(1)}, u32[]{:S(2)}, u32[]{:S(2)}) async-start(f32[16,2,128]{2,1,0:T(2,128)} %get-tuple-element.251), calls=%async_computation.16 | async-start | bytes 32768 | tf_op jit(solution)/shard_map/all_to_all | solution.py:306
  336.8 1.6 copy-start.3
  343.4 2.3 copy-start.2
  347.2 11.6 %all-to-all-start.16 = ((f32[16,2,128]{2,1,0:T(2,128)}), f32[16,2,128]{2,1,0:T(2,128)S(1)}, u32[]{:S(2)}, u32[]{:S(2)}) async-start(f32[16,2,128]{2,1,0:T(2,128)} %get-tuple-element.255), calls=%async_computation.17 | async-start | bytes 32768 | tf_op jit(solution)/shard_map/all_to_all | solution.py:306
Sparse Core Ops, SparseCore 0:
  10.7 75.4 all-gather.5
  96.6 114.0 all-reduce.1
  213.1 51.8 all-gather.3
  268.7 82.4 reduce-scatter.1

commit v12 on v11

--- a/solution.py
+++ b/solution.py
@@ -342,6 +342,8 @@
     )(where, psi_rows, both, carry[3], summed)
     recv, vecs, images, marks = narrow(jnp.int32(PB - 1), carry)
 
+    tile_shape = (row_tiles, 1, tile_size, col_tiles, 1, tile_size)
+    tile, correlation = lax.optimization_barrier((tile, correlation.reshape(tile_shape)))
     updated = pl.pallas_call(
         functools.partial(last_body, row_count=row_count, col_count=col_count),
         out_shape=jax.ShapeDtypeStruct((height, width), F32),
@@ -354,7 +356,7 @@
 
     tile_shape = (row_tiles, 1, tile_size, col_tiles, 1, tile_size)
     return (
-        correlation.reshape(tile_shape),
+        correlation,
         updated.reshape(tile_shape),
         marks[0, :PB],
         marks[1, :PB],

time: 371 us -> 369 us (level)
  no operation moved by 1% of the time
where the time goes in v12:
time: 369 us; the launch traced here: 368 us
  waiting for transfers between devices  140 us (38%)
  blocking collectives  106 us (29%)
  Pallas kernels  48 us (13%)
  starting transfers between devices  44.2 us (12%)
  between operations  13.9 us (4%)
  local copies, waits for them, and re-layouts  12.7 us (3%)
    all_to_all x12, blocking collectives, narrow(): return (lax.all_to_all(send, 'row', 0, 0, tiled=True), vecs, images, marks)  106 us
    all_gather x1, waiting for transfers between devices, on_device(): both = lax.all_gather(jnp.stack([psi, hpsi, folded]), 'row')  75 us
    psum x1, waiting for transfers between devices, on_device(): summed = lax.psum(matrix, 'col')  24.4 us
    all_to_all x2, starting transfers between devices, wide(): lax.all_to_all(send, ('row', 'col'), 0, 0, tiled=True)  24.3 us
    pallas_call x16, Pallas kernels, advance(): pl.pallas_call(functools.partial(step_body, row_count=row_count), out_sha...  23.3 us
    all_to_all x2, waiting for transfers between devices, wide(): lax.all_to_all(send, ('row', 'col'), 0, 0, tiled=True)  21.4 us
    pallas_call x2, Pallas kernels, products(): pl.pallas_call(body, out_shape=made, grid_spec=pltpu.PrefetchScalarGridSp...  19 us
    all_to_all x2, starting transfers between devices, narrow(): return (lax.all_to_all(send, 'row', 0, 0, tiled=True), vecs, images, marks)  9.45 us
  transfers between devices with their start and end apart: 10, of which 7 were waited for; matrix products, arithmetic and copies ran while one was open for 1% of the time, Pallas kernels for 10%

profile of v12, /device:TPU:1, one launch (start us, length us, event | category | flops | bytes accessed | tf_op | source)
XLA Modules:
  0.0 367.9 jit_solution(11441442042809970938)
XLA Ops:
  7.2 1.1 reshape.32
  8.6 2.0 pad_maximum_fusion
  11.3 75.0 %all-gather.6.cloned.1.call-done = bf16[48,32,4096]{2,1,0:T(8,128)(2,1)} async-done(((bf16[3,32,4096]{2,1,0:T(8,128)(2,1)}), bf16[48,32,4096]{2,1,0:T(8,128)(2,1)}) %all-gather.6.cloned.1.call-update) | async-done | bytes 12582928 | tf_op jit(solution)/shard_map/all_gather | solution.py:225
  86.2 10.3 %products.1 = (f32[8,256,512]{2,1,0:T(8,128)}, f32[8,16,512]{2,1,0:T(8,128)}) custom-call(s32[2]{0:T(128)} %pad_add_fusion.where_ref, bf16[16,3,32,4096]{3,2,1,0:T(8,128)(2,1)} %bitcast.22, bf16[16,3,32,4096]{3,2,1,0:T(8,128)(2,1)} %bitcast.23, bf16[16,3,32,4096]{3,2,1,0:T(8,128)(2,1)} %bitcast.24, bf16[16,3,32,4096]{3,2,1,0:T(8,128)(2,1)} %bitcast.25, ...), custom_call_target="tpu_custom_call" | custom-call | tf_op jit(solution)/shard_map/products/pallas_call | solution.py:245
  96.5 6.4 %all-to-all-start.1 = ((f32[8,16,512]{2,1,0:T(8,128)}), f32[8,16,512]{2,1,0:T(8,128)S(1)}, u32[]{:S(2)}, u32[]{:S(2)}) async-start(f32[8,16,512]{2,1,0:T(8,128)} %get-tuple-element.194), calls=%async_computation.1 | async-start | bytes 524288 | tf_op jit(solution)/shard_map/all_to_all | solution.py:267
  103.0 7.6 %all-to-all-done.1 = f32[8,16,512]{2,1,0:T(8,128)S(1)} async-done(((f32[8,16,512]{2,1,0:T(8,128)}), f32[8,16,512]{2,1,0:T(8,128)S(1)}, u32[]{:S(2)}, u32[]{:S(2)}) %all-to-all-start.1) | async-done | bytes 262176 | tf_op jit(solution)/shard_map/all_to_all | solution.py:267
  111.3 3.8 %all-to-all-start.2 = ((f32[8,16,512]{2,1,0:T(8,128)}), f32[8,16,512]{2,1,0:T(8,128)S(1)}, u32[]{:S(2)}, u32[]{:S(2)}) async-start(f32[8,16,512]{2,1,0:T(8,128)} %broadcast_in_dim.14), calls=%async_computation.2 | async-start | bytes 524288 | tf_op jit(solution)/shard_map/all_to_all | solution.py:269
  115.2 8.7 %overlaps.1 = f32[8,256,512]{2,1,0:T(8,128)} custom-call(s32[2]{0:T(128)} %pad_add_fusion.where_ref, bf16[16,3,32,4096]{3,2,1,0:T(8,128)(2,1)} %bitcast.29, bf16[16,3,32,4096]{3,2,1,0:T(8,128)(2,1)} %bitcast.30, bf16[16,3,32,4096]{3,2,1,0:T(8,128)(2,1)} %bitcast.31, bf16[16,3,32,4096]{3,2,1,0:T(8,128)(2,1)} %bitcast.32, bf16[16,3,32,4096]{3,2,1,0:T(8,128)(2,1)} %bitcast.33, ...), custom_call_target="tpu_custom_call" | custom-call | tf_op jit(solution)/shard_map/overlaps/pallas_call | solution.py:245
  123.9 7.7 %all-to-all-done.2 = f32[8,16,512]{2,1,0:T(8,128)S(1)} async-done(((f32[8,16,512]{2,1,0:T(8,128)}), f32[8,16,512]{2,1,0:T(8,128)S(1)}, u32[]{:S(2)}, u32[]{:S(2)}) %all-to-all-start.2) | async-done | bytes 262176 | tf_op jit(solution)/shard_map/all_to_all | solution.py:269
  132.0 53.8 %while.19 = (s32[]{:T(128)}, f32[128,2,128]{2,1,0:T(2,128)S(1)}, f32[16,32,128]{2,1,0:T(8,128)S(1)}, f32[16,32,128]{2,1,0:T(8,128)S(1)}, f32[8,128]{1,0:T(8,128)...) while((s32[]{:T(128)}, f32[128,2,128]{2,1,0:T(2,128)S(1)}, ...), condition=%wide.region_2.0_spmd, body=%wide.region_1.0_spmd.sunk | while | flops 2 | bytes 393333 | solution.py:314
  132.0 3.9 %reflect.33 = (f32[16,32,128]{2,1,0:T(8,128)S(1)}, f32[16,32,128]{2,1,0:T(8,128)S(1)}, f32[8,128]{1,0:T(8,128)S(1)}, f32[128,2,128]{2,1,0:T(2,128)}) custom-call(s32[1]{0:T(128)} %bitcast.21.step_ref, f32[128,2,128]{2,1,0:T(2,128)S(1)} %get-tuple-element.357.recv_ref, ...), custom_call_target="tpu_custom_call", output_to_operand_aliasing={{0}: (3, {}), {1}: (4, {}), {2}: (5, {})} | custom-call | tf_op jit(solution)/shard_map/while/body/eval_jaxpr/reflect/pallas_call | solution.py:286
  135.9 19.9 %all-to-all-start = ((f32[128,2,128]{2,1,0:T(2,128)}), f32[128,2,128]{2,1,0:T(2,128)S(1)}, u32[]{:S(2)}, u32[]{:S(2)}) async-start(f32[128,2,128]{2,1,0:T(2,128)} %get-tuple-element.344), calls=%async_computation | async-start | bytes 262144 | tf_op jit(solution)/shard_map/while/body/eval_jaxpr/all_to_all | solution.py:302
  155.9 9.6 %all-to-all-done = f32[128,2,128]{2,1,0:T(2,128)S(1)} async-done(((f32[128,2,128]{2,1,0:T(2,128)}), f32[128,2,128]{2,1,0:T(2,128)S(1)}, u32[]{:S(2)}, u32[]{:S(2)}) %all-to-all-start) | async-done | bytes 131104 | tf_op jit(solution)/shard_map/while/body/eval_jaxpr/all_to_all | solution.py:302
  165.4 4.0 %reflect.33 = (f32[16,32,128]{2,1,0:T(8,128)S(1)}, f32[16,32,128]{2,1,0:T(8,128)S(1)}, f32[8,128]{1,0:T(8,128)S(1)}, f32[128,2,128]{2,1,0:T(2,128)}) custom-call(s32[1]{0:T(128)} %bitcast.21.step_ref, f32[128,2,128]{2,1,0:T(2,128)S(1)} %get-tuple-element.357.recv_ref, ...), custom_call_target="tpu_custom_call", output_to_operand_aliasing={{0}: (3, {}), {1}: (4, {}), {2}: (5, {})} | custom-call | tf_op jit(solution)/shard_map/while/body/eval_jaxpr/reflect/pallas_call | solution.py:286
  169.5 4.4 %all-to-all-start = ((f32[128,2,128]{2,1,0:T(2,128)}), f32[128,2,128]{2,1,0:T(2,128)S(1)}, u32[]{:S(2)}, u32[]{:S(2)}) async-start(f32[128,2,128]{2,1,0:T(2,128)} %get-tuple-element.344), calls=%async_computation | async-start | bytes 262144 | tf_op jit(solution)/shard_map/while/body/eval_jaxpr/all_to_all | solution.py:302
  173.9 11.9 %all-to-all-done = f32[128,2,128]{2,1,0:T(2,128)S(1)} async-done(((f32[128,2,128]{2,1,0:T(2,128)}), f32[128,2,128]{2,1,0:T(2,128)S(1)}, u32[]{:S(2)}, u32[]{:S(2)}) %all-to-all-start) | async-done | bytes 131104 | tf_op jit(solution)/shard_map/while/body/eval_jaxpr/all_to_all | solution.py:302
  186.4 24.4 %all-reduce.2.cloned.1.call-done.matrix_ref.block_ref = f32[8,256,512]{2,1,0:T(8,128)} async-done(((f32[8,256,512]{2,1,0:T(8,128)}), f32[8,256,512]{2,1,0:T(8,128)}) %all-reduce.2.cloned.1.call-update) | async-done | bytes 4194320 | tf_op jit(solution)/shard_map/psum | solution.py:266
  210.8 2.2 copy-done
  213.0 1.0 reflect.19
  214.0 11.0 %all_to_all.90.recv_ref = f32[16,2,128]{2,1,0:T(2,128)S(1)} all-to-all(f32[16,2,128]{2,1,0:T(2,128)S(1)} %get-tuple-element.205), channel_id=1, replica_groups=mesh['row'=16,'col'=8] {'row'}, dimensions={0} | all-to-all | bytes 32768 | tf_op jit(solution)/shard_map/all_to_all | solution.py:306
  225.0 1.0 reflect.20
  226.0 8.6 %all_to_all.91.recv_ref = f32[16,2,128]{2,1,0:T(2,128)S(1)} all-to-all(f32[16,2,128]{2,1,0:T(2,128)S(1)} %get-tuple-element.209), channel_id=1, replica_groups=mesh['row'=16,'col'=8] {'row'}, dimensions={0} | all-to-all | bytes 32768 | tf_op jit(solution)/shard_map/all_to_all | solution.py:306
  234.7 1.0 reflect.21
  235.7 8.6 %all_to_all.92.recv_ref = f32[16,2,128]{2,1,0:T(2,128)S(1)} all-to-all(f32[16,2,128]{2,1,0:T(2,128)S(1)} %get-tuple-element.213), channel_id=1, replica_groups=mesh['row'=16,'col'=8] {'row'}, dimensions={0} | all-to-all | bytes 32768 | tf_op jit(solution)/shard_map/all_to_all | solution.py:306
  245.3 8.8 %all_to_all.93.recv_ref = f32[16,2,128]{2,1,0:T(2,128)S(1)} all-to-all(f32[16,2,128]{2,1,0:T(2,128)S(1)} %get-tuple-element.217), channel_id=1, replica_groups=mesh['row'=16,'col'=8] {'row'}, dimensions={0} | all-to-all | bytes 32768 | tf_op jit(solution)/shard_map/all_to_all | solution.py:306
  254.1 1.0 reflect.23
  255.1 8.6 %all_to_all.94.recv_ref = f32[16,2,128]{2,1,0:T(2,128)S(1)} all-to-all(f32[16,2,128]{2,1,0:T(2,128)S(1)} %get-tuple-element.221), channel_id=1, replica_groups=mesh['row'=16,'col'=8] {'row'}, dimensions={0} | all-to-all | bytes 32768 | tf_op jit(solution)/shard_map/all_to_all | solution.py:306
  263.8 1.0 reflect.24
  264.8 8.6 %all_to_all.95.recv_ref = f32[16,2,128]{2,1,0:T(2,128)S(1)} all-to-all(f32[16,2,128]{2,1,0:T(2,128)S(1)} %get-tuple-element.225), channel_id=1, replica_groups=mesh['row'=16,'col'=8] {'row'}, dimensions={0} | all-to-all | bytes 32768 | tf_op jit(solution)/shard_map/all_to_all | solution.py:306
  274.4 8.7 %all_to_all.96.recv_ref = f32[16,2,128]{2,1,0:T(2,128)S(1)} all-to-all(f32[16,2,128]{2,1,0:T(2,128)S(1)} %get-tuple-element.229), channel_id=1, replica_groups=mesh['row'=16,'col'=8] {'row'}, dimensions={0} | all-to-all | bytes 32768 | tf_op jit(solution)/shard_map/all_to_all | solution.py:306
  283.2 1.0 reflect.26
  284.2 8.6 %all_to_all.97.recv_ref = f32[16,2,128]{2,1,0:T(2,128)S(1)} all-to-all(f32[16,2,128]{2,1,0:T(2,128)S(1)} %get-tuple-element.233), channel_id=1, replica_groups=mesh['row'=16,'col'=8] {'row'}, dimensions={0} | all-to-all | bytes 32768 | tf_op jit(solution)/shard_map/all_to_all | solution.py:306
  293.9 8.6 %all_to_all.98.recv_ref = f32[16,2,128]{2,1,0:T(2,128)S(1)} all-to-all(f32[16,2,128]{2,1,0:T(2,128)S(1)} %get-tuple-element.237), channel_id=1, replica_groups=mesh['row'=16,'col'=8] {'row'}, dimensions={0} | all-to-all | bytes 32768 | tf_op jit(solution)/shard_map/all_to_all | solution.py:306
  303.5 8.6 %all_to_all.99.recv_ref = f32[16,2,128]{2,1,0:T(2,128)S(1)} all-to-all(f32[16,2,128]{2,1,0:T(2,128)S(1)} %get-tuple-element.241), channel_id=1, replica_groups=mesh['row'=16,'col'=8] {'row'}, dimensions={0} | all-to-all | bytes 32768 | tf_op jit(solution)/shard_map/all_to_all | solution.py:306
  312.2 1.0 reflect.29
  313.2 8.6 %all_to_all.100.recv_ref = f32[16,2,128]{2,1,0:T(2,128)S(1)} all-to-all(f32[16,2,128]{2,1,0:T(2,128)S(1)} %get-tuple-element.245), channel_id=1, replica_groups=mesh['row'=16,'col'=8] {'row'}, dimensions={0} | all-to-all | bytes 32768 | tf_op jit(solution)/shard_map/all_to_all | solution.py:306
  321.8 1.0 reflect.30
  322.8 8.6 %all_to_all.101.recv_ref = f32[16,2,128]{2,1,0:T(2,128)S(1)} all-to-all(f32[16,2,128]{2,1,0:T(2,128)S(1)} %get-tuple-element.249), channel_id=1, replica_groups=mesh['row'=16,'col'=8] {'row'}, dimensions={0} | all-to-all | bytes 32768 | tf_op jit(solution)/shard_map/all_to_all | solution.py:306
  331.5 1.6 reflect.31
  333.1 3.7 all-to-all-start.15
  336.8 1.6 copy-done.3
  338.4 4.2 %rotate.1 = (bf16[256,512]{1,0:T(8,128)(2,1)S(1)}, f32[256,512]{1,0:T(8,128)S(1)}) custom-call(s32[2]{0:T(128)S(1)} %copy-done.4, bf16[256,4096]{1,0:T(8,128)(2,1)S(1)} %copy-done.3, bf16[16,3,32,4096]{3,2,1,0:T(8,128)(2,1)} %bitcast.35, f32[8,128]{1,0:T(8,128)S(1)} %get-tuple-element.253.marks_ref, ...), custom_call_target="tpu_custom_call" | custom-call | tf_op jit(solution)/shard_map/rotate/pallas_call | solution.py:320
  343.4 2.3 copy-done.2
  345.6 1.6 reflect.32
  347.2 5.8 %all-to-all-start.16 = ((f32[16,2,128]{2,1,0:T(2,128)}), f32[16,2,128]{2,1,0:T(2,128)S(1)}, u32[]{:S(2)}, u32[]{:S(2)}) async-start(f32[16,2,128]{2,1,0:T(2,128)} %get-tuple-element.260), calls=%async_computation.17 | async-start | bytes 32768 | tf_op jit(solution)/shard_map/all_to_all | solution.py:306
  353.5 2.0 reshape.35
  355.6 3.3 all-to-all-done.16.recv_ref
  358.8 1.6 update.1
  (36 shorter events, 9.0 us)
Async XLA Ops:
  7.2 79.1 %all-gather.6.cloned.1.call-start = ((), (), s32[]{:S(2)}) async-start(), calls=%async_computation.21 | async-start | bytes 13369344 | tf_op jit(solution)/shard_map/all_gather | solution.py:225
  10.6 200.2 %all-reduce.2.cloned.1.call-start = ((), (), s32[]{:S(2)}) async-start(), calls=%async_computation.19 | async-start | bytes 8388608 | tf_op jit(solution)/shard_map/psum | solution.py:266
  96.5 14.1 %all-to-all-start.1 = ((f32[8,16,512]{2,1,0:T(8,128)}), f32[8,16,512]{2,1,0:T(8,128)S(1)}, u32[]{:S(2)}, u32[]{:S(2)}) async-start(f32[8,16,512]{2,1,0:T(8,128)} %get-tuple-element.194), calls=%async_computation.1 | async-start | bytes 524288 | tf_op jit(solution)/shard_map/all_to_all | solution.py:267
  111.3 20.2 %all-to-all-start.2 = ((f32[8,16,512]{2,1,0:T(8,128)}), f32[8,16,512]{2,1,0:T(8,128)S(1)}, u32[]{:S(2)}, u32[]{:S(2)}) async-start(f32[8,16,512]{2,1,0:T(8,128)} %broadcast_in_dim.14), calls=%async_computation.2 | async-start | bytes 524288 | tf_op jit(solution)/shard_map/all_to_all | solution.py:269
  115.1 221.7 %all-gather.4.cloned.1.call-start = ((), (), s32[]{:S(2)}) async-start(), calls=%async_computation.18 | async-start | bytes 2359296 | tf_op jit(solution)/shard_map/all_gather | solution.py:316
  135.9 29.5 %all-to-all-start = ((f32[128,2,128]{2,1,0:T(2,128)}), f32[128,2,128]{2,1,0:T(2,128)S(1)}, u32[]{:S(2)}, u32[]{:S(2)}) async-start(f32[128,2,128]{2,1,0:T(2,128)} %get-tuple-element.344), calls=%async_computation | async-start | bytes 262144 | tf_op jit(solution)/shard_map/while/body/eval_jaxpr/all_to_all | solution.py:302
  169.5 16.3 %all-to-all-start = ((f32[128,2,128]{2,1,0:T(2,128)}), f32[128,2,128]{2,1,0:T(2,128)S(1)}, u32[]{:S(2)}, u32[]{:S(2)}) async-start(f32[128,2,128]{2,1,0:T(2,128)} %get-tuple-element.344), calls=%async_computation | async-start | bytes 262144 | tf_op jit(solution)/shard_map/while/body/eval_jaxpr/all_to_all | solution.py:302
  185.8 167.7 %reduce-scatter.2.cloned.1.call-start = ((), (), s32[]{:S(2)}) async-start(), calls=%async_computation.20 | async-start | bytes 4718592 | tf_op jit(solution)/shard_map/reduce_scatter | solution.py:317
  210.8 2.2 copy-start
  213.0 12.0 %copy-start.1 = (f32[8,256,512]{2,1,0:T(8,128)S(1)}, f32[8,256,512]{2,1,0:T(8,128)}, u32[]{:S(2)}) copy-start(f32[8,256,512]{2,1,0:T(8,128)} %all-reduce.2.cloned.1.call-done.matrix_ref.block_ref) | copy-start | bytes 12582916
  321.8 15.0 %copy-start.4 = (s32[2]{0:T(128)S(1)}, s32[2]{0:T(128)}, u32[]{:S(2)}) copy-start(s32[2]{0:T(128)} %pad_add_fusion.where_ref) | copy-start | bytes 28
  333.1 10.3 %all-to-all-start.15 = ((f32[16,2,128]{2,1,0:T(2,128)}), f32[16,2,128]{2,1,0:T(2,128)S(1)}, u32[]{:S(2)}, u32[]{:S(2)}) async-start(f32[16,2,128]{2,1,0:T(2,128)} %get-tuple-element.257), calls=%async_computation.16 | async-start | bytes 32768 | tf_op jit(solution)/shard_map/all_to_all | solution.py:306
  336.8 1.6 copy-start.3
  343.4 2.3 copy-start.2
  347.2 11.6 %all-to-all-start.16 = ((f32[16,2,128]{2,1,0:T(2,128)}), f32[16,2,128]{2,1,0:T(2,128)S(1)}, u32[]{:S(2)}, u32[]{:S(2)}) async-start(f32[16,2,128]{2,1,0:T(2,128)} %get-tuple-element.260), calls=%async_computation.17 | async-start | bytes 32768 | tf_op jit(solution)/shard_map/all_to_all | solution.py:306
Sparse Core Ops, SparseCore 0:
  10.7 75.4 all-gather.5
  96.6 114.0 all-reduce.1
  213.1 51.8 all-gather.3
  268.7 82.4 reduce-scatter.1
